TPU v7x, 128 devices: a whole 4x4x4 slice. The times are simulated.
128 devices in a mesh: tm: 8 (over x, core), space: 16 (over z, y).
Axes of the slice: x: 4, y: 4, z: 4, core: 2. Of those that a mesh axis runs over, the one named last changes fastest.
Arguments:
- speed: float32 [32, 16, 128], P('space'), may hold values from 0.5 to 1.5
- forcing: float32 [32, 32, 16, 128], P('tm', 'space'), may hold values from -1.8 to 1.8
- guess: float32 [8, 4, 32, 16, 128], P('tm', None, 'space'), may hold values from -8 to 8
- basis: float32 [8, 64, 4, 32, 16, 128], P('tm', None, None, 'space'), may hold values from -1 to 1, as said below
Outputs:
- states: float32 [32, 4, 32, 16, 128], P('tm', None, 'space')
- coords: float32 [8, 64], P('tm')
Inputs may be any that keep to these rules, and one draw needn't show every extreme that they name: The columns of each basis[k] are linearly independent.
All inputs are finite; a program needn't handle non-finite values.
Results may differ from a plain program's by a relative error of at most 0.00018.
Values sent between devices are 32-bit elements; how exact they have to be, the bound alone decides.
No kernel may reach another device: no remote copies, remote signals or barrier semaphores. Data moves between devices by JAX's collectives and lax.ppermute only.
A program may use at most 128 MiB of HBM per device.

v0:
```python
import jax
import jax.numpy as jnp
from jax import lax
from jax.sharding import PartitionSpec as P

DT = 0.045
exact_mode = lax.Precision.HIGHEST


def from_behind(value, axis, by):
    size = lax.axis_size(axis)
    pairs = [(i, i + by) for i in range(size) if 0 <= i + by < size]
    return lax.ppermute(value, axis, pairs)


def from_behind_2(value, axis, steps):
    count = lax.axis_size(axis)
    pairs = [(source, (source + steps) % count) for source in range(count)]
    return lax.ppermute(value, axis, pairs)


def sent_to_all(value, axis):
    size = lax.axis_size(axis)
    return lax.all_to_all(
        jnp.broadcast_to(value[None], (size, *value.shape)), axis, 0, 0, tiled=True
    )


def taken_together(value, axis):
    everything = sent_to_all(value, axis)
    return jnp.sum(everything, axis=0)


def shifted_ahead(values, axis):
    size = values.shape[axis]
    rest = lax.slice_in_dim(values, 1, size, axis=axis)
    border = jnp.zeros_like(lax.slice_in_dim(values, 0, 1, axis=axis))
    return jnp.concatenate([rest, border], axis=axis)


def shifted_behind(values, axis):
    size = values.shape[axis]
    rest = lax.slice_in_dim(values, 0, size - 1, axis=axis)
    border = jnp.zeros_like(lax.slice_in_dim(values, 0, 1, axis=axis))
    return jnp.concatenate([border, rest], axis=axis)


def update_flow(state, upper_plane, delta_time):
    pressure = state[..., 0, :, :, :]
    depth = pressure.ndim
    above = jnp.concatenate([pressure[..., 1:, :, :], upper_plane], axis=depth - 3)
    flow_x = state[..., 1, :, :, :] - delta_time * (shifted_ahead(pressure, depth - 2) - pressure)
    flow_y = state[..., 2, :, :, :] - delta_time * (shifted_ahead(pressure, depth - 1) - pressure)
    flow_z = state[..., 3, :, :, :] - delta_time * (above - pressure)
    return (pressure, flow_x, flow_y, flow_z)


def update_pressure(pressure, flow_x, flow_y, flow_z, lower_plane, speed_sq, delta_time):
    depth = pressure.ndim
    below = jnp.concatenate([lower_plane, flow_z[..., :-1, :, :]], axis=depth - 3)
    diverge = (
        flow_x
        - shifted_behind(flow_x, depth - 2)
        + (flow_y - shifted_behind(flow_y, depth - 1))
        + (flow_z - below)
    )
    fresh = pressure - delta_time * speed_sq * diverge
    return jnp.stack([fresh, flow_x, flow_y, flow_z], axis=depth - 3)


def advance_field(state, speed_sq, delta_time, bottom_index):
    upper = from_behind(state[0, :1], "space", -1)
    pressure, flow_x, flow_y, flow_z = update_flow(state, upper, delta_time)
    paired = from_behind(jnp.stack([pressure[-1:], state[3, -1:]], axis=0), "space", 1)
    ghost = paired[1] - delta_time * (pressure[:1] - paired[0])
    lower = jnp.where(bottom_index == 0, jnp.zeros_like(ghost), ghost)
    return update_pressure(pressure, flow_x, flow_y, flow_z, lower, speed_sq, delta_time)


def advance_basis(state, speed_sq, delta_time, bottom_index):
    upper = from_behind(state[:, 0, :1], "space", -1)
    pressure, flow_x, flow_y, flow_z = update_flow(state, upper, delta_time)
    paired = from_behind(jnp.stack([pressure[:, -1:], state[:, 3, -1:]], axis=0), "space", 1)
    ghost = paired[1] - delta_time * (pressure[:, :1] - paired[0])
    lower = jnp.where(bottom_index == 0, jnp.zeros_like(ghost), ghost)
    return update_pressure(pressure, flow_x, flow_y, flow_z, lower, speed_sq, delta_time)


def solve_gram(chol, coef):
    lifted = lax.linalg.triangular_solve(chol, coef[..., None], left_side=True, lower=True)
    solved = lax.linalg.triangular_solve(chol, lifted, left_side=True, lower=True, transpose_a=True)
    return solved[..., 0]


def body(speed, forcing, guess, basis):
    bottom_index = lax.axis_index("space")
    speed_sq = speed * speed

    def fine_step(state, row_index):
        moved = advance_field(state, speed_sq, DT, bottom_index)
        return moved.at[0].add(forcing[row_index])

    def sweep(left):
        points = []
        current = left
        for row_index in range(3):
            current = fine_step(current, row_index)
            points.append(current)
        return points

    left = from_behind_2(guess[0], "tm", 1)
    first_points = sweep(left)
    relaxed = fine_step(first_points[-1], 3)
    left = from_behind_2(relaxed, "tm", 1)
    second_points = sweep(left)
    residue = fine_step(second_points[-1], 3) - relaxed
    columns = basis[0]
    moved_columns = columns
    for repeat in range(4):
        moved_columns = advance_basis(moved_columns, speed_sq, DT, bottom_index)
    coarse_columns = advance_basis(columns, speed_sq, 4 * DT, bottom_index)
    corrections = (moved_columns - coarse_columns).reshape(columns.shape[0], -1)
    flat_basis = columns.reshape(columns.shape[0], -1)
    gram = taken_together(jnp.dot(flat_basis, flat_basis.T, precision=exact_mode), "space")
    chol = jnp.linalg.cholesky(gram)

    def candidate(levels):
        left_value = from_behind_2(levels, "tm", 1)
        moved = advance_field(left_value, speed_sq, 4 * DT, bottom_index)
        partial_value = jnp.dot(flat_basis, left_value.reshape(-1), precision=exact_mode)
        coef = taken_together(partial_value, "space")
        weights = solve_gram(chol, coef)
        extra = jnp.dot(weights, corrections, precision=exact_mode).reshape(left_value.shape)
        return moved + extra + residue

    levels = candidate(residue)
    levels = candidate(levels)
    gap = candidate(levels) - levels
    total = gap
    total = (
        advance_field(
            advance_field(from_behind(total, "tm", 4), speed_sq, 8 * DT, bottom_index),
            speed_sq,
            8 * DT,
            bottom_index,
        )
        + gap
    )
    levels = candidate(levels + total)
    final_c = relaxed + levels
    left = from_behind_2(final_c, "tm", 1)
    third_points = sweep(left)
    states = jnp.stack(third_points + [final_c], axis=0)
    partial_value = jnp.dot(flat_basis, final_c.reshape(-1), precision=exact_mode)
    coef = taken_together(partial_value, "space")
    coords = solve_gram(chol, coef)[None, :]
    return (states, coords)


def solution(mesh):
    placed = (
        P("space", None, None),
        P("tm", "space", None, None),
        P("tm", None, "space", None, None),
        P("tm", None, None, "space", None, None),
    )
    return jax.shard_map(
        body,
        mesh=mesh,
        in_specs=placed,
        out_specs=(P("tm", None, "space", None, None), P("tm", None)),
        check_vma=False,
    )
```

profile of v0, /device:TPU:38, one launch (start us, length us, event | category | flops | bytes accessed | tf_op | source)
XLA Modules:
  0.0 460.0 jit_solution(17763336401703002379)
XLA Ops:
  0.7 3.9 collective-permute-done
  4.5 4.5 collective-permute-start.1
  11.1 5.8 %collective-permute-done.2 = f32[2,1,16,128]{3,2,1,0:T(8,128)S(1)} collective-permute-done((f32[2,1,16,128]{3,2,1,0:T(8,128)S(1)}, f32[2,1,16,128]{3,2,1,0:T(8,128)S(1)}, u32[]{:S(2)}, u32[]{:S(2)}) %collective-permute-start.2) | collective-permute-done | bytes 16416 | tf_op jit(solution)/shard_map/ppermute | solution.py:13
  19.7 3.5 collective-permute-done.3
  25.2 5.8 %collective-permute-done.4 = f32[2,1,16,128]{3,2,1,0:T(8,128)S(1)} collective-permute-done((f32[2,1,16,128]{3,2,1,0:T(8,128)S(1)}, f32[2,1,16,128]{3,2,1,0:T(8,128)S(1)}, u32[]{:S(2)}, u32[]{:S(2)}) %collective-permute-start.4) | collective-permute-done | bytes 16416 | tf_op jit(solution)/shard_map/ppermute | solution.py:13
  33.8 3.5 collective-permute-done.5
  39.4 5.8 %collective-permute-done.6 = f32[2,1,16,128]{3,2,1,0:T(8,128)S(1)} collective-permute-done((f32[2,1,16,128]{3,2,1,0:T(8,128)S(1)}, f32[2,1,16,128]{3,2,1,0:T(8,128)S(1)}, u32[]{:S(2)}, u32[]{:S(2)}) %collective-permute-start.6) | collective-permute-done | bytes 16416 | tf_op jit(solution)/shard_map/ppermute | solution.py:13
  48.0 3.5 collective-permute-done.7
  53.5 5.8 %collective-permute-done.8 = f32[2,1,16,128]{3,2,1,0:T(8,128)S(1)} collective-permute-done((f32[2,1,16,128]{3,2,1,0:T(8,128)S(1)}, f32[2,1,16,128]{3,2,1,0:T(8,128)S(1)}, u32[]{:S(2)}, u32[]{:S(2)}) %collective-permute-start.8) | collective-permute-done | bytes 16416 | tf_op jit(solution)/shard_map/ppermute | solution.py:13
  60.8 3.7 collective-permute-done.9
  66.6 3.9 collective-permute-start.11
  70.5 3.8 collective-permute-done.11
  77.1 3.5 collective-permute-done.12
  82.6 5.8 %collective-permute-done.13 = f32[2,1,16,128]{3,2,1,0:T(8,128)S(1)} collective-permute-done((f32[2,1,16,128]{3,2,1,0:T(8,128)S(1)}, f32[2,1,16,128]{3,2,1,0:T(8,128)S(1)}, u32[]{:S(2)}, u32[]{:S(2)}) %collective-permute-start.13) | collective-permute-done | bytes 16416 | tf_op jit(solution)/shard_map/ppermute | solution.py:13
  98.3 4.3 collective-permute-done.15
  104.8 3.5 collective-permute-done.16
  110.2 5.8 %collective-permute-done.17 = f32[2,1,16,128]{3,2,1,0:T(8,128)S(1)} collective-permute-done((f32[2,1,16,128]{3,2,1,0:T(8,128)S(1)}, f32[2,1,16,128]{3,2,1,0:T(8,128)S(1)}, u32[]{:S(2)}, u32[]{:S(2)}) %collective-permute-start.17) | collective-permute-done | bytes 16416 | tf_op jit(solution)/shard_map/ppermute | solution.py:13
  118.2 6.0 %collective-permute-start.21 = (f32[64,1,16,128]{3,2,0,1:T(8,128)S(1)}, f32[64,1,16,128]{3,2,0,1:T(8,128)S(1)}, u32[]{:S(2)}, u32[]{:S(2)}) collective-permute-start(f32[64,1,16,128]{3,2,0,1:T(8,128)S(1)} %get-tuple-element.159), channel_id=1, source_target_pairs={{1,0},{2,1},{3,2},{4,3},{5,4},{6,5},{7,6},{8,7},{9,8},{10,9},{11,1... | collective-permute-start | bytes 1572872 | tf_op jit(solution)/shard_map/ppermute | solution.py:13
  126.6 3.9 collective-permute-start.20
  130.6 4.4 collective-permute-done.19
  135.1 9.6 %collective-permute-done.20 = f32[2,1,16,128]{3,2,1,0:T(8,128)S(1)} collective-permute-done((f32[2,1,16,128]{3,2,1,0:T(8,128)S(1)}, f32[2,1,16,128]{3,2,1,0:T(8,128)S(1)}, u32[]{:S(2)}, u32[]{:S(2)}) %collective-permute-start.20) | collective-permute-done | bytes 16416 | tf_op jit(solution)/shard_map/ppermute | solution.py:13
  151.9 6.0 %collective-permute-start.23 = (f32[64,1,16,128]{3,2,0,1:T(8,128)S(1)}, f32[64,1,16,128]{3,2,0,1:T(8,128)S(1)}, u32[]{:S(2)}, u32[]{:S(2)}) collective-permute-start(f32[64,1,16,128]{3,2,0,1:T(8,128)S(1)} %slice_bitcast_fusion.10), channel_id=1, source_target_pairs={{1,0},{2,1},{3,2},{4,3},{5,4},{6,5},{7,6},{8,7},{9,8},{10,9},{11,1... | collective-permute-start | bytes 1572872 | tf_op jit(solution)/shard_map/ppermute | solution.py:13
  158.4 20.7 %collective-permute-done.24 = f32[2,64,1,16,128]{4,3,1,2,0:T(8,128)S(1)} collective-permute-done((f32[2,64,1,16,128]{4,3,1,2,0:T(8,128)S(1)}, f32[2,64,1,16,128]{4,3,1,2,0:T(8,128)S(1)}, u32[]{:S(2)}, u32[]{:S(2)}) %collective-permute-start.24) | collective-permute-done | bytes 1048608 | tf_op jit(solution)/shard_map/ppermute | solution.py:13
  184.3 8.2 %fusion.10 = f32[64,64]{1,0:T(8,128)S(1)} fusion(f32[64,4,2,16,128]{4,3,2,1,0:T(8,128)S(1)} %bitcast.1043), kind=kOutput, calls=%fused_computation.12 | convolution fusion | flops 805306368 | bytes 4210688 | tf_op jit(solution)/shard_map/dot_general | solution.py:124
  193.6 9.3 %all-to-all-start = ((f32[16,1,4096]{2,1,0:T(1,128)}), f32[16,1,4096]{2,1,0:T(1,128)S(1)}, u32[]{:S(2)}, u32[]{:S(2)}) async-start(f32[16,1,4096]{2,1,0:T(1,128)} %reshape.1304), calls=%async_computation | async-start | bytes 524288 | tf_op jit(solution)/shard_map/all_to_all | solution.py:24
  202.9 5.0 %reshape_squeeze.3 = f32[64,16384]{1,0:T(8,128)} reshape(f32[1,64,4,2,16,128]{5,4,3,2,1,0:T(8,128)} %param.33) | data formatting | bytes 8388608 | tf_op jit(solution)/shard_map/reshape;squeeze | solution.py:123
  207.8 9.5 %all-to-all-done = f32[16,1,4096]{2,1,0:T(1,128)S(1)} async-done(((f32[16,1,4096]{2,1,0:T(1,128)}), f32[16,1,4096]{2,1,0:T(1,128)S(1)}, u32[]{:S(2)}, u32[]{:S(2)}) %all-to-all-start) | async-done | bytes 262176 | tf_op jit(solution)/shard_map/all_to_all | solution.py:24
  222.3 6.6 %cholesky.18 = f32[64,64]{1,0:T(8,128)S(1)} custom-call(f32[64,64]{1,0:T(8,128)} %fusion.69), custom_call_target="Cholesky" | custom-call | tf_op jit(solution)/shard_map/jit(cholesky)/cholesky | solution.py:125
  242.2 3.3 convolution_bitcast_fusion.13
  246.2 7.2 %all-to-all-start.1 = ((f32[16,1,64]{2,1,0:T(1,128)}), f32[16,1,64]{2,1,0:T(1,128)S(1)}, u32[]{:S(2)}, u32[]{:S(2)}) async-start(f32[16,1,64]{2,1,0:T(1,128)} %broadcast_in_dim.25), calls=%async_computation.1 | async-start | bytes 16384 | tf_op jit(solution)/shard_map/all_to_all | solution.py:24
  254.0 4.9 %custom-call.18 = f32[1,64,64]{1,2,0:T(8,128)S(1)} custom-call(f32[1,64,64]{2,1,0:T(8,128)S(1)} %fusion.57), custom_call_target="InvertDiagBlocksLowerTriangular" | custom-call | tf_op jit(solution)/shard_map/triangular_solve/custom-call.2 | solution.py:91
  258.9 9.3 %all-to-all-done.1 = f32[16,1,64]{2,1,0:T(1,128)S(1)} async-done(((f32[16,1,64]{2,1,0:T(1,128)}), f32[16,1,64]{2,1,0:T(1,128)S(1)}, u32[]{:S(2)}, u32[]{:S(2)}) %all-to-all-start.1) | async-done | bytes 4128 | tf_op jit(solution)/shard_map/all_to_all | solution.py:24
  268.3 4.1 collective-permute-start.27
  274.5 7.4 %collective-permute-done.27 = f32[64,1,16,128]{3,2,0,1:T(8,128)S(1)} collective-permute-done((f32[64,1,16,128]{3,2,0,1:T(8,128)S(1)}, f32[64,1,16,128]{3,2,0,1:T(8,128)S(1)}, u32[]{:S(2)}, u32[]{:S(2)}) %collective-permute-start.27) | collective-permute-done | bytes 524320 | tf_op jit(solution)/shard_map/ppermute | solution.py:13
  289.5 4.3 fusion.8
  293.9 3.7 collective-permute-done.29
  297.6 3.3 convolution_bitcast_fusion.12
  301.5 6.8 %all-to-all-start.2 = ((f32[16,1,64]{2,1,0:T(1,128)}), f32[16,1,64]{2,1,0:T(1,128)S(1)}, u32[]{:S(2)}, u32[]{:S(2)}) async-start(f32[16,1,64]{2,1,0:T(1,128)} %broadcast_in_dim.27), calls=%async_computation.2 | async-start | bytes 16384 | tf_op jit(solution)/shard_map/all_to_all | solution.py:24
  308.3 3.4 collective-permute-start.31
  311.7 4.8 %collective-permute-start.30 = (f32[1,16,128]{2,1,0:T(8,128)S(1)}, f32[1,16,128]{2,1,0:T(8,128)S(1)}, u32[]{:S(2)}, u32[]{:S(2)}) collective-permute-start(f32[1,16,128]{2,1,0:T(8,128)S(1)} %get-tuple-element.237), channel_id=1, source_target_pairs={{1,0},{2,1},{3,2},{4,3},{5,4},{6,5},{7,6},{8,7},{9,8},{10,9},{11,1... | collective-permute-start | bytes 24584 | tf_op jit(solution)/shard_map/ppermute | solution.py:13
  316.8 6.6 %fusion.6 = f32[1,4,2,16,128]{4,0,3,2,1:T(1,128)S(1)} fusion(f32[64,1,1,1,1]{0,1,4,3,2:T(1,128)S(1)} %convolution_bitcast_fusion.5, f32[4,2,16,128,64]{3,2,1,0,4:T(8,128)} %bitcast.1035), kind=kOutput, calls=%fused_computation.8 | convolution fusion | flops 12582912 | bytes 4260096 | tf_op jit(solution)/shard_map/dot_general | solution.py:133
  323.7 3.7 collective-permute-done.32
  331.3 5.1 %all-to-all-start.3 = ((f32[16,1,64]{2,1,0:T(1,128)}), f32[16,1,64]{2,1,0:T(1,128)S(1)}, u32[]{:S(2)}, u32[]{:S(2)}) async-start(f32[16,1,64]{2,1,0:T(1,128)} %broadcast_in_dim.29), calls=%async_computation.3 | async-start | bytes 16384 | tf_op jit(solution)/shard_map/all_to_all | solution.py:24
  336.5 3.4 collective-permute-start.34
  339.8 4.8 %collective-permute-start.33 = (f32[1,16,128]{2,1,0:T(8,128)S(1)}, f32[1,16,128]{2,1,0:T(8,128)S(1)}, u32[]{:S(2)}, u32[]{:S(2)}) collective-permute-start(f32[1,16,128]{2,1,0:T(8,128)S(1)} %get-tuple-element.228), channel_id=1, source_target_pairs={{1,0},{2,1},{3,2},{4,3},{5,4},{6,5},{7,6},{8,7},{9,8},{10,9},{11,1... | collective-permute-start | bytes 24584 | tf_op jit(solution)/shard_map/ppermute | solution.py:13
  345.0 6.6 %fusion.4 = f32[1,4,2,16,128]{4,0,3,2,1:T(1,128)S(1)} fusion(f32[64,1,1,1,1]{0,1,4,3,2:T(1,128)S(1)} %convolution_bitcast_fusion.3, f32[4,2,16,128,64]{3,2,1,0,4:T(8,128)} %bitcast.1036), kind=kOutput, calls=%fused_computation.6 | convolution fusion | flops 12582912 | bytes 4260096 | tf_op jit(solution)/shard_map/dot_general | solution.py:133
  353.2 6.4 %collective-permute-done.35 = f32[4,2,16,128]{3,2,1,0:T(8,128)S(1)} collective-permute-done((f32[4,2,16,128]{3,2,1,0:T(8,128)S(1)}, f32[4,2,16,128]{3,2,1,0:T(8,128)S(1)}, u32[]{:S(2)}, u32[]{:S(2)}) %collective-permute-start.35) | collective-permute-done | bytes 65568 | tf_op jit(solution)/shard_map/ppermute | solution.py:13
  362.1 3.4 collective-permute-start.37
  365.5 4.3 collective-permute-done.37
  372.0 6.0 %collective-permute-start.38 = (f32[1,16,128]{2,1,0:T(8,128)S(1)}, f32[1,16,128]{2,1,0:T(8,128)S(1)}, u32[]{:S(2)}, u32[]{:S(2)}) collective-permute-start(f32[1,16,128]{2,1,0:T(8,128)S(1)} %slice_bitcast_fusion.56), channel_id=1, source_target_pairs={{1,0},{2,1},{3,2},{4,3},{5,4},{6,5},{7,6},{8,7},{9,8},{10,9},{11,1... | collective-permute-start | bytes 24584 | tf_op jit(solution)/shard_map/ppermute | solution.py:13
  379.5 3.7 collective-permute-done.40
  387.1 8.7 %all-to-all-start.4 = ((f32[16,1,64]{2,1,0:T(1,128)}), f32[16,1,64]{2,1,0:T(1,128)S(1)}, u32[]{:S(2)}, u32[]{:S(2)}) async-start(f32[16,1,64]{2,1,0:T(1,128)} %broadcast_in_dim.31), calls=%async_computation.4 | async-start | bytes 16384 | tf_op jit(solution)/shard_map/all_to_all | solution.py:24
  395.8 3.4 collective-permute-start.42
  399.2 4.8 %collective-permute-start.41 = (f32[1,16,128]{2,1,0:T(8,128)S(1)}, f32[1,16,128]{2,1,0:T(8,128)S(1)}, u32[]{:S(2)}, u32[]{:S(2)}) collective-permute-start(f32[1,16,128]{2,1,0:T(8,128)S(1)} %get-tuple-element.209), channel_id=1, source_target_pairs={{1,0},{2,1},{3,2},{4,3},{5,4},{6,5},{7,6},{8,7},{9,8},{10,9},{11,1... | collective-permute-start | bytes 24584 | tf_op jit(solution)/shard_map/ppermute | solution.py:13
  404.4 6.6 %fusion.2 = f32[1,4,2,16,128]{4,0,3,2,1:T(1,128)S(1)} fusion(f32[64,1,1,1,1]{0,1,4,3,2:T(1,128)S(1)} %convolution_bitcast_fusion.1, f32[4,2,16,128,64]{3,2,1,0,4:T(8,128)} %bitcast.1037), kind=kOutput, calls=%fused_computation.4 | convolution fusion | flops 12582912 | bytes 4260096 | tf_op jit(solution)/shard_map/dot_general | solution.py:133
  411.2 3.3 convolution_bitcast_fusion.9
  415.2 5.1 %all-to-all-start.5 = ((f32[16,1,64]{2,1,0:T(1,128)}), f32[16,1,64]{2,1,0:T(1,128)S(1)}, u32[]{:S(2)}, u32[]{:S(2)}) async-start(f32[16,1,64]{2,1,0:T(1,128)} %broadcast_in_dim.33), calls=%async_computation.5 | async-start | bytes 16384 | tf_op jit(solution)/shard_map/all_to_all | solution.py:24
  420.3 6.1 %all-to-all-done.5 = f32[16,1,64]{2,1,0:T(1,128)S(1)} async-done(((f32[16,1,64]{2,1,0:T(1,128)}), f32[16,1,64]{2,1,0:T(1,128)S(1)}, u32[]{:S(2)}, u32[]{:S(2)}) %all-to-all-start.5) | async-done | bytes 4128 | tf_op jit(solution)/shard_map/all_to_all | solution.py:24
  427.3 4.0 collective-permute-start.44
  433.4 5.7 %collective-permute-done.45 = f32[2,1,16,128]{3,2,1,0:T(8,128)S(1)} collective-permute-done((f32[2,1,16,128]{3,2,1,0:T(8,128)S(1)}, f32[2,1,16,128]{3,2,1,0:T(8,128)S(1)}, u32[]{:S(2)}, u32[]{:S(2)}) %collective-permute-start.45) | collective-permute-done | bytes 16416 | tf_op jit(solution)/shard_map/ppermute | solution.py:13
  441.2 3.9 collective-permute-start.47
  445.2 3.8 collective-permute-done.47
  451.1 3.9 collective-permute-start.49
  455.1 3.8 collective-permute-done.49
  (360 shorter events, 112.2 us)
Async XLA Ops:
  0.6 3.9 collective-permute-start
  4.5 6.5 %collective-permute-start.1 = (f32[1,16,128]{2,1,0:T(8,128)S(1)}, f32[1,16,128]{2,1,0:T(8,128)S(1)}, u32[]{:S(2)}, u32[]{:S(2)}) collective-permute-start(f32[1,16,128]{2,1,0:T(8,128)S(1)} %get-tuple-element.266), channel_id=1, source_target_pairs={{1,0},{2,1},{3,2},{4,3},{5,4},{6,5},{7,6},{8,7},{9,8},{10,9},{11,1... | collective-permute-start | bytes 24584 | tf_op jit(solution)/shard_map/ppermute | solution.py:13
  9.1 7.7 %collective-permute-start.2 = (f32[2,1,16,128]{3,2,1,0:T(8,128)S(1)}, f32[2,1,16,128]{3,2,1,0:T(8,128)S(1)}, u32[]{:S(2)}, u32[]{:S(2)}) collective-permute-start(f32[2,1,16,128]{3,2,1,0:T(8,128)S(1)} %pad_maximum_fusion.9), channel_id=1, source_target_pairs={{0,1},{1,2},{2,3},{3,4},{4,5},{5,6},{6,7},{7,8},{8,9},{9,10},{10,1... | collective-permute-start | bytes 49160 | tf_op jit(solution)/shard_map/ppermute | solution.py:13
  17.7 5.5 %collective-permute-start.3 = (f32[1,16,128]{2,1,0:T(8,128)S(1)}, f32[1,16,128]{2,1,0:T(8,128)S(1)}, u32[]{:S(2)}, u32[]{:S(2)}) collective-permute-start(f32[1,16,128]{2,1,0:T(8,128)S(1)} %get-tuple-element.322), channel_id=1, source_target_pairs={{1,0},{2,1},{3,2},{4,3},{5,4},{6,5},{7,6},{8,7},{9,8},{10,9},{11,1... | collective-permute-start | bytes 24584 | tf_op jit(solution)/shard_map/ppermute | solution.py:13
  23.3 7.7 %collective-permute-start.4 = (f32[2,1,16,128]{3,2,1,0:T(8,128)S(1)}, f32[2,1,16,128]{3,2,1,0:T(8,128)S(1)}, u32[]{:S(2)}, u32[]{:S(2)}) collective-permute-start(f32[2,1,16,128]{3,2,1,0:T(8,128)S(1)} %pad_maximum_fusion.10), channel_id=1, source_target_pairs={{0,1},{1,2},{2,3},{3,4},{4,5},{5,6},{6,7},{7,8},{8,9},{9,10},{10,1... | collective-permute-start | bytes 49160 | tf_op jit(solution)/shard_map/ppermute | solution.py:13
  31.8 5.5 %collective-permute-start.5 = (f32[1,16,128]{2,1,0:T(8,128)S(1)}, f32[1,16,128]{2,1,0:T(8,128)S(1)}, u32[]{:S(2)}, u32[]{:S(2)}) collective-permute-start(f32[1,16,128]{2,1,0:T(8,128)S(1)} %get-tuple-element.315), channel_id=1, source_target_pairs={{1,0},{2,1},{3,2},{4,3},{5,4},{6,5},{7,6},{8,7},{9,8},{10,9},{11,1... | collective-permute-start | bytes 24584 | tf_op jit(solution)/shard_map/ppermute | solution.py:13
  37.4 7.7 %collective-permute-start.6 = (f32[2,1,16,128]{3,2,1,0:T(8,128)S(1)}, f32[2,1,16,128]{3,2,1,0:T(8,128)S(1)}, u32[]{:S(2)}, u32[]{:S(2)}) collective-permute-start(f32[2,1,16,128]{3,2,1,0:T(8,128)S(1)} %pad_maximum_fusion.11), channel_id=1, source_target_pairs={{0,1},{1,2},{2,3},{3,4},{4,5},{5,6},{6,7},{7,8},{8,9},{9,10},{10,1... | collective-permute-start | bytes 49160 | tf_op jit(solution)/shard_map/ppermute | solution.py:13
  46.0 5.5 %collective-permute-start.7 = (f32[1,16,128]{2,1,0:T(8,128)S(1)}, f32[1,16,128]{2,1,0:T(8,128)S(1)}, u32[]{:S(2)}, u32[]{:S(2)}) collective-permute-start(f32[1,16,128]{2,1,0:T(8,128)S(1)} %get-tuple-element.308), channel_id=1, source_target_pairs={{1,0},{2,1},{3,2},{4,3},{5,4},{6,5},{7,6},{8,7},{9,8},{10,9},{11,1... | collective-permute-start | bytes 24584 | tf_op jit(solution)/shard_map/ppermute | solution.py:13
  51.6 7.7 %collective-permute-start.8 = (f32[2,1,16,128]{3,2,1,0:T(8,128)S(1)}, f32[2,1,16,128]{3,2,1,0:T(8,128)S(1)}, u32[]{:S(2)}, u32[]{:S(2)}) collective-permute-start(f32[2,1,16,128]{3,2,1,0:T(8,128)S(1)} %pad_maximum_fusion.12), channel_id=1, source_target_pairs={{0,1},{1,2},{2,3},{3,4},{4,5},{5,6},{6,7},{7,8},{8,9},{9,10},{10,1... | collective-permute-start | bytes 49160 | tf_op jit(solution)/shard_map/ppermute | solution.py:13
  60.8 3.7 collective-permute-start.9
  64.5 5.9 %collective-permute-start.10 = (f32[1,16,128]{2,1,0:T(8,128)S(1)}, f32[1,16,128]{2,1,0:T(8,128)S(1)}, u32[]{:S(2)}, u32[]{:S(2)}) collective-permute-start(f32[1,16,128]{2,1,0:T(8,128)S(1)} %get-tuple-element.259), channel_id=1, source_target_pairs={{1,0},{2,1},{3,2},{4,3},{5,4},{6,5},{7,6},{8,7},{9,8},{10,9},{11,1... | collective-permute-start | bytes 24584 | tf_op jit(solution)/shard_map/ppermute | solution.py:13
  66.6 7.7 %collective-permute-start.11 = (f32[2,1,16,128]{3,2,1,0:T(8,128)S(1)}, f32[2,1,16,128]{3,2,1,0:T(8,128)S(1)}, u32[]{:S(2)}, u32[]{:S(2)}) collective-permute-start(f32[2,1,16,128]{3,2,1,0:T(8,128)S(1)} %pad_maximum_fusion.13), channel_id=1, source_target_pairs={{0,1},{1,2},{2,3},{3,4},{4,5},{5,6},{6,7},{7,8},{8,9},{9,10},{10,1... | collective-permute-start | bytes 49160 | tf_op jit(solution)/shard_map/ppermute | solution.py:13
  75.1 5.5 %collective-permute-start.12 = (f32[1,16,128]{2,1,0:T(8,128)S(1)}, f32[1,16,128]{2,1,0:T(8,128)S(1)}, u32[]{:S(2)}, u32[]{:S(2)}) collective-permute-start(f32[1,16,128]{2,1,0:T(8,128)S(1)} %get-tuple-element.301), channel_id=1, source_target_pairs={{1,0},{2,1},{3,2},{4,3},{5,4},{6,5},{7,6},{8,7},{9,8},{10,9},{11,1... | collective-permute-start | bytes 24584 | tf_op jit(solution)/shard_map/ppermute | solution.py:13
  80.7 7.7 %collective-permute-start.13 = (f32[2,1,16,128]{3,2,1,0:T(8,128)S(1)}, f32[2,1,16,128]{3,2,1,0:T(8,128)S(1)}, u32[]{:S(2)}, u32[]{:S(2)}) collective-permute-start(f32[2,1,16,128]{3,2,1,0:T(8,128)S(1)} %pad_maximum_fusion.14), channel_id=1, source_target_pairs={{0,1},{1,2},{2,3},{3,4},{4,5},{5,6},{6,7},{7,8},{8,9},{9,10},{10,1... | collective-permute-start | bytes 49160 | tf_op jit(solution)/shard_map/ppermute | solution.py:13
  89.3 5.5 %collective-permute-start.14 = (f32[1,16,128]{2,1,0:T(8,128)S(1)}, f32[1,16,128]{2,1,0:T(8,128)S(1)}, u32[]{:S(2)}, u32[]{:S(2)}) collective-permute-start(f32[1,16,128]{2,1,0:T(8,128)S(1)} %get-tuple-element.294), channel_id=1, source_target_pairs={{1,0},{2,1},{3,2},{4,3},{5,4},{6,5},{7,6},{8,7},{9,8},{10,9},{11,1... | collective-permute-start | bytes 24584 | tf_op jit(solution)/shard_map/ppermute | solution.py:13
  94.0 8.6 %copy-start.17 = (f32[2,16,128]{2,1,0:T(8,128)S(1)}, f32[2,16,128]{2,1,0:T(8,128)}, u32[]{:S(2)}) copy-start(f32[2,16,128]{2,1,0:T(8,128)} %param.30) | copy-start | bytes 49156
  94.0 8.6 %copy-start.21 = (f32[4,2,16,128]{3,2,1,0:T(8,128)S(1)}, f32[4,2,16,128]{3,2,1,0:T(8,128)}, u32[]{:S(2)}) copy-start(f32[4,2,16,128]{3,2,1,0:T(8,128)} %param.31) | copy-start | bytes 196612
  94.9 7.7 %collective-permute-start.15 = (f32[2,1,16,128]{3,2,1,0:T(8,128)S(1)}, f32[2,1,16,128]{3,2,1,0:T(8,128)S(1)}, u32[]{:S(2)}, u32[]{:S(2)}) collective-permute-start(f32[2,1,16,128]{3,2,1,0:T(8,128)S(1)} %pad_maximum_fusion.15), channel_id=1, source_target_pairs={{0,1},{1,2},{2,3},{3,4},{4,5},{5,6},{6,7},{7,8},{8,9},{9,10},{10,1... | collective-permute-start | bytes 49160 | tf_op jit(solution)/shard_map/ppermute | solution.py:13
  102.7 5.5 %collective-permute-start.16 = (f32[1,16,128]{2,1,0:T(8,128)S(1)}, f32[1,16,128]{2,1,0:T(8,128)S(1)}, u32[]{:S(2)}, u32[]{:S(2)}) collective-permute-start(f32[1,16,128]{2,1,0:T(8,128)S(1)} %get-tuple-element.287), channel_id=1, source_target_pairs={{1,0},{2,1},{3,2},{4,3},{5,4},{6,5},{7,6},{8,7},{9,8},{10,9},{11,1... | collective-permute-start | bytes 24584 | tf_op jit(solution)/shard_map/ppermute | solution.py:13
  108.3 7.7 %collective-permute-start.17 = (f32[2,1,16,128]{3,2,1,0:T(8,128)S(1)}, f32[2,1,16,128]{3,2,1,0:T(8,128)S(1)}, u32[]{:S(2)}, u32[]{:S(2)}) collective-permute-start(f32[2,1,16,128]{3,2,1,0:T(8,128)S(1)} %pad_maximum_fusion.16), channel_id=1, source_target_pairs={{0,1},{1,2},{2,3},{3,4},{4,5},{5,6},{6,7},{7,8},{8,9},{9,10},{10,1... | collective-permute-start | bytes 49160 | tf_op jit(solution)/shard_map/ppermute | solution.py:13
  116.2 8.5 %collective-permute-start.18 = (f32[4,2,16,128]{3,2,1,0:T(8,128)S(1)}, f32[4,2,16,128]{3,2,1,0:T(8,128)S(1)}, u32[]{:S(2)}, u32[]{:S(2)}) collective-permute-start(f32[4,2,16,128]{3,2,1,0:T(8,128)S(1)} %sub.1271), channel_id=1, source_target_pairs={{0,16},{16,32},{32,48},{48,64},{64,80},{80,96},{96,112},{112,0},{1... | collective-permute-start | bytes 196616 | tf_op jit(solution)/shard_map/ppermute | solution.py:19
  116.3 29.0 %collective-permute-start.22 = (f32[2,64,1,16,128]{4,3,1,2,0:T(8,128)S(1)}, f32[2,64,1,16,128]{4,3,1,2,0:T(8,128)S(1)}, u32[]{:S(2)}, u32[]{:S(2)}) collective-permute-start(f32[2,64,1,16,128]{4,3,1,2,0:T(8,128)S(1)} %pad_maximum_fusion), channel_id=1, source_target_pairs={{0,1},{1,2},{2,3},{3,4},{4,5},{5,6},{6,7},{7,8},{8,9},{9,10},{10,1... | collective-permute-start | bytes 3145736 | tf_op jit(solution)/shard_map/ppermute | solution.py:13
  118.2 27.3 %collective-permute-start.21 = (f32[64,1,16,128]{3,2,0,1:T(8,128)S(1)}, f32[64,1,16,128]{3,2,0,1:T(8,128)S(1)}, u32[]{:S(2)}, u32[]{:S(2)}) collective-permute-start(f32[64,1,16,128]{3,2,0,1:T(8,128)S(1)} %get-tuple-element.159), channel_id=1, source_target_pairs={{1,0},{2,1},{3,2},{4,3},{5,4},{6,5},{7,6},{8,7},{9,8},{10,9},{11,1... | collective-permute-start | bytes 1572872 | tf_op jit(solution)/shard_map/ppermute | solution.py:13
  124.7 10.3 %collective-permute-start.19 = (f32[1,16,128]{2,1,0:T(8,128)S(1)}, f32[1,16,128]{2,1,0:T(8,128)S(1)}, u32[]{:S(2)}, u32[]{:S(2)}) collective-permute-start(f32[1,16,128]{2,1,0:T(8,128)S(1)} %get-tuple-element.246), channel_id=1, source_target_pairs={{1,0},{2,1},{3,2},{4,3},{5,4},{6,5},{7,6},{8,7},{9,8},{10,9},{11,1... | collective-permute-start | bytes 24584 | tf_op jit(solution)/shard_map/ppermute | solution.py:13
  126.6 18.0 %collective-permute-start.20 = (f32[2,1,16,128]{3,2,1,0:T(8,128)S(1)}, f32[2,1,16,128]{3,2,1,0:T(8,128)S(1)}, u32[]{:S(2)}, u32[]{:S(2)}) collective-permute-start(f32[2,1,16,128]{3,2,1,0:T(8,128)S(1)} %pad_maximum_fusion.17), channel_id=1, source_target_pairs={{0,1},{1,2},{2,3},{3,4},{4,5},{5,6},{6,7},{7,8},{8,9},{9,10},{10,1... | collective-permute-start | bytes 49160 | tf_op jit(solution)/shard_map/ppermute | solution.py:13
  149.9 29.2 %collective-permute-start.24 = (f32[2,64,1,16,128]{4,3,1,2,0:T(8,128)S(1)}, f32[2,64,1,16,128]{4,3,1,2,0:T(8,128)S(1)}, u32[]{:S(2)}, u32[]{:S(2)}) collective-permute-start(f32[2,64,1,16,128]{4,3,1,2,0:T(8,128)S(1)} %pad_maximum_fusion.1), channel_id=1, source_target_pairs={{0,1},{1,2},{2,3},{3,4},{4,5},{5,6},{6,7},{7,8},{8,9},{9,10},{10,1... | collective-permute-start | bytes 3145736 | tf_op jit(solution)/shard_map/ppermute | solution.py:13
  151.9 27.3 %collective-permute-start.23 = (f32[64,1,16,128]{3,2,0,1:T(8,128)S(1)}, f32[64,1,16,128]{3,2,0,1:T(8,128)S(1)}, u32[]{:S(2)}, u32[]{:S(2)}) collective-permute-start(f32[64,1,16,128]{3,2,0,1:T(8,128)S(1)} %slice_bitcast_fusion.10), channel_id=1, source_target_pairs={{1,0},{2,1},{3,2},{4,3},{5,4},{6,5},{7,6},{8,7},{9,8},{10,9},{11,1... | collective-permute-start | bytes 1572872 | tf_op jit(solution)/shard_map/ppermute | solution.py:13
  182.2 47.8 %collective-permute-start.26 = (f32[2,64,1,16,128]{4,3,1,2,0:T(8,128)}, f32[2,64,1,16,128]{4,3,1,2,0:T(8,128)}, u32[]{:S(2)}, u32[]{:S(2)}) collective-permute-start(f32[2,64,1,16,128]{4,3,1,2,0:T(8,128)} %pad_maximum_fusion.2), channel_id=1, source_target_pairs={{0,1},{1,2},{2,3},{3,4},{4,5},{5,6},{6,7},{7,8},{8,9},{9,10},{10,1... | collective-permute-start | bytes 3145736 | tf_op jit(solution)/shard_map/ppermute | solution.py:13
  193.6 23.8 %all-to-all-start = ((f32[16,1,4096]{2,1,0:T(1,128)}), f32[16,1,4096]{2,1,0:T(1,128)S(1)}, u32[]{:S(2)}, u32[]{:S(2)}) async-start(f32[16,1,4096]{2,1,0:T(1,128)} %reshape.1304), calls=%async_computation | async-start | bytes 524288 | tf_op jit(solution)/shard_map/all_to_all | solution.py:24
  219.6 15.1 %collective-permute-start.25 = (f32[64,1,16,128]{3,2,0,1:T(8,128)S(1)}, f32[64,1,16,128]{3,2,0,1:T(8,128)S(1)}, u32[]{:S(2)}, u32[]{:S(2)}) collective-permute-start(f32[64,1,16,128]{3,2,0,1:T(8,128)S(1)} %slice_bitcast_fusion.7), channel_id=1, source_target_pairs={{1,0},{2,1},{3,2},{4,3},{5,4},{6,5},{7,6},{8,7},{9,8},{10,9},{11,1... | collective-permute-start | bytes 1572872 | tf_op jit(solution)/shard_map/ppermute | solution.py:13
  240.1 33.0 %collective-permute-start.28 = (f32[2,64,1,16,128]{4,3,1,2,0:T(8,128)}, f32[2,64,1,16,128]{4,3,1,2,0:T(8,128)}, u32[]{:S(2)}, u32[]{:S(2)}) collective-permute-start(f32[2,64,1,16,128]{4,3,1,2,0:T(8,128)} %pad_maximum_fusion.3), channel_id=1, source_target_pairs={{0,1},{1,2},{2,3},{3,4},{4,5},{5,6},{6,7},{7,8},{8,9},{9,10},{10,1... | collective-permute-start | bytes 3145736 | tf_op jit(solution)/shard_map/ppermute | solution.py:13
  246.2 22.1 %all-to-all-start.1 = ((f32[16,1,64]{2,1,0:T(1,128)}), f32[16,1,64]{2,1,0:T(1,128)S(1)}, u32[]{:S(2)}, u32[]{:S(2)}) async-start(f32[16,1,64]{2,1,0:T(1,128)} %broadcast_in_dim.25), calls=%async_computation.1 | async-start | bytes 16384 | tf_op jit(solution)/shard_map/all_to_all | solution.py:24
  268.2 13.7 %copy-start.10 = (f32[64,2,16,128]{3,2,0,1:T(8,128)S(1)}, f32[64,2,16,128]{3,2,0,1:T(8,128)}, u32[]{:S(2)}) copy-start(f32[64,2,16,128]{3,2,0,1:T(8,128)} %copy-done.9) | copy-start | bytes 3145732
  268.3 13.7 %copy-start.12 = (f32[64,2,16,128]{3,2,0,1:T(8,128)S(1)}, f32[64,2,16,128]{3,2,0,1:T(8,128)}, u32[]{:S(2)}) copy-start(f32[64,2,16,128]{3,2,0,1:T(8,128)} %copy-done.11) | copy-start | bytes 3145732
  268.3 13.6 %collective-permute-start.27 = (f32[64,1,16,128]{3,2,0,1:T(8,128)S(1)}, f32[64,1,16,128]{3,2,0,1:T(8,128)S(1)}, u32[]{:S(2)}, u32[]{:S(2)}) collective-permute-start(f32[64,1,16,128]{3,2,0,1:T(8,128)S(1)} %slice_bitcast_fusion.3), channel_id=1, source_target_pairs={{1,0},{2,1},{3,2},{4,3},{5,4},{6,5},{7,6},{8,7},{9,8},{10,9},{11,1... | collective-permute-start | bytes 1572872 | tf_op jit(solution)/shard_map/ppermute | solution.py:13
  289.4 11.5 %copy-start.5 = (f32[8,8,128,128]{3,2,1,0:T(8,128)}, f32[8,8,128,128]{3,2,1,0:T(8,128)S(1)}, u32[]{:S(2)}) copy-start(f32[8,8,128,128]{3,2,1,0:T(8,128)S(1)} %copy.62) | copy-start | bytes 12582916
  289.5 8.1 %copy-start.1 = (f32[64,16384]{1,0:T(8,128)S(1)}, f32[64,16384]{1,0:T(8,128)}, u32[]{:S(2)}) copy-start(f32[64,16384]{1,0:T(8,128)} %reshape_squeeze.3) | copy-start | bytes 12582916
  293.8 3.7 collective-permute-start.29
  301.5 14.9 %all-to-all-start.2 = ((f32[16,1,64]{2,1,0:T(1,128)}), f32[16,1,64]{2,1,0:T(1,128)S(1)}, u32[]{:S(2)}, u32[]{:S(2)}) async-start(f32[16,1,64]{2,1,0:T(1,128)} %broadcast_in_dim.27), calls=%async_computation.2 | async-start | bytes 16384 | tf_op jit(solution)/shard_map/all_to_all | solution.py:24
  308.3 15.2 %collective-permute-start.31 = (f32[2,1,16,128]{3,2,1,0:T(8,128)S(1)}, f32[2,1,16,128]{3,2,1,0:T(8,128)S(1)}, u32[]{:S(2)}, u32[]{:S(2)}) collective-permute-start(f32[2,1,16,128]{3,2,1,0:T(8,128)S(1)} %pad_maximum_fusion.18), channel_id=1, source_target_pairs={{0,1},{1,2},{2,3},{3,4},{4,5},{5,6},{6,7},{7,8},{8,9},{9,10},{10,1... | collective-permute-start | bytes 49160 | tf_op jit(solution)/shard_map/ppermute | solution.py:13
  311.7 11.7 %collective-permute-start.30 = (f32[1,16,128]{2,1,0:T(8,128)S(1)}, f32[1,16,128]{2,1,0:T(8,128)S(1)}, u32[]{:S(2)}, u32[]{:S(2)}) collective-permute-start(f32[1,16,128]{2,1,0:T(8,128)S(1)} %get-tuple-element.237), channel_id=1, source_target_pairs={{1,0},{2,1},{3,2},{4,3},{5,4},{6,5},{7,6},{8,7},{9,8},{10,9},{11,1... | collective-permute-start | bytes 24584 | tf_op jit(solution)/shard_map/ppermute | solution.py:13
  316.5 10.9 %copy-start.2 = (f32[64,16384]{1,0:T(8,128)S(1)}, f32[64,16384]{1,0:T(8,128)}, u32[]{:S(2)}) copy-start(f32[64,16384]{1,0:T(8,128)} %reshape_squeeze.3) | copy-start | bytes 12582916
  323.7 3.7 collective-permute-start.32
  331.3 13.3 %all-to-all-start.3 = ((f32[16,1,64]{2,1,0:T(1,128)}), f32[16,1,64]{2,1,0:T(1,128)S(1)}, u32[]{:S(2)}, u32[]{:S(2)}) async-start(f32[16,1,64]{2,1,0:T(1,128)} %broadcast_in_dim.29), calls=%async_computation.3 | async-start | bytes 16384 | tf_op jit(solution)/shard_map/all_to_all | solution.py:24
  336.5 15.3 %collective-permute-start.34 = (f32[2,1,16,128]{3,2,1,0:T(8,128)S(1)}, f32[2,1,16,128]{3,2,1,0:T(8,128)S(1)}, u32[]{:S(2)}, u32[]{:S(2)}) collective-permute-start(f32[2,1,16,128]{3,2,1,0:T(8,128)S(1)} %pad_maximum_fusion.19), channel_id=1, source_target_pairs={{0,1},{1,2},{2,3},{3,4},{4,5},{5,6},{6,7},{7,8},{8,9},{9,10},{10,1... | collective-permute-start | bytes 49160 | tf_op jit(solution)/shard_map/ppermute | solution.py:13
  339.8 11.7 %collective-permute-start.33 = (f32[1,16,128]{2,1,0:T(8,128)S(1)}, f32[1,16,128]{2,1,0:T(8,128)S(1)}, u32[]{:S(2)}, u32[]{:S(2)}) collective-permute-start(f32[1,16,128]{2,1,0:T(8,128)S(1)} %get-tuple-element.228), channel_id=1, source_target_pairs={{1,0},{2,1},{3,2},{4,3},{5,4},{6,5},{7,6},{8,7},{9,8},{10,9},{11,1... | collective-permute-start | bytes 24584 | tf_op jit(solution)/shard_map/ppermute | solution.py:13
  344.7 38.5 %copy-start.3 = (f32[64,16384]{1,0:T(8,128)S(1)}, f32[64,16384]{1,0:T(8,128)}, u32[]{:S(2)}) copy-start(f32[64,16384]{1,0:T(8,128)} %reshape_squeeze.3) | copy-start | bytes 12582916
  351.9 7.7 %collective-permute-start.35 = (f32[4,2,16,128]{3,2,1,0:T(8,128)S(1)}, f32[4,2,16,128]{3,2,1,0:T(8,128)S(1)}, u32[]{:S(2)}, u32[]{:S(2)}) collective-permute-start(f32[4,2,16,128]{3,2,1,0:T(8,128)S(1)} %fusion.53), channel_id=1, source_target_pairs={{0,64},{16,80},{32,96},{48,112},{1,65},{17,81},{33,97},{49,113},{2... | collective-permute-start | bytes 196616 | tf_op jit(solution)/shard_map/ppermute | solution.py:13
  359.5 6.0 %collective-permute-start.36 = (f32[1,16,128]{2,1,0:T(8,128)S(1)}, f32[1,16,128]{2,1,0:T(8,128)S(1)}, u32[]{:S(2)}, u32[]{:S(2)}) collective-permute-start(f32[1,16,128]{2,1,0:T(8,128)S(1)} %get-tuple-element.225), channel_id=1, source_target_pairs={{1,0},{2,1},{3,2},{4,3},{5,4},{6,5},{7,6},{8,7},{9,8},{10,9},{11,1... | collective-permute-start | bytes 24584 | tf_op jit(solution)/shard_map/ppermute | solution.py:13
  362.1 7.7 %collective-permute-start.37 = (f32[2,1,16,128]{3,2,1,0:T(8,128)S(1)}, f32[2,1,16,128]{3,2,1,0:T(8,128)S(1)}, u32[]{:S(2)}, u32[]{:S(2)}) collective-permute-start(f32[2,1,16,128]{3,2,1,0:T(8,128)S(1)} %pad_maximum_fusion.20), channel_id=1, source_target_pairs={{0,1},{1,2},{2,3},{3,4},{4,5},{5,6},{6,7},{7,8},{8,9},{9,10},{10,1... | collective-permute-start | bytes 49160 | tf_op jit(solution)/shard_map/ppermute | solution.py:13
  369.9 8.0 %collective-permute-start.39 = (f32[2,1,16,128]{3,2,1,0:T(8,128)S(1)}, f32[2,1,16,128]{3,2,1,0:T(8,128)S(1)}, u32[]{:S(2)}, u32[]{:S(2)}) collective-permute-start(f32[2,1,16,128]{3,2,1,0:T(8,128)S(1)} %pad_maximum_fusion.21), channel_id=1, source_target_pairs={{0,1},{1,2},{2,3},{3,4},{4,5},{5,6},{6,7},{7,8},{8,9},{9,10},{10,1... | collective-permute-start | bytes 49160 | tf_op jit(solution)/shard_map/ppermute | solution.py:13
  372.0 7.4 %collective-permute-start.38 = (f32[1,16,128]{2,1,0:T(8,128)S(1)}, f32[1,16,128]{2,1,0:T(8,128)S(1)}, u32[]{:S(2)}, u32[]{:S(2)}) collective-permute-start(f32[1,16,128]{2,1,0:T(8,128)S(1)} %slice_bitcast_fusion.56), channel_id=1, source_target_pairs={{1,0},{2,1},{3,2},{4,3},{5,4},{6,5},{7,6},{8,7},{9,8},{10,9},{11,1... | collective-permute-start | bytes 24584 | tf_op jit(solution)/shard_map/ppermute | solution.py:13
  379.5 3.7 collective-permute-start.40
  387.1 16.9 %all-to-all-start.4 = ((f32[16,1,64]{2,1,0:T(1,128)}), f32[16,1,64]{2,1,0:T(1,128)S(1)}, u32[]{:S(2)}, u32[]{:S(2)}) async-start(f32[16,1,64]{2,1,0:T(1,128)} %broadcast_in_dim.31), calls=%async_computation.4 | async-start | bytes 16384 | tf_op jit(solution)/shard_map/all_to_all | solution.py:24
  395.8 15.3 %collective-permute-start.42 = (f32[2,1,16,128]{3,2,1,0:T(8,128)S(1)}, f32[2,1,16,128]{3,2,1,0:T(8,128)S(1)}, u32[]{:S(2)}, u32[]{:S(2)}) collective-permute-start(f32[2,1,16,128]{3,2,1,0:T(8,128)S(1)} %pad_maximum_fusion.22), channel_id=1, source_target_pairs={{0,1},{1,2},{2,3},{3,4},{4,5},{5,6},{6,7},{7,8},{8,9},{9,10},{10,1... | collective-permute-start | bytes 49160 | tf_op jit(solution)/shard_map/ppermute | solution.py:13
  399.2 11.8 %collective-permute-start.41 = (f32[1,16,128]{2,1,0:T(8,128)S(1)}, f32[1,16,128]{2,1,0:T(8,128)S(1)}, u32[]{:S(2)}, u32[]{:S(2)}) collective-permute-start(f32[1,16,128]{2,1,0:T(8,128)S(1)} %get-tuple-element.209), channel_id=1, source_target_pairs={{1,0},{2,1},{3,2},{4,3},{5,4},{6,5},{7,6},{8,7},{9,8},{10,9},{11,1... | collective-permute-start | bytes 24584 | tf_op jit(solution)/shard_map/ppermute | solution.py:13
  415.2 11.3 %all-to-all-start.5 = ((f32[16,1,64]{2,1,0:T(1,128)}), f32[16,1,64]{2,1,0:T(1,128)S(1)}, u32[]{:S(2)}, u32[]{:S(2)}) async-start(f32[16,1,64]{2,1,0:T(1,128)} %broadcast_in_dim.33), calls=%async_computation.5 | async-start | bytes 16384 | tf_op jit(solution)/shard_map/all_to_all | solution.py:24
  420.3 7.0 %collective-permute-start.43 = (f32[4,2,16,128]{3,2,1,0:T(8,128)S(1)}, f32[4,2,16,128]{3,2,1,0:T(8,128)S(1)}, u32[]{:S(2)}, u32[]{:S(2)}) collective-permute-start(f32[4,2,16,128]{3,2,1,0:T(8,128)S(1)} %fusion.56), channel_id=1, source_target_pairs={{0,16},{16,32},{32,48},{48,64},{64,80},{80,96},{96,112},{112,0},{1... | collective-permute-start | bytes 196616 | tf_op jit(solution)/shard_map/ppermute | solution.py:19
  427.3 5.9 %collective-permute-start.44 = (f32[1,16,128]{2,1,0:T(8,128)S(1)}, f32[1,16,128]{2,1,0:T(8,128)S(1)}, u32[]{:S(2)}, u32[]{:S(2)}) collective-permute-start(f32[1,16,128]{2,1,0:T(8,128)S(1)} %get-tuple-element.200), channel_id=1, source_target_pairs={{1,0},{2,1},{3,2},{4,3},{5,4},{6,5},{7,6},{8,7},{9,8},{10,9},{11,1... | collective-permute-start | bytes 24584 | tf_op jit(solution)/shard_map/ppermute | solution.py:13
  431.3 7.7 %collective-permute-start.45 = (f32[2,1,16,128]{3,2,1,0:T(8,128)S(1)}, f32[2,1,16,128]{3,2,1,0:T(8,128)S(1)}, u32[]{:S(2)}, u32[]{:S(2)}) collective-permute-start(f32[2,1,16,128]{3,2,1,0:T(8,128)S(1)} %pad_maximum_fusion.23), channel_id=1, source_target_pairs={{0,1},{1,2},{2,3},{3,4},{4,5},{5,6},{6,7},{7,8},{8,9},{9,10},{10,1... | collective-permute-start | bytes 49160 | tf_op jit(solution)/shard_map/ppermute | solution.py:13
  439.2 5.9 %collective-permute-start.46 = (f32[1,16,128]{2,1,0:T(8,128)S(1)}, f32[1,16,128]{2,1,0:T(8,128)S(1)}, u32[]{:S(2)}, u32[]{:S(2)}) collective-permute-start(f32[1,16,128]{2,1,0:T(8,128)S(1)} %get-tuple-element.271), channel_id=1, source_target_pairs={{1,0},{2,1},{3,2},{4,3},{5,4},{6,5},{7,6},{8,7},{9,8},{10,9},{11,1... | collective-permute-start | bytes 24584 | tf_op jit(solution)/shard_map/ppermute | solution.py:13
  441.2 7.7 %collective-permute-start.47 = (f32[2,1,16,128]{3,2,1,0:T(8,128)S(1)}, f32[2,1,16,128]{3,2,1,0:T(8,128)S(1)}, u32[]{:S(2)}, u32[]{:S(2)}) collective-permute-start(f32[2,1,16,128]{3,2,1,0:T(8,128)S(1)} %pad_maximum_fusion.24), channel_id=1, source_target_pairs={{0,1},{1,2},{2,3},{3,4},{4,5},{5,6},{6,7},{7,8},{8,9},{9,10},{10,1... | collective-permute-start | bytes 49160 | tf_op jit(solution)/shard_map/ppermute | solution.py:13
  449.1 5.9 %collective-permute-start.48 = (f32[1,16,128]{2,1,0:T(8,128)S(1)}, f32[1,16,128]{2,1,0:T(8,128)S(1)}, u32[]{:S(2)}, u32[]{:S(2)}) collective-permute-start(f32[1,16,128]{2,1,0:T(8,128)S(1)} %get-tuple-element.268), channel_id=1, source_target_pairs={{1,0},{2,1},{3,2},{4,3},{5,4},{6,5},{7,6},{8,7},{9,8},{10,9},{11,1... | collective-permute-start | bytes 24584 | tf_op jit(solution)/shard_map/ppermute | solution.py:13
  451.1 7.7 %collective-permute-start.49 = (f32[2,1,16,128]{3,2,1,0:T(8,128)S(1)}, f32[2,1,16,128]{3,2,1,0:T(8,128)S(1)}, u32[]{:S(2)}, u32[]{:S(2)}) collective-permute-start(f32[2,1,16,128]{3,2,1,0:T(8,128)S(1)} %pad_maximum_fusion.25), channel_id=1, source_target_pairs={{0,1},{1,2},{2,3},{3,4},{4,5},{5,6},{6,7},{7,8},{8,9},{9,10},{10,1... | collective-permute-start | bytes 49160 | tf_op jit(solution)/shard_map/ppermute | solution.py:13
  (15 other events, 38.0 us)
where the time goes:
time: 469 us; the launch traced here: 460 us
  waiting for transfers between devices  175 us (37%)
  starting transfers between devices  168 us (36%)
  matrix products  51 us (11%)
  other arithmetic  38.7 us (8%)
  local copies, waits for them, and re-layouts  24.2 us (5%)
    ppermute x43, waiting for transfers between devices, from_behind(): return lax.ppermute(value, axis, pairs)  132 us
    ppermute x43, starting transfers between devices, from_behind(): return lax.ppermute(value, axis, pairs)  126 us
    all_to_all x6, starting transfers between devices, sent_to_all(): lax.all_to_all(jnp.broadcast_to(value[None], (size, *value.shape)), axis,...  42.1 us
    all_to_all x6, waiting for transfers between devices, sent_to_all(): lax.all_to_all(jnp.broadcast_to(value[None], (size, *value.shape)), axis,...  25 us
    dot_general x4, matrix products, candidate(): jnp.dot(weights, corrections, precision=exact_mode)  24.1 us
    ppermute x7, waiting for transfers between devices, from_behind_2(): return lax.ppermute(value, axis, pairs)  18.6 us
    dot_general x4, matrix products, candidate(): jnp.dot(flat_basis, left_value.reshape(-1), precision=exact_mode)  13.4 us
  transfers between devices with their start and end apart: 56, of which 33 were waited for; matrix products, arithmetic and copies ran while one was open for 14% of the time, Pallas kernels for 0%

commit v1 on v0

v1 whole, which is shorter than its diff:
```python
import jax
import jax.numpy as jnp
from jax import lax
from jax.experimental import pallas as pl
from jax.experimental.pallas import tpu as pltpu
from jax.sharding import PartitionSpec as P

DT = 0.045
N_TM = 8
N_SP = 16
RANK = 64
NX = 16
NY = 128
F32 = jnp.float32
BF16 = jnp.bfloat16
VMEM = pl.BlockSpec(memory_space=pltpu.VMEM)
SMEM = pl.BlockSpec(memory_space=pltpu.SMEM)


def hop(value, by_tm, by_space):
    pairs = []
    for k in range(N_TM):
        for s in range(N_SP):
            target = ((k + by_tm) % N_TM) * N_SP + (s + by_space) % N_SP
            pairs.append((k * N_SP + s, target))
    return lax.ppermute(value, ("tm", "space"), pairs)


def share(copies):
    return lax.all_to_all(copies, "space", 0, 0, tiled=True)


def next_x(v):
    row = lax.broadcasted_iota(jnp.int32, v.shape, 1)
    return jnp.where(row < NX - 1, pltpu.roll(v, NX - 1, 1), 0.0)


def prev_x(v):
    row = lax.broadcasted_iota(jnp.int32, v.shape, 1)
    return jnp.where(row > 0, pltpu.roll(v, 1, 1), 0.0)


def next_y(v):
    lane = lax.broadcasted_iota(jnp.int32, v.shape, 2)
    return jnp.where(lane < NY - 1, pltpu.roll(v, NY - 1, 2), 0.0)


def prev_y(v):
    lane = lax.broadcasted_iota(jnp.int32, v.shape, 2)
    return jnp.where(lane > 0, pltpu.roll(v, 1, 2), 0.0)


def cat(*parts):
    parts = [part for part in parts if part.shape[0]]
    return parts[0] if len(parts) == 1 else jnp.concatenate(parts, axis=0)


def only(ok, v):
    return jnp.where(ok, v, jnp.zeros_like(v))


def without_floor(vz, low, ok1, ok2):
    far = max(0, low - 2)
    return cat(only(ok2, vz[:far]), only(ok1, vz[far:low]), vz[low:])


def advance(p, vx, vy, vz, c2, h, low, ok1, ok2, load=None):
    mid = p[1:-1]
    vx = vx - h * (next_x(mid) - mid)
    vy = vy - h * (next_y(mid) - mid)
    vz = vz - h * (p[1:] - p[:-1])
    vz = without_floor(vz, low, ok1, ok2)
    diverge = (vx - prev_x(vx)) + (vy - prev_y(vy)) + (vz[1:] - vz[:-1])
    fresh = mid - h * c2 * diverge
    if load is not None:
        fresh = fresh + load
    return fresh, vx, vy, vz[1:]


def advance_many(p, vx, vy, vz, c2, h, steps, ok1, ok2, loads=None):
    points = []
    for i in range(steps):
        low = steps - i
        load = None if loads is None else loads[i]
        p, vx, vy, vz = advance(p, vx, vy, vz, c2, h, low, ok1, ok2, load)
        edge = low - 1
        n = p.shape[0]
        points.append(
            cat(p[edge : n - edge], vx[edge : n - edge], vy[edge : n - edge], vz[edge : n - edge])
        )
        vx, vy, vz, c2 = vx[1:-1], vy[1:-1], vz[: n - 1], c2[1:-1]
    return points


def put(ref, at, planes):
    n = planes.shape[0]
    ref[at : at + n] = planes
    return at + n


def put_up_far(ref, u, at=0):
    at = put(ref, at, u[0:2])
    at = put(ref, at, u[6:8])
    at = put(ref, at, u[3:4])
    return put(ref, at, u[5:6])


def put_down_far(ref, u, at=0):
    at = put(ref, at, u[0:2])
    at = put(ref, at, u[2:3])
    at = put(ref, at, u[4:5])
    return put(ref, at, u[6:7])


def wide(own, b1, a1, b2, a2, ok_b1, ok_a1, ok_b2, ok_a2):
    p = cat(
        only(ok_b2, b2[0:2]), only(ok_b1, b1[0:2]), own[0:2], only(ok_a1, a1[0:2]), only(ok_a2, a2[0:2])
    )
    vx = cat(b2[4:5], b1[2:4], own[2:4], a1[2:4], a2[2:3])
    vy = cat(b2[5:6], b1[4:6], own[4:6], a1[4:6], a2[3:4])
    vz = cat(b2[2:4], b1[6:8], own[6:8], a1[6:8], a2[4:5])
    return p, vx, vy, vz


def flags(where_ref):
    s = where_ref[0]
    return s >= 1, s < N_SP - 1, s >= 2, s < N_SP - 2


def call(kernel, outs, *args, scratch=(), flops=1_000_000):
    shapes = [jax.ShapeDtypeStruct(shape, F32) for shape in outs]
    return pl.pallas_call(
        kernel,
        out_shape=shapes,
        in_specs=[SMEM if arg.dtype == jnp.int32 else VMEM for arg in args],
        out_specs=[VMEM] * len(shapes),
        scratch_shapes=list(scratch),
        cost_estimate=pl.CostEstimate(flops=flops, bytes_accessed=100_000, transcendentals=0),
    )(*args)


def pack_kernel(g_ref, f_ref, c_ref, up1, dn1, up2, dn2):
    u = g_ref[...]
    c2 = c_ref[...] * c_ref[...]
    for ref, inner in ((up1, 1), (dn1, 0)):
        put(ref, 0, u)
        put(ref, 8, f_ref[0])
        put(ref, 10, f_ref[1])
        put(ref, 12, f_ref[2, inner : inner + 1])
        put(ref, 13, c2)
    at = put_up_far(up2, u)
    at = put(up2, at, f_ref[0, 1:2])
    put(up2, at, c2[1:2])
    at = put_down_far(dn2, u)
    at = put(dn2, at, f_ref[0, 0:1])
    put(dn2, at, c2[0:1])


def load_medium(c_ref, b1, a1, b2, a2, ok):
    ok_b1, ok_a1, ok_b2, ok_a2 = ok
    own = c_ref[...] * c_ref[...]
    return cat(
        only(ok_b2, b2[7:8]), only(ok_b1, b1[13:15]), own, only(ok_a1, a1[13:15]), only(ok_a2, a2[6:7])
    )


def load_forcing(f_ref, b1, a1, b2, a2, ok):
    ok_b1, ok_a1, ok_b2, ok_a2 = ok
    return [
        cat(
            only(ok_b2, b2[6:7]), only(ok_b1, b1[8:10]), f_ref[0], only(ok_a1, a1[8:10]), only(ok_a2, a2[5:6])
        ),
        cat(only(ok_b1, b1[10:12]), f_ref[1], only(ok_a1, a1[10:12])),
        cat(only(ok_b1, b1[12:13]), f_ref[2], only(ok_a1, a1[12:13])),
        f_ref[3],
    ]


def relax_kernel(where, g_ref, f_ref, c_ref, b1, a1, b2, a2, out, up2, dn2):
    ok = flags(where)
    c2 = load_medium(c_ref, b1, a1, b2, a2, ok)
    loads = load_forcing(f_ref, b1, a1, b2, a2, ok)
    p, vx, vy, vz = wide(g_ref[...], b1[...], a1[...], b2[...], a2[...], *ok)
    u = advance_many(p, vx, vy, vz, c2, DT, 4, ok[0], ok[2], loads)[-1]
    out[...] = u
    put_up_far(up2, u)
    put_down_far(dn2, u)


def residue_kernel(where, relaxed, f_ref, c_ref, hb1, ha1, hb2, ha2, own, b1, a1, b2, a2, out, med):
    ok = flags(where)
    c2 = load_medium(c_ref, hb1, ha1, hb2, ha2, ok)
    loads = load_forcing(f_ref, hb1, ha1, hb2, ha2, ok)
    p, vx, vy, vz = wide(own[...], b1[...], a1[...], b2[...], a2[...], *ok)
    u = advance_many(p, vx, vy, vz, c2, DT, 4, ok[0], ok[2], loads)[-1]
    out[...] = u - relaxed[...]
    med[...] = c2


def gram_kernel(basis, out, split):
    rows = 16

    def step(i, total):
        for j in range(rows):
            values = basis[pl.ds(i * rows + j, RANK, stride=8 * NX), :]
            high = values.astype(BF16)
            rest = values - high.astype(F32)
            middle = rest.astype(BF16)
            low = (rest - middle.astype(F32)).astype(BF16)
            lanes = slice(j * NY, (j + 1) * NY)
            split[0:RANK, lanes] = high
            split[RANK : 2 * RANK, lanes] = middle
            split[2 * RANK : 3 * RANK, lanes] = low
        both = split[...]
        return total + lax.dot_general(
            both, both, (((1,), (1,)), ((), ())), preferred_element_type=F32
        )

    total = lax.fori_loop(0, 8 * NX // rows, step, jnp.zeros((3 * RANK, 3 * RANK), F32))
    part = total[0:RANK] + total[RANK : 2 * RANK] + total[2 * RANK :]
    gram = part[:, 0:RANK] + part[:, RANK : 2 * RANK] + part[:, 2 * RANK :]
    out[...] = jnp.concatenate([gram, gram], axis=1)


def inner_products(basis, u, scratch):
    tiles = u.reshape(8 * NX, NY)
    pieces = [tiles[8 * i : 8 * i + 8] for i in range(NX)]
    for r in range(RANK):
        at = r * 8 * NX
        sums = []
        for lane in range(4):
            part = basis[at + 32 * lane : at + 32 * lane + 8, :] * pieces[4 * lane]
            for i in range(1, 4):
                low = at + 32 * lane + 8 * i
                part = part + basis[low : low + 8, :] * pieces[4 * lane + i]
            sums.append(part)
        total = (sums[0] + sums[1]) + (sums[2] + sums[3])
        scratch[r : r + 1, :] = jnp.sum(total, axis=0, keepdims=True)
    column = jnp.sum(scratch[...], axis=1, keepdims=True)
    return to_row(column)


def to_row(column):
    r = lax.broadcasted_iota(jnp.int32, (RANK, NY), 0)
    lane = lax.broadcasted_iota(jnp.int32, (RANK, NY), 1)
    return jnp.sum(jnp.where(r == lane, column, 0.0), axis=0, keepdims=True)


def first_kernel(basis, x_ref, gram, out, scratch):
    row = inner_products(basis, x_ref[...], scratch)
    g = gram[...]
    lane = lax.broadcasted_iota(jnp.int32, (RANK // 2, NY), 1)
    packed = jnp.where(lane < RANK, g[: RANK // 2], g[RANK // 2 :])
    rows = jnp.concatenate([packed, jnp.broadcast_to(row, (8, NY))], axis=0)
    for j in range(N_SP):
        out[j] = rows


def inverse(g):
    lane = lax.broadcasted_iota(jnp.int32, (RANK, NY), 1)
    row = lax.broadcasted_iota(jnp.int32, (RANK, NY), 0)
    work = jnp.where(lane < RANK, g, jnp.where(lane - RANK == row, 1.0, 0.0))
    for j in range(RANK):
        pivot_row = work[j : j + 1, :]
        pivot = work[j : j + 1, j : j + 1]
        scaled = pivot_row * (1.0 / pivot)
        factor = jnp.where(row[:, 0:1] == j, 0.0, work[:, j : j + 1])
        work = work - factor * scaled
    diagonal = jnp.sum(jnp.where(lane == row, work, 0.0), axis=1, keepdims=True)
    solved = pltpu.roll(work, RANK, 1) * (1.0 / diagonal)
    return jnp.where(lane < RANK, solved, 0.0)


def project(basis, ginv, coef, x, scratch, outs):
    weights = jnp.sum(ginv * coef, axis=1, keepdims=True)
    scratch[...] = jnp.broadcast_to(weights, (RANK, NY))
    total = [jnp.zeros((8, NY), F32) for i in range(NX)]
    for r in range(RANK):
        w = scratch[r : r + 1, :]
        at = r * 8 * NX
        for i in range(NX):
            total[i] = total[i] + w * basis[at + 8 * i : at + 8 * i + 8, :]
    y = jnp.concatenate(total, axis=0).reshape(8, NX, NY)
    z = x - y
    center, up1, dn1, up2, dn2 = outs
    put(center, 0, y)
    put(center, 8, z)
    put(up1, 0, y)
    put(up1, 8, z[1:2])
    put(up1, 9, z[7:8])
    put(dn1, 0, y)
    put(dn1, 8, z[0:1])
    put_up_far(up2, y)
    put_down_far(dn2, y)


PROJECTED = [(16, NX, NY), (10, NX, NY), (9, NX, NY), (6, NX, NY), (5, NX, NY)]


def first_project_kernel(got, basis, x_ref, ginv_ref, *rest):
    outs, scratch = rest[:5], rest[5]
    total = got[0]
    for j in range(1, N_SP):
        total = total + got[j]
    packed = total[: RANK // 2]
    g = jnp.concatenate([packed, pltpu.roll(packed, RANK, 1)], axis=0)
    ginv = inverse(g)
    ginv_ref[...] = ginv
    project(basis, ginv, total[RANK // 2 : RANK // 2 + 1], x_ref[...], scratch, outs)


def project_kernel(got, ginv_ref, basis, x_ref, *rest):
    outs, scratch = rest[:5], rest[5]
    coef = jnp.sum(got[...], axis=0)
    project(basis, ginv_ref[...], coef, x_ref[...], scratch, outs)


def q_of(where, med, center, b1, a1, b2, a2):
    ok = flags(where)
    ok_b1, ok_a1 = ok[0], ok[1]
    c2 = med[...]
    y = center[0:8]
    z = center[8:16]
    p, vx, vy, vz = wide(y, b1[...], a1[...], b2[...], a2[...], *ok)
    fine = advance_many(p, vx, vy, vz, c2, DT, 4, ok[0], ok[2])[-1]
    zp = cat(only(ok_b1, b1[8:9]), z[0:2], only(ok_a1, a1[8:9]))
    zz = cat(b1[9:10], z[6:8])
    coarse = advance_many(zp, z[2:4], z[4:6], zz, c2[3:5], 4 * DT, 1, ok[0], ok[2])[-1]
    return fine + coarse


def level_kernel(where, med, center, b1, a1, b2, a2, acc, basis, u_out, acc_out, row_out, scratch):
    u = q_of(where, med, center, b1, a1, b2, a2)
    u_out[...] = u
    acc_out[...] = acc[...] + u
    row = inner_products(basis, u, scratch)
    for j in range(N_SP):
        row_out[j] = row


def gap_kernel(where, med, center, b1, a1, b2, a2, acc, u_out, acc_out, up2, dn2):
    u = q_of(where, med, center, b1, a1, b2, a2)
    u_out[...] = u
    acc_out[...] = acc[...] + u
    put_up_far(up2, u)
    put_down_far(dn2, u)


def chain_kernel(where, med, own, b, a, acc, basis, x_out, row_out, scratch):
    ok = flags(where)
    c2 = med[...]
    p = cat(only(ok[0], b[0:2]), own[0:2], only(ok[1], a[0:2]))
    vx = cat(b[4:5], own[2:4], a[2:3])
    vy = cat(b[5:6], own[4:6], a[3:4])
    vz = cat(b[2:4], own[6:8], a[4:5])
    moved = advance_many(p, vx, vy, vz, c2[2:6], 8 * DT, 2, ok[0], ok[2])[-1]
    chained = (where[1] >= 5) | (where[1] == 0)
    x = acc[...] + only(chained, moved)
    x_out[...] = x
    row = inner_products(basis, x, scratch)
    for j in range(N_SP):
        row_out[j] = row


def final_kernel(where, med, center, b1, a1, b2, a2, relaxed, residue, basis, out, up2, dn2, row_out, scratch):
    u = relaxed[...] + (q_of(where, med, center, b1, a1, b2, a2) + residue[...])
    out[...] = u
    put(up2, put(up2, 0, u[1:2]), u[7:8])
    put(dn2, 0, u[0:1])
    row = inner_products(basis, u, scratch)
    for j in range(N_SP):
        row_out[j] = row


def sweep_kernel(where, f_ref, c_ref, hb1, ha1, hb2, ha2, final, own, b1, a1, b2, a2, got, ginv, out, coords):
    ok = flags(where)
    c2 = load_medium(c_ref, hb1, ha1, hb2, ha2, ok)[1:7]
    loads = [load[1:-1] for load in load_forcing(f_ref, hb1, ha1, hb2, ha2, ok)[:3]]
    u = own[...]
    p = cat(
        only(ok[2], b2[0:1]), only(ok[0], b1[0:2]), u[0:2], only(ok[1], a1[0:2]), only(ok[3], a2[0:1])
    )
    vx = cat(b1[2:4], u[2:4], a1[2:4])
    vy = cat(b1[4:6], u[4:6], a1[4:6])
    vz = cat(b2[1:2], b1[6:8], u[6:8], a1[6:8])
    points = advance_many(p, vx, vy, vz, c2, DT, 3, ok[0], ok[2], loads)
    for i in range(3):
        out[i] = points[i]
    out[3] = final[...]
    coef = jnp.sum(got[...], axis=0)
    coords[...] = to_row(jnp.sum(ginv[...] * coef, axis=1, keepdims=True))


def body(speed, forcing, guess, basis):
    where = jnp.stack([lax.axis_index("space"), lax.axis_index("tm")]).astype(jnp.int32)
    columns = basis.reshape(RANK * 8 * NX, NY)
    state = (8, NX, NY)
    table = pltpu.VMEM((RANK, NY), F32)
    copies = (N_SP, 1, NY)

    start = hop(guess.reshape(state), 1, 0)
    up1, dn1, up2, dn2 = call(
        pack_kernel, [(15, NX, NY), (15, NX, NY), (8, NX, NY), (7, NX, NY)], start, forcing, speed
    )
    halo = (hop(up1, 0, 1), hop(dn1, 0, -1), hop(up2, 0, 2), hop(dn2, 0, -2))
    far = [(6, NX, NY), (5, NX, NY)]
    relaxed, up2, dn2 = call(relax_kernel, [state, *far], where, start, forcing, speed, *halo)
    near = [hop(relaxed, 1, 0), hop(relaxed, 1, 1), hop(relaxed, 1, -1), hop(up2, 1, 2), hop(dn2, 1, -2)]
    (gram,) = call(
        gram_kernel,
        [(RANK, NY)],
        columns,
        scratch=[pltpu.VMEM((3 * RANK, 16 * NY), BF16)],
        flops=50_000_000,
    )
    residue, med = call(
        residue_kernel, [state, (8, NX, NY)], where, relaxed, forcing, speed, *halo, *near
    )
    x = hop(residue, 1, 0)
    (rows,) = call(first_kernel, [(N_SP, RANK // 2 + 8, NY)], columns, x, gram, scratch=[table])
    ginv, *packed = call(
        first_project_kernel, [(RANK, NY), *PROJECTED], share(rows), columns, x, scratch=[table]
    )

    def exchanged(packed, by_tm):
        center, up1, dn1, up2, dn2 = packed
        if by_tm:
            center = hop(center, by_tm, 0)
        return [center, hop(up1, by_tm, 1), hop(dn1, by_tm, -1), hop(up2, by_tm, 2), hop(dn2, by_tm, -2)]

    acc = x
    for level in range(2):
        u, acc, rows = call(
            level_kernel, [state, state, copies], where, med, *exchanged(packed, 1), acc, columns, scratch=[table]
        )
        packed = call(project_kernel, PROJECTED, share(rows), ginv, columns, u, scratch=[table])
    gap, acc, up, dn = call(gap_kernel, [state, state, *far], where, med, *exchanged(packed, 1), acc)
    x, rows = call(
        chain_kernel,
        [state, copies],
        where,
        med,
        hop(gap, 4, 0),
        hop(up, 4, 1),
        hop(dn, 4, -1),
        acc,
        columns,
        scratch=[table],
    )
    packed = call(project_kernel, PROJECTED, share(rows), ginv, columns, x, scratch=[table])
    final, up2, dn2, rows = call(
        final_kernel,
        [state, (2, NX, NY), (1, NX, NY), copies],
        where,
        med,
        *exchanged(packed, 0),
        relaxed,
        residue,
        columns,
        scratch=[table],
    )
    got = share(rows)
    near = [hop(final, 1, 0), hop(final, 1, 1), hop(final, 1, -1)]
    near += [hop(up2, 1, 2), hop(dn2, 1, -2)]
    states, coords = call(
        sweep_kernel, [(4, 8, NX, NY), (1, NY)], where, forcing, speed, *halo, final, *near, got, ginv
    )
    return states.reshape(4, 4, 2, NX, NY), coords[:, :RANK]


def solution(mesh):
    placed = (
        P("space", None, None),
        P("tm", "space", None, None),
        P("tm", None, "space", None, None),
        P("tm", None, None, "space", None, None),
    )
    return jax.shard_map(
        body,
        mesh=mesh,
        in_specs=placed,
        out_specs=(P("tm", None, "space", None, None), P("tm", None)),
        check_vma=False,
    )
```

time: 469 us -> 254 us (0.54)
  the two profiles are of different devices: /device:TPU:38 before, /device:TPU:1 now
where the time goes in v1:
time: 254 us; the launch traced here: 253 us
  starting transfers between devices  98.6 us (39%)
  blocking collectives  65.1 us (26%)
  Pallas kernels  57.5 us (23%)
  waiting for transfers between devices  22.1 us (9%)
  local copies, waits for them, and re-layouts  8.48 us (3%)
    ppermute x38, starting transfers between devices, hop(): return lax.ppermute(value, ('tm', 'space'), pairs)  98.6 us
    all_to_all x5, blocking collectives, share(): return lax.all_to_all(copies, 'space', 0, 0, tiled=True)  65.1 us
    pallas_call x15, Pallas kernels, call(): pl.pallas_call(kernel, out_shape=shapes, in_specs=[SMEM if arg.dtype == j...  57.5 us
    ppermute x38, waiting for transfers between devices, hop(): return lax.ppermute(value, ('tm', 'space'), pairs)  22.1 us
    unnamed x76, local copies, waits for them, and re-layouts  8.48 us
  transfers between devices with their start and end apart: 38, of which 15 were waited for; matrix products, arithmetic and copies ran while one was open for 0% of the time, Pallas kernels for 3%

profile of v1, /device:TPU:1, one launch (start us, length us, event | category | flops | bytes accessed | tf_op | source)
XLA Modules:
  0.0 253.3 jit_solution(17152918237112844575)
XLA Ops:
  0.6 2.6 %collective-permute-start = (f32[8,16,128]{2,1,0:T(8,128)}, f32[8,16,128]{2,1,0:T(8,128)S(1)}, u32[]{:S(2)}, u32[]{:S(2)}) collective-permute-start(f32[8,16,128]{2,1,0:T(8,128)} %bitcast.17), channel_id=1, source_target_pairs={{0,16},{1,17},{2,18},{3,19},{4,20},{5,21},{6,22},{7,23},{8,24},{9,... | collective-permute-start | bytes 196616 | tf_op jit(solution)/shard_map/ppermute | solution.py:26
  3.2 1.6 collective-permute-done.g_ref
  4.9 0.6 copy-done.5
  5.5 1.6 shard_map.59
  7.1 1.3 collective-permute-start.1
  8.4 4.9 %collective-permute-start.2 = (f32[15,16,128]{2,1,0:T(8,128)}, f32[15,16,128]{2,1,0:T(8,128)S(1)}, u32[]{:S(2)}, u32[]{:S(2)}) collective-permute-start(f32[15,16,128]{2,1,0:T(8,128)} %get-tuple-element.51), channel_id=1, source_target_pairs={{0,15},{1,0},{2,1},{3,2},{4,3},{5,4},{6,5},{7,6},{8,7},{9,8},{10,9... | collective-permute-start | bytes 368648 | tf_op jit(solution)/shard_map/ppermute | solution.py:26
  13.3 1.6 collective-permute-start.4
  15.0 1.3 collective-permute-start.3
  16.3 0.6 pad_add_fusion.where
  16.9 1.5 collective-permute-done.4.a2.ha2
  18.4 3.8 %collective-permute-done.3.b2.hb2 = f32[8,16,128]{2,1,0:T(8,128)S(1)} collective-permute-done((f32[8,16,128]{2,1,0:T(8,128)}, f32[8,16,128]{2,1,0:T(8,128)S(1)}, u32[]{:S(2)}, u32[]{:S(2)}) %collective-permute-start.3) | collective-permute-done | bytes 65568 | tf_op jit(solution)/shard_map/ppermute | solution.py:26
  22.2 0.6 copy-done.3
  22.8 0.6 copy-done.1
  23.5 2.3 shard_map.60
  25.8 3.5 %collective-permute-start.7 = (f32[8,16,128]{2,1,0:T(8,128)}, f32[8,16,128]{2,1,0:T(8,128)S(1)}, u32[]{:S(2)}, u32[]{:S(2)}) collective-permute-start(f32[8,16,128]{2,1,0:T(8,128)} %get-tuple-element.54.relaxed), channel_id=1, source_target_pairs={{0,31},{1,16},{2,17},{3,18},{4,19},{5,20},{6,21},{7,22},{8,23},{9,... | collective-permute-start | bytes 196616 | tf_op jit(solution)/shard_map/ppermute | solution.py:26
  29.3 0.6 collective-permute-start.6
  29.9 2.6 %collective-permute-start.5 = (f32[8,16,128]{2,1,0:T(8,128)}, f32[8,16,128]{2,1,0:T(8,128)S(1)}, u32[]{:S(2)}, u32[]{:S(2)}) collective-permute-start(f32[8,16,128]{2,1,0:T(8,128)} %get-tuple-element.54.relaxed), channel_id=1, source_target_pairs={{0,16},{1,17},{2,18},{3,19},{4,20},{5,21},{6,22},{7,23},{8,24},{9,... | collective-permute-start | bytes 196616 | tf_op jit(solution)/shard_map/ppermute | solution.py:26
  33.1 5.4 %collective-permute-start.9 = (f32[5,16,128]{2,1,0:T(8,128)}, f32[5,16,128]{2,1,0:T(8,128)S(1)}, u32[]{:S(2)}, u32[]{:S(2)}) collective-permute-start(f32[5,16,128]{2,1,0:T(8,128)} %get-tuple-element.56), channel_id=1, source_target_pairs={{0,30},{1,31},{2,16},{3,17},{4,18},{5,19},{6,20},{7,21},{8,22},{9,... | collective-permute-start | bytes 122888 | tf_op jit(solution)/shard_map/ppermute | solution.py:26
  38.5 1.4 collective-permute-done.9.a2
  39.9 0.9 collective-permute-done.8.b2
  41.5 0.6 copy-done.23
  42.1 2.4 shard_map.61
  44.5 8.6 %shard_map.62.gram = f32[64,128]{1,0:T(8,128)} custom-call(f32[8192,128]{1,0:T(8,128)} %bitcast.6), custom_call_target="tpu_custom_call" | custom-call | flops 50000000 | bytes 100000 | tf_op jit(solution)/shard_map/pallas_call | solution.py:132
  53.2 0.6 copy-done.2
  53.8 3.4 %shard_map.63 = f32[16,40,128]{2,1,0:T(8,128)} custom-call(f32[8192,128]{1,0:T(8,128)} %bitcast.7, f32[8,16,128]{2,1,0:T(8,128)} %copy-done.2, f32[64,128]{1,0:T(8,128)} %shard_map.62.gram), custom_call_target="tpu_custom_call" | custom-call | flops 1000000 | bytes 100000 | tf_op jit(solution)/shard_map/pallas_call | solution.py:132
  57.2 16.4 %all_to_all.25.got = f32[16,40,128]{2,1,0:T(8,128)} all-to-all(f32[16,40,128]{2,1,0:T(8,128)} %shard_map.63), channel_id=1, replica_groups=mesh['tm'=8,'space'=16] {'space'}, dimensions={0} | all-to-all | bytes 655360 | tf_op jit(solution)/shard_map/all_to_all | solution.py:30
  73.6 8.9 %shard_map.64 = (f32[64,128]{1,0:T(8,128)}, f32[16,16,128]{2,1,0:T(8,128)}, f32[10,16,128]{2,1,0:T(8,128)}, f32[9,16,128]{2,1,0:T(8,128)}, f32[6,16,128]{2,1,0:T(8,128)}, /*index=5*/f32[5,16,128]{2,1,0:T(8,128)}) custom-call(f32[16,40,128]{2,1,0:T(8,128)} %all_to_all.25.got, f32[8192,128]{1,0:T(8,128)} %bitcast.8, f32[8,16,128]{2,1,0:T(8,128)} %copy-done.2), custom_call_target="tpu_custom_call" | custom-call | flops 1000000 | bytes 100000 | tf_op jit(solution)/shard_map/pallas_call | solution.py:132
  82.4 1.8 collective-permute-start.11
  84.6 5.5 %collective-permute-start.13 = (f32[9,16,128]{2,1,0:T(8,128)}, f32[9,16,128]{2,1,0:T(8,128)S(1)}, u32[]{:S(2)}, u32[]{:S(2)}) collective-permute-start(f32[9,16,128]{2,1,0:T(8,128)} %get-tuple-element.61), channel_id=1, source_target_pairs={{0,31},{1,16},{2,17},{3,18},{4,19},{5,20},{6,21},{7,22},{8,23},{9,... | collective-permute-start | bytes 221192 | tf_op jit(solution)/shard_map/ppermute | solution.py:26
  90.1 4.4 %collective-permute-start.15 = (f32[5,16,128]{2,1,0:T(8,128)}, f32[5,16,128]{2,1,0:T(8,128)S(1)}, u32[]{:S(2)}, u32[]{:S(2)}) collective-permute-start(f32[5,16,128]{2,1,0:T(8,128)} %get-tuple-element.63), channel_id=1, source_target_pairs={{0,30},{1,31},{2,16},{3,17},{4,18},{5,19},{6,20},{7,21},{8,22},{9,... | collective-permute-start | bytes 122888 | tf_op jit(solution)/shard_map/ppermute | solution.py:26
  94.5 1.4 collective-permute-done.15.a2
  95.9 1.8 collective-permute-done.14.b2
  98.4 4.0 %shard_map.65 = (f32[8,16,128]{2,1,0:T(8,128)}, f32[8,16,128]{2,1,0:T(8,128)}, f32[16,1,128]{2,1,0:T(1,128)}) custom-call(s32[2]{0:T(128)} %pad_add_fusion.where, f32[8,16,128]{2,1,0:T(8,128)} %get-tuple-element.57.med, f32[16,16,128]{2,1,0:T(8,128)} %copy-done.8, f32[10,16,128]{2,1,0:T(8,128)} %copy-done.11, f32[9,16,128]{2,1,0:T(8,128)} %copy-done.15, ...), custom_call_target="tpu_custom_call" | custom-call | flops 1000000 | bytes 100000 | tf_op jit(solution)/shard_map/pallas_call | solution.py:132
  102.4 12.2 %all_to_all.26.got = f32[16,1,128]{2,1,0:T(1,128)} all-to-all(f32[16,1,128]{2,1,0:T(1,128)} %get-tuple-element.64), channel_id=1, replica_groups=mesh['tm'=8,'space'=16] {'space'}, dimensions={0} | all-to-all | bytes 16384 | tf_op jit(solution)/shard_map/all_to_all | solution.py:30
  114.6 3.3 %shard_map.66 = (f32[16,16,128]{2,1,0:T(8,128)}, f32[10,16,128]{2,1,0:T(8,128)}, f32[9,16,128]{2,1,0:T(8,128)}, f32[6,16,128]{2,1,0:T(8,128)}, f32[5,16,128]{2,1,0:T(8,128)}) custom-call(f32[16,1,128]{2,1,0:T(1,128)} %all_to_all.26.got, f32[64,128]{1,0:T(8,128)} %get-tuple-element.65.ginv_ref.ginv, f32[8192,128]{1,0:T(8,128)} %bitcast.10, ...), custom_call_target="tpu_custom_call" | custom-call | flops 1000000 | bytes 100000 | tf_op jit(solution)/shard_map/pallas_call | solution.py:132
  117.9 2.4 collective-permute-start.16
  120.4 7.6 %collective-permute-start.18 = (f32[9,16,128]{2,1,0:T(8,128)}, f32[9,16,128]{2,1,0:T(8,128)S(1)}, u32[]{:S(2)}, u32[]{:S(2)}) collective-permute-start(f32[9,16,128]{2,1,0:T(8,128)} %get-tuple-element.69), channel_id=1, source_target_pairs={{0,31},{1,16},{2,17},{3,18},{4,19},{5,20},{6,21},{7,22},{8,23},{9,... | collective-permute-start | bytes 221192 | tf_op jit(solution)/shard_map/ppermute | solution.py:26
  127.9 5.4 %collective-permute-start.20 = (f32[5,16,128]{2,1,0:T(8,128)}, f32[5,16,128]{2,1,0:T(8,128)S(1)}, u32[]{:S(2)}, u32[]{:S(2)}) collective-permute-start(f32[5,16,128]{2,1,0:T(8,128)} %get-tuple-element.71), channel_id=1, source_target_pairs={{0,30},{1,31},{2,16},{3,17},{4,18},{5,19},{6,20},{7,21},{8,22},{9,... | collective-permute-start | bytes 122888 | tf_op jit(solution)/shard_map/ppermute | solution.py:26
  133.3 1.4 collective-permute-done.20.a2
  136.0 4.0 %shard_map.67 = (f32[8,16,128]{2,1,0:T(8,128)}, f32[8,16,128]{2,1,0:T(8,128)}, f32[16,1,128]{2,1,0:T(1,128)}) custom-call(s32[2]{0:T(128)} %pad_add_fusion.where, f32[8,16,128]{2,1,0:T(8,128)} %get-tuple-element.57.med, f32[16,16,128]{2,1,0:T(8,128)} %copy-done.7, f32[10,16,128]{2,1,0:T(8,128)} %copy-done.10, f32[9,16,128]{2,1,0:T(8,128)} %copy-done.14, ...), custom_call_target="tpu_custom_call" | custom-call | flops 1000000 | bytes 100000 | tf_op jit(solution)/shard_map/pallas_call | solution.py:132
  140.0 12.7 %all_to_all.27.got = f32[16,1,128]{2,1,0:T(1,128)} all-to-all(f32[16,1,128]{2,1,0:T(1,128)} %get-tuple-element.73), channel_id=1, replica_groups=mesh['tm'=8,'space'=16] {'space'}, dimensions={0} | all-to-all | bytes 16384 | tf_op jit(solution)/shard_map/all_to_all | solution.py:30
  152.7 3.3 %shard_map.68 = (f32[16,16,128]{2,1,0:T(8,128)}, f32[10,16,128]{2,1,0:T(8,128)}, f32[9,16,128]{2,1,0:T(8,128)}, f32[6,16,128]{2,1,0:T(8,128)}, f32[5,16,128]{2,1,0:T(8,128)}) custom-call(f32[16,1,128]{2,1,0:T(1,128)} %all_to_all.27.got, f32[64,128]{1,0:T(8,128)} %get-tuple-element.65.ginv_ref.ginv, f32[8192,128]{1,0:T(8,128)} %bitcast.12, ...), custom_call_target="tpu_custom_call" | custom-call | flops 1000000 | bytes 100000 | tf_op jit(solution)/shard_map/pallas_call | solution.py:132
  156.0 2.9 %collective-permute-start.21 = (f32[16,16,128]{2,1,0:T(8,128)}, f32[16,16,128]{2,1,0:T(8,128)S(1)}, u32[]{:S(2)}, u32[]{:S(2)}) collective-permute-start(f32[16,16,128]{2,1,0:T(8,128)} %get-tuple-element.75), channel_id=1, source_target_pairs={{0,16},{1,17},{2,18},{3,19},{4,20},{5,21},{6,22},{7,23},{8,24},{9,... | collective-permute-start | bytes 393224 | tf_op jit(solution)/shard_map/ppermute | solution.py:26
  159.1 6.9 %collective-permute-start.23 = (f32[9,16,128]{2,1,0:T(8,128)}, f32[9,16,128]{2,1,0:T(8,128)S(1)}, u32[]{:S(2)}, u32[]{:S(2)}) collective-permute-start(f32[9,16,128]{2,1,0:T(8,128)} %get-tuple-element.77), channel_id=1, source_target_pairs={{0,31},{1,16},{2,17},{3,18},{4,19},{5,20},{6,21},{7,22},{8,23},{9,... | collective-permute-start | bytes 221192 | tf_op jit(solution)/shard_map/ppermute | solution.py:26
  166.0 3.2 %collective-permute-start.25 = (f32[5,16,128]{2,1,0:T(8,128)}, f32[5,16,128]{2,1,0:T(8,128)S(1)}, u32[]{:S(2)}, u32[]{:S(2)}) collective-permute-start(f32[5,16,128]{2,1,0:T(8,128)} %get-tuple-element.79), channel_id=1, source_target_pairs={{0,30},{1,31},{2,16},{3,17},{4,18},{5,19},{6,20},{7,21},{8,22},{9,... | collective-permute-start | bytes 122888 | tf_op jit(solution)/shard_map/ppermute | solution.py:26
  169.2 2.3 collective-permute-done.25.a2
  171.5 2.1 collective-permute-done.24.b2
  174.3 2.3 shard_map.69
  176.7 2.2 collective-permute-start.26
  178.9 7.2 %collective-permute-start.28 = (f32[5,16,128]{2,1,0:T(8,128)}, f32[5,16,128]{2,1,0:T(8,128)S(1)}, u32[]{:S(2)}, u32[]{:S(2)}) collective-permute-start(f32[5,16,128]{2,1,0:T(8,128)} %get-tuple-element.83), channel_id=1, source_target_pairs={{0,79},{1,64},{2,65},{3,66},{4,67},{5,68},{6,69},{7,70},{8,71},{9,... | collective-permute-start | bytes 122888 | tf_op jit(solution)/shard_map/ppermute | solution.py:26
  186.0 1.4 collective-permute-done.28.a
  188.4 3.6 %shard_map.70 = (f32[8,16,128]{2,1,0:T(8,128)}, f32[16,1,128]{2,1,0:T(1,128)}) custom-call(s32[2]{0:T(128)} %pad_add_fusion.where, f32[8,16,128]{2,1,0:T(8,128)} %get-tuple-element.57.med, f32[8,16,128]{2,1,0:T(8,128)} %copy-done.17, f32[6,16,128]{2,1,0:T(8,128)} %copy-done.27, f32[5,16,128]{2,1,0:T(8,128)} %copy-done.33, ...), custom_call_target="tpu_custom_call" | custom-call | flops 1000000 | bytes 100000 | tf_op jit(solution)/shard_map/pallas_call | solution.py:132
  191.9 13.0 %all_to_all.28.got = f32[16,1,128]{2,1,0:T(1,128)} all-to-all(f32[16,1,128]{2,1,0:T(1,128)} %get-tuple-element.85), channel_id=1, replica_groups=mesh['tm'=8,'space'=16] {'space'}, dimensions={0} | all-to-all | bytes 16384 | tf_op jit(solution)/shard_map/all_to_all | solution.py:30
  204.9 3.3 %shard_map.71 = (f32[16,16,128]{2,1,0:T(8,128)}, f32[10,16,128]{2,1,0:T(8,128)}, f32[9,16,128]{2,1,0:T(8,128)}, f32[6,16,128]{2,1,0:T(8,128)}, f32[5,16,128]{2,1,0:T(8,128)}) custom-call(f32[16,1,128]{2,1,0:T(1,128)} %all_to_all.28.got, f32[64,128]{1,0:T(8,128)} %get-tuple-element.65.ginv_ref.ginv, f32[8192,128]{1,0:T(8,128)} %bitcast.14, ...), custom_call_target="tpu_custom_call" | custom-call | flops 1000000 | bytes 100000 | tf_op jit(solution)/shard_map/pallas_call | solution.py:132
  208.7 4.3 %collective-permute-start.30 = (f32[9,16,128]{2,1,0:T(8,128)}, f32[9,16,128]{2,1,0:T(8,128)S(1)}, u32[]{:S(2)}, u32[]{:S(2)}) collective-permute-start(f32[9,16,128]{2,1,0:T(8,128)} %get-tuple-element.89), channel_id=1, source_target_pairs={{0,15},{1,0},{2,1},{3,2},{4,3},{5,4},{6,5},{7,6},{8,7},{9,8},{10,9... | collective-permute-start | bytes 221192 | tf_op jit(solution)/shard_map/ppermute | solution.py:26
  213.0 5.1 %collective-permute-start.32 = (f32[5,16,128]{2,1,0:T(8,128)}, f32[5,16,128]{2,1,0:T(8,128)S(1)}, u32[]{:S(2)}, u32[]{:S(2)}) collective-permute-start(f32[5,16,128]{2,1,0:T(8,128)} %get-tuple-element.91), channel_id=1, source_target_pairs={{0,14},{1,15},{2,0},{3,1},{4,2},{5,3},{6,4},{7,5},{8,6},{9,7},{10,... | collective-permute-start | bytes 122888 | tf_op jit(solution)/shard_map/ppermute | solution.py:26
  218.1 1.4 collective-permute-done.32.a2
  220.5 4.0 %shard_map.72 = (f32[8,16,128]{2,1,0:T(8,128)}, f32[2,16,128]{2,1,0:T(8,128)}, f32[1,16,128]{2,1,0:T(8,128)}, f32[16,1,128]{2,1,0:T(1,128)}) custom-call(s32[2]{0:T(128)} %pad_add_fusion.where, f32[8,16,128]{2,1,0:T(8,128)} %get-tuple-element.57.med, f32[16,16,128]{2,1,0:T(8,128)} %get-tuple-element.87.center, f32[10,16,128]{2,1,0:T(8,128)} %copy-done.12, ...), custom_call_target="tpu_custom_call" | custom-call | flops 1000000 | bytes 100000 | tf_op jit(solution)/shard_map/pallas_call | solution.py:132
  224.5 6.8 %collective-permute-start.35 = (f32[8,16,128]{2,1,0:T(8,128)}, f32[8,16,128]{2,1,0:T(8,128)S(1)}, u32[]{:S(2)}, u32[]{:S(2)}) collective-permute-start(f32[8,16,128]{2,1,0:T(8,128)} %get-tuple-element.92.final), channel_id=1, source_target_pairs={{0,31},{1,16},{2,17},{3,18},{4,19},{5,20},{6,21},{7,22},{8,23},{9,... | collective-permute-start | bytes 196616 | tf_op jit(solution)/shard_map/ppermute | solution.py:26
  231.3 1.2 collective-permute-start.33
  233.0 5.8 %collective-permute-start.37 = (f32[1,16,128]{2,1,0:T(8,128)}, f32[1,16,128]{2,1,0:T(8,128)S(1)}, u32[]{:S(2)}, u32[]{:S(2)}) collective-permute-start(f32[1,16,128]{2,1,0:T(8,128)} %get-tuple-element.94), channel_id=1, source_target_pairs={{0,30},{1,31},{2,16},{3,17},{4,18},{5,19},{6,20},{7,21},{8,22},{9,... | collective-permute-start | bytes 24584 | tf_op jit(solution)/shard_map/ppermute | solution.py:26
  238.8 10.8 %all_to_all.29.got = f32[16,1,128]{2,1,0:T(1,128)} all-to-all(f32[16,1,128]{2,1,0:T(1,128)} %get-tuple-element.95), channel_id=1, replica_groups=mesh['tm'=8,'space'=16] {'space'}, dimensions={0} | all-to-all | bytes 16384 | tf_op jit(solution)/shard_map/all_to_all | solution.py:30
  250.3 0.6 copy-done.20
  250.9 2.3 shard_map.73
  (109 shorter events, 7.9 us)
Async XLA Ops:
  0.6 4.2 %collective-permute-start = (f32[8,16,128]{2,1,0:T(8,128)}, f32[8,16,128]{2,1,0:T(8,128)S(1)}, u32[]{:S(2)}, u32[]{:S(2)}) collective-permute-start(f32[8,16,128]{2,1,0:T(8,128)} %bitcast.17), channel_id=1, source_target_pairs={{0,16},{1,17},{2,18},{3,19},{4,20},{5,21},{6,22},{7,23},{8,24},{9,... | collective-permute-start | bytes 196616 | tf_op jit(solution)/shard_map/ppermute | solution.py:26
  4.9 0.6 copy-start.5
  7.1 15.0 %collective-permute-start.1 = (f32[15,16,128]{2,1,0:T(8,128)}, f32[15,16,128]{2,1,0:T(8,128)S(1)}, u32[]{:S(2)}, u32[]{:S(2)}) collective-permute-start(f32[15,16,128]{2,1,0:T(8,128)} %get-tuple-element.50), channel_id=1, source_target_pairs={{0,1},{1,2},{2,3},{3,4},{4,5},{5,6},{6,7},{7,8},{8,9},{9,10},{10,1... | collective-permute-start | bytes 368648 | tf_op jit(solution)/shard_map/ppermute | solution.py:26
  8.4 13.7 %collective-permute-start.2 = (f32[15,16,128]{2,1,0:T(8,128)}, f32[15,16,128]{2,1,0:T(8,128)S(1)}, u32[]{:S(2)}, u32[]{:S(2)}) collective-permute-start(f32[15,16,128]{2,1,0:T(8,128)} %get-tuple-element.51), channel_id=1, source_target_pairs={{0,15},{1,0},{2,1},{3,2},{4,3},{5,4},{6,5},{7,6},{8,7},{9,8},{10,9... | collective-permute-start | bytes 368648 | tf_op jit(solution)/shard_map/ppermute | solution.py:26
  13.3 5.0 %collective-permute-start.4 = (f32[7,16,128]{2,1,0:T(8,128)}, f32[7,16,128]{2,1,0:T(8,128)S(1)}, u32[]{:S(2)}, u32[]{:S(2)}) collective-permute-start(f32[7,16,128]{2,1,0:T(8,128)} %get-tuple-element.53), channel_id=1, source_target_pairs={{0,14},{1,15},{2,0},{3,1},{4,2},{5,3},{6,4},{7,5},{8,6},{9,7},{10,... | collective-permute-start | bytes 172040 | tf_op jit(solution)/shard_map/ppermute | solution.py:26
  15.0 7.2 %collective-permute-start.3 = (f32[8,16,128]{2,1,0:T(8,128)}, f32[8,16,128]{2,1,0:T(8,128)S(1)}, u32[]{:S(2)}, u32[]{:S(2)}) collective-permute-start(f32[8,16,128]{2,1,0:T(8,128)} %get-tuple-element.52), channel_id=1, source_target_pairs={{0,2},{1,3},{2,4},{3,5},{4,6},{5,7},{6,8},{7,9},{8,10},{9,11},{10,... | collective-permute-start | bytes 196616 | tf_op jit(solution)/shard_map/ppermute | solution.py:26
  18.4 3.8 %copy-start.4 = (f32[7,16,128]{2,1,0:T(8,128)}, f32[7,16,128]{2,1,0:T(8,128)S(1)}, u32[]{:S(2)}) copy-start(f32[7,16,128]{2,1,0:T(8,128)S(1)} %collective-permute-done.4.a2.ha2) | copy-start | bytes 172036
  22.1 0.7 copy-start
  22.8 0.7 copy-start.1
  25.8 15.0 %collective-permute-start.7 = (f32[8,16,128]{2,1,0:T(8,128)}, f32[8,16,128]{2,1,0:T(8,128)S(1)}, u32[]{:S(2)}, u32[]{:S(2)}) collective-permute-start(f32[8,16,128]{2,1,0:T(8,128)} %get-tuple-element.54.relaxed), channel_id=1, source_target_pairs={{0,31},{1,16},{2,17},{3,18},{4,19},{5,20},{6,21},{7,22},{8,23},{9,... | collective-permute-start | bytes 196616 | tf_op jit(solution)/shard_map/ppermute | solution.py:26
  29.3 11.5 %collective-permute-start.6 = (f32[8,16,128]{2,1,0:T(8,128)}, f32[8,16,128]{2,1,0:T(8,128)S(1)}, u32[]{:S(2)}, u32[]{:S(2)}) collective-permute-start(f32[8,16,128]{2,1,0:T(8,128)} %get-tuple-element.54.relaxed), channel_id=1, source_target_pairs={{0,17},{1,18},{2,19},{3,20},{4,21},{5,22},{6,23},{7,24},{8,25},{9,... | collective-permute-start | bytes 196616 | tf_op jit(solution)/shard_map/ppermute | solution.py:26
  29.9 10.9 %collective-permute-start.5 = (f32[8,16,128]{2,1,0:T(8,128)}, f32[8,16,128]{2,1,0:T(8,128)S(1)}, u32[]{:S(2)}, u32[]{:S(2)}) collective-permute-start(f32[8,16,128]{2,1,0:T(8,128)} %get-tuple-element.54.relaxed), channel_id=1, source_target_pairs={{0,16},{1,17},{2,18},{3,19},{4,20},{5,21},{6,22},{7,23},{8,24},{9,... | collective-permute-start | bytes 196616 | tf_op jit(solution)/shard_map/ppermute | solution.py:26
  32.5 8.3 %collective-permute-start.8 = (f32[6,16,128]{2,1,0:T(8,128)}, f32[6,16,128]{2,1,0:T(8,128)S(1)}, u32[]{:S(2)}, u32[]{:S(2)}) collective-permute-start(f32[6,16,128]{2,1,0:T(8,128)} %get-tuple-element.55), channel_id=1, source_target_pairs={{0,18},{1,19},{2,20},{3,21},{4,22},{5,23},{6,24},{7,25},{8,26},{9,... | collective-permute-start | bytes 147464 | tf_op jit(solution)/shard_map/ppermute | solution.py:26
  33.1 6.9 %collective-permute-start.9 = (f32[5,16,128]{2,1,0:T(8,128)}, f32[5,16,128]{2,1,0:T(8,128)S(1)}, u32[]{:S(2)}, u32[]{:S(2)}) collective-permute-start(f32[5,16,128]{2,1,0:T(8,128)} %get-tuple-element.56), channel_id=1, source_target_pairs={{0,30},{1,31},{2,16},{3,17},{4,18},{5,19},{6,20},{7,21},{8,22},{9,... | collective-permute-start | bytes 122888 | tf_op jit(solution)/shard_map/ppermute | solution.py:26
  39.9 0.9 copy-start.35
  40.8 0.7 copy-start.21
  40.8 0.7 copy-start.22
  41.5 0.6 copy-start.23
  44.5 8.7 %collective-permute-start.10 = (f32[8,16,128]{2,1,0:T(8,128)}, f32[8,16,128]{2,1,0:T(8,128)S(1)}, u32[]{:S(2)}, u32[]{:S(2)}) collective-permute-start(f32[8,16,128]{2,1,0:T(8,128)} %get-tuple-element.58.residue), channel_id=1, source_target_pairs={{0,16},{1,17},{2,18},{3,19},{4,20},{5,21},{6,22},{7,23},{8,24},{9,... | collective-permute-start | bytes 196616 | tf_op jit(solution)/shard_map/ppermute | solution.py:26
  53.2 0.6 copy-start.2
  82.4 15.3 %collective-permute-start.11 = (f32[16,16,128]{2,1,0:T(8,128)}, f32[16,16,128]{2,1,0:T(8,128)S(1)}, u32[]{:S(2)}, u32[]{:S(2)}) collective-permute-start(f32[16,16,128]{2,1,0:T(8,128)} %get-tuple-element.59), channel_id=1, source_target_pairs={{0,16},{1,17},{2,18},{3,19},{4,20},{5,21},{6,22},{7,23},{8,24},{9,... | collective-permute-start | bytes 393224 | tf_op jit(solution)/shard_map/ppermute | solution.py:26
  84.2 13.5 %collective-permute-start.12 = (f32[10,16,128]{2,1,0:T(8,128)}, f32[10,16,128]{2,1,0:T(8,128)S(1)}, u32[]{:S(2)}, u32[]{:S(2)}) collective-permute-start(f32[10,16,128]{2,1,0:T(8,128)} %get-tuple-element.60), channel_id=1, source_target_pairs={{0,17},{1,18},{2,19},{3,20},{4,21},{5,22},{6,23},{7,24},{8,25},{9,... | collective-permute-start | bytes 245768 | tf_op jit(solution)/shard_map/ppermute | solution.py:26
  84.6 13.1 %collective-permute-start.13 = (f32[9,16,128]{2,1,0:T(8,128)}, f32[9,16,128]{2,1,0:T(8,128)S(1)}, u32[]{:S(2)}, u32[]{:S(2)}) collective-permute-start(f32[9,16,128]{2,1,0:T(8,128)} %get-tuple-element.61), channel_id=1, source_target_pairs={{0,31},{1,16},{2,17},{3,18},{4,19},{5,20},{6,21},{7,22},{8,23},{9,... | collective-permute-start | bytes 221192 | tf_op jit(solution)/shard_map/ppermute | solution.py:26
  90.1 7.6 %collective-permute-start.14 = (f32[6,16,128]{2,1,0:T(8,128)}, f32[6,16,128]{2,1,0:T(8,128)S(1)}, u32[]{:S(2)}, u32[]{:S(2)}) collective-permute-start(f32[6,16,128]{2,1,0:T(8,128)} %get-tuple-element.62), channel_id=1, source_target_pairs={{0,18},{1,19},{2,20},{3,21},{4,22},{5,23},{6,24},{7,25},{8,26},{9,... | collective-permute-start | bytes 147464 | tf_op jit(solution)/shard_map/ppermute | solution.py:26
  90.1 5.8 %collective-permute-start.15 = (f32[5,16,128]{2,1,0:T(8,128)}, f32[5,16,128]{2,1,0:T(8,128)S(1)}, u32[]{:S(2)}, u32[]{:S(2)}) collective-permute-start(f32[5,16,128]{2,1,0:T(8,128)} %get-tuple-element.63), channel_id=1, source_target_pairs={{0,30},{1,31},{2,16},{3,17},{4,18},{5,19},{6,20},{7,21},{8,22},{9,... | collective-permute-start | bytes 122888 | tf_op jit(solution)/shard_map/ppermute | solution.py:26
  95.9 1.8 copy-start.30
  97.7 0.6 copy-start.15
  97.7 0.7 copy-start.11
  97.7 0.7 copy-start.8
  117.9 17.4 %collective-permute-start.16 = (f32[16,16,128]{2,1,0:T(8,128)}, f32[16,16,128]{2,1,0:T(8,128)S(1)}, u32[]{:S(2)}, u32[]{:S(2)}) collective-permute-start(f32[16,16,128]{2,1,0:T(8,128)} %get-tuple-element.67), channel_id=1, source_target_pairs={{0,16},{1,17},{2,18},{3,19},{4,20},{5,21},{6,22},{7,23},{8,24},{9,... | collective-permute-start | bytes 393224 | tf_op jit(solution)/shard_map/ppermute | solution.py:26
  120.4 14.9 %collective-permute-start.17 = (f32[10,16,128]{2,1,0:T(8,128)}, f32[10,16,128]{2,1,0:T(8,128)S(1)}, u32[]{:S(2)}, u32[]{:S(2)}) collective-permute-start(f32[10,16,128]{2,1,0:T(8,128)} %get-tuple-element.68), channel_id=1, source_target_pairs={{0,17},{1,18},{2,19},{3,20},{4,21},{5,22},{6,23},{7,24},{8,25},{9,... | collective-permute-start | bytes 245768 | tf_op jit(solution)/shard_map/ppermute | solution.py:26
  120.4 14.9 %collective-permute-start.18 = (f32[9,16,128]{2,1,0:T(8,128)}, f32[9,16,128]{2,1,0:T(8,128)S(1)}, u32[]{:S(2)}, u32[]{:S(2)}) collective-permute-start(f32[9,16,128]{2,1,0:T(8,128)} %get-tuple-element.69), channel_id=1, source_target_pairs={{0,31},{1,16},{2,17},{3,18},{4,19},{5,20},{6,21},{7,22},{8,23},{9,... | collective-permute-start | bytes 221192 | tf_op jit(solution)/shard_map/ppermute | solution.py:26
  127.9 7.3 %collective-permute-start.19 = (f32[6,16,128]{2,1,0:T(8,128)}, f32[6,16,128]{2,1,0:T(8,128)S(1)}, u32[]{:S(2)}, u32[]{:S(2)}) collective-permute-start(f32[6,16,128]{2,1,0:T(8,128)} %get-tuple-element.70), channel_id=1, source_target_pairs={{0,18},{1,19},{2,20},{3,21},{4,22},{5,23},{6,24},{7,25},{8,26},{9,... | collective-permute-start | bytes 147464 | tf_op jit(solution)/shard_map/ppermute | solution.py:26
  127.9 6.8 %collective-permute-start.20 = (f32[5,16,128]{2,1,0:T(8,128)}, f32[5,16,128]{2,1,0:T(8,128)S(1)}, u32[]{:S(2)}, u32[]{:S(2)}) collective-permute-start(f32[5,16,128]{2,1,0:T(8,128)} %get-tuple-element.71), channel_id=1, source_target_pairs={{0,30},{1,31},{2,16},{3,17},{4,18},{5,19},{6,20},{7,21},{8,22},{9,... | collective-permute-start | bytes 122888 | tf_op jit(solution)/shard_map/ppermute | solution.py:26
  135.3 0.6 copy-start.14
  135.3 0.7 copy-start.10
  135.3 0.7 copy-start.7
  156.0 17.6 %collective-permute-start.21 = (f32[16,16,128]{2,1,0:T(8,128)}, f32[16,16,128]{2,1,0:T(8,128)S(1)}, u32[]{:S(2)}, u32[]{:S(2)}) collective-permute-start(f32[16,16,128]{2,1,0:T(8,128)} %get-tuple-element.75), channel_id=1, source_target_pairs={{0,16},{1,17},{2,18},{3,19},{4,20},{5,21},{6,22},{7,23},{8,24},{9,... | collective-permute-start | bytes 393224 | tf_op jit(solution)/shard_map/ppermute | solution.py:26
  158.9 14.7 %collective-permute-start.22 = (f32[10,16,128]{2,1,0:T(8,128)}, f32[10,16,128]{2,1,0:T(8,128)S(1)}, u32[]{:S(2)}, u32[]{:S(2)}) collective-permute-start(f32[10,16,128]{2,1,0:T(8,128)} %get-tuple-element.76), channel_id=1, source_target_pairs={{0,17},{1,18},{2,19},{3,20},{4,21},{5,22},{6,23},{7,24},{8,25},{9,... | collective-permute-start | bytes 245768 | tf_op jit(solution)/shard_map/ppermute | solution.py:26
  159.1 14.5 %collective-permute-start.23 = (f32[9,16,128]{2,1,0:T(8,128)}, f32[9,16,128]{2,1,0:T(8,128)S(1)}, u32[]{:S(2)}, u32[]{:S(2)}) collective-permute-start(f32[9,16,128]{2,1,0:T(8,128)} %get-tuple-element.77), channel_id=1, source_target_pairs={{0,31},{1,16},{2,17},{3,18},{4,19},{5,20},{6,21},{7,22},{8,23},{9,... | collective-permute-start | bytes 221192 | tf_op jit(solution)/shard_map/ppermute | solution.py:26
  166.0 7.6 %collective-permute-start.24 = (f32[6,16,128]{2,1,0:T(8,128)}, f32[6,16,128]{2,1,0:T(8,128)S(1)}, u32[]{:S(2)}, u32[]{:S(2)}) collective-permute-start(f32[6,16,128]{2,1,0:T(8,128)} %get-tuple-element.78), channel_id=1, source_target_pairs={{0,18},{1,19},{2,20},{3,21},{4,22},{5,23},{6,24},{7,25},{8,26},{9,... | collective-permute-start | bytes 147464 | tf_op jit(solution)/shard_map/ppermute | solution.py:26
  166.0 5.5 %collective-permute-start.25 = (f32[5,16,128]{2,1,0:T(8,128)}, f32[5,16,128]{2,1,0:T(8,128)S(1)}, u32[]{:S(2)}, u32[]{:S(2)}) collective-permute-start(f32[5,16,128]{2,1,0:T(8,128)} %get-tuple-element.79), channel_id=1, source_target_pairs={{0,30},{1,31},{2,16},{3,17},{4,18},{5,19},{6,20},{7,21},{8,22},{9,... | collective-permute-start | bytes 122888 | tf_op jit(solution)/shard_map/ppermute | solution.py:26
  171.5 2.1 copy-start.34
  173.6 0.6 copy-start.13
  173.6 0.7 copy-start.9
  173.6 0.7 copy-start.6
  176.7 11.1 %collective-permute-start.26 = (f32[8,16,128]{2,1,0:T(8,128)}, f32[8,16,128]{2,1,0:T(8,128)S(1)}, u32[]{:S(2)}, u32[]{:S(2)}) collective-permute-start(f32[8,16,128]{2,1,0:T(8,128)} %get-tuple-element.81), channel_id=1, source_target_pairs={{0,64},{1,65},{2,66},{3,67},{4,68},{5,69},{6,70},{7,71},{8,72},{9,... | collective-permute-start | bytes 196616 | tf_op jit(solution)/shard_map/ppermute | solution.py:26
  178.8 8.9 %collective-permute-start.27 = (f32[6,16,128]{2,1,0:T(8,128)}, f32[6,16,128]{2,1,0:T(8,128)S(1)}, u32[]{:S(2)}, u32[]{:S(2)}) collective-permute-start(f32[6,16,128]{2,1,0:T(8,128)} %get-tuple-element.82), channel_id=1, source_target_pairs={{0,65},{1,66},{2,67},{3,68},{4,69},{5,70},{6,71},{7,72},{8,73},{9,... | collective-permute-start | bytes 147464 | tf_op jit(solution)/shard_map/ppermute | solution.py:26
  178.9 8.6 %collective-permute-start.28 = (f32[5,16,128]{2,1,0:T(8,128)}, f32[5,16,128]{2,1,0:T(8,128)S(1)}, u32[]{:S(2)}, u32[]{:S(2)}) collective-permute-start(f32[5,16,128]{2,1,0:T(8,128)} %get-tuple-element.83), channel_id=1, source_target_pairs={{0,79},{1,64},{2,65},{3,66},{4,67},{5,68},{6,69},{7,70},{8,71},{9,... | collective-permute-start | bytes 122888 | tf_op jit(solution)/shard_map/ppermute | solution.py:26
  187.7 0.6 copy-start.17
  208.3 11.6 %collective-permute-start.29 = (f32[10,16,128]{2,1,0:T(8,128)}, f32[10,16,128]{2,1,0:T(8,128)S(1)}, u32[]{:S(2)}, u32[]{:S(2)}) collective-permute-start(f32[10,16,128]{2,1,0:T(8,128)} %get-tuple-element.88), channel_id=1, source_target_pairs={{0,1},{1,2},{2,3},{3,4},{4,5},{5,6},{6,7},{7,8},{8,9},{9,10},{10,1... | collective-permute-start | bytes 245768 | tf_op jit(solution)/shard_map/ppermute | solution.py:26
  208.7 11.1 %collective-permute-start.30 = (f32[9,16,128]{2,1,0:T(8,128)}, f32[9,16,128]{2,1,0:T(8,128)S(1)}, u32[]{:S(2)}, u32[]{:S(2)}) collective-permute-start(f32[9,16,128]{2,1,0:T(8,128)} %get-tuple-element.89), channel_id=1, source_target_pairs={{0,15},{1,0},{2,1},{3,2},{4,3},{5,4},{6,5},{7,6},{8,7},{9,8},{10,9... | collective-permute-start | bytes 221192 | tf_op jit(solution)/shard_map/ppermute | solution.py:26
  213.0 6.8 %collective-permute-start.31 = (f32[6,16,128]{2,1,0:T(8,128)}, f32[6,16,128]{2,1,0:T(8,128)S(1)}, u32[]{:S(2)}, u32[]{:S(2)}) collective-permute-start(f32[6,16,128]{2,1,0:T(8,128)} %get-tuple-element.90), channel_id=1, source_target_pairs={{0,2},{1,3},{2,4},{3,5},{4,6},{5,7},{6,8},{7,9},{8,10},{9,11},{10,... | collective-permute-start | bytes 147464 | tf_op jit(solution)/shard_map/ppermute | solution.py:26
  213.0 6.5 %collective-permute-start.32 = (f32[5,16,128]{2,1,0:T(8,128)}, f32[5,16,128]{2,1,0:T(8,128)S(1)}, u32[]{:S(2)}, u32[]{:S(2)}) collective-permute-start(f32[5,16,128]{2,1,0:T(8,128)} %get-tuple-element.91), channel_id=1, source_target_pairs={{0,14},{1,15},{2,0},{3,1},{4,2},{5,3},{6,4},{7,5},{8,6},{9,7},{10,... | collective-permute-start | bytes 122888 | tf_op jit(solution)/shard_map/ppermute | solution.py:26
  219.8 0.6 copy-start.16
  219.8 0.7 copy-start.12
  224.5 25.1 %collective-permute-start.35 = (f32[8,16,128]{2,1,0:T(8,128)}, f32[8,16,128]{2,1,0:T(8,128)S(1)}, u32[]{:S(2)}, u32[]{:S(2)}) collective-permute-start(f32[8,16,128]{2,1,0:T(8,128)} %get-tuple-element.92.final), channel_id=1, source_target_pairs={{0,31},{1,16},{2,17},{3,18},{4,19},{5,20},{6,21},{7,22},{8,23},{9,... | collective-permute-start | bytes 196616 | tf_op jit(solution)/shard_map/ppermute | solution.py:26
  231.3 18.3 %collective-permute-start.34 = (f32[8,16,128]{2,1,0:T(8,128)}, f32[8,16,128]{2,1,0:T(8,128)S(1)}, u32[]{:S(2)}, u32[]{:S(2)}) collective-permute-start(f32[8,16,128]{2,1,0:T(8,128)} %get-tuple-element.92.final), channel_id=1, source_target_pairs={{0,17},{1,18},{2,19},{3,20},{4,21},{5,22},{6,23},{7,24},{8,25},{9,... | collective-permute-start | bytes 196616 | tf_op jit(solution)/shard_map/ppermute | solution.py:26
  231.3 18.3 %collective-permute-start.33 = (f32[8,16,128]{2,1,0:T(8,128)}, f32[8,16,128]{2,1,0:T(8,128)S(1)}, u32[]{:S(2)}, u32[]{:S(2)}) collective-permute-start(f32[8,16,128]{2,1,0:T(8,128)} %get-tuple-element.92.final), channel_id=1, source_target_pairs={{0,16},{1,17},{2,18},{3,19},{4,20},{5,21},{6,22},{7,23},{8,24},{9,... | collective-permute-start | bytes 196616 | tf_op jit(solution)/shard_map/ppermute | solution.py:26
  232.5 17.1 %collective-permute-start.36 = (f32[2,16,128]{2,1,0:T(8,128)}, f32[2,16,128]{2,1,0:T(8,128)S(1)}, u32[]{:S(2)}, u32[]{:S(2)}) collective-permute-start(f32[2,16,128]{2,1,0:T(8,128)} %get-tuple-element.93), channel_id=1, source_target_pairs={{0,18},{1,19},{2,20},{3,21},{4,22},{5,23},{6,24},{7,25},{8,26},{9,... | collective-permute-start | bytes 49160 | tf_op jit(solution)/shard_map/ppermute | solution.py:26
  233.0 16.6 %collective-permute-start.37 = (f32[1,16,128]{2,1,0:T(8,128)}, f32[1,16,128]{2,1,0:T(8,128)S(1)}, u32[]{:S(2)}, u32[]{:S(2)}) collective-permute-start(f32[1,16,128]{2,1,0:T(8,128)} %get-tuple-element.94), channel_id=1, source_target_pairs={{0,30},{1,31},{2,16},{3,17},{4,18},{5,19},{6,20},{7,21},{8,22},{9,... | collective-permute-start | bytes 24584 | tf_op jit(solution)/shard_map/ppermute | solution.py:26
  249.6 0.6 copy-start.18
  249.7 0.6 copy-start.19
  250.3 0.6 copy-start.20
  (12 other events, 7.3 us)

commit v2 on v1

--- a/solution.py
+++ b/solution.py
@@ -127,14 +127,19 @@
     return s >= 1, s < N_SP - 1, s >= 2, s < N_SP - 2
 
 
-def call(kernel, outs, *args, scratch=(), flops=1_000_000):
-    shapes = [jax.ShapeDtypeStruct(shape, F32) for shape in outs]
+def call(kernel, outs, *args, scratch=(), flops=1_000_000, limit=4):
+    shapes = [pltpu.VMEM(shape, F32) for shape in outs]
+    args = [
+        arg if arg.dtype == jnp.int32 else pltpu.with_memory_space_constraint(arg, pltpu.VMEM)
+        for arg in args
+    ]
     return pl.pallas_call(
         kernel,
         out_shape=shapes,
         in_specs=[SMEM if arg.dtype == jnp.int32 else VMEM for arg in args],
         out_specs=[VMEM] * len(shapes),
         scratch_shapes=list(scratch),
+        compiler_params=pltpu.CompilerParams(vmem_limit_bytes=limit * 1024 * 1024),
         cost_estimate=pl.CostEstimate(flops=flops, bytes_accessed=100_000, transcendentals=0),
     )(*args)
 

time: 254 us -> 217 us (0.85)
  Pallas kernels: 57.5 us -> 23.3 us
    pallas_call x15, Pallas kernels: 57.5 us -> 23.3 us  [call(): pl.pallas_call(kernel, out_shape=shapes, in_specs=[SMEM if arg.dtype == j...]
    unnamed x76 -> x21, local copies, waits for them, and re-layouts: 8.48 us -> 7.36 us
where the time goes in v2:
time: 217 us; the launch traced here: 216 us
  starting transfers between devices  99 us (46%)
  blocking collectives  64.5 us (30%)
  Pallas kernels  23.3 us (11%)
  waiting for transfers between devices  21.1 us (10%)
  local copies, waits for them, and re-layouts  7.36 us (3%)
    ppermute x38, starting transfers between devices, hop(): return lax.ppermute(value, ('tm', 'space'), pairs)  99 us
    all_to_all x5, blocking collectives, share(): return lax.all_to_all(copies, 'space', 0, 0, tiled=True)  64.5 us
    pallas_call x15, Pallas kernels, call(): pl.pallas_call(kernel, out_shape=shapes, in_specs=[SMEM if arg.dtype == j...  23.3 us
    ppermute x38, waiting for transfers between devices, hop(): return lax.ppermute(value, ('tm', 'space'), pairs)  21.1 us
    unnamed x21, local copies, waits for them, and re-layouts  7.36 us
  transfers between devices with their start and end apart: 38, of which 15 were waited for; matrix products, arithmetic and copies ran while one was open for 0% of the time, Pallas kernels for 3%

profile of v2, /device:TPU:1, one launch (start us, length us, event | category | flops | bytes accessed | tf_op | source)
XLA Modules:
  0.0 216.2 jit_solution(9174773075849002262)
XLA Ops:
  0.6 2.6 %collective-permute-start = (f32[8,16,128]{2,1,0:T(8,128)}, f32[8,16,128]{2,1,0:T(8,128)S(1)}, u32[]{:S(2)}, u32[]{:S(2)}) collective-permute-start(f32[8,16,128]{2,1,0:T(8,128)} %bitcast.18), channel_id=1, source_target_pairs={{0,16},{1,17},{2,18},{3,19},{4,20},{5,21},{6,22},{7,23},{8,24},{9,... | collective-permute-start | bytes 196616 | tf_op jit(solution)/shard_map/ppermute | solution.py:26
  3.2 1.6 collective-permute-done.g_ref
  4.9 0.8 copy-done.2
  5.7 0.7 copy-done.6
  6.5 1.4 collective-permute-start.1
  7.8 5.0 %collective-permute-start.2 = (f32[15,16,128]{2,1,0:T(8,128)S(1)}, f32[15,16,128]{2,1,0:T(8,128)S(1)}, u32[]{:S(2)}, u32[]{:S(2)}) collective-permute-start(f32[15,16,128]{2,1,0:T(8,128)S(1)} %get-tuple-element.51), channel_id=1, source_target_pairs={{0,15},{1,0},{2,1},{3,2},{4,3},{5,4},{6,5},{7,6},{8,7},{9,8},{10,9... | collective-permute-start | bytes 368648 | tf_op jit(solution)/shard_map/ppermute | solution.py:26
  12.8 1.6 collective-permute-start.4
  14.4 1.4 collective-permute-start.3
  15.9 1.8 collective-permute-done.4.a2.ha2
  17.7 3.7 %collective-permute-done.3.b2.hb2 = f32[8,16,128]{2,1,0:T(8,128)S(1)} collective-permute-done((f32[8,16,128]{2,1,0:T(8,128)S(1)}, f32[8,16,128]{2,1,0:T(8,128)S(1)}, u32[]{:S(2)}, u32[]{:S(2)}) %collective-permute-start.3) | collective-permute-done | bytes 65568 | tf_op jit(solution)/shard_map/ppermute | solution.py:26
  21.4 0.8 copy-done.3
  22.2 0.7 copy-done.7
  22.9 1.1 shard_map.60
  24.0 4.3 %collective-permute-start.7 = (f32[8,16,128]{2,1,0:T(8,128)S(1)}, f32[8,16,128]{2,1,0:T(8,128)S(1)}, u32[]{:S(2)}, u32[]{:S(2)}) collective-permute-start(f32[8,16,128]{2,1,0:T(8,128)S(1)} %get-tuple-element.54.relaxed), channel_id=1, source_target_pairs={{0,31},{1,16},{2,17},{3,18},{4,19},{5,20},{6,21},{7,22},{8,23},{9,... | collective-permute-start | bytes 196616 | tf_op jit(solution)/shard_map/ppermute | solution.py:26
  28.4 2.4 %collective-permute-start.5 = (f32[8,16,128]{2,1,0:T(8,128)S(1)}, f32[8,16,128]{2,1,0:T(8,128)S(1)}, u32[]{:S(2)}, u32[]{:S(2)}) collective-permute-start(f32[8,16,128]{2,1,0:T(8,128)S(1)} %get-tuple-element.54.relaxed), channel_id=1, source_target_pairs={{0,16},{1,17},{2,18},{3,19},{4,20},{5,21},{6,22},{7,23},{8,24},{9,... | collective-permute-start | bytes 196616 | tf_op jit(solution)/shard_map/ppermute | solution.py:26
  30.8 0.6 collective-permute-start.8
  31.4 5.4 %collective-permute-start.9 = (f32[5,16,128]{2,1,0:T(8,128)S(1)}, f32[5,16,128]{2,1,0:T(8,128)S(1)}, u32[]{:S(2)}, u32[]{:S(2)}) collective-permute-start(f32[5,16,128]{2,1,0:T(8,128)S(1)} %get-tuple-element.56), channel_id=1, source_target_pairs={{0,30},{1,31},{2,16},{3,17},{4,18},{5,19},{6,20},{7,21},{8,22},{9,... | collective-permute-start | bytes 122888 | tf_op jit(solution)/shard_map/ppermute | solution.py:26
  36.8 1.1 collective-permute-done.9.a2
  37.9 1.0 collective-permute-done.8.b2
  38.9 0.8 copy-done.4
  39.8 1.1 shard_map.61
  40.9 2.2 %copy-done = f32[1,64,4,2,16,128]{5,4,3,2,1,0:T(8,128)S(1)} copy-done((f32[1,64,4,2,16,128]{5,4,3,2,1,0:T(8,128)S(1)}, f32[1,64,4,2,16,128]{5,4,3,2,1,0:T(8,128)}, u32[]{:S(2)}) %copy-start) | copy-done | bytes 4194328
  43.1 5.8 %shard_map.62.gram = f32[64,128]{1,0:T(8,128)S(1)} custom-call(f32[8192,128]{1,0:T(8,128)S(1)} %bitcast.7), custom_call_target="tpu_custom_call" | custom-call | flops 50000000 | bytes 100000 | tf_op jit(solution)/shard_map/pallas_call | solution.py:136
  49.0 0.4 shard_map.63
  49.4 16.3 %all_to_all.25.got = f32[16,40,128]{2,1,0:T(8,128)S(1)} all-to-all(f32[16,40,128]{2,1,0:T(8,128)S(1)} %shard_map.63), channel_id=1, replica_groups=mesh['tm'=8,'space'=16] {'space'}, dimensions={0} | all-to-all | bytes 655360 | tf_op jit(solution)/shard_map/all_to_all | solution.py:30
  65.7 5.9 %shard_map.64 = (f32[64,128]{1,0:T(8,128)S(1)}, f32[16,16,128]{2,1,0:T(8,128)S(1)}, f32[10,16,128]{2,1,0:T(8,128)S(1)}, f32[9,16,128]{2,1,0:T(8,128)S(1)}, f32[6...) custom-call(f32[16,40,128]{2,1,0:T(8,128)S(1)} %all_to_all.25.got, f32[8192,128]{1,0:T(8,128)S(1)} %bitcast.9, ...), custom_call_target="tpu_custom_call" | custom-call | flops 1000000 | bytes 100000 | tf_op jit(solution)/shard_map/pallas_call | solution.py:136
  71.6 1.8 collective-permute-start.11
  73.8 5.5 %collective-permute-start.13 = (f32[9,16,128]{2,1,0:T(8,128)S(1)}, f32[9,16,128]{2,1,0:T(8,128)S(1)}, u32[]{:S(2)}, u32[]{:S(2)}) collective-permute-start(f32[9,16,128]{2,1,0:T(8,128)S(1)} %get-tuple-element.61), channel_id=1, source_target_pairs={{0,31},{1,16},{2,17},{3,18},{4,19},{5,20},{6,21},{7,22},{8,23},{9,... | collective-permute-start | bytes 221192 | tf_op jit(solution)/shard_map/ppermute | solution.py:26
  79.3 4.4 %collective-permute-start.15 = (f32[5,16,128]{2,1,0:T(8,128)S(1)}, f32[5,16,128]{2,1,0:T(8,128)S(1)}, u32[]{:S(2)}, u32[]{:S(2)}) collective-permute-start(f32[5,16,128]{2,1,0:T(8,128)S(1)} %get-tuple-element.63), channel_id=1, source_target_pairs={{0,30},{1,31},{2,16},{3,17},{4,18},{5,19},{6,20},{7,21},{8,22},{9,... | collective-permute-start | bytes 122888 | tf_op jit(solution)/shard_map/ppermute | solution.py:26
  83.7 1.1 collective-permute-done.15.a2
  84.8 1.9 collective-permute-done.14.b2
  86.7 1.5 shard_map.65
  88.2 12.1 %all_to_all.26.got = f32[16,1,128]{2,1,0:T(1,128)S(1)} all-to-all(f32[16,1,128]{2,1,0:T(1,128)S(1)} %get-tuple-element.64), channel_id=1, replica_groups=mesh['tm'=8,'space'=16] {'space'}, dimensions={0} | all-to-all | bytes 16384 | tf_op jit(solution)/shard_map/all_to_all | solution.py:30
  100.7 2.2 %collective-permute-start.16 = (f32[16,16,128]{2,1,0:T(8,128)S(1)}, f32[16,16,128]{2,1,0:T(8,128)S(1)}, u32[]{:S(2)}, u32[]{:S(2)}) collective-permute-start(f32[16,16,128]{2,1,0:T(8,128)S(1)} %get-tuple-element.67), channel_id=1, source_target_pairs={{0,16},{1,17},{2,18},{3,19},{4,20},{5,21},{6,22},{7,23},{8,24},{9,... | collective-permute-start | bytes 393224 | tf_op jit(solution)/shard_map/ppermute | solution.py:26
  103.0 7.5 %collective-permute-start.18 = (f32[9,16,128]{2,1,0:T(8,128)S(1)}, f32[9,16,128]{2,1,0:T(8,128)S(1)}, u32[]{:S(2)}, u32[]{:S(2)}) collective-permute-start(f32[9,16,128]{2,1,0:T(8,128)S(1)} %get-tuple-element.69), channel_id=1, source_target_pairs={{0,31},{1,16},{2,17},{3,18},{4,19},{5,20},{6,21},{7,22},{8,23},{9,... | collective-permute-start | bytes 221192 | tf_op jit(solution)/shard_map/ppermute | solution.py:26
  110.4 5.4 %collective-permute-start.20 = (f32[5,16,128]{2,1,0:T(8,128)S(1)}, f32[5,16,128]{2,1,0:T(8,128)S(1)}, u32[]{:S(2)}, u32[]{:S(2)}) collective-permute-start(f32[5,16,128]{2,1,0:T(8,128)S(1)} %get-tuple-element.71), channel_id=1, source_target_pairs={{0,30},{1,31},{2,16},{3,17},{4,18},{5,19},{6,20},{7,21},{8,22},{9,... | collective-permute-start | bytes 122888 | tf_op jit(solution)/shard_map/ppermute | solution.py:26
  115.8 1.1 collective-permute-done.20.a2
  116.9 0.6 collective-permute-done.19.b2
  117.6 1.5 shard_map.67
  119.1 12.4 %all_to_all.27.got = f32[16,1,128]{2,1,0:T(1,128)S(1)} all-to-all(f32[16,1,128]{2,1,0:T(1,128)S(1)} %get-tuple-element.73), channel_id=1, replica_groups=mesh['tm'=8,'space'=16] {'space'}, dimensions={0} | all-to-all | bytes 16384 | tf_op jit(solution)/shard_map/all_to_all | solution.py:30
  131.9 3.1 %collective-permute-start.21 = (f32[16,16,128]{2,1,0:T(8,128)S(1)}, f32[16,16,128]{2,1,0:T(8,128)S(1)}, u32[]{:S(2)}, u32[]{:S(2)}) collective-permute-start(f32[16,16,128]{2,1,0:T(8,128)S(1)} %get-tuple-element.75), channel_id=1, source_target_pairs={{0,16},{1,17},{2,18},{3,19},{4,20},{5,21},{6,22},{7,23},{8,24},{9,... | collective-permute-start | bytes 393224 | tf_op jit(solution)/shard_map/ppermute | solution.py:26
  135.1 7.0 %collective-permute-start.23 = (f32[9,16,128]{2,1,0:T(8,128)S(1)}, f32[9,16,128]{2,1,0:T(8,128)S(1)}, u32[]{:S(2)}, u32[]{:S(2)}) collective-permute-start(f32[9,16,128]{2,1,0:T(8,128)S(1)} %get-tuple-element.77), channel_id=1, source_target_pairs={{0,31},{1,16},{2,17},{3,18},{4,19},{5,20},{6,21},{7,22},{8,23},{9,... | collective-permute-start | bytes 221192 | tf_op jit(solution)/shard_map/ppermute | solution.py:26
  142.1 3.2 %collective-permute-start.25 = (f32[5,16,128]{2,1,0:T(8,128)S(1)}, f32[5,16,128]{2,1,0:T(8,128)S(1)}, u32[]{:S(2)}, u32[]{:S(2)}) collective-permute-start(f32[5,16,128]{2,1,0:T(8,128)S(1)} %get-tuple-element.79), channel_id=1, source_target_pairs={{0,30},{1,31},{2,16},{3,17},{4,18},{5,19},{6,20},{7,21},{8,22},{9,... | collective-permute-start | bytes 122888 | tf_op jit(solution)/shard_map/ppermute | solution.py:26
  145.3 2.0 collective-permute-done.25.a2
  147.3 2.2 %collective-permute-done.24.b2 = f32[6,16,128]{2,1,0:T(8,128)S(1)} collective-permute-done((f32[6,16,128]{2,1,0:T(8,128)S(1)}, f32[6,16,128]{2,1,0:T(8,128)S(1)}, u32[]{:S(2)}, u32[]{:S(2)}) %collective-permute-start.24) | collective-permute-done | bytes 49184 | tf_op jit(solution)/shard_map/ppermute | solution.py:26
  149.5 1.1 shard_map.69
  150.7 2.2 %collective-permute-start.26 = (f32[8,16,128]{2,1,0:T(8,128)S(1)}, f32[8,16,128]{2,1,0:T(8,128)S(1)}, u32[]{:S(2)}, u32[]{:S(2)}) collective-permute-start(f32[8,16,128]{2,1,0:T(8,128)S(1)} %get-tuple-element.81), channel_id=1, source_target_pairs={{0,64},{1,65},{2,66},{3,67},{4,68},{5,69},{6,70},{7,71},{8,72},{9,... | collective-permute-start | bytes 196616 | tf_op jit(solution)/shard_map/ppermute | solution.py:26
  152.9 7.2 %collective-permute-start.28 = (f32[5,16,128]{2,1,0:T(8,128)S(1)}, f32[5,16,128]{2,1,0:T(8,128)S(1)}, u32[]{:S(2)}, u32[]{:S(2)}) collective-permute-start(f32[5,16,128]{2,1,0:T(8,128)S(1)} %get-tuple-element.83), channel_id=1, source_target_pairs={{0,79},{1,64},{2,65},{3,66},{4,67},{5,68},{6,69},{7,70},{8,71},{9,... | collective-permute-start | bytes 122888 | tf_op jit(solution)/shard_map/ppermute | solution.py:26
  160.1 1.1 collective-permute-done.28.a
  161.6 1.2 shard_map.70
  162.7 12.8 %all_to_all.28.got = f32[16,1,128]{2,1,0:T(1,128)S(1)} all-to-all(f32[16,1,128]{2,1,0:T(1,128)S(1)} %get-tuple-element.85), channel_id=1, replica_groups=mesh['tm'=8,'space'=16] {'space'}, dimensions={0} | all-to-all | bytes 16384 | tf_op jit(solution)/shard_map/all_to_all | solution.py:30
  175.6 0.4 shard_map.71
  176.3 4.5 %collective-permute-start.30 = (f32[9,16,128]{2,1,0:T(8,128)S(1)}, f32[9,16,128]{2,1,0:T(8,128)S(1)}, u32[]{:S(2)}, u32[]{:S(2)}) collective-permute-start(f32[9,16,128]{2,1,0:T(8,128)S(1)} %get-tuple-element.89), channel_id=1, source_target_pairs={{0,15},{1,0},{2,1},{3,2},{4,3},{5,4},{6,5},{7,6},{8,7},{9,8},{10,9... | collective-permute-start | bytes 221192 | tf_op jit(solution)/shard_map/ppermute | solution.py:26
  180.8 5.1 %collective-permute-start.32 = (f32[5,16,128]{2,1,0:T(8,128)S(1)}, f32[5,16,128]{2,1,0:T(8,128)S(1)}, u32[]{:S(2)}, u32[]{:S(2)}) collective-permute-start(f32[5,16,128]{2,1,0:T(8,128)S(1)} %get-tuple-element.91), channel_id=1, source_target_pairs={{0,14},{1,15},{2,0},{3,1},{4,2},{5,3},{6,4},{7,5},{8,6},{9,7},{10,... | collective-permute-start | bytes 122888 | tf_op jit(solution)/shard_map/ppermute | solution.py:26
  185.9 1.1 collective-permute-done.32.a2
  187.4 1.5 shard_map.72
  188.9 7.0 %collective-permute-start.35 = (f32[8,16,128]{2,1,0:T(8,128)S(1)}, f32[8,16,128]{2,1,0:T(8,128)S(1)}, u32[]{:S(2)}, u32[]{:S(2)}) collective-permute-start(f32[8,16,128]{2,1,0:T(8,128)S(1)} %get-tuple-element.92.final), channel_id=1, source_target_pairs={{0,31},{1,16},{2,17},{3,18},{4,19},{5,20},{6,21},{7,22},{8,23},{9,... | collective-permute-start | bytes 196616 | tf_op jit(solution)/shard_map/ppermute | solution.py:26
  195.9 0.9 collective-permute-start.33
  196.8 0.5 collective-permute-start.36
  197.3 5.9 %collective-permute-start.37 = (f32[1,16,128]{2,1,0:T(8,128)S(1)}, f32[1,16,128]{2,1,0:T(8,128)S(1)}, u32[]{:S(2)}, u32[]{:S(2)}) collective-permute-start(f32[1,16,128]{2,1,0:T(8,128)S(1)} %get-tuple-element.94), channel_id=1, source_target_pairs={{0,30},{1,31},{2,16},{3,17},{4,18},{5,19},{6,20},{7,21},{8,22},{9,... | collective-permute-start | bytes 24584 | tf_op jit(solution)/shard_map/ppermute | solution.py:26
  203.1 10.8 %all_to_all.29.got = f32[16,1,128]{2,1,0:T(1,128)S(1)} all-to-all(f32[16,1,128]{2,1,0:T(1,128)S(1)} %get-tuple-element.95), channel_id=1, replica_groups=mesh['tm'=8,'space'=16] {'space'}, dimensions={0} | all-to-all | bytes 16384 | tf_op jit(solution)/shard_map/all_to_all | solution.py:30
  214.0 1.0 shard_map.73
  215.0 0.5 copy-done.9
  215.5 0.7 copy.6
  (54 shorter events, 2.6 us)
Async XLA Ops:
  0.6 4.2 %collective-permute-start = (f32[8,16,128]{2,1,0:T(8,128)}, f32[8,16,128]{2,1,0:T(8,128)S(1)}, u32[]{:S(2)}, u32[]{:S(2)}) collective-permute-start(f32[8,16,128]{2,1,0:T(8,128)} %bitcast.18), channel_id=1, source_target_pairs={{0,16},{1,17},{2,18},{3,19},{4,20},{5,21},{6,22},{7,23},{8,24},{9,... | collective-permute-start | bytes 196616 | tf_op jit(solution)/shard_map/ppermute | solution.py:26
  4.9 0.8 copy-start.2
  5.7 0.7 copy-start.6
  6.5 14.9 %collective-permute-start.1 = (f32[15,16,128]{2,1,0:T(8,128)S(1)}, f32[15,16,128]{2,1,0:T(8,128)S(1)}, u32[]{:S(2)}, u32[]{:S(2)}) collective-permute-start(f32[15,16,128]{2,1,0:T(8,128)S(1)} %get-tuple-element.50), channel_id=1, source_target_pairs={{0,1},{1,2},{2,3},{3,4},{4,5},{5,6},{6,7},{7,8},{8,9},{9,10},{10,1... | collective-permute-start | bytes 368648 | tf_op jit(solution)/shard_map/ppermute | solution.py:26
  7.8 13.5 %collective-permute-start.2 = (f32[15,16,128]{2,1,0:T(8,128)S(1)}, f32[15,16,128]{2,1,0:T(8,128)S(1)}, u32[]{:S(2)}, u32[]{:S(2)}) collective-permute-start(f32[15,16,128]{2,1,0:T(8,128)S(1)} %get-tuple-element.51), channel_id=1, source_target_pairs={{0,15},{1,0},{2,1},{3,2},{4,3},{5,4},{6,5},{7,6},{8,7},{9,8},{10,9... | collective-permute-start | bytes 368648 | tf_op jit(solution)/shard_map/ppermute | solution.py:26
  12.8 4.8 %collective-permute-start.4 = (f32[7,16,128]{2,1,0:T(8,128)S(1)}, f32[7,16,128]{2,1,0:T(8,128)S(1)}, u32[]{:S(2)}, u32[]{:S(2)}) collective-permute-start(f32[7,16,128]{2,1,0:T(8,128)S(1)} %get-tuple-element.53), channel_id=1, source_target_pairs={{0,14},{1,15},{2,0},{3,1},{4,2},{5,3},{6,4},{7,5},{8,6},{9,7},{10,... | collective-permute-start | bytes 172040 | tf_op jit(solution)/shard_map/ppermute | solution.py:26
  14.4 7.0 %collective-permute-start.3 = (f32[8,16,128]{2,1,0:T(8,128)S(1)}, f32[8,16,128]{2,1,0:T(8,128)S(1)}, u32[]{:S(2)}, u32[]{:S(2)}) collective-permute-start(f32[8,16,128]{2,1,0:T(8,128)S(1)} %get-tuple-element.52), channel_id=1, source_target_pairs={{0,2},{1,3},{2,4},{3,5},{4,6},{5,7},{6,8},{7,9},{8,10},{9,11},{10,... | collective-permute-start | bytes 196616 | tf_op jit(solution)/shard_map/ppermute | solution.py:26
  21.3 0.8 copy-start.3
  22.2 0.7 copy-start.7
  24.0 14.9 %collective-permute-start.7 = (f32[8,16,128]{2,1,0:T(8,128)S(1)}, f32[8,16,128]{2,1,0:T(8,128)S(1)}, u32[]{:S(2)}, u32[]{:S(2)}) collective-permute-start(f32[8,16,128]{2,1,0:T(8,128)S(1)} %get-tuple-element.54.relaxed), channel_id=1, source_target_pairs={{0,31},{1,16},{2,17},{3,18},{4,19},{5,20},{6,21},{7,22},{8,23},{9,... | collective-permute-start | bytes 196616 | tf_op jit(solution)/shard_map/ppermute | solution.py:26
  28.4 10.5 %collective-permute-start.6 = (f32[8,16,128]{2,1,0:T(8,128)S(1)}, f32[8,16,128]{2,1,0:T(8,128)S(1)}, u32[]{:S(2)}, u32[]{:S(2)}) collective-permute-start(f32[8,16,128]{2,1,0:T(8,128)S(1)} %get-tuple-element.54.relaxed), channel_id=1, source_target_pairs={{0,17},{1,18},{2,19},{3,20},{4,21},{5,22},{6,23},{7,24},{8,25},{9,... | collective-permute-start | bytes 196616 | tf_op jit(solution)/shard_map/ppermute | solution.py:26
  28.4 10.5 %collective-permute-start.5 = (f32[8,16,128]{2,1,0:T(8,128)S(1)}, f32[8,16,128]{2,1,0:T(8,128)S(1)}, u32[]{:S(2)}, u32[]{:S(2)}) collective-permute-start(f32[8,16,128]{2,1,0:T(8,128)S(1)} %get-tuple-element.54.relaxed), channel_id=1, source_target_pairs={{0,16},{1,17},{2,18},{3,19},{4,20},{5,21},{6,22},{7,23},{8,24},{9,... | collective-permute-start | bytes 196616 | tf_op jit(solution)/shard_map/ppermute | solution.py:26
  30.8 8.1 %collective-permute-start.8 = (f32[6,16,128]{2,1,0:T(8,128)S(1)}, f32[6,16,128]{2,1,0:T(8,128)S(1)}, u32[]{:S(2)}, u32[]{:S(2)}) collective-permute-start(f32[6,16,128]{2,1,0:T(8,128)S(1)} %get-tuple-element.55), channel_id=1, source_target_pairs={{0,18},{1,19},{2,20},{3,21},{4,22},{5,23},{6,24},{7,25},{8,26},{9,... | collective-permute-start | bytes 147464 | tf_op jit(solution)/shard_map/ppermute | solution.py:26
  31.4 6.5 %collective-permute-start.9 = (f32[5,16,128]{2,1,0:T(8,128)S(1)}, f32[5,16,128]{2,1,0:T(8,128)S(1)}, u32[]{:S(2)}, u32[]{:S(2)}) collective-permute-start(f32[5,16,128]{2,1,0:T(8,128)S(1)} %get-tuple-element.56), channel_id=1, source_target_pairs={{0,30},{1,31},{2,16},{3,17},{4,18},{5,19},{6,20},{7,21},{8,22},{9,... | collective-permute-start | bytes 122888 | tf_op jit(solution)/shard_map/ppermute | solution.py:26
  38.9 0.8 copy-start.4
  40.9 8.1 %collective-permute-start.10 = (f32[8,16,128]{2,1,0:T(8,128)S(1)}, f32[8,16,128]{2,1,0:T(8,128)S(1)}, u32[]{:S(2)}, u32[]{:S(2)}) collective-permute-start(f32[8,16,128]{2,1,0:T(8,128)S(1)} %get-tuple-element.58.residue), channel_id=1, source_target_pairs={{0,16},{1,17},{2,18},{3,19},{4,20},{5,21},{6,22},{7,23},{8,24},{9,... | collective-permute-start | bytes 196616 | tf_op jit(solution)/shard_map/ppermute | solution.py:26
  40.9 2.2 %copy-start = (f32[1,64,4,2,16,128]{5,4,3,2,1,0:T(8,128)S(1)}, f32[1,64,4,2,16,128]{5,4,3,2,1,0:T(8,128)}, u32[]{:S(2)}) copy-start(f32[1,64,4,2,16,128]{5,4,3,2,1,0:T(8,128)} %param.7) | copy-start | bytes 12582916
  48.9 37.8 %copy-start.1 = (f32[1,64,4,2,16,128]{5,4,3,2,1,0:T(8,128)S(1)}, f32[1,64,4,2,16,128]{5,4,3,2,1,0:T(8,128)}, u32[]{:S(2)}) copy-start(f32[1,64,4,2,16,128]{5,4,3,2,1,0:T(8,128)} %param.7) | copy-start | bytes 12582916
  71.6 15.1 %collective-permute-start.11 = (f32[16,16,128]{2,1,0:T(8,128)S(1)}, f32[16,16,128]{2,1,0:T(8,128)S(1)}, u32[]{:S(2)}, u32[]{:S(2)}) collective-permute-start(f32[16,16,128]{2,1,0:T(8,128)S(1)} %get-tuple-element.59), channel_id=1, source_target_pairs={{0,16},{1,17},{2,18},{3,19},{4,20},{5,21},{6,22},{7,23},{8,24},{9,... | collective-permute-start | bytes 393224 | tf_op jit(solution)/shard_map/ppermute | solution.py:26
  73.4 13.3 %collective-permute-start.12 = (f32[10,16,128]{2,1,0:T(8,128)S(1)}, f32[10,16,128]{2,1,0:T(8,128)S(1)}, u32[]{:S(2)}, u32[]{:S(2)}) collective-permute-start(f32[10,16,128]{2,1,0:T(8,128)S(1)} %get-tuple-element.60), channel_id=1, source_target_pairs={{0,17},{1,18},{2,19},{3,20},{4,21},{5,22},{6,23},{7,24},{8,25},{9,... | collective-permute-start | bytes 245768 | tf_op jit(solution)/shard_map/ppermute | solution.py:26
  73.8 12.9 %collective-permute-start.13 = (f32[9,16,128]{2,1,0:T(8,128)S(1)}, f32[9,16,128]{2,1,0:T(8,128)S(1)}, u32[]{:S(2)}, u32[]{:S(2)}) collective-permute-start(f32[9,16,128]{2,1,0:T(8,128)S(1)} %get-tuple-element.61), channel_id=1, source_target_pairs={{0,31},{1,16},{2,17},{3,18},{4,19},{5,20},{6,21},{7,22},{8,23},{9,... | collective-permute-start | bytes 221192 | tf_op jit(solution)/shard_map/ppermute | solution.py:26
  79.3 7.4 %collective-permute-start.14 = (f32[6,16,128]{2,1,0:T(8,128)S(1)}, f32[6,16,128]{2,1,0:T(8,128)S(1)}, u32[]{:S(2)}, u32[]{:S(2)}) collective-permute-start(f32[6,16,128]{2,1,0:T(8,128)S(1)} %get-tuple-element.62), channel_id=1, source_target_pairs={{0,18},{1,19},{2,20},{3,21},{4,22},{5,23},{6,24},{7,25},{8,26},{9,... | collective-permute-start | bytes 147464 | tf_op jit(solution)/shard_map/ppermute | solution.py:26
  79.3 5.5 %collective-permute-start.15 = (f32[5,16,128]{2,1,0:T(8,128)S(1)}, f32[5,16,128]{2,1,0:T(8,128)S(1)}, u32[]{:S(2)}, u32[]{:S(2)}) collective-permute-start(f32[5,16,128]{2,1,0:T(8,128)S(1)} %get-tuple-element.63), channel_id=1, source_target_pairs={{0,30},{1,31},{2,16},{3,17},{4,18},{5,19},{6,20},{7,21},{8,22},{9,... | collective-permute-start | bytes 122888 | tf_op jit(solution)/shard_map/ppermute | solution.py:26
  100.7 16.9 %collective-permute-start.16 = (f32[16,16,128]{2,1,0:T(8,128)S(1)}, f32[16,16,128]{2,1,0:T(8,128)S(1)}, u32[]{:S(2)}, u32[]{:S(2)}) collective-permute-start(f32[16,16,128]{2,1,0:T(8,128)S(1)} %get-tuple-element.67), channel_id=1, source_target_pairs={{0,16},{1,17},{2,18},{3,19},{4,20},{5,21},{6,22},{7,23},{8,24},{9,... | collective-permute-start | bytes 393224 | tf_op jit(solution)/shard_map/ppermute | solution.py:26
  102.9 14.7 %collective-permute-start.17 = (f32[10,16,128]{2,1,0:T(8,128)S(1)}, f32[10,16,128]{2,1,0:T(8,128)S(1)}, u32[]{:S(2)}, u32[]{:S(2)}) collective-permute-start(f32[10,16,128]{2,1,0:T(8,128)S(1)} %get-tuple-element.68), channel_id=1, source_target_pairs={{0,17},{1,18},{2,19},{3,20},{4,21},{5,22},{6,23},{7,24},{8,25},{9,... | collective-permute-start | bytes 245768 | tf_op jit(solution)/shard_map/ppermute | solution.py:26
  103.0 14.6 %collective-permute-start.18 = (f32[9,16,128]{2,1,0:T(8,128)S(1)}, f32[9,16,128]{2,1,0:T(8,128)S(1)}, u32[]{:S(2)}, u32[]{:S(2)}) collective-permute-start(f32[9,16,128]{2,1,0:T(8,128)S(1)} %get-tuple-element.69), channel_id=1, source_target_pairs={{0,31},{1,16},{2,17},{3,18},{4,19},{5,20},{6,21},{7,22},{8,23},{9,... | collective-permute-start | bytes 221192 | tf_op jit(solution)/shard_map/ppermute | solution.py:26
  110.4 7.1 %collective-permute-start.19 = (f32[6,16,128]{2,1,0:T(8,128)S(1)}, f32[6,16,128]{2,1,0:T(8,128)S(1)}, u32[]{:S(2)}, u32[]{:S(2)}) collective-permute-start(f32[6,16,128]{2,1,0:T(8,128)S(1)} %get-tuple-element.70), channel_id=1, source_target_pairs={{0,18},{1,19},{2,20},{3,21},{4,22},{5,23},{6,24},{7,25},{8,26},{9,... | collective-permute-start | bytes 147464 | tf_op jit(solution)/shard_map/ppermute | solution.py:26
  110.4 6.5 %collective-permute-start.20 = (f32[5,16,128]{2,1,0:T(8,128)S(1)}, f32[5,16,128]{2,1,0:T(8,128)S(1)}, u32[]{:S(2)}, u32[]{:S(2)}) collective-permute-start(f32[5,16,128]{2,1,0:T(8,128)S(1)} %get-tuple-element.71), channel_id=1, source_target_pairs={{0,30},{1,31},{2,16},{3,17},{4,18},{5,19},{6,20},{7,21},{8,22},{9,... | collective-permute-start | bytes 122888 | tf_op jit(solution)/shard_map/ppermute | solution.py:26
  131.9 17.7 %collective-permute-start.21 = (f32[16,16,128]{2,1,0:T(8,128)S(1)}, f32[16,16,128]{2,1,0:T(8,128)S(1)}, u32[]{:S(2)}, u32[]{:S(2)}) collective-permute-start(f32[16,16,128]{2,1,0:T(8,128)S(1)} %get-tuple-element.75), channel_id=1, source_target_pairs={{0,16},{1,17},{2,18},{3,19},{4,20},{5,21},{6,22},{7,23},{8,24},{9,... | collective-permute-start | bytes 393224 | tf_op jit(solution)/shard_map/ppermute | solution.py:26
  135.0 14.5 %collective-permute-start.22 = (f32[10,16,128]{2,1,0:T(8,128)S(1)}, f32[10,16,128]{2,1,0:T(8,128)S(1)}, u32[]{:S(2)}, u32[]{:S(2)}) collective-permute-start(f32[10,16,128]{2,1,0:T(8,128)S(1)} %get-tuple-element.76), channel_id=1, source_target_pairs={{0,17},{1,18},{2,19},{3,20},{4,21},{5,22},{6,23},{7,24},{8,25},{9,... | collective-permute-start | bytes 245768 | tf_op jit(solution)/shard_map/ppermute | solution.py:26
  135.1 14.4 %collective-permute-start.23 = (f32[9,16,128]{2,1,0:T(8,128)S(1)}, f32[9,16,128]{2,1,0:T(8,128)S(1)}, u32[]{:S(2)}, u32[]{:S(2)}) collective-permute-start(f32[9,16,128]{2,1,0:T(8,128)S(1)} %get-tuple-element.77), channel_id=1, source_target_pairs={{0,31},{1,16},{2,17},{3,18},{4,19},{5,20},{6,21},{7,22},{8,23},{9,... | collective-permute-start | bytes 221192 | tf_op jit(solution)/shard_map/ppermute | solution.py:26
  142.1 7.4 %collective-permute-start.24 = (f32[6,16,128]{2,1,0:T(8,128)S(1)}, f32[6,16,128]{2,1,0:T(8,128)S(1)}, u32[]{:S(2)}, u32[]{:S(2)}) collective-permute-start(f32[6,16,128]{2,1,0:T(8,128)S(1)} %get-tuple-element.78), channel_id=1, source_target_pairs={{0,18},{1,19},{2,20},{3,21},{4,22},{5,23},{6,24},{7,25},{8,26},{9,... | collective-permute-start | bytes 147464 | tf_op jit(solution)/shard_map/ppermute | solution.py:26
  142.1 5.2 %collective-permute-start.25 = (f32[5,16,128]{2,1,0:T(8,128)S(1)}, f32[5,16,128]{2,1,0:T(8,128)S(1)}, u32[]{:S(2)}, u32[]{:S(2)}) collective-permute-start(f32[5,16,128]{2,1,0:T(8,128)S(1)} %get-tuple-element.79), channel_id=1, source_target_pairs={{0,30},{1,31},{2,16},{3,17},{4,18},{5,19},{6,20},{7,21},{8,22},{9,... | collective-permute-start | bytes 122888 | tf_op jit(solution)/shard_map/ppermute | solution.py:26
  150.7 10.9 %collective-permute-start.26 = (f32[8,16,128]{2,1,0:T(8,128)S(1)}, f32[8,16,128]{2,1,0:T(8,128)S(1)}, u32[]{:S(2)}, u32[]{:S(2)}) collective-permute-start(f32[8,16,128]{2,1,0:T(8,128)S(1)} %get-tuple-element.81), channel_id=1, source_target_pairs={{0,64},{1,65},{2,66},{3,67},{4,68},{5,69},{6,70},{7,71},{8,72},{9,... | collective-permute-start | bytes 196616 | tf_op jit(solution)/shard_map/ppermute | solution.py:26
  152.9 8.7 %collective-permute-start.27 = (f32[6,16,128]{2,1,0:T(8,128)S(1)}, f32[6,16,128]{2,1,0:T(8,128)S(1)}, u32[]{:S(2)}, u32[]{:S(2)}) collective-permute-start(f32[6,16,128]{2,1,0:T(8,128)S(1)} %get-tuple-element.82), channel_id=1, source_target_pairs={{0,65},{1,66},{2,67},{3,68},{4,69},{5,70},{6,71},{7,72},{8,73},{9,... | collective-permute-start | bytes 147464 | tf_op jit(solution)/shard_map/ppermute | solution.py:26
  152.9 8.3 %collective-permute-start.28 = (f32[5,16,128]{2,1,0:T(8,128)S(1)}, f32[5,16,128]{2,1,0:T(8,128)S(1)}, u32[]{:S(2)}, u32[]{:S(2)}) collective-permute-start(f32[5,16,128]{2,1,0:T(8,128)S(1)} %get-tuple-element.83), channel_id=1, source_target_pairs={{0,79},{1,64},{2,65},{3,66},{4,67},{5,68},{6,69},{7,70},{8,71},{9,... | collective-permute-start | bytes 122888 | tf_op jit(solution)/shard_map/ppermute | solution.py:26
  175.6 38.4 %copy-start.5 = (f32[4,2,16,128]{3,2,1,0:T(8,128)S(1)}, f32[4,2,16,128]{3,2,1,0:T(8,128)}, u32[]{:S(2)}) copy-start(f32[4,2,16,128]{3,2,1,0:T(8,128)} %f_ref.7) | copy-start | bytes 196612
  175.6 38.4 %copy-start.8 = (f32[2,16,128]{2,1,0:T(8,128)S(1)}, f32[2,16,128]{2,1,0:T(8,128)}, u32[]{:S(2)}) copy-start(f32[2,16,128]{2,1,0:T(8,128)} %c_ref.7) | copy-start | bytes 49156
  176.0 11.4 %collective-permute-start.29 = (f32[10,16,128]{2,1,0:T(8,128)S(1)}, f32[10,16,128]{2,1,0:T(8,128)S(1)}, u32[]{:S(2)}, u32[]{:S(2)}) collective-permute-start(f32[10,16,128]{2,1,0:T(8,128)S(1)} %get-tuple-element.88), channel_id=1, source_target_pairs={{0,1},{1,2},{2,3},{3,4},{4,5},{5,6},{6,7},{7,8},{8,9},{9,10},{10,1... | collective-permute-start | bytes 245768 | tf_op jit(solution)/shard_map/ppermute | solution.py:26
  176.3 11.1 %collective-permute-start.30 = (f32[9,16,128]{2,1,0:T(8,128)S(1)}, f32[9,16,128]{2,1,0:T(8,128)S(1)}, u32[]{:S(2)}, u32[]{:S(2)}) collective-permute-start(f32[9,16,128]{2,1,0:T(8,128)S(1)} %get-tuple-element.89), channel_id=1, source_target_pairs={{0,15},{1,0},{2,1},{3,2},{4,3},{5,4},{6,5},{7,6},{8,7},{9,8},{10,9... | collective-permute-start | bytes 221192 | tf_op jit(solution)/shard_map/ppermute | solution.py:26
  180.8 6.6 %collective-permute-start.31 = (f32[6,16,128]{2,1,0:T(8,128)S(1)}, f32[6,16,128]{2,1,0:T(8,128)S(1)}, u32[]{:S(2)}, u32[]{:S(2)}) collective-permute-start(f32[6,16,128]{2,1,0:T(8,128)S(1)} %get-tuple-element.90), channel_id=1, source_target_pairs={{0,2},{1,3},{2,4},{3,5},{4,6},{5,7},{6,8},{7,9},{8,10},{9,11},{10,... | collective-permute-start | bytes 147464 | tf_op jit(solution)/shard_map/ppermute | solution.py:26
  180.8 6.2 %collective-permute-start.32 = (f32[5,16,128]{2,1,0:T(8,128)S(1)}, f32[5,16,128]{2,1,0:T(8,128)S(1)}, u32[]{:S(2)}, u32[]{:S(2)}) collective-permute-start(f32[5,16,128]{2,1,0:T(8,128)S(1)} %get-tuple-element.91), channel_id=1, source_target_pairs={{0,14},{1,15},{2,0},{3,1},{4,2},{5,3},{6,4},{7,5},{8,6},{9,7},{10,... | collective-permute-start | bytes 122888 | tf_op jit(solution)/shard_map/ppermute | solution.py:26
  188.9 25.1 %collective-permute-start.35 = (f32[8,16,128]{2,1,0:T(8,128)S(1)}, f32[8,16,128]{2,1,0:T(8,128)S(1)}, u32[]{:S(2)}, u32[]{:S(2)}) collective-permute-start(f32[8,16,128]{2,1,0:T(8,128)S(1)} %get-tuple-element.92.final), channel_id=1, source_target_pairs={{0,31},{1,16},{2,17},{3,18},{4,19},{5,20},{6,21},{7,22},{8,23},{9,... | collective-permute-start | bytes 196616 | tf_op jit(solution)/shard_map/ppermute | solution.py:26
  195.9 18.1 %collective-permute-start.34 = (f32[8,16,128]{2,1,0:T(8,128)S(1)}, f32[8,16,128]{2,1,0:T(8,128)S(1)}, u32[]{:S(2)}, u32[]{:S(2)}) collective-permute-start(f32[8,16,128]{2,1,0:T(8,128)S(1)} %get-tuple-element.92.final), channel_id=1, source_target_pairs={{0,17},{1,18},{2,19},{3,20},{4,21},{5,22},{6,23},{7,24},{8,25},{9,... | collective-permute-start | bytes 196616 | tf_op jit(solution)/shard_map/ppermute | solution.py:26
  195.9 18.1 %collective-permute-start.33 = (f32[8,16,128]{2,1,0:T(8,128)S(1)}, f32[8,16,128]{2,1,0:T(8,128)S(1)}, u32[]{:S(2)}, u32[]{:S(2)}) collective-permute-start(f32[8,16,128]{2,1,0:T(8,128)S(1)} %get-tuple-element.92.final), channel_id=1, source_target_pairs={{0,16},{1,17},{2,18},{3,19},{4,20},{5,21},{6,22},{7,23},{8,24},{9,... | collective-permute-start | bytes 196616 | tf_op jit(solution)/shard_map/ppermute | solution.py:26
  196.8 17.1 %collective-permute-start.36 = (f32[2,16,128]{2,1,0:T(8,128)S(1)}, f32[2,16,128]{2,1,0:T(8,128)S(1)}, u32[]{:S(2)}, u32[]{:S(2)}) collective-permute-start(f32[2,16,128]{2,1,0:T(8,128)S(1)} %get-tuple-element.93), channel_id=1, source_target_pairs={{0,18},{1,19},{2,20},{3,21},{4,22},{5,23},{6,24},{7,25},{8,26},{9,... | collective-permute-start | bytes 49160 | tf_op jit(solution)/shard_map/ppermute | solution.py:26
  197.3 16.6 %collective-permute-start.37 = (f32[1,16,128]{2,1,0:T(8,128)S(1)}, f32[1,16,128]{2,1,0:T(8,128)S(1)}, u32[]{:S(2)}, u32[]{:S(2)}) collective-permute-start(f32[1,16,128]{2,1,0:T(8,128)S(1)} %get-tuple-element.94), channel_id=1, source_target_pairs={{0,30},{1,31},{2,16},{3,17},{4,18},{5,19},{6,20},{7,21},{8,22},{9,... | collective-permute-start | bytes 24584 | tf_op jit(solution)/shard_map/ppermute | solution.py:26
  215.0 0.5 copy-start.9

commit v3 on v2

v3 whole, which is shorter than its diff:
```python
import functools

import jax
import jax.numpy as jnp
from jax import lax
from jax.experimental import pallas as pl
from jax.experimental.pallas import tpu as pltpu
from jax.sharding import PartitionSpec as P

DT = 0.045
N_TM = 8
N_SP = 16
RANK = 64
NX = 16
NY = 128
F32 = jnp.float32
BF16 = jnp.bfloat16
VMEM = pl.BlockSpec(memory_space=pltpu.VMEM)
SMEM = pl.BlockSpec(memory_space=pltpu.SMEM)


def moved(value, by_tm, other):
    pairs = []
    for k in range(N_TM):
        for s in range(N_SP):
            slab = other(s)
            if 0 <= slab < N_SP:
                target = ((k + by_tm) % N_TM) * N_SP + slab
            else:
                target = ((k + (by_tm or 1)) % N_TM) * N_SP + s
            pairs.append((k * N_SP + s, target))
    return lax.ppermute(value, ("tm", "space"), pairs)


def hop(value, by_tm):
    return moved(value, by_tm, lambda s: s)


def trade(value, by_tm, step, first):
    low = 0 if first else 1

    def other(s):
        return s + step if (s // step) % 2 == low else s - step

    return moved(value, by_tm, other)


def share(copies):
    return lax.all_to_all(copies, "space", 0, 0, tiled=True)


def next_x(v):
    row = lax.broadcasted_iota(jnp.int32, v.shape, 1)
    return jnp.where(row < NX - 1, pltpu.roll(v, NX - 1, 1), 0.0)


def prev_x(v):
    row = lax.broadcasted_iota(jnp.int32, v.shape, 1)
    return jnp.where(row > 0, pltpu.roll(v, 1, 1), 0.0)


def next_y(v):
    lane = lax.broadcasted_iota(jnp.int32, v.shape, 2)
    return jnp.where(lane < NY - 1, pltpu.roll(v, NY - 1, 2), 0.0)


def prev_y(v):
    lane = lax.broadcasted_iota(jnp.int32, v.shape, 2)
    return jnp.where(lane > 0, pltpu.roll(v, 1, 2), 0.0)


def cat(*parts):
    parts = [part for part in parts if part.shape[0]]
    return parts[0] if len(parts) == 1 else jnp.concatenate(parts, axis=0)


def only(ok, v):
    return jnp.where(ok, v, jnp.zeros_like(v))


def without_floor(vz, low, ok1, ok2):
    far = max(0, low - 2)
    return cat(only(ok2, vz[:far]), only(ok1, vz[far:low]), vz[low:])


def advance_many(p, vx, vy, vz, c2, h, steps, ok1, ok2, loads=None):
    wx, wy = prev_x(vx), prev_y(vy)
    points = []
    for i in range(steps):
        low = steps - i
        mid = p[1:-1]
        row = lax.broadcasted_iota(jnp.int32, mid.shape, 1)
        lane = lax.broadcasted_iota(jnp.int32, mid.shape, 2)
        vx = vx - h * (next_x(mid) - mid)
        vy = vy - h * (next_y(mid) - mid)
        wx = jnp.where(row > 0, wx - h * (mid - pltpu.roll(mid, 1, 1)), 0.0)
        wy = jnp.where(lane > 0, wy - h * (mid - pltpu.roll(mid, 1, 2)), 0.0)
        vz = vz - h * (p[1:] - p[:-1])
        vz = without_floor(vz, low, ok1, ok2)
        diverge = (vx - wx) + (vy - wy) + (vz[1:] - vz[:-1])
        p = mid - h * c2 * diverge
        if loads is not None:
            p = p + loads[i]
        edge = low - 1
        n = p.shape[0]
        own = slice(edge, n - edge)
        points.append(cat(p[own], vx[own], vy[own], vz[1:][own]))
        vx, vy, wx, wy, c2 = (v[1:-1] for v in (vx, vy, wx, wy, c2))
        vz = vz[1:n]
    return points


def put(ref, at, planes):
    n = planes.shape[0]
    ref[at : at + n] = planes
    return at + n


def put_both(refs, up_first, at, both, up=(), down=()):
    first, second = refs
    for planes in both:
        put(first, at, planes)
        at = put(second, at, planes)
    for rising, falling in zip(up, down):
        put(first, at, jnp.where(up_first, rising, falling))
        at = put(second, at, jnp.where(up_first, falling, rising))
    return at


def put_far(refs, up_first, u, more_up=(), more_down=()):
    up = [u[3:4], u[5:6], *more_up]
    down = [u[2:3], u[4:5], *more_down]
    put_both(refs, up_first, 0, [u[0:2], u[6:8]], up, down)


def below_above(up_first, first, second):
    a, b = first[...], second[...]
    return jnp.where(up_first, b, a), jnp.where(up_first, a, b)


def wide(own, b1, a1, b2, a2, ok):
    ok_b1, ok_a1, ok_b2, ok_a2 = ok
    p = cat(
        only(ok_b2, b2[0:2]), only(ok_b1, b1[0:2]), own[0:2], only(ok_a1, a1[0:2]), only(ok_a2, a2[0:2])
    )
    vx = cat(b2[4:5], b1[2:4], own[2:4], a1[2:4], a2[4:5])
    vy = cat(b2[5:6], b1[4:6], own[4:6], a1[4:6], a2[5:6])
    vz = cat(b2[2:4], b1[6:8], own[6:8], a1[6:8], a2[2:3])
    return p, vx, vy, vz


def flags(where_ref):
    s = where_ref[0]
    return s >= 1, s < N_SP - 1, s >= 2, s < N_SP - 2


def ways(where_ref):
    return where_ref[2] == 0, where_ref[3] == 0


def halo_of(where_ref, near, far):
    up1, up2 = ways(where_ref)
    return *below_above(up1, *near), *below_above(up2, *far)


def call(kernel, outs, *args, scratch=(), flops=1_000_000, limit=4):
    shapes = [pltpu.VMEM(shape, F32) for shape in outs]
    args = [
        arg if arg.dtype == jnp.int32 else pltpu.with_memory_space_constraint(arg, pltpu.VMEM)
        for arg in args
    ]
    return pl.pallas_call(
        kernel,
        out_shape=shapes,
        in_specs=[SMEM if arg.dtype == jnp.int32 else VMEM for arg in args],
        out_specs=[VMEM] * len(shapes),
        scratch_shapes=list(scratch),
        compiler_params=pltpu.CompilerParams(vmem_limit_bytes=limit * 1024 * 1024),
        cost_estimate=pl.CostEstimate(flops=flops, bytes_accessed=100_000, transcendentals=0),
    )(*args)


def stage_kernel(f_ref, c_ref, basis, f_out, c2_out):
    f_out[...] = f_ref[...]
    c2_out[...] = c_ref[...] * c_ref[...]


def pack_kernel(where, g_ref, f_ref, c2_ref, e1, o1, e2, o2):
    up1, up2 = ways(where)
    u = g_ref[...]
    c2 = c2_ref[...]
    put_both((e1, o1), up1, 0, [u, f_ref[0], f_ref[1], c2], [f_ref[2, 1:2]], [f_ref[2, 0:1]])
    put_far((e2, o2), up2, u, [f_ref[0, 1:2], c2[1:2]], [f_ref[0, 0:1], c2[0:1]])


def load_medium(own, b1, a1, b2, a2, ok):
    ok_b1, ok_a1, ok_b2, ok_a2 = ok
    return cat(
        only(ok_b2, b2[7:8]), only(ok_b1, b1[12:14]), own, only(ok_a1, a1[12:14]), only(ok_a2, a2[7:8])
    )


def load_forcing(f_ref, b1, a1, b2, a2, ok):
    ok_b1, ok_a1, ok_b2, ok_a2 = ok
    return [
        cat(
            only(ok_b2, b2[6:7]), only(ok_b1, b1[8:10]), f_ref[0], only(ok_a1, a1[8:10]), only(ok_a2, a2[6:7])
        ),
        cat(only(ok_b1, b1[10:12]), f_ref[1], only(ok_a1, a1[10:12])),
        cat(only(ok_b1, b1[14:15]), f_ref[2], only(ok_a1, a1[14:15])),
        f_ref[3],
    ]


LOADS = [8, 6, 4, 2]


def relax_kernel(where, g_ref, f_ref, c2_ref, e1, o1, e2, o2, out, far_e, far_o, med, loads_out):
    ok = flags(where)
    halo = halo_of(where, (e1, o1), (e2, o2))
    c2 = load_medium(c2_ref[...], *halo, ok)
    loads = load_forcing(f_ref, *halo, ok)
    p, vx, vy, vz = wide(g_ref[...], *halo, ok)
    u = advance_many(p, vx, vy, vz, c2, DT, 4, ok[0], ok[2], loads)[-1]
    out[...] = u
    put_far((far_e, far_o), ways(where)[1], u)
    med[...] = c2
    at = 0
    for load in loads:
        at = put(loads_out, at, load)


def kept_loads(loads_ref):
    starts = [sum(LOADS[:i]) for i in range(4)]
    return [loads_ref[start : start + n] for start, n in zip(starts, LOADS)]


def residue_kernel(where, relaxed, loads_ref, med, e2, o2, e1, o1, own, out):
    ok = flags(where)
    p, vx, vy, vz = wide(own[...], *halo_of(where, (e1, o1), (e2, o2)), ok)
    u = advance_many(p, vx, vy, vz, med[...], DT, 4, ok[0], ok[2], kept_loads(loads_ref))[-1]
    out[...] = u - relaxed[...]


def gram_kernel(parts, basis, *refs):
    before = refs[0] if len(refs) == 3 else None
    out, split = refs[-2:]
    rows = 16

    def step(i, total):
        for j in range(rows):
            values = basis[pl.ds(i * rows + j, RANK, stride=8 * NX), :]
            high = values.astype(BF16)
            rest = values - high.astype(F32)
            middle = rest.astype(BF16)
            low = (rest - middle.astype(F32)).astype(BF16)
            lanes = slice(j * NY, (j + 1) * NY)
            split[0:RANK, lanes] = high
            split[RANK : 2 * RANK, lanes] = middle
            split[2 * RANK : 3 * RANK, lanes] = low
        both = split[...]
        return total + lax.dot_general(
            both, both, (((1,), (1,)), ((), ())), preferred_element_type=F32
        )

    total = lax.fori_loop(*parts, step, jnp.zeros((3 * RANK, 3 * RANK), F32))
    part = total[0:RANK] + total[RANK : 2 * RANK] + total[2 * RANK :]
    gram = part[:, 0:RANK] + part[:, RANK : 2 * RANK] + part[:, 2 * RANK :]
    gram = jnp.concatenate([gram, gram], axis=1)
    out[...] = gram if before is None else gram + before[...]


def inner_products(basis, u, scratch):
    tiles = u.reshape(8 * NX, NY)
    pieces = [tiles[8 * i : 8 * i + 8] for i in range(NX)]
    for r in range(RANK):
        at = r * 8 * NX
        sums = []
        for lane in range(4):
            part = basis[at + 32 * lane : at + 32 * lane + 8, :] * pieces[4 * lane]
            for i in range(1, 4):
                low = at + 32 * lane + 8 * i
                part = part + basis[low : low + 8, :] * pieces[4 * lane + i]
            sums.append(part)
        total = (sums[0] + sums[1]) + (sums[2] + sums[3])
        scratch[r : r + 1, :] = jnp.sum(total, axis=0, keepdims=True)
    column = jnp.sum(scratch[...], axis=1, keepdims=True)
    return to_row(column)


def to_row(column):
    r = lax.broadcasted_iota(jnp.int32, (RANK, NY), 0)
    lane = lax.broadcasted_iota(jnp.int32, (RANK, NY), 1)
    return jnp.sum(jnp.where(r == lane, column, 0.0), axis=0, keepdims=True)


def first_kernel(basis, x_ref, gram, out, scratch):
    row = inner_products(basis, x_ref[...], scratch)
    g = gram[...]
    lane = lax.broadcasted_iota(jnp.int32, (RANK // 2, NY), 1)
    packed = jnp.where(lane < RANK, g[: RANK // 2], g[RANK // 2 :])
    rows = jnp.concatenate([packed, jnp.broadcast_to(row, (8, NY))], axis=0)
    for j in range(N_SP):
        out[j] = rows


def inverse(g):
    lane = lax.broadcasted_iota(jnp.int32, (RANK, NY), 1)
    row = lax.broadcasted_iota(jnp.int32, (RANK, NY), 0)
    work = jnp.where(lane < RANK, g, jnp.where(lane - RANK == row, 1.0, 0.0))
    block = 4
    for start in range(0, RANK, block):
        columns = [
            jnp.broadcast_to(work[:, j : j + 1], (RANK, NY)) for j in range(start, start + block)
        ]
        for i in range(block):
            j = start + i
            reciprocal = 1.0 / columns[i][j : j + 1, :]
            factor = jnp.where(row == j, 0.0, columns[i])
            for later in range(i + 1, block):
                scaled = columns[later][j : j + 1, :] * reciprocal
                columns[later] = columns[later] - factor * scaled
            work = work - factor * (work[j : j + 1, :] * reciprocal)
    diagonal = jnp.sum(jnp.where(lane == row, work, 0.0), axis=1, keepdims=True)
    solved = pltpu.roll(work, RANK, 1) * (1.0 / diagonal)
    return jnp.where(lane < RANK, solved, 0.0)


def project(where, basis, ginv, coef, x, scratch, outs):
    weights = jnp.sum(ginv * coef, axis=1, keepdims=True)
    scratch[...] = jnp.broadcast_to(weights, (RANK, NY))
    total = [jnp.zeros((8, NY), F32) for i in range(NX)]
    for r in range(RANK):
        w = scratch[r : r + 1, :]
        at = r * 8 * NX
        for i in range(NX):
            total[i] = total[i] + w * basis[at + 8 * i : at + 8 * i + 8, :]
    y = jnp.concatenate(total, axis=0).reshape(8, NX, NY)
    z = x - y
    center, e1, o1, e2, o2 = outs
    put(center, 0, y)
    put(center, 8, z)
    up1, up2 = ways(where)
    put_both((e1, o1), up1, 0, [y], [z[1:2], z[7:8]], [z[0:1], z[6:7]])
    put_far((e2, o2), up2, y)


PROJECTED = [(16, NX, NY), (10, NX, NY), (10, NX, NY), (6, NX, NY), (6, NX, NY)]


def first_project_kernel(where, got, basis, x_ref, ginv_ref, *rest):
    outs, scratch = rest[:5], rest[5]
    total = got[0]
    for j in range(1, N_SP):
        total = total + got[j]
    packed = total[: RANK // 2]
    g = jnp.concatenate([packed, pltpu.roll(packed, RANK, 1)], axis=0)
    ginv = inverse(g)
    ginv_ref[...] = ginv
    project(where, basis, ginv, total[RANK // 2 : RANK // 2 + 1], x_ref[...], scratch, outs)


def project_kernel(where, got, ginv_ref, basis, x_ref, *rest):
    outs, scratch = rest[:5], rest[5]
    coef = jnp.sum(got[...], axis=0)
    project(where, basis, ginv_ref[...], coef, x_ref[...], scratch, outs)


def q_of(where, med, e2, o2, e1, o1, center):
    ok = flags(where)
    c2 = med[...]
    y = center[0:8]
    z = center[8:16]
    halo = halo_of(where, (e1, o1), (e2, o2))
    b1, a1 = halo[:2]
    p, vx, vy, vz = wide(y, *halo, ok)
    fine = advance_many(p, vx, vy, vz, c2, DT, 4, ok[0], ok[2])[-1]
    zp = cat(only(ok[0], b1[8:9]), z[0:2], only(ok[1], a1[8:9]))
    zz = cat(b1[9:10], z[6:8])
    coarse = advance_many(zp, z[2:4], z[4:6], zz, c2[3:5], 4 * DT, 1, ok[0], ok[2])[-1]
    return fine + coarse


def put_copies(ref, row):
    for j in range(N_SP):
        ref[j] = row


def level_kernel(where, med, e2, o2, e1, o1, center, acc, basis, u_out, acc_out, row_out, scratch):
    u = q_of(where, med, e2, o2, e1, o1, center)
    u_out[...] = u
    acc_out[...] = acc[...] + u
    put_copies(row_out, inner_products(basis, u, scratch))


def gap_kernel(where, med, e2, o2, e1, o1, center, acc, u_out, acc_out, e_out, o_out):
    u = q_of(where, med, e2, o2, e1, o1, center)
    u_out[...] = u
    acc_out[...] = acc[...] + u
    put_far((e_out, o_out), ways(where)[0], u)


def chain_kernel(where, med, o1, e1, own, acc, basis, x_out, row_out, scratch):
    ok = flags(where)
    b, a = below_above(ways(where)[0], e1, o1)
    p = cat(only(ok[0], b[0:2]), own[0:2], only(ok[1], a[0:2]))
    vx = cat(b[4:5], own[2:4], a[4:5])
    vy = cat(b[5:6], own[4:6], a[5:6])
    vz = cat(b[2:4], own[6:8], a[2:3])
    c2 = med[...]
    moved_on = advance_many(p, vx, vy, vz, c2[2:6], 8 * DT, 2, ok[0], ok[2])[-1]
    chained = (where[1] >= 5) | (where[1] == 0)
    x = acc[...] + only(chained, moved_on)
    x_out[...] = x
    put_copies(row_out, inner_products(basis, x, scratch))


def final_kernel(where, med, e2, o2, e1, o1, center, relaxed, residue, basis, out, e_out, o_out, row_out, scratch):
    u = relaxed[...] + (q_of(where, med, e2, o2, e1, o1, center) + residue[...])
    out[...] = u
    up2 = ways(where)[1]
    put_both((e_out, o_out), up2, 0, [], [u[1:2], u[7:8]], [u[0:1], u[6:7]])
    put_copies(row_out, inner_products(basis, u, scratch))


def sweep_kernel(where, loads_ref, med, final, e2, o2, e1, o1, own, got, ginv, out, coords):
    ok = flags(where)
    loads = [load[1:-1] for load in kept_loads(loads_ref)[:3]]
    b1, a1, b2, a2 = halo_of(where, (e1, o1), (e2, o2))
    u = own[...]
    p = cat(
        only(ok[2], b2[0:1]), only(ok[0], b1[0:2]), u[0:2], only(ok[1], a1[0:2]), only(ok[3], a2[0:1])
    )
    vx = cat(b1[2:4], u[2:4], a1[2:4])
    vy = cat(b1[4:6], u[4:6], a1[4:6])
    vz = cat(b2[1:2], b1[6:8], u[6:8], a1[6:8])
    points = advance_many(p, vx, vy, vz, med[1:7], DT, 3, ok[0], ok[2], loads)
    for i in range(3):
        out[i] = points[i]
    out[3] = final[...]
    coef = jnp.sum(got[...], axis=0)
    coords[...] = to_row(jnp.sum(ginv[...] * coef, axis=1, keepdims=True))


def body(speed, forcing, guess, basis):
    slab, block = lax.axis_index("space"), lax.axis_index("tm")
    where = jnp.stack([slab, block, slab % 2, slab // 2 % 2]).astype(jnp.int32)
    columns = basis.reshape(RANK * 8 * NX, NY)
    state = (8, NX, NY)
    table = [pltpu.VMEM((RANK, NY), F32)]
    split = [pltpu.VMEM((3 * RANK, 16 * NY), BF16)]
    copies = (N_SP, 1, NY)
    far = [(6, NX, NY), (6, NX, NY)]

    def traded(near, distant, center, by_tm):
        result = [
            trade(distant[1], by_tm, 2, False),
            trade(distant[0], by_tm, 2, True),
            trade(near[1], by_tm, 1, False),
            trade(near[0], by_tm, 1, True),
        ]
        result = [result[1], result[0], result[3], result[2]]
        return result + ([hop(center, by_tm)] if by_tm else [])

    start = hop(guess.reshape(state), 1)
    load, c2 = call(stage_kernel, [(4, 2, NX, NY), (2, NX, NY)], forcing, speed, columns)
    e1, o1, e2, o2 = call(
        pack_kernel,
        [(15, NX, NY), (15, NX, NY), (8, NX, NY), (8, NX, NY)],
        where,
        start,
        load,
        c2,
    )
    e2, o2, e1, o1 = traded((e1, o1), (e2, o2), None, 0)
    (gram,) = call(
        functools.partial(gram_kernel, (0, 4)), [(RANK, NY)], columns, scratch=split, flops=50_000_000
    )
    relaxed, e, o, med, loads = call(
        relax_kernel,
        [state, *far, (8, NX, NY), (sum(LOADS), NX, NY)],
        where,
        start,
        load,
        c2,
        e1,
        o1,
        e2,
        o2,
    )
    near = traded((relaxed, relaxed), (e, o), relaxed, 1)
    (residue,) = call(residue_kernel, [state], where, relaxed, loads, med, *near)
    x = hop(residue, 1)
    (gram,) = call(
        functools.partial(gram_kernel, (4, 8)), [(RANK, NY)], columns, gram, scratch=split, flops=50_000_000
    )
    (rows,) = call(first_kernel, [(N_SP, RANK // 2 + 8, NY)], columns, x, gram, scratch=table)
    ginv, *packed = call(
        first_project_kernel, [(RANK, NY), *PROJECTED], where, share(rows), columns, x, scratch=table
    )

    def exchanged(packed, by_tm):
        center, e1, o1, e2, o2 = packed
        result = traded((e1, o1), (e2, o2), center, by_tm)
        return result if by_tm else result + [center]

    acc = x
    for level in range(2):
        u, acc, rows = call(
            level_kernel, [state, state, copies], where, med, *exchanged(packed, 1), acc, columns, scratch=table
        )
        packed = call(project_kernel, PROJECTED, where, share(rows), ginv, columns, u, scratch=table)
    gap, acc, e, o = call(gap_kernel, [state, state, *far], where, med, *exchanged(packed, 1), acc)
    o = trade(o, 4, 1, False)
    e = trade(e, 4, 1, True)
    x, rows = call(
        chain_kernel, [state, copies], where, med, o, e, hop(gap, 4), acc, columns, scratch=table
    )
    packed = call(project_kernel, PROJECTED, where, share(rows), ginv, columns, x, scratch=table)
    final, e, o, rows = call(
        final_kernel,
        [state, (2, NX, NY), (2, NX, NY), copies],
        where,
        med,
        *exchanged(packed, 0),
        relaxed,
        residue,
        columns,
        scratch=table,
    )
    got = share(rows)
    near = traded((final, final), (e, o), final, 1)
    states, coords = call(
        sweep_kernel, [(4, 8, NX, NY), (1, NY)], where, loads, med, final, *near, got, ginv
    )
    return states.reshape(4, 4, 2, NX, NY), coords[:, :RANK]


def solution(mesh):
    placed = (
        P("space", None, None),
        P("tm", "space", None, None),
        P("tm", None, "space", None, None),
        P("tm", None, None, "space", None, None),
    )
    return jax.shard_map(
        body,
        mesh=mesh,
        in_specs=placed,
        out_specs=(P("tm", None, "space", None, None), P("tm", None)),
        check_vma=False,
    )
```

time: 217 us -> 184 us (0.85)
  starting transfers between devices: 99 us -> 70.7 us
  waiting for transfers between devices: 21.1 us -> 17.3 us
  local copies, waits for them, and re-layouts: 7.36 us -> 4.95 us
    ppermute x38, starting transfers between devices: 99 us -> 70.7 us  [moved(): return lax.ppermute(value, ('tm', 'space'), pairs)]
    ppermute x38, waiting for transfers between devices: 21.1 us -> 17.3 us  [moved(): return lax.ppermute(value, ('tm', 'space'), pairs)]
    unnamed x21 -> x11, local copies, waits for them, and re-layouts: 7.36 us -> 4.95 us
    pallas_call x15 -> x17, Pallas kernels: 23.3 us -> 21.5 us  [call(): pl.pallas_call(kernel, out_shape=shapes, in_specs=[SMEM if arg.dtype == j...]
  transfers between devices with their start and end apart: 38 -> 38, of which waited for: 15 -> 9; matrix products, arithmetic and copies ran while one was open for 0% -> 0% of each run, Pallas kernels for 3% -> 3%
where the time goes in v3:
time: 184 us; the launch traced here: 182 us
  starting transfers between devices  70.7 us (38%)
  blocking collectives  66.4 us (36%)
  Pallas kernels  21.5 us (12%)
  waiting for transfers between devices  17.3 us (9%)
  local copies, waits for them, and re-layouts  4.95 us (3%)
    ppermute x38, starting transfers between devices, moved(): return lax.ppermute(value, ('tm', 'space'), pairs)  70.7 us
    all_to_all x5, blocking collectives, share(): return lax.all_to_all(copies, 'space', 0, 0, tiled=True)  66.4 us
    pallas_call x17, Pallas kernels, call(): pl.pallas_call(kernel, out_shape=shapes, in_specs=[SMEM if arg.dtype == j...  21.5 us
    ppermute x38, waiting for transfers between devices, moved(): return lax.ppermute(value, ('tm', 'space'), pairs)  17.3 us
    unnamed x11, local copies, waits for them, and re-layouts  4.95 us
  transfers between devices with their start and end apart: 38, of which 9 were waited for; matrix products, arithmetic and copies ran while one was open for 0% of the time, Pallas kernels for 3%

profile of v3, /device:TPU:1, one launch (start us, length us, event | category | flops | bytes accessed | tf_op | source)
XLA Modules:
  0.0 181.8 jit_solution(15154054776698839645)
XLA Ops:
  0.6 2.6 %collective-permute-start = (f32[8,16,128]{2,1,0:T(8,128)}, f32[8,16,128]{2,1,0:T(8,128)S(1)}, u32[]{:S(2)}, u32[]{:S(2)}) collective-permute-start(f32[8,16,128]{2,1,0:T(8,128)} %bitcast.22), channel_id=1, source_target_pairs={{0,16},{1,17},{2,18},{3,19},{4,20},{5,21},{6,22},{7,23},{8,24},{9,... | collective-permute-start | bytes 196616 | tf_op jit(solution)/shard_map/ppermute | solution.py:32
  3.2 2.2 %copy-done = f32[1,64,4,2,16,128]{5,4,3,2,1,0:T(8,128)S(1)} copy-done((f32[1,64,4,2,16,128]{5,4,3,2,1,0:T(8,128)S(1)}, f32[1,64,4,2,16,128]{5,4,3,2,1,0:T(8,128)}, u32[]{:S(2)}) %copy-start) | copy-done | bytes 4194328
  5.4 0.8 copy-done.2
  6.3 0.7 copy-done.3
  7.1 0.6 shard_map.60
  7.6 1.4 collective-permute-start.1
  9.4 2.3 %collective-permute-start.3 = (f32[8,16,128]{2,1,0:T(8,128)S(1)}, f32[8,16,128]{2,1,0:T(8,128)S(1)}, u32[]{:S(2)}, u32[]{:S(2)}) collective-permute-start(f32[8,16,128]{2,1,0:T(8,128)S(1)} %get-tuple-element.56), channel_id=1, source_target_pairs={{0,2},{1,3},{2,0},{3,1},{4,6},{5,7},{6,4},{7,5},{8,10},{9,11},{10,... | collective-permute-start | bytes 196616 | tf_op jit(solution)/shard_map/ppermute | solution.py:32
  11.6 0.6 collective-permute-start.4
  12.3 4.0 %collective-permute-done.3.e2 = f32[8,16,128]{2,1,0:T(8,128)S(1)} collective-permute-done((f32[8,16,128]{2,1,0:T(8,128)S(1)}, f32[8,16,128]{2,1,0:T(8,128)S(1)}, u32[]{:S(2)}, u32[]{:S(2)}) %collective-permute-start.3) | collective-permute-done | bytes 65568 | tf_op jit(solution)/shard_map/ppermute | solution.py:32
  16.3 0.9 shard_map.61
  17.2 1.1 collective-permute-start.9
  18.3 0.4 collective-permute-start.8
  18.7 4.4 %collective-permute-start.7 = (f32[8,16,128]{2,1,0:T(8,128)S(1)}, f32[8,16,128]{2,1,0:T(8,128)S(1)}, u32[]{:S(2)}, u32[]{:S(2)}) collective-permute-start(f32[8,16,128]{2,1,0:T(8,128)S(1)} %get-tuple-element.60.relaxed), channel_id=1, source_target_pairs={{0,17},{1,16},{2,19},{3,18},{4,21},{5,20},{6,23},{7,22},{8,25},{9,... | collective-permute-start | bytes 196616 | tf_op jit(solution)/shard_map/ppermute | solution.py:32
  23.1 4.5 %collective-permute-start.5 = (f32[6,16,128]{2,1,0:T(8,128)S(1)}, f32[6,16,128]{2,1,0:T(8,128)S(1)}, u32[]{:S(2)}, u32[]{:S(2)}) collective-permute-start(f32[6,16,128]{2,1,0:T(8,128)S(1)} %get-tuple-element.61), channel_id=1, source_target_pairs={{0,18},{1,19},{2,16},{3,17},{4,22},{5,23},{6,20},{7,21},{8,26},{9,... | collective-permute-start | bytes 147464 | tf_op jit(solution)/shard_map/ppermute | solution.py:32
  27.6 0.7 collective-permute-start.6
  28.3 0.6 collective-permute-done.5.e2
  28.9 0.6 collective-permute-done.6.o2
  29.5 0.9 shard_map.62.residue
  30.4 2.4 %collective-permute-start.10 = (f32[8,16,128]{2,1,0:T(8,128)S(1)}, f32[8,16,128]{2,1,0:T(8,128)S(1)}, u32[]{:S(2)}, u32[]{:S(2)}) collective-permute-start(f32[8,16,128]{2,1,0:T(8,128)S(1)} %shard_map.62.residue), channel_id=1, source_target_pairs={{0,16},{1,17},{2,18},{3,19},{4,20},{5,21},{6,22},{7,23},{8,24},{9,... | collective-permute-start | bytes 196616 | tf_op jit(solution)/shard_map/ppermute | solution.py:32
  32.7 3.0 %shard_map.63.refs_0_ = f32[64,128]{1,0:T(8,128)S(1)} custom-call(f32[8192,128]{1,0:T(8,128)S(1)} %bitcast.10), custom_call_target="tpu_custom_call" | custom-call | flops 50000000 | bytes 100000 | tf_op jit(solution)/shard_map/pallas_call | solution.py:172
  35.8 3.0 %shard_map.64.gram = f32[64,128]{1,0:T(8,128)S(1)} custom-call(f32[8192,128]{1,0:T(8,128)S(1)} %bitcast.11, f32[64,128]{1,0:T(8,128)S(1)} %shard_map.63.refs_0_), custom_call_target="tpu_custom_call" | custom-call | flops 50000000 | bytes 100000 | tf_op jit(solution)/shard_map/pallas_call | solution.py:172
  38.8 0.4 shard_map.65
  39.3 15.9 %all_to_all.25.got = f32[16,40,128]{2,1,0:T(8,128)S(1)} all-to-all(f32[16,40,128]{2,1,0:T(8,128)S(1)} %shard_map.65), channel_id=1, replica_groups=mesh['tm'=8,'space'=16] {'space'}, dimensions={0} | all-to-all | bytes 655360 | tf_op jit(solution)/shard_map/all_to_all | solution.py:49
  55.2 3.2 %shard_map.66 = (f32[64,128]{1,0:T(8,128)S(1)}, f32[16,16,128]{2,1,0:T(8,128)S(1)}, f32[10,16,128]{2,1,0:T(8,128)S(1)}, f32[10,16,128]{2,1,0:T(8,128)S(1)}, f32[...) custom-call(s32[4]{0:T(128)S(1)} %pad_add_fusion.where, f32[16,40,128]{2,1,0:T(8,128)S(1)} %all_to_all.25.got, ...), custom_call_target="tpu_custom_call" | custom-call | flops 1000000 | bytes 100000 | tf_op jit(solution)/shard_map/pallas_call | solution.py:172
  58.4 2.7 %collective-permute-start.15 = (f32[16,16,128]{2,1,0:T(8,128)S(1)}, f32[16,16,128]{2,1,0:T(8,128)S(1)}, u32[]{:S(2)}, u32[]{:S(2)}) collective-permute-start(f32[16,16,128]{2,1,0:T(8,128)S(1)} %get-tuple-element.67), channel_id=1, source_target_pairs={{0,16},{1,17},{2,18},{3,19},{4,20},{5,21},{6,22},{7,23},{8,24},{9,... | collective-permute-start | bytes 393224 | tf_op jit(solution)/shard_map/ppermute | solution.py:32
  61.3 1.7 collective-permute-start.14
  63.0 2.5 %collective-permute-start.11 = (f32[6,16,128]{2,1,0:T(8,128)S(1)}, f32[6,16,128]{2,1,0:T(8,128)S(1)}, u32[]{:S(2)}, u32[]{:S(2)}) collective-permute-start(f32[6,16,128]{2,1,0:T(8,128)S(1)} %get-tuple-element.63), channel_id=1, source_target_pairs={{0,18},{1,19},{2,16},{3,17},{4,22},{5,23},{6,20},{7,21},{8,26},{9,... | collective-permute-start | bytes 147464 | tf_op jit(solution)/shard_map/ppermute | solution.py:32
  65.5 0.6 collective-permute-start.12
  66.1 1.9 %collective-permute-done.11.e2 = f32[6,16,128]{2,1,0:T(8,128)S(1)} collective-permute-done((f32[6,16,128]{2,1,0:T(8,128)S(1)}, f32[6,16,128]{2,1,0:T(8,128)S(1)}, u32[]{:S(2)}, u32[]{:S(2)}) %collective-permute-start.11) | collective-permute-done | bytes 49184 | tf_op jit(solution)/shard_map/ppermute | solution.py:32
  68.1 1.3 shard_map.67
  69.4 13.3 %all_to_all.26.got = f32[16,1,128]{2,1,0:T(1,128)S(1)} all-to-all(f32[16,1,128]{2,1,0:T(1,128)S(1)} %get-tuple-element.68), channel_id=1, replica_groups=mesh['tm'=8,'space'=16] {'space'}, dimensions={0} | all-to-all | bytes 16384 | tf_op jit(solution)/shard_map/all_to_all | solution.py:49
  82.6 0.9 shard_map.68
  83.6 2.8 %collective-permute-start.20 = (f32[16,16,128]{2,1,0:T(8,128)S(1)}, f32[16,16,128]{2,1,0:T(8,128)S(1)}, u32[]{:S(2)}, u32[]{:S(2)}) collective-permute-start(f32[16,16,128]{2,1,0:T(8,128)S(1)} %get-tuple-element.75), channel_id=1, source_target_pairs={{0,16},{1,17},{2,18},{3,19},{4,20},{5,21},{6,22},{7,23},{8,24},{9,... | collective-permute-start | bytes 393224 | tf_op jit(solution)/shard_map/ppermute | solution.py:32
  86.4 2.1 %collective-permute-start.19 = (f32[10,16,128]{2,1,0:T(8,128)S(1)}, f32[10,16,128]{2,1,0:T(8,128)S(1)}, u32[]{:S(2)}, u32[]{:S(2)}) collective-permute-start(f32[10,16,128]{2,1,0:T(8,128)S(1)} %get-tuple-element.74), channel_id=1, source_target_pairs={{0,16},{1,18},{2,17},{3,20},{4,19},{5,22},{6,21},{7,24},{8,23},{9,... | collective-permute-start | bytes 245768 | tf_op jit(solution)/shard_map/ppermute | solution.py:32
  88.5 2.5 %collective-permute-start.16 = (f32[6,16,128]{2,1,0:T(8,128)S(1)}, f32[6,16,128]{2,1,0:T(8,128)S(1)}, u32[]{:S(2)}, u32[]{:S(2)}) collective-permute-start(f32[6,16,128]{2,1,0:T(8,128)S(1)} %get-tuple-element.71), channel_id=1, source_target_pairs={{0,18},{1,19},{2,16},{3,17},{4,22},{5,23},{6,20},{7,21},{8,26},{9,... | collective-permute-start | bytes 147464 | tf_op jit(solution)/shard_map/ppermute | solution.py:32
  91.0 1.0 collective-permute-start.17
  92.0 2.7 %collective-permute-done.16.e2 = f32[6,16,128]{2,1,0:T(8,128)S(1)} collective-permute-done((f32[6,16,128]{2,1,0:T(8,128)S(1)}, f32[6,16,128]{2,1,0:T(8,128)S(1)}, u32[]{:S(2)}, u32[]{:S(2)}) %collective-permute-start.16) | collective-permute-done | bytes 49184 | tf_op jit(solution)/shard_map/ppermute | solution.py:32
  94.8 1.3 shard_map.69
  96.0 12.4 %all_to_all.27.got = f32[16,1,128]{2,1,0:T(1,128)S(1)} all-to-all(f32[16,1,128]{2,1,0:T(1,128)S(1)} %get-tuple-element.77), channel_id=1, replica_groups=mesh['tm'=8,'space'=16] {'space'}, dimensions={0} | all-to-all | bytes 16384 | tf_op jit(solution)/shard_map/all_to_all | solution.py:49
  108.4 0.9 shard_map.70
  109.4 3.2 %collective-permute-start.25 = (f32[16,16,128]{2,1,0:T(8,128)S(1)}, f32[16,16,128]{2,1,0:T(8,128)S(1)}, u32[]{:S(2)}, u32[]{:S(2)}) collective-permute-start(f32[16,16,128]{2,1,0:T(8,128)S(1)} %get-tuple-element.83), channel_id=1, source_target_pairs={{0,16},{1,17},{2,18},{3,19},{4,20},{5,21},{6,22},{7,23},{8,24},{9,... | collective-permute-start | bytes 393224 | tf_op jit(solution)/shard_map/ppermute | solution.py:32
  112.7 3.0 %collective-permute-start.24 = (f32[10,16,128]{2,1,0:T(8,128)S(1)}, f32[10,16,128]{2,1,0:T(8,128)S(1)}, u32[]{:S(2)}, u32[]{:S(2)}) collective-permute-start(f32[10,16,128]{2,1,0:T(8,128)S(1)} %get-tuple-element.82), channel_id=1, source_target_pairs={{0,16},{1,18},{2,17},{3,20},{4,19},{5,22},{6,21},{7,24},{8,23},{9,... | collective-permute-start | bytes 245768 | tf_op jit(solution)/shard_map/ppermute | solution.py:32
  115.7 2.5 %collective-permute-start.21 = (f32[6,16,128]{2,1,0:T(8,128)S(1)}, f32[6,16,128]{2,1,0:T(8,128)S(1)}, u32[]{:S(2)}, u32[]{:S(2)}) collective-permute-start(f32[6,16,128]{2,1,0:T(8,128)S(1)} %get-tuple-element.79), channel_id=1, source_target_pairs={{0,18},{1,19},{2,16},{3,17},{4,22},{5,23},{6,20},{7,21},{8,26},{9,... | collective-permute-start | bytes 147464 | tf_op jit(solution)/shard_map/ppermute | solution.py:32
  118.2 3.0 %collective-permute-done.21.e2 = f32[6,16,128]{2,1,0:T(8,128)S(1)} collective-permute-done((f32[6,16,128]{2,1,0:T(8,128)S(1)}, f32[6,16,128]{2,1,0:T(8,128)S(1)}, u32[]{:S(2)}, u32[]{:S(2)}) %collective-permute-start.21) | collective-permute-done | bytes 49184 | tf_op jit(solution)/shard_map/ppermute | solution.py:32
  121.2 0.9 shard_map.71
  122.1 1.6 collective-permute-start.28
  123.7 1.5 collective-permute-start.26
  125.2 4.2 %collective-permute-start.27 = (f32[6,16,128]{2,1,0:T(8,128)S(1)}, f32[6,16,128]{2,1,0:T(8,128)S(1)}, u32[]{:S(2)}, u32[]{:S(2)}) collective-permute-start(f32[6,16,128]{2,1,0:T(8,128)S(1)} %get-tuple-element.86), channel_id=1, source_target_pairs={{0,65},{1,64},{2,67},{3,66},{4,69},{5,68},{6,71},{7,70},{8,73},{9,... | collective-permute-start | bytes 147464 | tf_op jit(solution)/shard_map/ppermute | solution.py:32
  129.4 2.0 %collective-permute-done.27.e1 = f32[6,16,128]{2,1,0:T(8,128)S(1)} collective-permute-done((f32[6,16,128]{2,1,0:T(8,128)S(1)}, f32[6,16,128]{2,1,0:T(8,128)S(1)}, u32[]{:S(2)}, u32[]{:S(2)}) %collective-permute-start.27) | collective-permute-done | bytes 49184 | tf_op jit(solution)/shard_map/ppermute | solution.py:32
  131.4 1.1 shard_map.72
  132.4 14.1 %all_to_all.28.got = f32[16,1,128]{2,1,0:T(1,128)S(1)} all-to-all(f32[16,1,128]{2,1,0:T(1,128)S(1)} %get-tuple-element.89), channel_id=1, replica_groups=mesh['tm'=8,'space'=16] {'space'}, dimensions={0} | all-to-all | bytes 16384 | tf_op jit(solution)/shard_map/all_to_all | solution.py:49
  146.6 0.9 shard_map.73
  147.9 3.8 %collective-permute-start.32 = (f32[10,16,128]{2,1,0:T(8,128)S(1)}, f32[10,16,128]{2,1,0:T(8,128)S(1)}, u32[]{:S(2)}, u32[]{:S(2)}) collective-permute-start(f32[10,16,128]{2,1,0:T(8,128)S(1)} %get-tuple-element.94), channel_id=1, source_target_pairs={{0,16},{1,2},{2,1},{3,4},{4,3},{5,6},{6,5},{7,8},{8,7},{9,10},{10,... | collective-permute-start | bytes 245768 | tf_op jit(solution)/shard_map/ppermute | solution.py:32
  151.7 3.5 %collective-permute-start.30 = (f32[6,16,128]{2,1,0:T(8,128)S(1)}, f32[6,16,128]{2,1,0:T(8,128)S(1)}, u32[]{:S(2)}, u32[]{:S(2)}) collective-permute-start(f32[6,16,128]{2,1,0:T(8,128)S(1)} %get-tuple-element.92), channel_id=1, source_target_pairs={{0,16},{1,17},{2,4},{3,5},{4,2},{5,3},{6,8},{7,9},{8,6},{9,7},{10,... | collective-permute-start | bytes 147464 | tf_op jit(solution)/shard_map/ppermute | solution.py:32
  155.2 0.9 collective-permute-done.29.e2
  156.1 1.6 collective-permute-done.30.o2
  157.7 1.3 shard_map.74
  159.0 1.1 collective-permute-start.37
  160.2 4.3 %collective-permute-start.35 = (f32[8,16,128]{2,1,0:T(8,128)S(1)}, f32[8,16,128]{2,1,0:T(8,128)S(1)}, u32[]{:S(2)}, u32[]{:S(2)}) collective-permute-start(f32[8,16,128]{2,1,0:T(8,128)S(1)} %get-tuple-element.96.final), channel_id=1, source_target_pairs={{0,17},{1,16},{2,19},{3,18},{4,21},{5,20},{6,23},{7,22},{8,25},{9,... | collective-permute-start | bytes 196616 | tf_op jit(solution)/shard_map/ppermute | solution.py:32
  164.5 4.3 %collective-permute-start.33 = (f32[2,16,128]{2,1,0:T(8,128)S(1)}, f32[2,16,128]{2,1,0:T(8,128)S(1)}, u32[]{:S(2)}, u32[]{:S(2)}) collective-permute-start(f32[2,16,128]{2,1,0:T(8,128)S(1)} %get-tuple-element.97), channel_id=1, source_target_pairs={{0,18},{1,19},{2,16},{3,17},{4,22},{5,23},{6,20},{7,21},{8,26},{9,... | collective-permute-start | bytes 49160 | tf_op jit(solution)/shard_map/ppermute | solution.py:32
  169.1 10.7 %all_to_all.29.got = f32[16,1,128]{2,1,0:T(1,128)S(1)} all-to-all(f32[16,1,128]{2,1,0:T(1,128)S(1)} %get-tuple-element.99), channel_id=1, replica_groups=mesh['tm'=8,'space'=16] {'space'}, dimensions={0} | all-to-all | bytes 16384 | tf_op jit(solution)/shard_map/all_to_all | solution.py:49
  179.8 0.8 shard_map.75
  180.6 0.5 copy-done.4
  181.1 0.7 copy.6
  (46 shorter events, 1.8 us)
Async XLA Ops:
  0.6 6.4 %collective-permute-start = (f32[8,16,128]{2,1,0:T(8,128)}, f32[8,16,128]{2,1,0:T(8,128)S(1)}, u32[]{:S(2)}, u32[]{:S(2)}) collective-permute-start(f32[8,16,128]{2,1,0:T(8,128)} %bitcast.22), channel_id=1, source_target_pairs={{0,16},{1,17},{2,18},{3,19},{4,20},{5,21},{6,22},{7,23},{8,24},{9,... | collective-permute-start | bytes 196616 | tf_op jit(solution)/shard_map/ppermute | solution.py:32
  3.2 2.2 %copy-start = (f32[1,64,4,2,16,128]{5,4,3,2,1,0:T(8,128)S(1)}, f32[1,64,4,2,16,128]{5,4,3,2,1,0:T(8,128)}, u32[]{:S(2)}) copy-start(f32[1,64,4,2,16,128]{5,4,3,2,1,0:T(8,128)} %param.7) | copy-start | bytes 12582916
  5.4 0.8 copy-start.2
  6.3 0.7 copy-start.3
  7.0 25.8 %copy-start.1 = (f32[1,64,4,2,16,128]{5,4,3,2,1,0:T(8,128)S(1)}, f32[1,64,4,2,16,128]{5,4,3,2,1,0:T(8,128)}, u32[]{:S(2)}) copy-start(f32[1,64,4,2,16,128]{5,4,3,2,1,0:T(8,128)} %param.7) | copy-start | bytes 12582916
  7.6 8.7 %collective-permute-start.1 = (f32[15,16,128]{2,1,0:T(8,128)S(1)}, f32[15,16,128]{2,1,0:T(8,128)S(1)}, u32[]{:S(2)}, u32[]{:S(2)}) collective-permute-start(f32[15,16,128]{2,1,0:T(8,128)S(1)} %get-tuple-element.54), channel_id=1, source_target_pairs={{0,1},{1,0},{2,3},{3,2},{4,5},{5,4},{6,7},{7,6},{8,9},{9,8},{10,11... | collective-permute-start | bytes 368648 | tf_op jit(solution)/shard_map/ppermute | solution.py:32
  9.0 7.3 %collective-permute-start.2 = (f32[15,16,128]{2,1,0:T(8,128)S(1)}, f32[15,16,128]{2,1,0:T(8,128)S(1)}, u32[]{:S(2)}, u32[]{:S(2)}) collective-permute-start(f32[15,16,128]{2,1,0:T(8,128)S(1)} %get-tuple-element.55), channel_id=1, source_target_pairs={{0,16},{1,2},{2,1},{3,4},{4,3},{5,6},{6,5},{7,8},{8,7},{9,10},{10,... | collective-permute-start | bytes 368648 | tf_op jit(solution)/shard_map/ppermute | solution.py:32
  9.4 6.9 %collective-permute-start.3 = (f32[8,16,128]{2,1,0:T(8,128)S(1)}, f32[8,16,128]{2,1,0:T(8,128)S(1)}, u32[]{:S(2)}, u32[]{:S(2)}) collective-permute-start(f32[8,16,128]{2,1,0:T(8,128)S(1)} %get-tuple-element.56), channel_id=1, source_target_pairs={{0,2},{1,3},{2,0},{3,1},{4,6},{5,7},{6,4},{7,5},{8,10},{9,11},{10,... | collective-permute-start | bytes 196616 | tf_op jit(solution)/shard_map/ppermute | solution.py:32
  11.6 4.6 %collective-permute-start.4 = (f32[8,16,128]{2,1,0:T(8,128)S(1)}, f32[8,16,128]{2,1,0:T(8,128)S(1)}, u32[]{:S(2)}, u32[]{:S(2)}) collective-permute-start(f32[8,16,128]{2,1,0:T(8,128)S(1)} %get-tuple-element.57), channel_id=1, source_target_pairs={{0,16},{1,17},{2,4},{3,5},{4,2},{5,3},{6,8},{7,9},{8,6},{9,7},{10,... | collective-permute-start | bytes 196616 | tf_op jit(solution)/shard_map/ppermute | solution.py:32
  17.2 12.3 %collective-permute-start.9 = (f32[8,16,128]{2,1,0:T(8,128)S(1)}, f32[8,16,128]{2,1,0:T(8,128)S(1)}, u32[]{:S(2)}, u32[]{:S(2)}) collective-permute-start(f32[8,16,128]{2,1,0:T(8,128)S(1)} %get-tuple-element.60.relaxed), channel_id=1, source_target_pairs={{0,16},{1,17},{2,18},{3,19},{4,20},{5,21},{6,22},{7,23},{8,24},{9,... | collective-permute-start | bytes 196616 | tf_op jit(solution)/shard_map/ppermute | solution.py:32
  18.3 11.2 %collective-permute-start.8 = (f32[8,16,128]{2,1,0:T(8,128)S(1)}, f32[8,16,128]{2,1,0:T(8,128)S(1)}, u32[]{:S(2)}, u32[]{:S(2)}) collective-permute-start(f32[8,16,128]{2,1,0:T(8,128)S(1)} %get-tuple-element.60.relaxed), channel_id=1, source_target_pairs={{0,16},{1,18},{2,17},{3,20},{4,19},{5,22},{6,21},{7,24},{8,23},{9,... | collective-permute-start | bytes 196616 | tf_op jit(solution)/shard_map/ppermute | solution.py:32
  18.7 10.8 %collective-permute-start.7 = (f32[8,16,128]{2,1,0:T(8,128)S(1)}, f32[8,16,128]{2,1,0:T(8,128)S(1)}, u32[]{:S(2)}, u32[]{:S(2)}) collective-permute-start(f32[8,16,128]{2,1,0:T(8,128)S(1)} %get-tuple-element.60.relaxed), channel_id=1, source_target_pairs={{0,17},{1,16},{2,19},{3,18},{4,21},{5,20},{6,23},{7,22},{8,25},{9,... | collective-permute-start | bytes 196616 | tf_op jit(solution)/shard_map/ppermute | solution.py:32
  23.1 5.8 %collective-permute-start.5 = (f32[6,16,128]{2,1,0:T(8,128)S(1)}, f32[6,16,128]{2,1,0:T(8,128)S(1)}, u32[]{:S(2)}, u32[]{:S(2)}) collective-permute-start(f32[6,16,128]{2,1,0:T(8,128)S(1)} %get-tuple-element.61), channel_id=1, source_target_pairs={{0,18},{1,19},{2,16},{3,17},{4,22},{5,23},{6,20},{7,21},{8,26},{9,... | collective-permute-start | bytes 147464 | tf_op jit(solution)/shard_map/ppermute | solution.py:32
  27.6 1.8 %collective-permute-start.6 = (f32[6,16,128]{2,1,0:T(8,128)S(1)}, f32[6,16,128]{2,1,0:T(8,128)S(1)}, u32[]{:S(2)}, u32[]{:S(2)}) collective-permute-start(f32[6,16,128]{2,1,0:T(8,128)S(1)} %get-tuple-element.62), channel_id=1, source_target_pairs={{0,16},{1,17},{2,20},{3,21},{4,18},{5,19},{6,24},{7,25},{8,22},{9,... | collective-permute-start | bytes 147464 | tf_op jit(solution)/shard_map/ppermute | solution.py:32
  30.4 8.5 %collective-permute-start.10 = (f32[8,16,128]{2,1,0:T(8,128)S(1)}, f32[8,16,128]{2,1,0:T(8,128)S(1)}, u32[]{:S(2)}, u32[]{:S(2)}) collective-permute-start(f32[8,16,128]{2,1,0:T(8,128)S(1)} %shard_map.62.residue), channel_id=1, source_target_pairs={{0,16},{1,17},{2,18},{3,19},{4,20},{5,21},{6,22},{7,23},{8,24},{9,... | collective-permute-start | bytes 196616 | tf_op jit(solution)/shard_map/ppermute | solution.py:32
  58.4 9.6 %collective-permute-start.15 = (f32[16,16,128]{2,1,0:T(8,128)S(1)}, f32[16,16,128]{2,1,0:T(8,128)S(1)}, u32[]{:S(2)}, u32[]{:S(2)}) collective-permute-start(f32[16,16,128]{2,1,0:T(8,128)S(1)} %get-tuple-element.67), channel_id=1, source_target_pairs={{0,16},{1,17},{2,18},{3,19},{4,20},{5,21},{6,22},{7,23},{8,24},{9,... | collective-permute-start | bytes 393224 | tf_op jit(solution)/shard_map/ppermute | solution.py:32
  61.2 6.9 %collective-permute-start.13 = (f32[10,16,128]{2,1,0:T(8,128)S(1)}, f32[10,16,128]{2,1,0:T(8,128)S(1)}, u32[]{:S(2)}, u32[]{:S(2)}) collective-permute-start(f32[10,16,128]{2,1,0:T(8,128)S(1)} %get-tuple-element.65), channel_id=1, source_target_pairs={{0,17},{1,16},{2,19},{3,18},{4,21},{5,20},{6,23},{7,22},{8,25},{9,... | collective-permute-start | bytes 245768 | tf_op jit(solution)/shard_map/ppermute | solution.py:32
  61.3 6.7 %collective-permute-start.14 = (f32[10,16,128]{2,1,0:T(8,128)S(1)}, f32[10,16,128]{2,1,0:T(8,128)S(1)}, u32[]{:S(2)}, u32[]{:S(2)}) collective-permute-start(f32[10,16,128]{2,1,0:T(8,128)S(1)} %get-tuple-element.66), channel_id=1, source_target_pairs={{0,16},{1,18},{2,17},{3,20},{4,19},{5,22},{6,21},{7,24},{8,23},{9,... | collective-permute-start | bytes 245768 | tf_op jit(solution)/shard_map/ppermute | solution.py:32
  63.0 5.0 %collective-permute-start.11 = (f32[6,16,128]{2,1,0:T(8,128)S(1)}, f32[6,16,128]{2,1,0:T(8,128)S(1)}, u32[]{:S(2)}, u32[]{:S(2)}) collective-permute-start(f32[6,16,128]{2,1,0:T(8,128)S(1)} %get-tuple-element.63), channel_id=1, source_target_pairs={{0,18},{1,19},{2,16},{3,17},{4,22},{5,23},{6,20},{7,21},{8,26},{9,... | collective-permute-start | bytes 147464 | tf_op jit(solution)/shard_map/ppermute | solution.py:32
  65.5 2.5 %collective-permute-start.12 = (f32[6,16,128]{2,1,0:T(8,128)S(1)}, f32[6,16,128]{2,1,0:T(8,128)S(1)}, u32[]{:S(2)}, u32[]{:S(2)}) collective-permute-start(f32[6,16,128]{2,1,0:T(8,128)S(1)} %get-tuple-element.64), channel_id=1, source_target_pairs={{0,16},{1,17},{2,20},{3,21},{4,18},{5,19},{6,24},{7,25},{8,22},{9,... | collective-permute-start | bytes 147464 | tf_op jit(solution)/shard_map/ppermute | solution.py:32
  83.6 11.2 %collective-permute-start.20 = (f32[16,16,128]{2,1,0:T(8,128)S(1)}, f32[16,16,128]{2,1,0:T(8,128)S(1)}, u32[]{:S(2)}, u32[]{:S(2)}) collective-permute-start(f32[16,16,128]{2,1,0:T(8,128)S(1)} %get-tuple-element.75), channel_id=1, source_target_pairs={{0,16},{1,17},{2,18},{3,19},{4,20},{5,21},{6,22},{7,23},{8,24},{9,... | collective-permute-start | bytes 393224 | tf_op jit(solution)/shard_map/ppermute | solution.py:32
  86.3 8.4 %collective-permute-start.18 = (f32[10,16,128]{2,1,0:T(8,128)S(1)}, f32[10,16,128]{2,1,0:T(8,128)S(1)}, u32[]{:S(2)}, u32[]{:S(2)}) collective-permute-start(f32[10,16,128]{2,1,0:T(8,128)S(1)} %get-tuple-element.73), channel_id=1, source_target_pairs={{0,17},{1,16},{2,19},{3,18},{4,21},{5,20},{6,23},{7,22},{8,25},{9,... | collective-permute-start | bytes 245768 | tf_op jit(solution)/shard_map/ppermute | solution.py:32
  86.4 8.3 %collective-permute-start.19 = (f32[10,16,128]{2,1,0:T(8,128)S(1)}, f32[10,16,128]{2,1,0:T(8,128)S(1)}, u32[]{:S(2)}, u32[]{:S(2)}) collective-permute-start(f32[10,16,128]{2,1,0:T(8,128)S(1)} %get-tuple-element.74), channel_id=1, source_target_pairs={{0,16},{1,18},{2,17},{3,20},{4,19},{5,22},{6,21},{7,24},{8,23},{9,... | collective-permute-start | bytes 245768 | tf_op jit(solution)/shard_map/ppermute | solution.py:32
  88.5 6.2 %collective-permute-start.16 = (f32[6,16,128]{2,1,0:T(8,128)S(1)}, f32[6,16,128]{2,1,0:T(8,128)S(1)}, u32[]{:S(2)}, u32[]{:S(2)}) collective-permute-start(f32[6,16,128]{2,1,0:T(8,128)S(1)} %get-tuple-element.71), channel_id=1, source_target_pairs={{0,18},{1,19},{2,16},{3,17},{4,22},{5,23},{6,20},{7,21},{8,26},{9,... | collective-permute-start | bytes 147464 | tf_op jit(solution)/shard_map/ppermute | solution.py:32
  91.0 3.7 %collective-permute-start.17 = (f32[6,16,128]{2,1,0:T(8,128)S(1)}, f32[6,16,128]{2,1,0:T(8,128)S(1)}, u32[]{:S(2)}, u32[]{:S(2)}) collective-permute-start(f32[6,16,128]{2,1,0:T(8,128)S(1)} %get-tuple-element.72), channel_id=1, source_target_pairs={{0,16},{1,17},{2,20},{3,21},{4,18},{5,19},{6,24},{7,25},{8,22},{9,... | collective-permute-start | bytes 147464 | tf_op jit(solution)/shard_map/ppermute | solution.py:32
  109.4 11.8 %collective-permute-start.25 = (f32[16,16,128]{2,1,0:T(8,128)S(1)}, f32[16,16,128]{2,1,0:T(8,128)S(1)}, u32[]{:S(2)}, u32[]{:S(2)}) collective-permute-start(f32[16,16,128]{2,1,0:T(8,128)S(1)} %get-tuple-element.83), channel_id=1, source_target_pairs={{0,16},{1,17},{2,18},{3,19},{4,20},{5,21},{6,22},{7,23},{8,24},{9,... | collective-permute-start | bytes 393224 | tf_op jit(solution)/shard_map/ppermute | solution.py:32
  112.6 8.6 %collective-permute-start.23 = (f32[10,16,128]{2,1,0:T(8,128)S(1)}, f32[10,16,128]{2,1,0:T(8,128)S(1)}, u32[]{:S(2)}, u32[]{:S(2)}) collective-permute-start(f32[10,16,128]{2,1,0:T(8,128)S(1)} %get-tuple-element.81), channel_id=1, source_target_pairs={{0,17},{1,16},{2,19},{3,18},{4,21},{5,20},{6,23},{7,22},{8,25},{9,... | collective-permute-start | bytes 245768 | tf_op jit(solution)/shard_map/ppermute | solution.py:32
  112.7 8.5 %collective-permute-start.24 = (f32[10,16,128]{2,1,0:T(8,128)S(1)}, f32[10,16,128]{2,1,0:T(8,128)S(1)}, u32[]{:S(2)}, u32[]{:S(2)}) collective-permute-start(f32[10,16,128]{2,1,0:T(8,128)S(1)} %get-tuple-element.82), channel_id=1, source_target_pairs={{0,16},{1,18},{2,17},{3,20},{4,19},{5,22},{6,21},{7,24},{8,23},{9,... | collective-permute-start | bytes 245768 | tf_op jit(solution)/shard_map/ppermute | solution.py:32
  115.7 5.5 %collective-permute-start.21 = (f32[6,16,128]{2,1,0:T(8,128)S(1)}, f32[6,16,128]{2,1,0:T(8,128)S(1)}, u32[]{:S(2)}, u32[]{:S(2)}) collective-permute-start(f32[6,16,128]{2,1,0:T(8,128)S(1)} %get-tuple-element.79), channel_id=1, source_target_pairs={{0,18},{1,19},{2,16},{3,17},{4,22},{5,23},{6,20},{7,21},{8,26},{9,... | collective-permute-start | bytes 147464 | tf_op jit(solution)/shard_map/ppermute | solution.py:32
  118.2 3.0 %collective-permute-start.22 = (f32[6,16,128]{2,1,0:T(8,128)S(1)}, f32[6,16,128]{2,1,0:T(8,128)S(1)}, u32[]{:S(2)}, u32[]{:S(2)}) collective-permute-start(f32[6,16,128]{2,1,0:T(8,128)S(1)} %get-tuple-element.80), channel_id=1, source_target_pairs={{0,16},{1,17},{2,20},{3,21},{4,18},{5,19},{6,24},{7,25},{8,22},{9,... | collective-permute-start | bytes 147464 | tf_op jit(solution)/shard_map/ppermute | solution.py:32
  122.1 9.3 %collective-permute-start.28 = (f32[8,16,128]{2,1,0:T(8,128)S(1)}, f32[8,16,128]{2,1,0:T(8,128)S(1)}, u32[]{:S(2)}, u32[]{:S(2)}) collective-permute-start(f32[8,16,128]{2,1,0:T(8,128)S(1)} %get-tuple-element.87), channel_id=1, source_target_pairs={{0,64},{1,65},{2,66},{3,67},{4,68},{5,69},{6,70},{7,71},{8,72},{9,... | collective-permute-start | bytes 196616 | tf_op jit(solution)/shard_map/ppermute | solution.py:32
  123.7 5.7 %collective-permute-start.26 = (f32[6,16,128]{2,1,0:T(8,128)S(1)}, f32[6,16,128]{2,1,0:T(8,128)S(1)}, u32[]{:S(2)}, u32[]{:S(2)}) collective-permute-start(f32[6,16,128]{2,1,0:T(8,128)S(1)} %get-tuple-element.85), channel_id=1, source_target_pairs={{0,64},{1,66},{2,65},{3,68},{4,67},{5,70},{6,69},{7,72},{8,71},{9,... | collective-permute-start | bytes 147464 | tf_op jit(solution)/shard_map/ppermute | solution.py:32
  125.2 6.2 %collective-permute-start.27 = (f32[6,16,128]{2,1,0:T(8,128)S(1)}, f32[6,16,128]{2,1,0:T(8,128)S(1)}, u32[]{:S(2)}, u32[]{:S(2)}) collective-permute-start(f32[6,16,128]{2,1,0:T(8,128)S(1)} %get-tuple-element.86), channel_id=1, source_target_pairs={{0,65},{1,64},{2,67},{3,66},{4,69},{5,68},{6,71},{7,70},{8,73},{9,... | collective-permute-start | bytes 147464 | tf_op jit(solution)/shard_map/ppermute | solution.py:32
  147.5 10.2 %collective-permute-start.31 = (f32[10,16,128]{2,1,0:T(8,128)S(1)}, f32[10,16,128]{2,1,0:T(8,128)S(1)}, u32[]{:S(2)}, u32[]{:S(2)}) collective-permute-start(f32[10,16,128]{2,1,0:T(8,128)S(1)} %get-tuple-element.93), channel_id=1, source_target_pairs={{0,1},{1,0},{2,3},{3,2},{4,5},{5,4},{6,7},{7,6},{8,9},{9,8},{10,11... | collective-permute-start | bytes 245768 | tf_op jit(solution)/shard_map/ppermute | solution.py:32
  147.9 9.8 %collective-permute-start.32 = (f32[10,16,128]{2,1,0:T(8,128)S(1)}, f32[10,16,128]{2,1,0:T(8,128)S(1)}, u32[]{:S(2)}, u32[]{:S(2)}) collective-permute-start(f32[10,16,128]{2,1,0:T(8,128)S(1)} %get-tuple-element.94), channel_id=1, source_target_pairs={{0,16},{1,2},{2,1},{3,4},{4,3},{5,6},{6,5},{7,8},{8,7},{9,10},{10,... | collective-permute-start | bytes 245768 | tf_op jit(solution)/shard_map/ppermute | solution.py:32
  151.7 4.4 %collective-permute-start.29 = (f32[6,16,128]{2,1,0:T(8,128)S(1)}, f32[6,16,128]{2,1,0:T(8,128)S(1)}, u32[]{:S(2)}, u32[]{:S(2)}) collective-permute-start(f32[6,16,128]{2,1,0:T(8,128)S(1)} %get-tuple-element.91), channel_id=1, source_target_pairs={{0,2},{1,3},{2,0},{3,1},{4,6},{5,7},{6,4},{7,5},{8,10},{9,11},{10,... | collective-permute-start | bytes 147464 | tf_op jit(solution)/shard_map/ppermute | solution.py:32
  151.7 6.0 %collective-permute-start.30 = (f32[6,16,128]{2,1,0:T(8,128)S(1)}, f32[6,16,128]{2,1,0:T(8,128)S(1)}, u32[]{:S(2)}, u32[]{:S(2)}) collective-permute-start(f32[6,16,128]{2,1,0:T(8,128)S(1)} %get-tuple-element.92), channel_id=1, source_target_pairs={{0,16},{1,17},{2,4},{3,5},{4,2},{5,3},{6,8},{7,9},{8,6},{9,7},{10,... | collective-permute-start | bytes 147464 | tf_op jit(solution)/shard_map/ppermute | solution.py:32
  159.0 20.8 %collective-permute-start.37 = (f32[8,16,128]{2,1,0:T(8,128)S(1)}, f32[8,16,128]{2,1,0:T(8,128)S(1)}, u32[]{:S(2)}, u32[]{:S(2)}) collective-permute-start(f32[8,16,128]{2,1,0:T(8,128)S(1)} %get-tuple-element.96.final), channel_id=1, source_target_pairs={{0,16},{1,17},{2,18},{3,19},{4,20},{5,21},{6,22},{7,23},{8,24},{9,... | collective-permute-start | bytes 196616 | tf_op jit(solution)/shard_map/ppermute | solution.py:32
  160.0 19.7 %collective-permute-start.36 = (f32[8,16,128]{2,1,0:T(8,128)S(1)}, f32[8,16,128]{2,1,0:T(8,128)S(1)}, u32[]{:S(2)}, u32[]{:S(2)}) collective-permute-start(f32[8,16,128]{2,1,0:T(8,128)S(1)} %get-tuple-element.96.final), channel_id=1, source_target_pairs={{0,16},{1,18},{2,17},{3,20},{4,19},{5,22},{6,21},{7,24},{8,23},{9,... | collective-permute-start | bytes 196616 | tf_op jit(solution)/shard_map/ppermute | solution.py:32
  160.2 19.6 %collective-permute-start.35 = (f32[8,16,128]{2,1,0:T(8,128)S(1)}, f32[8,16,128]{2,1,0:T(8,128)S(1)}, u32[]{:S(2)}, u32[]{:S(2)}) collective-permute-start(f32[8,16,128]{2,1,0:T(8,128)S(1)} %get-tuple-element.96.final), channel_id=1, source_target_pairs={{0,17},{1,16},{2,19},{3,18},{4,21},{5,20},{6,23},{7,22},{8,25},{9,... | collective-permute-start | bytes 196616 | tf_op jit(solution)/shard_map/ppermute | solution.py:32
  164.5 15.3 %collective-permute-start.33 = (f32[2,16,128]{2,1,0:T(8,128)S(1)}, f32[2,16,128]{2,1,0:T(8,128)S(1)}, u32[]{:S(2)}, u32[]{:S(2)}) collective-permute-start(f32[2,16,128]{2,1,0:T(8,128)S(1)} %get-tuple-element.97), channel_id=1, source_target_pairs={{0,18},{1,19},{2,16},{3,17},{4,22},{5,23},{6,20},{7,21},{8,26},{9,... | collective-permute-start | bytes 49160 | tf_op jit(solution)/shard_map/ppermute | solution.py:32
  168.8 11.0 %collective-permute-start.34 = (f32[2,16,128]{2,1,0:T(8,128)S(1)}, f32[2,16,128]{2,1,0:T(8,128)S(1)}, u32[]{:S(2)}, u32[]{:S(2)}) collective-permute-start(f32[2,16,128]{2,1,0:T(8,128)S(1)} %get-tuple-element.98), channel_id=1, source_target_pairs={{0,16},{1,17},{2,20},{3,21},{4,18},{5,19},{6,24},{7,25},{8,22},{9,... | collective-permute-start | bytes 49160 | tf_op jit(solution)/shard_map/ppermute | solution.py:32
  180.6 0.5 copy-start.4

commit v4 on v3

--- a/solution.py
+++ b/solution.py
@@ -6,6 +6,7 @@
 from jax.experimental import pallas as pl
 from jax.experimental.pallas import tpu as pltpu
 from jax.sharding import PartitionSpec as P
+
 
 DT = 0.045
 N_TM = 8
@@ -16,7 +17,6 @@
 F32 = jnp.float32
 BF16 = jnp.bfloat16
 VMEM = pl.BlockSpec(memory_space=pltpu.VMEM)
-SMEM = pl.BlockSpec(memory_space=pltpu.SMEM)
 
 
 def moved(value, by_tm, other):
@@ -149,31 +149,30 @@
     return p, vx, vy, vz
 
 
-def flags(where_ref):
-    s = where_ref[0]
+def flags():
+    s = lax.axis_index("space")
     return s >= 1, s < N_SP - 1, s >= 2, s < N_SP - 2
 
 
-def ways(where_ref):
-    return where_ref[2] == 0, where_ref[3] == 0
-
-
-def halo_of(where_ref, near, far):
-    up1, up2 = ways(where_ref)
+def ways():
+    s = lax.axis_index("space")
+    return (s & 1) == 0, (s & 2) == 0
+
+
+def halo_of(near, far):
+    up1, up2 = ways()
     return *below_above(up1, *near), *below_above(up2, *far)
 
 
-def call(kernel, outs, *args, scratch=(), flops=1_000_000, limit=4):
-    shapes = [pltpu.VMEM(shape, F32) for shape in outs]
-    args = [
-        arg if arg.dtype == jnp.int32 else pltpu.with_memory_space_constraint(arg, pltpu.VMEM)
-        for arg in args
-    ]
+def call(kernel, outs, *args, scratch=(), flops=1_000_000, limit=4, outward=False):
+    kind = pltpu.HBM if outward else pltpu.VMEM
+    shapes = [kind(shape, F32) for shape in outs]
+    args = [pltpu.with_memory_space_constraint(arg, pltpu.VMEM) for arg in args]
     return pl.pallas_call(
         kernel,
         out_shape=shapes,
-        in_specs=[SMEM if arg.dtype == jnp.int32 else VMEM for arg in args],
-        out_specs=[VMEM] * len(shapes),
+        in_specs=[VMEM] * len(args),
+        out_specs=[pl.BlockSpec(memory_space=kind)] * len(shapes),
         scratch_shapes=list(scratch),
         compiler_params=pltpu.CompilerParams(vmem_limit_bytes=limit * 1024 * 1024),
         cost_estimate=pl.CostEstimate(flops=flops, bytes_accessed=100_000, transcendentals=0),
@@ -185,8 +184,8 @@
     c2_out[...] = c_ref[...] * c_ref[...]
 
 
-def pack_kernel(where, g_ref, f_ref, c2_ref, e1, o1, e2, o2):
-    up1, up2 = ways(where)
+def pack_kernel(g_ref, f_ref, c2_ref, e1, o1, e2, o2):
+    up1, up2 = ways()
     u = g_ref[...]
     c2 = c2_ref[...]
     put_both((e1, o1), up1, 0, [u, f_ref[0], f_ref[1], c2], [f_ref[2, 1:2]], [f_ref[2, 0:1]])
@@ -215,15 +214,15 @@
 LOADS = [8, 6, 4, 2]
 
 
-def relax_kernel(where, g_ref, f_ref, c2_ref, e1, o1, e2, o2, out, far_e, far_o, med, loads_out):
-    ok = flags(where)
-    halo = halo_of(where, (e1, o1), (e2, o2))
+def relax_kernel(g_ref, f_ref, c2_ref, e1, o1, e2, o2, out, far_e, far_o, med, loads_out):
+    ok = flags()
+    halo = halo_of((e1, o1), (e2, o2))
     c2 = load_medium(c2_ref[...], *halo, ok)
     loads = load_forcing(f_ref, *halo, ok)
     p, vx, vy, vz = wide(g_ref[...], *halo, ok)
     u = advance_many(p, vx, vy, vz, c2, DT, 4, ok[0], ok[2], loads)[-1]
     out[...] = u
-    put_far((far_e, far_o), ways(where)[1], u)
+    put_far((far_e, far_o), ways()[1], u)
     med[...] = c2
     at = 0
     for load in loads:
@@ -235,9 +234,9 @@
     return [loads_ref[start : start + n] for start, n in zip(starts, LOADS)]
 
 
-def residue_kernel(where, relaxed, loads_ref, med, e2, o2, e1, o1, own, out):
-    ok = flags(where)
-    p, vx, vy, vz = wide(own[...], *halo_of(where, (e1, o1), (e2, o2)), ok)
+def residue_kernel(relaxed, loads_ref, med, e2, o2, e1, o1, own, out):
+    ok = flags()
+    p, vx, vy, vz = wide(own[...], *halo_of((e1, o1), (e2, o2)), ok)
     u = advance_many(p, vx, vy, vz, med[...], DT, 4, ok[0], ok[2], kept_loads(loads_ref))[-1]
     out[...] = u - relaxed[...]
 
@@ -326,10 +325,10 @@
     return jnp.where(lane < RANK, solved, 0.0)
 
 
-def project(where, basis, ginv, coef, x, scratch, outs):
+def project(basis, ginv, coef, x, scratch, outs):
     weights = jnp.sum(ginv * coef, axis=1, keepdims=True)
     scratch[...] = jnp.broadcast_to(weights, (RANK, NY))
-    total = [jnp.zeros((8, NY), F32) for i in range(NX)]
+    total = [jnp.zeros((8, NY), F32) for _ in range(NX)]
     for r in range(RANK):
         w = scratch[r : r + 1, :]
         at = r * 8 * NX
@@ -340,7 +339,7 @@
     center, e1, o1, e2, o2 = outs
     put(center, 0, y)
     put(center, 8, z)
-    up1, up2 = ways(where)
+    up1, up2 = ways()
     put_both((e1, o1), up1, 0, [y], [z[1:2], z[7:8]], [z[0:1], z[6:7]])
     put_far((e2, o2), up2, y)
 
@@ -348,7 +347,7 @@
 PROJECTED = [(16, NX, NY), (10, NX, NY), (10, NX, NY), (6, NX, NY), (6, NX, NY)]
 
 
-def first_project_kernel(where, got, basis, x_ref, ginv_ref, *rest):
+def first_project_kernel(got, basis, x_ref, ginv_ref, *rest):
     outs, scratch = rest[:5], rest[5]
     total = got[0]
     for j in range(1, N_SP):
@@ -357,21 +356,21 @@
     g = jnp.concatenate([packed, pltpu.roll(packed, RANK, 1)], axis=0)
     ginv = inverse(g)
     ginv_ref[...] = ginv
-    project(where, basis, ginv, total[RANK // 2 : RANK // 2 + 1], x_ref[...], scratch, outs)
-
-
-def project_kernel(where, got, ginv_ref, basis, x_ref, *rest):
+    project(basis, ginv, total[RANK // 2 : RANK // 2 + 1], x_ref[...], scratch, outs)
+
+
+def project_kernel(got, ginv_ref, basis, x_ref, *rest):
     outs, scratch = rest[:5], rest[5]
     coef = jnp.sum(got[...], axis=0)
-    project(where, basis, ginv_ref[...], coef, x_ref[...], scratch, outs)
-
-
-def q_of(where, med, e2, o2, e1, o1, center):
-    ok = flags(where)
+    project(basis, ginv_ref[...], coef, x_ref[...], scratch, outs)
+
+
+def q_of(med, e2, o2, e1, o1, center):
+    ok = flags()
     c2 = med[...]
     y = center[0:8]
     z = center[8:16]
-    halo = halo_of(where, (e1, o1), (e2, o2))
+    halo = halo_of((e1, o1), (e2, o2))
     b1, a1 = halo[:2]
     p, vx, vy, vz = wide(y, *halo, ok)
     fine = advance_many(p, vx, vy, vz, c2, DT, 4, ok[0], ok[2])[-1]
@@ -386,47 +385,57 @@
         ref[j] = row
 
 
-def level_kernel(where, med, e2, o2, e1, o1, center, acc, basis, u_out, acc_out, row_out, scratch):
-    u = q_of(where, med, e2, o2, e1, o1, center)
+def level_kernel(med, e2, o2, e1, o1, center, acc, basis, u_out, acc_out, row_out, scratch):
+    u = q_of(med, e2, o2, e1, o1, center)
     u_out[...] = u
     acc_out[...] = acc[...] + u
     put_copies(row_out, inner_products(basis, u, scratch))
 
 
-def gap_kernel(where, med, e2, o2, e1, o1, center, acc, u_out, acc_out, e_out, o_out):
-    u = q_of(where, med, e2, o2, e1, o1, center)
+def gap_kernel(med, e2, o2, e1, o1, center, acc, u_out, acc_out, e_out, o_out):
+    u = q_of(med, e2, o2, e1, o1, center)
     u_out[...] = u
     acc_out[...] = acc[...] + u
-    put_far((e_out, o_out), ways(where)[0], u)
-
-
-def chain_kernel(where, med, o1, e1, own, acc, basis, x_out, row_out, scratch):
-    ok = flags(where)
-    b, a = below_above(ways(where)[0], e1, o1)
+    put_far((e_out, o_out), ways()[0], u)
+
+
+def chain_kernel(med, o1, e1, own, acc, basis, x_out, row_out, scratch):
+    ok = flags()
+    b, a = below_above(ways()[0], e1, o1)
     p = cat(only(ok[0], b[0:2]), own[0:2], only(ok[1], a[0:2]))
     vx = cat(b[4:5], own[2:4], a[4:5])
     vy = cat(b[5:6], own[4:6], a[5:6])
     vz = cat(b[2:4], own[6:8], a[2:3])
     c2 = med[...]
     moved_on = advance_many(p, vx, vy, vz, c2[2:6], 8 * DT, 2, ok[0], ok[2])[-1]
-    chained = (where[1] >= 5) | (where[1] == 0)
+    row = lax.axis_index("tm")
+    chained = (row >= 5) | (row == 0)
     x = acc[...] + only(chained, moved_on)
     x_out[...] = x
     put_copies(row_out, inner_products(basis, x, scratch))
 
 
-def final_kernel(where, med, e2, o2, e1, o1, center, relaxed, residue, basis, out, e_out, o_out, row_out, scratch):
-    u = relaxed[...] + (q_of(where, med, e2, o2, e1, o1, center) + residue[...])
+def final_kernel(med, e2, o2, e1, o1, center, relaxed, residue, basis, out, e_out, o_out, row_out, scratch):
+    u = relaxed[...] + (q_of(med, e2, o2, e1, o1, center) + residue[...])
     out[...] = u
-    up2 = ways(where)[1]
+    up2 = ways()[1]
     put_both((e_out, o_out), up2, 0, [], [u[1:2], u[7:8]], [u[0:1], u[6:7]])
     put_copies(row_out, inner_products(basis, u, scratch))
 
 
-def sweep_kernel(where, loads_ref, med, final, e2, o2, e1, o1, own, got, ginv, out, coords):
-    ok = flags(where)
+def sweep_kernel(loads_ref, med, final, e2, o2, e1, o1, own, got, ginv, out, coords, kept, kept_row, sems):
+    def copy(row, source):
+        return pltpu.make_async_copy(source, out.at[row], sems.at[row])
+
+    copies = [copy(3, final)]
+    copies[0].start()
+    coef = jnp.sum(got[...], axis=0)
+    kept_row[...] = to_row(jnp.sum(ginv[...] * coef, axis=1, keepdims=True))
+    copies.append(pltpu.make_async_copy(kept_row, coords, sems.at[4]))
+    copies[1].start()
+    ok = flags()
     loads = [load[1:-1] for load in kept_loads(loads_ref)[:3]]
-    b1, a1, b2, a2 = halo_of(where, (e1, o1), (e2, o2))
+    b1, a1, b2, a2 = halo_of((e1, o1), (e2, o2))
     u = own[...]
     p = cat(
         only(ok[2], b2[0:1]), only(ok[0], b1[0:2]), u[0:2], only(ok[1], a1[0:2]), only(ok[3], a2[0:1])
@@ -436,15 +445,14 @@
     vz = cat(b2[1:2], b1[6:8], u[6:8], a1[6:8])
     points = advance_many(p, vx, vy, vz, med[1:7], DT, 3, ok[0], ok[2], loads)
     for i in range(3):
-        out[i] = points[i]
-    out[3] = final[...]
-    coef = jnp.sum(got[...], axis=0)
-    coords[...] = to_row(jnp.sum(ginv[...] * coef, axis=1, keepdims=True))
+        kept[i] = points[i]
+        copies.append(copy(i, kept.at[i]))
+        copies[-1].start()
+    for each in copies:
+        each.wait()
 
 
 def body(speed, forcing, guess, basis):
-    slab, block = lax.axis_index("space"), lax.axis_index("tm")
-    where = jnp.stack([slab, block, slab % 2, slab // 2 % 2]).astype(jnp.int32)
     columns = basis.reshape(RANK * 8 * NX, NY)
     state = (8, NX, NY)
     table = [pltpu.VMEM((RANK, NY), F32)]
@@ -453,21 +461,20 @@
     far = [(6, NX, NY), (6, NX, NY)]
 
     def traded(near, distant, center, by_tm):
-        result = [
-            trade(distant[1], by_tm, 2, False),
-            trade(distant[0], by_tm, 2, True),
-            trade(near[1], by_tm, 1, False),
-            trade(near[0], by_tm, 1, True),
-        ]
-        result = [result[1], result[0], result[3], result[2]]
-        return result + ([hop(center, by_tm)] if by_tm else [])
+        far_second = trade(distant[1], by_tm, 2, False)
+        far_first = trade(distant[0], by_tm, 2, True)
+        near_second = trade(near[1], by_tm, 1, False)
+        near_first = trade(near[0], by_tm, 1, True)
+        result = [far_first, far_second, near_first, near_second]
+        if by_tm:
+            result.append(hop(center, by_tm))
+        return result
 
     start = hop(guess.reshape(state), 1)
     load, c2 = call(stage_kernel, [(4, 2, NX, NY), (2, NX, NY)], forcing, speed, columns)
     e1, o1, e2, o2 = call(
         pack_kernel,
         [(15, NX, NY), (15, NX, NY), (8, NX, NY), (8, NX, NY)],
-        where,
         start,
         load,
         c2,
@@ -479,7 +486,6 @@
     relaxed, e, o, med, loads = call(
         relax_kernel,
         [state, *far, (8, NX, NY), (sum(LOADS), NX, NY)],
-        where,
         start,
         load,
         c2,
@@ -489,14 +495,14 @@
         o2,
     )
     near = traded((relaxed, relaxed), (e, o), relaxed, 1)
-    (residue,) = call(residue_kernel, [state], where, relaxed, loads, med, *near)
+    (residue,) = call(residue_kernel, [state], relaxed, loads, med, *near)
     x = hop(residue, 1)
     (gram,) = call(
         functools.partial(gram_kernel, (4, 8)), [(RANK, NY)], columns, gram, scratch=split, flops=50_000_000
     )
     (rows,) = call(first_kernel, [(N_SP, RANK // 2 + 8, NY)], columns, x, gram, scratch=table)
     ginv, *packed = call(
-        first_project_kernel, [(RANK, NY), *PROJECTED], where, share(rows), columns, x, scratch=table
+        first_project_kernel, [(RANK, NY), *PROJECTED], share(rows), columns, x, scratch=table
     )
 
     def exchanged(packed, by_tm):
@@ -505,22 +511,21 @@
         return result if by_tm else result + [center]
 
     acc = x
-    for level in range(2):
+    for _ in range(2):
         u, acc, rows = call(
-            level_kernel, [state, state, copies], where, med, *exchanged(packed, 1), acc, columns, scratch=table
+            level_kernel, [state, state, copies], med, *exchanged(packed, 1), acc, columns, scratch=table
         )
-        packed = call(project_kernel, PROJECTED, where, share(rows), ginv, columns, u, scratch=table)
-    gap, acc, e, o = call(gap_kernel, [state, state, *far], where, med, *exchanged(packed, 1), acc)
+        packed = call(project_kernel, PROJECTED, share(rows), ginv, columns, u, scratch=table)
+    gap, acc, e, o = call(gap_kernel, [state, state, *far], med, *exchanged(packed, 1), acc)
     o = trade(o, 4, 1, False)
     e = trade(e, 4, 1, True)
     x, rows = call(
-        chain_kernel, [state, copies], where, med, o, e, hop(gap, 4), acc, columns, scratch=table
-    )
-    packed = call(project_kernel, PROJECTED, where, share(rows), ginv, columns, x, scratch=table)
+        chain_kernel, [state, copies], med, o, e, hop(gap, 4), acc, columns, scratch=table
+    )
+    packed = call(project_kernel, PROJECTED, share(rows), ginv, columns, x, scratch=table)
     final, e, o, rows = call(
         final_kernel,
         [state, (2, NX, NY), (2, NX, NY), copies],
-        where,
         med,
         *exchanged(packed, 0),
         relaxed,
@@ -531,7 +536,16 @@
     got = share(rows)
     near = traded((final, final), (e, o), final, 1)
     states, coords = call(
-        sweep_kernel, [(4, 8, NX, NY), (1, NY)], where, loads, med, final, *near, got, ginv
+        sweep_kernel,
+        [(4, 8, NX, NY), (1, NY)],
+        loads,
+        med,
+        final,
+        *near,
+        got,
+        ginv,
+        scratch=[pltpu.VMEM((3, 8, NX, NY), F32), pltpu.VMEM((1, NY), F32), pltpu.SemaphoreType.DMA((5,))],
+        outward=True,
     )
     return states.reshape(4, 4, 2, NX, NY), coords[:, :RANK]
 

time: 184 us -> 176 us (0.957)
  Pallas kernels: 21.5 us -> 15 us
    pallas_call x17, Pallas kernels: 21.5 us -> 15 us  [call(): pl.pallas_call(kernel, out_shape=shapes, in_specs=[VMEM] * len(args), out...]
    unnamed x11 -> x8, local copies, waits for them, and re-layouts: 4.95 us -> 3.75 us
where the time goes in v4:
time: 176 us; the launch traced here: 174 us
  starting transfers between devices  71.3 us (41%)
  blocking collectives  66.2 us (38%)
  waiting for transfers between devices  16.9 us (10%)
  Pallas kernels  15 us (9%)
  local copies, waits for them, and re-layouts  3.75 us (2%)
    ppermute x38, starting transfers between devices, moved(): return lax.ppermute(value, ('tm', 'space'), pairs)  71.3 us
    all_to_all x5, blocking collectives, share(): return lax.all_to_all(copies, 'space', 0, 0, tiled=True)  66.2 us
    ppermute x38, waiting for transfers between devices, moved(): return lax.ppermute(value, ('tm', 'space'), pairs)  16.9 us
    pallas_call x17, Pallas kernels, call(): pl.pallas_call(kernel, out_shape=shapes, in_specs=[VMEM] * len(args), out...  15 us
    unnamed x8, local copies, waits for them, and re-layouts  3.75 us
  transfers between devices with their start and end apart: 38, of which 9 were waited for; matrix products, arithmetic and copies ran while one was open for 0% of the time, Pallas kernels for 3%

profile of v4, /device:TPU:1, one launch (start us, length us, event | category | flops | bytes accessed | tf_op | source)
XLA Modules:
  0.0 174.2 jit_solution(8557958005731342408)
XLA Ops:
  0.6 2.6 %collective-permute-start = (f32[8,16,128]{2,1,0:T(8,128)}, f32[8,16,128]{2,1,0:T(8,128)S(1)}, u32[]{:S(2)}, u32[]{:S(2)}) collective-permute-start(f32[8,16,128]{2,1,0:T(8,128)} %bitcast.17), channel_id=1, source_target_pairs={{0,16},{1,17},{2,18},{3,19},{4,20},{5,21},{6,22},{7,23},{8,24},{9,... | collective-permute-start | bytes 196616 | tf_op jit(solution)/shard_map/ppermute | solution.py:32
  3.2 2.2 %copy-done = f32[1,64,4,2,16,128]{5,4,3,2,1,0:T(8,128)S(1)} copy-done((f32[1,64,4,2,16,128]{5,4,3,2,1,0:T(8,128)S(1)}, f32[1,64,4,2,16,128]{5,4,3,2,1,0:T(8,128)}, u32[]{:S(2)}) %copy-start) | copy-done | bytes 4194328
  5.4 0.8 copy-done.2
  6.3 0.7 copy-done.3
  7.0 1.4 collective-permute-start.1
  8.4 0.4 collective-permute-start.2
  8.8 2.2 %collective-permute-start.3 = (f32[8,16,128]{2,1,0:T(8,128)S(1)}, f32[8,16,128]{2,1,0:T(8,128)S(1)}, u32[]{:S(2)}, u32[]{:S(2)}) collective-permute-start(f32[8,16,128]{2,1,0:T(8,128)S(1)} %get-tuple-element.56), channel_id=1, source_target_pairs={{0,2},{1,3},{2,0},{3,1},{4,6},{5,7},{6,4},{7,5},{8,10},{9,11},{10,... | collective-permute-start | bytes 196616 | tf_op jit(solution)/shard_map/ppermute | solution.py:32
  11.0 0.7 collective-permute-start.4
  11.7 3.6 %collective-permute-done.3.e2 = f32[8,16,128]{2,1,0:T(8,128)S(1)} collective-permute-done((f32[8,16,128]{2,1,0:T(8,128)S(1)}, f32[8,16,128]{2,1,0:T(8,128)S(1)}, u32[]{:S(2)}, u32[]{:S(2)}) %collective-permute-start.3) | collective-permute-done | bytes 65568 | tf_op jit(solution)/shard_map/ppermute | solution.py:32
  15.3 0.3 shard_map.61
  15.7 1.6 collective-permute-start.9
  17.3 0.3 collective-permute-start.8
  17.6 4.4 %collective-permute-start.7 = (f32[8,16,128]{2,1,0:T(8,128)S(1)}, f32[8,16,128]{2,1,0:T(8,128)S(1)}, u32[]{:S(2)}, u32[]{:S(2)}) collective-permute-start(f32[8,16,128]{2,1,0:T(8,128)S(1)} %get-tuple-element.60.relaxed), channel_id=1, source_target_pairs={{0,17},{1,16},{2,19},{3,18},{4,21},{5,20},{6,23},{7,22},{8,25},{9,... | collective-permute-start | bytes 196616 | tf_op jit(solution)/shard_map/ppermute | solution.py:32
  22.0 4.5 %collective-permute-start.5 = (f32[6,16,128]{2,1,0:T(8,128)S(1)}, f32[6,16,128]{2,1,0:T(8,128)S(1)}, u32[]{:S(2)}, u32[]{:S(2)}) collective-permute-start(f32[6,16,128]{2,1,0:T(8,128)S(1)} %get-tuple-element.61), channel_id=1, source_target_pairs={{0,18},{1,19},{2,16},{3,17},{4,22},{5,23},{6,20},{7,21},{8,26},{9,... | collective-permute-start | bytes 147464 | tf_op jit(solution)/shard_map/ppermute | solution.py:32
  26.4 0.7 collective-permute-start.6
  27.1 0.7 collective-permute-done.5.e2
  27.9 0.5 collective-permute-done.6.o2
  28.3 0.3 shard_map.62.residue
  28.7 2.4 %collective-permute-start.10 = (f32[8,16,128]{2,1,0:T(8,128)S(1)}, f32[8,16,128]{2,1,0:T(8,128)S(1)}, u32[]{:S(2)}, u32[]{:S(2)}) collective-permute-start(f32[8,16,128]{2,1,0:T(8,128)S(1)} %shard_map.62.residue), channel_id=1, source_target_pairs={{0,16},{1,17},{2,18},{3,19},{4,20},{5,21},{6,22},{7,23},{8,24},{9,... | collective-permute-start | bytes 196616 | tf_op jit(solution)/shard_map/ppermute | solution.py:32
  31.1 3.0 %shard_map.63.refs_0_ = f32[64,128]{1,0:T(8,128)S(1)} custom-call(f32[8192,128]{1,0:T(8,128)S(1)} %bitcast.5), custom_call_target="tpu_custom_call" | custom-call | flops 50000000 | bytes 100000 | tf_op jit(solution)/shard_map/pallas_call | solution.py:171
  34.1 3.0 %shard_map.64.gram = f32[64,128]{1,0:T(8,128)S(1)} custom-call(f32[8192,128]{1,0:T(8,128)S(1)} %bitcast.6, f32[64,128]{1,0:T(8,128)S(1)} %shard_map.63.refs_0_), custom_call_target="tpu_custom_call" | custom-call | flops 50000000 | bytes 100000 | tf_op jit(solution)/shard_map/pallas_call | solution.py:171
  37.1 0.4 shard_map.65
  37.5 15.9 %all_to_all.25.got = f32[16,40,128]{2,1,0:T(8,128)S(1)} all-to-all(f32[16,40,128]{2,1,0:T(8,128)S(1)} %shard_map.65), channel_id=1, replica_groups=mesh['tm'=8,'space'=16] {'space'}, dimensions={0} | all-to-all | bytes 655360 | tf_op jit(solution)/shard_map/all_to_all | solution.py:49
  53.4 2.7 %shard_map.66 = (f32[64,128]{1,0:T(8,128)S(1)}, f32[16,16,128]{2,1,0:T(8,128)S(1)}, f32[10,16,128]{2,1,0:T(8,128)S(1)}, f32[10,16,128]{2,1,0:T(8,128)S(1)}, f32[...) custom-call(f32[16,40,128]{2,1,0:T(8,128)S(1)} %all_to_all.25.got, f32[8192,128]{1,0:T(8,128)S(1)} %bitcast.8, ...), custom_call_target="tpu_custom_call" | custom-call | flops 1000000 | bytes 100000 | tf_op jit(solution)/shard_map/pallas_call | solution.py:171
  56.1 2.7 %collective-permute-start.15 = (f32[16,16,128]{2,1,0:T(8,128)S(1)}, f32[16,16,128]{2,1,0:T(8,128)S(1)}, u32[]{:S(2)}, u32[]{:S(2)}) collective-permute-start(f32[16,16,128]{2,1,0:T(8,128)S(1)} %get-tuple-element.67), channel_id=1, source_target_pairs={{0,16},{1,17},{2,18},{3,19},{4,20},{5,21},{6,22},{7,23},{8,24},{9,... | collective-permute-start | bytes 393224 | tf_op jit(solution)/shard_map/ppermute | solution.py:32
  59.0 1.7 collective-permute-start.14
  60.7 2.5 %collective-permute-start.11 = (f32[6,16,128]{2,1,0:T(8,128)S(1)}, f32[6,16,128]{2,1,0:T(8,128)S(1)}, u32[]{:S(2)}, u32[]{:S(2)}) collective-permute-start(f32[6,16,128]{2,1,0:T(8,128)S(1)} %get-tuple-element.63), channel_id=1, source_target_pairs={{0,18},{1,19},{2,16},{3,17},{4,22},{5,23},{6,20},{7,21},{8,26},{9,... | collective-permute-start | bytes 147464 | tf_op jit(solution)/shard_map/ppermute | solution.py:32
  63.2 0.6 collective-permute-start.12
  63.8 1.9 %collective-permute-done.11.e2 = f32[6,16,128]{2,1,0:T(8,128)S(1)} collective-permute-done((f32[6,16,128]{2,1,0:T(8,128)S(1)}, f32[6,16,128]{2,1,0:T(8,128)S(1)}, u32[]{:S(2)}, u32[]{:S(2)}) %collective-permute-start.11) | collective-permute-done | bytes 49184 | tf_op jit(solution)/shard_map/ppermute | solution.py:32
  65.7 0.7 shard_map.67
  66.5 13.2 %all_to_all.26.got = f32[16,1,128]{2,1,0:T(1,128)S(1)} all-to-all(f32[16,1,128]{2,1,0:T(1,128)S(1)} %get-tuple-element.68), channel_id=1, replica_groups=mesh['tm'=8,'space'=16] {'space'}, dimensions={0} | all-to-all | bytes 16384 | tf_op jit(solution)/shard_map/all_to_all | solution.py:49
  79.7 0.4 shard_map.68
  80.1 2.9 %collective-permute-start.20 = (f32[16,16,128]{2,1,0:T(8,128)S(1)}, f32[16,16,128]{2,1,0:T(8,128)S(1)}, u32[]{:S(2)}, u32[]{:S(2)}) collective-permute-start(f32[16,16,128]{2,1,0:T(8,128)S(1)} %get-tuple-element.75), channel_id=1, source_target_pairs={{0,16},{1,17},{2,18},{3,19},{4,20},{5,21},{6,22},{7,23},{8,24},{9,... | collective-permute-start | bytes 393224 | tf_op jit(solution)/shard_map/ppermute | solution.py:32
  83.1 2.1 %collective-permute-start.19 = (f32[10,16,128]{2,1,0:T(8,128)S(1)}, f32[10,16,128]{2,1,0:T(8,128)S(1)}, u32[]{:S(2)}, u32[]{:S(2)}) collective-permute-start(f32[10,16,128]{2,1,0:T(8,128)S(1)} %get-tuple-element.74), channel_id=1, source_target_pairs={{0,16},{1,18},{2,17},{3,20},{4,19},{5,22},{6,21},{7,24},{8,23},{9,... | collective-permute-start | bytes 245768 | tf_op jit(solution)/shard_map/ppermute | solution.py:32
  85.1 2.5 %collective-permute-start.16 = (f32[6,16,128]{2,1,0:T(8,128)S(1)}, f32[6,16,128]{2,1,0:T(8,128)S(1)}, u32[]{:S(2)}, u32[]{:S(2)}) collective-permute-start(f32[6,16,128]{2,1,0:T(8,128)S(1)} %get-tuple-element.71), channel_id=1, source_target_pairs={{0,18},{1,19},{2,16},{3,17},{4,22},{5,23},{6,20},{7,21},{8,26},{9,... | collective-permute-start | bytes 147464 | tf_op jit(solution)/shard_map/ppermute | solution.py:32
  87.6 1.0 collective-permute-start.17
  88.6 2.7 %collective-permute-done.16.e2 = f32[6,16,128]{2,1,0:T(8,128)S(1)} collective-permute-done((f32[6,16,128]{2,1,0:T(8,128)S(1)}, f32[6,16,128]{2,1,0:T(8,128)S(1)}, u32[]{:S(2)}, u32[]{:S(2)}) %collective-permute-start.16) | collective-permute-done | bytes 49184 | tf_op jit(solution)/shard_map/ppermute | solution.py:32
  91.4 0.7 shard_map.69
  92.1 12.3 %all_to_all.27.got = f32[16,1,128]{2,1,0:T(1,128)S(1)} all-to-all(f32[16,1,128]{2,1,0:T(1,128)S(1)} %get-tuple-element.77), channel_id=1, replica_groups=mesh['tm'=8,'space'=16] {'space'}, dimensions={0} | all-to-all | bytes 16384 | tf_op jit(solution)/shard_map/all_to_all | solution.py:49
  104.4 0.4 shard_map.70
  104.8 3.3 %collective-permute-start.25 = (f32[16,16,128]{2,1,0:T(8,128)S(1)}, f32[16,16,128]{2,1,0:T(8,128)S(1)}, u32[]{:S(2)}, u32[]{:S(2)}) collective-permute-start(f32[16,16,128]{2,1,0:T(8,128)S(1)} %get-tuple-element.83), channel_id=1, source_target_pairs={{0,16},{1,17},{2,18},{3,19},{4,20},{5,21},{6,22},{7,23},{8,24},{9,... | collective-permute-start | bytes 393224 | tf_op jit(solution)/shard_map/ppermute | solution.py:32
  108.1 2.9 %collective-permute-start.24 = (f32[10,16,128]{2,1,0:T(8,128)S(1)}, f32[10,16,128]{2,1,0:T(8,128)S(1)}, u32[]{:S(2)}, u32[]{:S(2)}) collective-permute-start(f32[10,16,128]{2,1,0:T(8,128)S(1)} %get-tuple-element.82), channel_id=1, source_target_pairs={{0,16},{1,18},{2,17},{3,20},{4,19},{5,22},{6,21},{7,24},{8,23},{9,... | collective-permute-start | bytes 245768 | tf_op jit(solution)/shard_map/ppermute | solution.py:32
  111.1 2.5 %collective-permute-start.21 = (f32[6,16,128]{2,1,0:T(8,128)S(1)}, f32[6,16,128]{2,1,0:T(8,128)S(1)}, u32[]{:S(2)}, u32[]{:S(2)}) collective-permute-start(f32[6,16,128]{2,1,0:T(8,128)S(1)} %get-tuple-element.79), channel_id=1, source_target_pairs={{0,18},{1,19},{2,16},{3,17},{4,22},{5,23},{6,20},{7,21},{8,26},{9,... | collective-permute-start | bytes 147464 | tf_op jit(solution)/shard_map/ppermute | solution.py:32
  113.6 3.0 %collective-permute-done.21.e2 = f32[6,16,128]{2,1,0:T(8,128)S(1)} collective-permute-done((f32[6,16,128]{2,1,0:T(8,128)S(1)}, f32[6,16,128]{2,1,0:T(8,128)S(1)}, u32[]{:S(2)}, u32[]{:S(2)}) %collective-permute-start.21) | collective-permute-done | bytes 49184 | tf_op jit(solution)/shard_map/ppermute | solution.py:32
  116.6 0.3 shard_map.71
  117.0 1.6 collective-permute-start.28
  118.6 1.4 collective-permute-start.26
  120.0 4.2 %collective-permute-start.27 = (f32[6,16,128]{2,1,0:T(8,128)S(1)}, f32[6,16,128]{2,1,0:T(8,128)S(1)}, u32[]{:S(2)}, u32[]{:S(2)}) collective-permute-start(f32[6,16,128]{2,1,0:T(8,128)S(1)} %get-tuple-element.86), channel_id=1, source_target_pairs={{0,65},{1,64},{2,67},{3,66},{4,69},{5,68},{6,71},{7,70},{8,73},{9,... | collective-permute-start | bytes 147464 | tf_op jit(solution)/shard_map/ppermute | solution.py:32
  124.3 2.0 %collective-permute-done.27.e1 = f32[6,16,128]{2,1,0:T(8,128)S(1)} collective-permute-done((f32[6,16,128]{2,1,0:T(8,128)S(1)}, f32[6,16,128]{2,1,0:T(8,128)S(1)}, u32[]{:S(2)}, u32[]{:S(2)}) %collective-permute-start.27) | collective-permute-done | bytes 49184 | tf_op jit(solution)/shard_map/ppermute | solution.py:32
  126.3 0.5 shard_map.72
  126.8 14.1 %all_to_all.28.got = f32[16,1,128]{2,1,0:T(1,128)S(1)} all-to-all(f32[16,1,128]{2,1,0:T(1,128)S(1)} %get-tuple-element.89), channel_id=1, replica_groups=mesh['tm'=8,'space'=16] {'space'}, dimensions={0} | all-to-all | bytes 16384 | tf_op jit(solution)/shard_map/all_to_all | solution.py:49
  140.9 0.4 shard_map.73
  141.3 0.4 collective-permute-start.31
  141.7 3.7 %collective-permute-start.32 = (f32[10,16,128]{2,1,0:T(8,128)S(1)}, f32[10,16,128]{2,1,0:T(8,128)S(1)}, u32[]{:S(2)}, u32[]{:S(2)}) collective-permute-start(f32[10,16,128]{2,1,0:T(8,128)S(1)} %get-tuple-element.94), channel_id=1, source_target_pairs={{0,16},{1,2},{2,1},{3,4},{4,3},{5,6},{6,5},{7,8},{8,7},{9,10},{10,... | collective-permute-start | bytes 245768 | tf_op jit(solution)/shard_map/ppermute | solution.py:32
  145.4 3.5 %collective-permute-start.30 = (f32[6,16,128]{2,1,0:T(8,128)S(1)}, f32[6,16,128]{2,1,0:T(8,128)S(1)}, u32[]{:S(2)}, u32[]{:S(2)}) collective-permute-start(f32[6,16,128]{2,1,0:T(8,128)S(1)} %get-tuple-element.92), channel_id=1, source_target_pairs={{0,16},{1,17},{2,4},{3,5},{4,2},{5,3},{6,8},{7,9},{8,6},{9,7},{10,... | collective-permute-start | bytes 147464 | tf_op jit(solution)/shard_map/ppermute | solution.py:32
  149.0 0.9 collective-permute-done.29.e2
  149.9 1.6 collective-permute-done.30.o2
  151.4 0.7 shard_map.74
  152.2 1.1 collective-permute-start.37
  153.4 4.3 %collective-permute-start.35 = (f32[8,16,128]{2,1,0:T(8,128)S(1)}, f32[8,16,128]{2,1,0:T(8,128)S(1)}, u32[]{:S(2)}, u32[]{:S(2)}) collective-permute-start(f32[8,16,128]{2,1,0:T(8,128)S(1)} %get-tuple-element.96.final), channel_id=1, source_target_pairs={{0,17},{1,16},{2,19},{3,18},{4,21},{5,20},{6,23},{7,22},{8,25},{9,... | collective-permute-start | bytes 196616 | tf_op jit(solution)/shard_map/ppermute | solution.py:32
  157.8 4.3 %collective-permute-start.33 = (f32[2,16,128]{2,1,0:T(8,128)S(1)}, f32[2,16,128]{2,1,0:T(8,128)S(1)}, u32[]{:S(2)}, u32[]{:S(2)}) collective-permute-start(f32[2,16,128]{2,1,0:T(8,128)S(1)} %get-tuple-element.97), channel_id=1, source_target_pairs={{0,18},{1,19},{2,16},{3,17},{4,22},{5,23},{6,20},{7,21},{8,26},{9,... | collective-permute-start | bytes 49160 | tf_op jit(solution)/shard_map/ppermute | solution.py:32
  162.0 0.4 collective-permute-start.34
  162.4 10.7 %all_to_all.29.got = f32[16,1,128]{2,1,0:T(1,128)S(1)} all-to-all(f32[16,1,128]{2,1,0:T(1,128)S(1)} %get-tuple-element.99), channel_id=1, replica_groups=mesh['tm'=8,'space'=16] {'space'}, dimensions={0} | all-to-all | bytes 16384 | tf_op jit(solution)/shard_map/all_to_all | solution.py:49
  173.1 0.9 shard_map.75
  (42 shorter events, 0.7 us)
Async XLA Ops:
  0.6 6.4 %collective-permute-start = (f32[8,16,128]{2,1,0:T(8,128)}, f32[8,16,128]{2,1,0:T(8,128)S(1)}, u32[]{:S(2)}, u32[]{:S(2)}) collective-permute-start(f32[8,16,128]{2,1,0:T(8,128)} %bitcast.17), channel_id=1, source_target_pairs={{0,16},{1,17},{2,18},{3,19},{4,20},{5,21},{6,22},{7,23},{8,24},{9,... | collective-permute-start | bytes 196616 | tf_op jit(solution)/shard_map/ppermute | solution.py:32
  3.2 2.2 %copy-start = (f32[1,64,4,2,16,128]{5,4,3,2,1,0:T(8,128)S(1)}, f32[1,64,4,2,16,128]{5,4,3,2,1,0:T(8,128)}, u32[]{:S(2)}) copy-start(f32[1,64,4,2,16,128]{5,4,3,2,1,0:T(8,128)} %param.7) | copy-start | bytes 12582916
  5.4 0.8 copy-start.2
  6.3 0.7 copy-start.3
  7.0 24.1 %copy-start.1 = (f32[1,64,4,2,16,128]{5,4,3,2,1,0:T(8,128)S(1)}, f32[1,64,4,2,16,128]{5,4,3,2,1,0:T(8,128)}, u32[]{:S(2)}) copy-start(f32[1,64,4,2,16,128]{5,4,3,2,1,0:T(8,128)} %param.7) | copy-start | bytes 12582916
  7.0 8.3 %collective-permute-start.1 = (f32[15,16,128]{2,1,0:T(8,128)S(1)}, f32[15,16,128]{2,1,0:T(8,128)S(1)}, u32[]{:S(2)}, u32[]{:S(2)}) collective-permute-start(f32[15,16,128]{2,1,0:T(8,128)S(1)} %get-tuple-element.54), channel_id=1, source_target_pairs={{0,1},{1,0},{2,3},{3,2},{4,5},{5,4},{6,7},{7,6},{8,9},{9,8},{10,11... | collective-permute-start | bytes 368648 | tf_op jit(solution)/shard_map/ppermute | solution.py:32
  8.4 6.9 %collective-permute-start.2 = (f32[15,16,128]{2,1,0:T(8,128)S(1)}, f32[15,16,128]{2,1,0:T(8,128)S(1)}, u32[]{:S(2)}, u32[]{:S(2)}) collective-permute-start(f32[15,16,128]{2,1,0:T(8,128)S(1)} %get-tuple-element.55), channel_id=1, source_target_pairs={{0,16},{1,2},{2,1},{3,4},{4,3},{5,6},{6,5},{7,8},{8,7},{9,10},{10,... | collective-permute-start | bytes 368648 | tf_op jit(solution)/shard_map/ppermute | solution.py:32
  8.8 6.5 %collective-permute-start.3 = (f32[8,16,128]{2,1,0:T(8,128)S(1)}, f32[8,16,128]{2,1,0:T(8,128)S(1)}, u32[]{:S(2)}, u32[]{:S(2)}) collective-permute-start(f32[8,16,128]{2,1,0:T(8,128)S(1)} %get-tuple-element.56), channel_id=1, source_target_pairs={{0,2},{1,3},{2,0},{3,1},{4,6},{5,7},{6,4},{7,5},{8,10},{9,11},{10,... | collective-permute-start | bytes 196616 | tf_op jit(solution)/shard_map/ppermute | solution.py:32
  11.0 4.3 %collective-permute-start.4 = (f32[8,16,128]{2,1,0:T(8,128)S(1)}, f32[8,16,128]{2,1,0:T(8,128)S(1)}, u32[]{:S(2)}, u32[]{:S(2)}) collective-permute-start(f32[8,16,128]{2,1,0:T(8,128)S(1)} %get-tuple-element.57), channel_id=1, source_target_pairs={{0,16},{1,17},{2,4},{3,5},{4,2},{5,3},{6,8},{7,9},{8,6},{9,7},{10,... | collective-permute-start | bytes 196616 | tf_op jit(solution)/shard_map/ppermute | solution.py:32
  15.7 12.6 %collective-permute-start.9 = (f32[8,16,128]{2,1,0:T(8,128)S(1)}, f32[8,16,128]{2,1,0:T(8,128)S(1)}, u32[]{:S(2)}, u32[]{:S(2)}) collective-permute-start(f32[8,16,128]{2,1,0:T(8,128)S(1)} %get-tuple-element.60.relaxed), channel_id=1, source_target_pairs={{0,16},{1,17},{2,18},{3,19},{4,20},{5,21},{6,22},{7,23},{8,24},{9,... | collective-permute-start | bytes 196616 | tf_op jit(solution)/shard_map/ppermute | solution.py:32
  17.3 11.1 %collective-permute-start.8 = (f32[8,16,128]{2,1,0:T(8,128)S(1)}, f32[8,16,128]{2,1,0:T(8,128)S(1)}, u32[]{:S(2)}, u32[]{:S(2)}) collective-permute-start(f32[8,16,128]{2,1,0:T(8,128)S(1)} %get-tuple-element.60.relaxed), channel_id=1, source_target_pairs={{0,16},{1,18},{2,17},{3,20},{4,19},{5,22},{6,21},{7,24},{8,23},{9,... | collective-permute-start | bytes 196616 | tf_op jit(solution)/shard_map/ppermute | solution.py:32
  17.6 10.7 %collective-permute-start.7 = (f32[8,16,128]{2,1,0:T(8,128)S(1)}, f32[8,16,128]{2,1,0:T(8,128)S(1)}, u32[]{:S(2)}, u32[]{:S(2)}) collective-permute-start(f32[8,16,128]{2,1,0:T(8,128)S(1)} %get-tuple-element.60.relaxed), channel_id=1, source_target_pairs={{0,17},{1,16},{2,19},{3,18},{4,21},{5,20},{6,23},{7,22},{8,25},{9,... | collective-permute-start | bytes 196616 | tf_op jit(solution)/shard_map/ppermute | solution.py:32
  22.0 5.9 %collective-permute-start.5 = (f32[6,16,128]{2,1,0:T(8,128)S(1)}, f32[6,16,128]{2,1,0:T(8,128)S(1)}, u32[]{:S(2)}, u32[]{:S(2)}) collective-permute-start(f32[6,16,128]{2,1,0:T(8,128)S(1)} %get-tuple-element.61), channel_id=1, source_target_pairs={{0,18},{1,19},{2,16},{3,17},{4,22},{5,23},{6,20},{7,21},{8,26},{9,... | collective-permute-start | bytes 147464 | tf_op jit(solution)/shard_map/ppermute | solution.py:32
  26.4 1.9 %collective-permute-start.6 = (f32[6,16,128]{2,1,0:T(8,128)S(1)}, f32[6,16,128]{2,1,0:T(8,128)S(1)}, u32[]{:S(2)}, u32[]{:S(2)}) collective-permute-start(f32[6,16,128]{2,1,0:T(8,128)S(1)} %get-tuple-element.62), channel_id=1, source_target_pairs={{0,16},{1,17},{2,20},{3,21},{4,18},{5,19},{6,24},{7,25},{8,22},{9,... | collective-permute-start | bytes 147464 | tf_op jit(solution)/shard_map/ppermute | solution.py:32
  28.7 8.4 %collective-permute-start.10 = (f32[8,16,128]{2,1,0:T(8,128)S(1)}, f32[8,16,128]{2,1,0:T(8,128)S(1)}, u32[]{:S(2)}, u32[]{:S(2)}) collective-permute-start(f32[8,16,128]{2,1,0:T(8,128)S(1)} %shard_map.62.residue), channel_id=1, source_target_pairs={{0,16},{1,17},{2,18},{3,19},{4,20},{5,21},{6,22},{7,23},{8,24},{9,... | collective-permute-start | bytes 196616 | tf_op jit(solution)/shard_map/ppermute | solution.py:32
  56.1 9.6 %collective-permute-start.15 = (f32[16,16,128]{2,1,0:T(8,128)S(1)}, f32[16,16,128]{2,1,0:T(8,128)S(1)}, u32[]{:S(2)}, u32[]{:S(2)}) collective-permute-start(f32[16,16,128]{2,1,0:T(8,128)S(1)} %get-tuple-element.67), channel_id=1, source_target_pairs={{0,16},{1,17},{2,18},{3,19},{4,20},{5,21},{6,22},{7,23},{8,24},{9,... | collective-permute-start | bytes 393224 | tf_op jit(solution)/shard_map/ppermute | solution.py:32
  58.8 6.9 %collective-permute-start.13 = (f32[10,16,128]{2,1,0:T(8,128)S(1)}, f32[10,16,128]{2,1,0:T(8,128)S(1)}, u32[]{:S(2)}, u32[]{:S(2)}) collective-permute-start(f32[10,16,128]{2,1,0:T(8,128)S(1)} %get-tuple-element.65), channel_id=1, source_target_pairs={{0,17},{1,16},{2,19},{3,18},{4,21},{5,20},{6,23},{7,22},{8,25},{9,... | collective-permute-start | bytes 245768 | tf_op jit(solution)/shard_map/ppermute | solution.py:32
  59.0 6.7 %collective-permute-start.14 = (f32[10,16,128]{2,1,0:T(8,128)S(1)}, f32[10,16,128]{2,1,0:T(8,128)S(1)}, u32[]{:S(2)}, u32[]{:S(2)}) collective-permute-start(f32[10,16,128]{2,1,0:T(8,128)S(1)} %get-tuple-element.66), channel_id=1, source_target_pairs={{0,16},{1,18},{2,17},{3,20},{4,19},{5,22},{6,21},{7,24},{8,23},{9,... | collective-permute-start | bytes 245768 | tf_op jit(solution)/shard_map/ppermute | solution.py:32
  60.7 5.1 %collective-permute-start.11 = (f32[6,16,128]{2,1,0:T(8,128)S(1)}, f32[6,16,128]{2,1,0:T(8,128)S(1)}, u32[]{:S(2)}, u32[]{:S(2)}) collective-permute-start(f32[6,16,128]{2,1,0:T(8,128)S(1)} %get-tuple-element.63), channel_id=1, source_target_pairs={{0,18},{1,19},{2,16},{3,17},{4,22},{5,23},{6,20},{7,21},{8,26},{9,... | collective-permute-start | bytes 147464 | tf_op jit(solution)/shard_map/ppermute | solution.py:32
  63.2 2.5 %collective-permute-start.12 = (f32[6,16,128]{2,1,0:T(8,128)S(1)}, f32[6,16,128]{2,1,0:T(8,128)S(1)}, u32[]{:S(2)}, u32[]{:S(2)}) collective-permute-start(f32[6,16,128]{2,1,0:T(8,128)S(1)} %get-tuple-element.64), channel_id=1, source_target_pairs={{0,16},{1,17},{2,20},{3,21},{4,18},{5,19},{6,24},{7,25},{8,22},{9,... | collective-permute-start | bytes 147464 | tf_op jit(solution)/shard_map/ppermute | solution.py:32
  80.1 11.3 %collective-permute-start.20 = (f32[16,16,128]{2,1,0:T(8,128)S(1)}, f32[16,16,128]{2,1,0:T(8,128)S(1)}, u32[]{:S(2)}, u32[]{:S(2)}) collective-permute-start(f32[16,16,128]{2,1,0:T(8,128)S(1)} %get-tuple-element.75), channel_id=1, source_target_pairs={{0,16},{1,17},{2,18},{3,19},{4,20},{5,21},{6,22},{7,23},{8,24},{9,... | collective-permute-start | bytes 393224 | tf_op jit(solution)/shard_map/ppermute | solution.py:32
  83.0 8.4 %collective-permute-start.18 = (f32[10,16,128]{2,1,0:T(8,128)S(1)}, f32[10,16,128]{2,1,0:T(8,128)S(1)}, u32[]{:S(2)}, u32[]{:S(2)}) collective-permute-start(f32[10,16,128]{2,1,0:T(8,128)S(1)} %get-tuple-element.73), channel_id=1, source_target_pairs={{0,17},{1,16},{2,19},{3,18},{4,21},{5,20},{6,23},{7,22},{8,25},{9,... | collective-permute-start | bytes 245768 | tf_op jit(solution)/shard_map/ppermute | solution.py:32
  83.1 8.3 %collective-permute-start.19 = (f32[10,16,128]{2,1,0:T(8,128)S(1)}, f32[10,16,128]{2,1,0:T(8,128)S(1)}, u32[]{:S(2)}, u32[]{:S(2)}) collective-permute-start(f32[10,16,128]{2,1,0:T(8,128)S(1)} %get-tuple-element.74), channel_id=1, source_target_pairs={{0,16},{1,18},{2,17},{3,20},{4,19},{5,22},{6,21},{7,24},{8,23},{9,... | collective-permute-start | bytes 245768 | tf_op jit(solution)/shard_map/ppermute | solution.py:32
  85.1 6.2 %collective-permute-start.16 = (f32[6,16,128]{2,1,0:T(8,128)S(1)}, f32[6,16,128]{2,1,0:T(8,128)S(1)}, u32[]{:S(2)}, u32[]{:S(2)}) collective-permute-start(f32[6,16,128]{2,1,0:T(8,128)S(1)} %get-tuple-element.71), channel_id=1, source_target_pairs={{0,18},{1,19},{2,16},{3,17},{4,22},{5,23},{6,20},{7,21},{8,26},{9,... | collective-permute-start | bytes 147464 | tf_op jit(solution)/shard_map/ppermute | solution.py:32
  87.6 3.8 %collective-permute-start.17 = (f32[6,16,128]{2,1,0:T(8,128)S(1)}, f32[6,16,128]{2,1,0:T(8,128)S(1)}, u32[]{:S(2)}, u32[]{:S(2)}) collective-permute-start(f32[6,16,128]{2,1,0:T(8,128)S(1)} %get-tuple-element.72), channel_id=1, source_target_pairs={{0,16},{1,17},{2,20},{3,21},{4,18},{5,19},{6,24},{7,25},{8,22},{9,... | collective-permute-start | bytes 147464 | tf_op jit(solution)/shard_map/ppermute | solution.py:32
  104.8 11.8 %collective-permute-start.25 = (f32[16,16,128]{2,1,0:T(8,128)S(1)}, f32[16,16,128]{2,1,0:T(8,128)S(1)}, u32[]{:S(2)}, u32[]{:S(2)}) collective-permute-start(f32[16,16,128]{2,1,0:T(8,128)S(1)} %get-tuple-element.83), channel_id=1, source_target_pairs={{0,16},{1,17},{2,18},{3,19},{4,20},{5,21},{6,22},{7,23},{8,24},{9,... | collective-permute-start | bytes 393224 | tf_op jit(solution)/shard_map/ppermute | solution.py:32
  108.0 8.6 %collective-permute-start.23 = (f32[10,16,128]{2,1,0:T(8,128)S(1)}, f32[10,16,128]{2,1,0:T(8,128)S(1)}, u32[]{:S(2)}, u32[]{:S(2)}) collective-permute-start(f32[10,16,128]{2,1,0:T(8,128)S(1)} %get-tuple-element.81), channel_id=1, source_target_pairs={{0,17},{1,16},{2,19},{3,18},{4,21},{5,20},{6,23},{7,22},{8,25},{9,... | collective-permute-start | bytes 245768 | tf_op jit(solution)/shard_map/ppermute | solution.py:32
  108.1 8.5 %collective-permute-start.24 = (f32[10,16,128]{2,1,0:T(8,128)S(1)}, f32[10,16,128]{2,1,0:T(8,128)S(1)}, u32[]{:S(2)}, u32[]{:S(2)}) collective-permute-start(f32[10,16,128]{2,1,0:T(8,128)S(1)} %get-tuple-element.82), channel_id=1, source_target_pairs={{0,16},{1,18},{2,17},{3,20},{4,19},{5,22},{6,21},{7,24},{8,23},{9,... | collective-permute-start | bytes 245768 | tf_op jit(solution)/shard_map/ppermute | solution.py:32
  111.1 5.5 %collective-permute-start.21 = (f32[6,16,128]{2,1,0:T(8,128)S(1)}, f32[6,16,128]{2,1,0:T(8,128)S(1)}, u32[]{:S(2)}, u32[]{:S(2)}) collective-permute-start(f32[6,16,128]{2,1,0:T(8,128)S(1)} %get-tuple-element.79), channel_id=1, source_target_pairs={{0,18},{1,19},{2,16},{3,17},{4,22},{5,23},{6,20},{7,21},{8,26},{9,... | collective-permute-start | bytes 147464 | tf_op jit(solution)/shard_map/ppermute | solution.py:32
  113.6 3.1 %collective-permute-start.22 = (f32[6,16,128]{2,1,0:T(8,128)S(1)}, f32[6,16,128]{2,1,0:T(8,128)S(1)}, u32[]{:S(2)}, u32[]{:S(2)}) collective-permute-start(f32[6,16,128]{2,1,0:T(8,128)S(1)} %get-tuple-element.80), channel_id=1, source_target_pairs={{0,16},{1,17},{2,20},{3,21},{4,18},{5,19},{6,24},{7,25},{8,22},{9,... | collective-permute-start | bytes 147464 | tf_op jit(solution)/shard_map/ppermute | solution.py:32
  117.0 9.3 %collective-permute-start.28 = (f32[8,16,128]{2,1,0:T(8,128)S(1)}, f32[8,16,128]{2,1,0:T(8,128)S(1)}, u32[]{:S(2)}, u32[]{:S(2)}) collective-permute-start(f32[8,16,128]{2,1,0:T(8,128)S(1)} %get-tuple-element.87), channel_id=1, source_target_pairs={{0,64},{1,65},{2,66},{3,67},{4,68},{5,69},{6,70},{7,71},{8,72},{9,... | collective-permute-start | bytes 196616 | tf_op jit(solution)/shard_map/ppermute | solution.py:32
  118.6 5.7 %collective-permute-start.26 = (f32[6,16,128]{2,1,0:T(8,128)S(1)}, f32[6,16,128]{2,1,0:T(8,128)S(1)}, u32[]{:S(2)}, u32[]{:S(2)}) collective-permute-start(f32[6,16,128]{2,1,0:T(8,128)S(1)} %get-tuple-element.85), channel_id=1, source_target_pairs={{0,64},{1,66},{2,65},{3,68},{4,67},{5,70},{6,69},{7,72},{8,71},{9,... | collective-permute-start | bytes 147464 | tf_op jit(solution)/shard_map/ppermute | solution.py:32
  120.0 6.2 %collective-permute-start.27 = (f32[6,16,128]{2,1,0:T(8,128)S(1)}, f32[6,16,128]{2,1,0:T(8,128)S(1)}, u32[]{:S(2)}, u32[]{:S(2)}) collective-permute-start(f32[6,16,128]{2,1,0:T(8,128)S(1)} %get-tuple-element.86), channel_id=1, source_target_pairs={{0,65},{1,64},{2,67},{3,66},{4,69},{5,68},{6,71},{7,70},{8,73},{9,... | collective-permute-start | bytes 147464 | tf_op jit(solution)/shard_map/ppermute | solution.py:32
  141.3 10.1 %collective-permute-start.31 = (f32[10,16,128]{2,1,0:T(8,128)S(1)}, f32[10,16,128]{2,1,0:T(8,128)S(1)}, u32[]{:S(2)}, u32[]{:S(2)}) collective-permute-start(f32[10,16,128]{2,1,0:T(8,128)S(1)} %get-tuple-element.93), channel_id=1, source_target_pairs={{0,1},{1,0},{2,3},{3,2},{4,5},{5,4},{6,7},{7,6},{8,9},{9,8},{10,11... | collective-permute-start | bytes 245768 | tf_op jit(solution)/shard_map/ppermute | solution.py:32
  141.7 9.7 %collective-permute-start.32 = (f32[10,16,128]{2,1,0:T(8,128)S(1)}, f32[10,16,128]{2,1,0:T(8,128)S(1)}, u32[]{:S(2)}, u32[]{:S(2)}) collective-permute-start(f32[10,16,128]{2,1,0:T(8,128)S(1)} %get-tuple-element.94), channel_id=1, source_target_pairs={{0,16},{1,2},{2,1},{3,4},{4,3},{5,6},{6,5},{7,8},{8,7},{9,10},{10,... | collective-permute-start | bytes 245768 | tf_op jit(solution)/shard_map/ppermute | solution.py:32
  145.4 4.4 %collective-permute-start.29 = (f32[6,16,128]{2,1,0:T(8,128)S(1)}, f32[6,16,128]{2,1,0:T(8,128)S(1)}, u32[]{:S(2)}, u32[]{:S(2)}) collective-permute-start(f32[6,16,128]{2,1,0:T(8,128)S(1)} %get-tuple-element.91), channel_id=1, source_target_pairs={{0,2},{1,3},{2,0},{3,1},{4,6},{5,7},{6,4},{7,5},{8,10},{9,11},{10,... | collective-permute-start | bytes 147464 | tf_op jit(solution)/shard_map/ppermute | solution.py:32
  145.4 6.0 %collective-permute-start.30 = (f32[6,16,128]{2,1,0:T(8,128)S(1)}, f32[6,16,128]{2,1,0:T(8,128)S(1)}, u32[]{:S(2)}, u32[]{:S(2)}) collective-permute-start(f32[6,16,128]{2,1,0:T(8,128)S(1)} %get-tuple-element.92), channel_id=1, source_target_pairs={{0,16},{1,17},{2,4},{3,5},{4,2},{5,3},{6,8},{7,9},{8,6},{9,7},{10,... | collective-permute-start | bytes 147464 | tf_op jit(solution)/shard_map/ppermute | solution.py:32
  152.2 20.9 %collective-permute-start.37 = (f32[8,16,128]{2,1,0:T(8,128)S(1)}, f32[8,16,128]{2,1,0:T(8,128)S(1)}, u32[]{:S(2)}, u32[]{:S(2)}) collective-permute-start(f32[8,16,128]{2,1,0:T(8,128)S(1)} %get-tuple-element.96.final), channel_id=1, source_target_pairs={{0,16},{1,17},{2,18},{3,19},{4,20},{5,21},{6,22},{7,23},{8,24},{9,... | collective-permute-start | bytes 196616 | tf_op jit(solution)/shard_map/ppermute | solution.py:32
  153.2 19.8 %collective-permute-start.36 = (f32[8,16,128]{2,1,0:T(8,128)S(1)}, f32[8,16,128]{2,1,0:T(8,128)S(1)}, u32[]{:S(2)}, u32[]{:S(2)}) collective-permute-start(f32[8,16,128]{2,1,0:T(8,128)S(1)} %get-tuple-element.96.final), channel_id=1, source_target_pairs={{0,16},{1,18},{2,17},{3,20},{4,19},{5,22},{6,21},{7,24},{8,23},{9,... | collective-permute-start | bytes 196616 | tf_op jit(solution)/shard_map/ppermute | solution.py:32
  153.4 19.6 %collective-permute-start.35 = (f32[8,16,128]{2,1,0:T(8,128)S(1)}, f32[8,16,128]{2,1,0:T(8,128)S(1)}, u32[]{:S(2)}, u32[]{:S(2)}) collective-permute-start(f32[8,16,128]{2,1,0:T(8,128)S(1)} %get-tuple-element.96.final), channel_id=1, source_target_pairs={{0,17},{1,16},{2,19},{3,18},{4,21},{5,20},{6,23},{7,22},{8,25},{9,... | collective-permute-start | bytes 196616 | tf_op jit(solution)/shard_map/ppermute | solution.py:32
  157.8 15.3 %collective-permute-start.33 = (f32[2,16,128]{2,1,0:T(8,128)S(1)}, f32[2,16,128]{2,1,0:T(8,128)S(1)}, u32[]{:S(2)}, u32[]{:S(2)}) collective-permute-start(f32[2,16,128]{2,1,0:T(8,128)S(1)} %get-tuple-element.97), channel_id=1, source_target_pairs={{0,18},{1,19},{2,16},{3,17},{4,22},{5,23},{6,20},{7,21},{8,26},{9,... | collective-permute-start | bytes 49160 | tf_op jit(solution)/shard_map/ppermute | solution.py:32
  162.0 11.0 %collective-permute-start.34 = (f32[2,16,128]{2,1,0:T(8,128)S(1)}, f32[2,16,128]{2,1,0:T(8,128)S(1)}, u32[]{:S(2)}, u32[]{:S(2)}) collective-permute-start(f32[2,16,128]{2,1,0:T(8,128)S(1)} %get-tuple-element.98), channel_id=1, source_target_pairs={{0,16},{1,17},{2,20},{3,21},{4,18},{5,19},{6,24},{7,25},{8,22},{9,... | collective-permute-start | bytes 49160 | tf_op jit(solution)/shard_map/ppermute | solution.py:32

commit v5 on v4

--- a/solution.py
+++ b/solution.py
@@ -179,8 +179,7 @@
     )(*args)
 
 
-def stage_kernel(f_ref, c_ref, basis, f_out, c2_out):
-    f_out[...] = f_ref[...]
+def stage_kernel(c_ref, basis, c2_out):
     c2_out[...] = c_ref[...] * c_ref[...]
 
 
@@ -229,16 +228,17 @@
         at = put(loads_out, at, load)
 
 
-def kept_loads(loads_ref):
-    starts = [sum(LOADS[:i]) for i in range(4)]
+def kept_loads(loads_ref, base=0):
+    starts = [base + sum(LOADS[:i]) for i in range(4)]
     return [loads_ref[start : start + n] for start, n in zip(starts, LOADS)]
 
 
-def residue_kernel(relaxed, loads_ref, med, e2, o2, e1, o1, own, out):
+def residue_kernel(relaxed, loads_ref, med, e2, o2, e1, o1, own, out, back):
     ok = flags()
     p, vx, vy, vz = wide(own[...], *halo_of((e1, o1), (e2, o2)), ok)
     u = advance_many(p, vx, vy, vz, med[...], DT, 4, ok[0], ok[2], kept_loads(loads_ref))[-1]
     out[...] = u - relaxed[...]
+    put(back, put(back, 0, u), loads_ref[...])
 
 
 def gram_kernel(parts, basis, *refs):
@@ -307,7 +307,7 @@
     lane = lax.broadcasted_iota(jnp.int32, (RANK, NY), 1)
     row = lax.broadcasted_iota(jnp.int32, (RANK, NY), 0)
     work = jnp.where(lane < RANK, g, jnp.where(lane - RANK == row, 1.0, 0.0))
-    block = 4
+    block = 8
     for start in range(0, RANK, block):
         columns = [
             jnp.broadcast_to(work[:, j : j + 1], (RANK, NY)) for j in range(start, start + block)
@@ -415,15 +415,15 @@
     put_copies(row_out, inner_products(basis, x, scratch))
 
 
-def final_kernel(med, e2, o2, e1, o1, center, relaxed, residue, basis, out, e_out, o_out, row_out, scratch):
-    u = relaxed[...] + (q_of(med, e2, o2, e1, o1, center) + residue[...])
+def final_kernel(med, e2, o2, e1, o1, center, back, basis, out, e_out, o_out, row_out, scratch):
+    u = q_of(med, e2, o2, e1, o1, center) + back[0:8]
     out[...] = u
     up2 = ways()[1]
     put_both((e_out, o_out), up2, 0, [], [u[1:2], u[7:8]], [u[0:1], u[6:7]])
     put_copies(row_out, inner_products(basis, u, scratch))
 
 
-def sweep_kernel(loads_ref, med, final, e2, o2, e1, o1, own, got, ginv, out, coords, kept, kept_row, sems):
+def sweep_kernel(back, med, final, e2, o2, e1, o1, own, got, ginv, out, coords, kept, kept_row, sems):
     def copy(row, source):
         return pltpu.make_async_copy(source, out.at[row], sems.at[row])
 
@@ -434,7 +434,7 @@
     copies.append(pltpu.make_async_copy(kept_row, coords, sems.at[4]))
     copies[1].start()
     ok = flags()
-    loads = [load[1:-1] for load in kept_loads(loads_ref)[:3]]
+    loads = [load[1:-1] for load in kept_loads(back, 8)[:3]]
     b1, a1, b2, a2 = halo_of((e1, o1), (e2, o2))
     u = own[...]
     p = cat(
@@ -470,14 +470,11 @@
             result.append(hop(center, by_tm))
         return result
 
-    start = hop(guess.reshape(state), 1)
-    load, c2 = call(stage_kernel, [(4, 2, NX, NY), (2, NX, NY)], forcing, speed, columns)
+    start = hop(guess.reshape(state), 2)
+    load = hop(forcing, 1)
+    (c2,) = call(stage_kernel, [(2, NX, NY)], speed, columns)
     e1, o1, e2, o2 = call(
-        pack_kernel,
-        [(15, NX, NY), (15, NX, NY), (8, NX, NY), (8, NX, NY)],
-        start,
-        load,
-        c2,
+        pack_kernel, [(15, NX, NY), (15, NX, NY), (8, NX, NY), (8, NX, NY)], start, load, c2
     )
     e2, o2, e1, o1 = traded((e1, o1), (e2, o2), None, 0)
     (gram,) = call(
@@ -495,11 +492,9 @@
         o2,
     )
     near = traded((relaxed, relaxed), (e, o), relaxed, 1)
-    (residue,) = call(residue_kernel, [state], relaxed, loads, med, *near)
-    x = hop(residue, 1)
-    (gram,) = call(
-        functools.partial(gram_kernel, (4, 8)), [(RANK, NY)], columns, gram, scratch=split, flops=50_000_000
-    )
+    (gram,) = call(functools.partial(gram_kernel, (4, 8)), [(RANK, NY)], columns, gram, scratch=split, flops=50_000_000)
+    x, back = call(residue_kernel, [state, (8 + sum(LOADS), NX, NY)], relaxed, loads, med, *near)
+    back = hop(back, -1)
     (rows,) = call(first_kernel, [(N_SP, RANK // 2 + 8, NY)], columns, x, gram, scratch=table)
     ginv, *packed = call(
         first_project_kernel, [(RANK, NY), *PROJECTED], share(rows), columns, x, scratch=table
@@ -528,8 +523,7 @@
         [state, (2, NX, NY), (2, NX, NY), copies],
         med,
         *exchanged(packed, 0),
-        relaxed,
-        residue,
+        back,
         columns,
         scratch=table,
     )
@@ -538,7 +532,7 @@
     states, coords = call(
         sweep_kernel,
         [(4, 8, NX, NY), (1, NY)],
-        loads,
+        back,
         med,
         final,
         *near,

time: 176 us -> 173 us (0.983)
    unnamed x8 -> x6, local copies, waits for them, and re-layouts: 3.75 us -> 2.91 us
    ppermute x38 -> x39, starting transfers between devices: 71.3 us -> 70.5 us  [moved(): return lax.ppermute(value, ('tm', 'space'), pairs)]
    ppermute x38 -> x39, waiting for transfers between devices: 16.9 us -> 17.2 us  [moved(): return lax.ppermute(value, ('tm', 'space'), pairs)]
  transfers between devices with their start and end apart: 38 -> 39, of which waited for: 9 -> 9; matrix products, arithmetic and copies ran while one was open for 0% -> 0% of each run, Pallas kernels for 3% -> 4%
where the time goes in v5:
time: 173 us; the launch traced here: 171 us
  starting transfers between devices  70.5 us (41%)
  blocking collectives  65.7 us (38%)
  waiting for transfers between devices  17.2 us (10%)
  Pallas kernels  14.3 us (8%)
  local copies, waits for them, and re-layouts  2.91 us (2%)
    ppermute x39, starting transfers between devices, moved(): return lax.ppermute(value, ('tm', 'space'), pairs)  70.5 us
    all_to_all x5, blocking collectives, share(): return lax.all_to_all(copies, 'space', 0, 0, tiled=True)  65.7 us
    ppermute x39, waiting for transfers between devices, moved(): return lax.ppermute(value, ('tm', 'space'), pairs)  17.2 us
    pallas_call x17, Pallas kernels, call(): pl.pallas_call(kernel, out_shape=shapes, in_specs=[VMEM] * len(args), out...  14.3 us
  transfers between devices with their start and end apart: 39, of which 9 were waited for; matrix products, arithmetic and copies ran while one was open for 0% of the time, Pallas kernels for 4%

profile of v5, /device:TPU:1, one launch (start us, length us, event | category | flops | bytes accessed | tf_op | source)
XLA Modules:
  0.0 171.5 jit_solution(11830125839868499949)
XLA Ops:
  0.6 2.6 %collective-permute-start.1 = (f32[4,2,16,128]{3,2,1,0:T(8,128)}, f32[4,2,16,128]{3,2,1,0:T(8,128)S(1)}, u32[]{:S(2)}, u32[]{:S(2)}) collective-permute-start(f32[4,2,16,128]{3,2,1,0:T(8,128)} %param.5), channel_id=1, source_target_pairs={{0,16},{1,17},{2,18},{3,19},{4,20},{5,21},{6,22},{7,23},{8,24},{9,... | collective-permute-start | bytes 196616 | tf_op jit(solution)/shard_map/ppermute | solution.py:32
  3.2 1.2 collective-permute-start
  4.4 2.2 %copy-done = f32[1,64,4,2,16,128]{5,4,3,2,1,0:T(8,128)S(1)} copy-done((f32[1,64,4,2,16,128]{5,4,3,2,1,0:T(8,128)S(1)}, f32[1,64,4,2,16,128]{5,4,3,2,1,0:T(8,128)}, u32[]{:S(2)}) %copy-start) | copy-done | bytes 4194328
  6.6 0.7 copy-done.2
  7.4 0.5 collective-permute-done.g_ref
  7.9 1.5 collective-permute-start.2
  9.4 0.3 collective-permute-start.3
  9.7 2.3 %collective-permute-start.4 = (f32[8,16,128]{2,1,0:T(8,128)S(1)}, f32[8,16,128]{2,1,0:T(8,128)S(1)}, u32[]{:S(2)}, u32[]{:S(2)}) collective-permute-start(f32[8,16,128]{2,1,0:T(8,128)S(1)} %get-tuple-element.54), channel_id=1, source_target_pairs={{0,2},{1,3},{2,0},{3,1},{4,6},{5,7},{6,4},{7,5},{8,10},{9,11},{10,... | collective-permute-start | bytes 196616 | tf_op jit(solution)/shard_map/ppermute | solution.py:32
  12.0 0.6 collective-permute-start.5
  12.6 4.0 %collective-permute-done.4.e2 = f32[8,16,128]{2,1,0:T(8,128)S(1)} collective-permute-done((f32[8,16,128]{2,1,0:T(8,128)S(1)}, f32[8,16,128]{2,1,0:T(8,128)S(1)}, u32[]{:S(2)}, u32[]{:S(2)}) %collective-permute-start.4) | collective-permute-done | bytes 65568 | tf_op jit(solution)/shard_map/ppermute | solution.py:32
  16.6 0.3 shard_map.61
  17.0 1.4 collective-permute-start.10
  18.4 4.0 %collective-permute-start.8 = (f32[8,16,128]{2,1,0:T(8,128)S(1)}, f32[8,16,128]{2,1,0:T(8,128)S(1)}, u32[]{:S(2)}, u32[]{:S(2)}) collective-permute-start(f32[8,16,128]{2,1,0:T(8,128)S(1)} %get-tuple-element.56.relaxed), channel_id=1, source_target_pairs={{0,17},{1,16},{2,19},{3,18},{4,21},{5,20},{6,23},{7,22},{8,25},{9,... | collective-permute-start | bytes 196616 | tf_op jit(solution)/shard_map/ppermute | solution.py:32
  22.4 4.2 %collective-permute-start.6 = (f32[6,16,128]{2,1,0:T(8,128)S(1)}, f32[6,16,128]{2,1,0:T(8,128)S(1)}, u32[]{:S(2)}, u32[]{:S(2)}) collective-permute-start(f32[6,16,128]{2,1,0:T(8,128)S(1)} %get-tuple-element.59), channel_id=1, source_target_pairs={{0,18},{1,19},{2,16},{3,17},{4,22},{5,23},{6,20},{7,21},{8,26},{9,... | collective-permute-start | bytes 147464 | tf_op jit(solution)/shard_map/ppermute | solution.py:32
  26.6 1.6 collective-permute-start.7
  28.1 3.0 %shard_map.63.refs_0_ = f32[64,128]{1,0:T(8,128)S(1)} custom-call(f32[8192,128]{1,0:T(8,128)S(1)} %bitcast.5), custom_call_target="tpu_custom_call" | custom-call | flops 50000000 | bytes 100000 | tf_op jit(solution)/shard_map/pallas_call | solution.py:171
  31.1 3.0 %shard_map.64.gram = f32[64,128]{1,0:T(8,128)S(1)} custom-call(f32[8192,128]{1,0:T(8,128)S(1)} %bitcast.6, f32[64,128]{1,0:T(8,128)S(1)} %shard_map.63.refs_0_), custom_call_target="tpu_custom_call" | custom-call | flops 50000000 | bytes 100000 | tf_op jit(solution)/shard_map/pallas_call | solution.py:171
  34.2 0.3 shard_map.62
  34.5 0.4 shard_map.65
  35.0 16.2 %all_to_all.25.got = f32[16,40,128]{2,1,0:T(8,128)S(1)} all-to-all(f32[16,40,128]{2,1,0:T(8,128)S(1)} %shard_map.65), channel_id=1, replica_groups=mesh['tm'=8,'space'=16] {'space'}, dimensions={0} | all-to-all | bytes 655360 | tf_op jit(solution)/shard_map/all_to_all | solution.py:49
  51.1 1.9 %shard_map.66 = (f32[64,128]{1,0:T(8,128)S(1)}, f32[16,16,128]{2,1,0:T(8,128)S(1)}, f32[10,16,128]{2,1,0:T(8,128)S(1)}, f32[10,16,128]{2,1,0:T(8,128)S(1)}, f32[...) custom-call(f32[16,40,128]{2,1,0:T(8,128)S(1)} %all_to_all.25.got, f32[8192,128]{1,0:T(8,128)S(1)} %bitcast.8, ...), custom_call_target="tpu_custom_call" | custom-call | flops 1000000 | bytes 100000 | tf_op jit(solution)/shard_map/pallas_call | solution.py:171
  53.1 1.1 collective-permute-start.16
  54.3 1.2 collective-permute-start.15
  55.5 2.5 %collective-permute-start.12 = (f32[6,16,128]{2,1,0:T(8,128)S(1)}, f32[6,16,128]{2,1,0:T(8,128)S(1)}, u32[]{:S(2)}, u32[]{:S(2)}) collective-permute-start(f32[6,16,128]{2,1,0:T(8,128)S(1)} %get-tuple-element.63), channel_id=1, source_target_pairs={{0,18},{1,19},{2,16},{3,17},{4,22},{5,23},{6,20},{7,21},{8,26},{9,... | collective-permute-start | bytes 147464 | tf_op jit(solution)/shard_map/ppermute | solution.py:32
  58.0 1.4 collective-permute-start.13
  59.4 1.3 collective-permute-done.12.e2
  60.7 0.7 shard_map.67
  61.5 12.8 %all_to_all.26.got = f32[16,1,128]{2,1,0:T(1,128)S(1)} all-to-all(f32[16,1,128]{2,1,0:T(1,128)S(1)} %get-tuple-element.68), channel_id=1, replica_groups=mesh['tm'=8,'space'=16] {'space'}, dimensions={0} | all-to-all | bytes 16384 | tf_op jit(solution)/shard_map/all_to_all | solution.py:49
  74.3 0.4 shard_map.68
  74.7 4.0 %collective-permute-start.21 = (f32[16,16,128]{2,1,0:T(8,128)S(1)}, f32[16,16,128]{2,1,0:T(8,128)S(1)}, u32[]{:S(2)}, u32[]{:S(2)}) collective-permute-start(f32[16,16,128]{2,1,0:T(8,128)S(1)} %get-tuple-element.75), channel_id=1, source_target_pairs={{0,16},{1,17},{2,18},{3,19},{4,20},{5,21},{6,22},{7,23},{8,24},{9,... | collective-permute-start | bytes 393224 | tf_op jit(solution)/shard_map/ppermute | solution.py:32
  78.8 1.6 collective-permute-start.20
  80.4 2.5 %collective-permute-start.17 = (f32[6,16,128]{2,1,0:T(8,128)S(1)}, f32[6,16,128]{2,1,0:T(8,128)S(1)}, u32[]{:S(2)}, u32[]{:S(2)}) collective-permute-start(f32[6,16,128]{2,1,0:T(8,128)S(1)} %get-tuple-element.71), channel_id=1, source_target_pairs={{0,18},{1,19},{2,16},{3,17},{4,22},{5,23},{6,20},{7,21},{8,26},{9,... | collective-permute-start | bytes 147464 | tf_op jit(solution)/shard_map/ppermute | solution.py:32
  82.9 1.1 collective-permute-start.18
  84.0 2.3 %collective-permute-done.17.e2 = f32[6,16,128]{2,1,0:T(8,128)S(1)} collective-permute-done((f32[6,16,128]{2,1,0:T(8,128)S(1)}, f32[6,16,128]{2,1,0:T(8,128)S(1)}, u32[]{:S(2)}, u32[]{:S(2)}) %collective-permute-start.17) | collective-permute-done | bytes 49184 | tf_op jit(solution)/shard_map/ppermute | solution.py:32
  86.3 0.7 shard_map.69
  87.1 12.5 %all_to_all.27.got = f32[16,1,128]{2,1,0:T(1,128)S(1)} all-to-all(f32[16,1,128]{2,1,0:T(1,128)S(1)} %get-tuple-element.77), channel_id=1, replica_groups=mesh['tm'=8,'space'=16] {'space'}, dimensions={0} | all-to-all | bytes 16384 | tf_op jit(solution)/shard_map/all_to_all | solution.py:49
  99.6 0.4 shard_map.70
  100.0 3.4 %collective-permute-start.26 = (f32[16,16,128]{2,1,0:T(8,128)S(1)}, f32[16,16,128]{2,1,0:T(8,128)S(1)}, u32[]{:S(2)}, u32[]{:S(2)}) collective-permute-start(f32[16,16,128]{2,1,0:T(8,128)S(1)} %get-tuple-element.83), channel_id=1, source_target_pairs={{0,16},{1,17},{2,18},{3,19},{4,20},{5,21},{6,22},{7,23},{8,24},{9,... | collective-permute-start | bytes 393224 | tf_op jit(solution)/shard_map/ppermute | solution.py:32
  103.4 0.7 collective-permute-start.22
  104.1 2.6 %collective-permute-start.24 = (f32[10,16,128]{2,1,0:T(8,128)S(1)}, f32[10,16,128]{2,1,0:T(8,128)S(1)}, u32[]{:S(2)}, u32[]{:S(2)}) collective-permute-start(f32[10,16,128]{2,1,0:T(8,128)S(1)} %get-tuple-element.81), channel_id=1, source_target_pairs={{0,17},{1,16},{2,19},{3,18},{4,21},{5,20},{6,23},{7,22},{8,25},{9,... | collective-permute-start | bytes 245768 | tf_op jit(solution)/shard_map/ppermute | solution.py:32
  106.8 0.4 collective-permute-start.11
  107.2 1.2 collective-permute-done.22.e2
  108.4 1.0 collective-permute-start.23
  109.4 2.7 %collective-permute-done.23.o2 = f32[6,16,128]{2,1,0:T(8,128)S(1)} collective-permute-done((f32[6,16,128]{2,1,0:T(8,128)S(1)}, f32[6,16,128]{2,1,0:T(8,128)S(1)}, u32[]{:S(2)}, u32[]{:S(2)}) %collective-permute-start.23) | collective-permute-done | bytes 49184 | tf_op jit(solution)/shard_map/ppermute | solution.py:32
  112.1 0.3 shard_map.71
  112.4 0.7 collective-permute-start.29
  113.1 2.3 %collective-permute-start.27 = (f32[6,16,128]{2,1,0:T(8,128)S(1)}, f32[6,16,128]{2,1,0:T(8,128)S(1)}, u32[]{:S(2)}, u32[]{:S(2)}) collective-permute-start(f32[6,16,128]{2,1,0:T(8,128)S(1)} %get-tuple-element.85), channel_id=1, source_target_pairs={{0,64},{1,66},{2,65},{3,68},{4,67},{5,70},{6,69},{7,72},{8,71},{9,... | collective-permute-start | bytes 147464 | tf_op jit(solution)/shard_map/ppermute | solution.py:32
  115.5 5.4 %collective-permute-start.28 = (f32[6,16,128]{2,1,0:T(8,128)S(1)}, f32[6,16,128]{2,1,0:T(8,128)S(1)}, u32[]{:S(2)}, u32[]{:S(2)}) collective-permute-start(f32[6,16,128]{2,1,0:T(8,128)S(1)} %get-tuple-element.86), channel_id=1, source_target_pairs={{0,65},{1,64},{2,67},{3,66},{4,69},{5,68},{6,71},{7,70},{8,73},{9,... | collective-permute-start | bytes 147464 | tf_op jit(solution)/shard_map/ppermute | solution.py:32
  120.9 2.0 %collective-permute-done.28.e1 = f32[6,16,128]{2,1,0:T(8,128)S(1)} collective-permute-done((f32[6,16,128]{2,1,0:T(8,128)S(1)}, f32[6,16,128]{2,1,0:T(8,128)S(1)}, u32[]{:S(2)}, u32[]{:S(2)}) %collective-permute-start.28) | collective-permute-done | bytes 49184 | tf_op jit(solution)/shard_map/ppermute | solution.py:32
  122.9 0.5 shard_map.72
  123.4 13.4 %all_to_all.28.got = f32[16,1,128]{2,1,0:T(1,128)S(1)} all-to-all(f32[16,1,128]{2,1,0:T(1,128)S(1)} %get-tuple-element.89), channel_id=1, replica_groups=mesh['tm'=8,'space'=16] {'space'}, dimensions={0} | all-to-all | bytes 16384 | tf_op jit(solution)/shard_map/all_to_all | solution.py:49
  136.8 0.4 shard_map.73
  137.2 0.4 collective-permute-start.32
  137.6 4.4 %collective-permute-start.33 = (f32[10,16,128]{2,1,0:T(8,128)S(1)}, f32[10,16,128]{2,1,0:T(8,128)S(1)}, u32[]{:S(2)}, u32[]{:S(2)}) collective-permute-start(f32[10,16,128]{2,1,0:T(8,128)S(1)} %get-tuple-element.94), channel_id=1, source_target_pairs={{0,16},{1,2},{2,1},{3,4},{4,3},{5,6},{6,5},{7,8},{8,7},{9,10},{10,... | collective-permute-start | bytes 245768 | tf_op jit(solution)/shard_map/ppermute | solution.py:32
  141.9 3.5 %collective-permute-start.31 = (f32[6,16,128]{2,1,0:T(8,128)S(1)}, f32[6,16,128]{2,1,0:T(8,128)S(1)}, u32[]{:S(2)}, u32[]{:S(2)}) collective-permute-start(f32[6,16,128]{2,1,0:T(8,128)S(1)} %get-tuple-element.92), channel_id=1, source_target_pairs={{0,16},{1,17},{2,4},{3,5},{4,2},{5,3},{6,8},{7,9},{8,6},{9,7},{10,... | collective-permute-start | bytes 147464 | tf_op jit(solution)/shard_map/ppermute | solution.py:32
  145.5 0.9 collective-permute-done.30.e2
  146.4 2.2 %collective-permute-done.31.o2 = f32[6,16,128]{2,1,0:T(8,128)S(1)} collective-permute-done((f32[6,16,128]{2,1,0:T(8,128)S(1)}, f32[6,16,128]{2,1,0:T(8,128)S(1)}, u32[]{:S(2)}, u32[]{:S(2)}) %collective-permute-start.31) | collective-permute-done | bytes 49184 | tf_op jit(solution)/shard_map/ppermute | solution.py:32
  148.6 0.7 shard_map.74
  149.3 0.4 collective-permute-start.38
  150.0 4.5 %collective-permute-start.36 = (f32[8,16,128]{2,1,0:T(8,128)S(1)}, f32[8,16,128]{2,1,0:T(8,128)S(1)}, u32[]{:S(2)}, u32[]{:S(2)}) collective-permute-start(f32[8,16,128]{2,1,0:T(8,128)S(1)} %get-tuple-element.96.final), channel_id=1, source_target_pairs={{0,17},{1,16},{2,19},{3,18},{4,21},{5,20},{6,23},{7,22},{8,25},{9,... | collective-permute-start | bytes 196616 | tf_op jit(solution)/shard_map/ppermute | solution.py:32
  154.5 4.1 %collective-permute-start.34 = (f32[2,16,128]{2,1,0:T(8,128)S(1)}, f32[2,16,128]{2,1,0:T(8,128)S(1)}, u32[]{:S(2)}, u32[]{:S(2)}) collective-permute-start(f32[2,16,128]{2,1,0:T(8,128)S(1)} %get-tuple-element.97), channel_id=1, source_target_pairs={{0,18},{1,19},{2,16},{3,17},{4,22},{5,23},{6,20},{7,21},{8,26},{9,... | collective-permute-start | bytes 49160 | tf_op jit(solution)/shard_map/ppermute | solution.py:32
  158.6 1.0 collective-permute-start.35
  159.6 10.7 %all_to_all.29.got = f32[16,1,128]{2,1,0:T(1,128)S(1)} all-to-all(f32[16,1,128]{2,1,0:T(1,128)S(1)} %get-tuple-element.99), channel_id=1, replica_groups=mesh['tm'=8,'space'=16] {'space'}, dimensions={0} | all-to-all | bytes 16384 | tf_op jit(solution)/shard_map/all_to_all | solution.py:49
  170.4 0.9 shard_map.75
  (42 shorter events, 0.7 us)
Async XLA Ops:
  0.6 6.7 %collective-permute-start.1 = (f32[4,2,16,128]{3,2,1,0:T(8,128)}, f32[4,2,16,128]{3,2,1,0:T(8,128)S(1)}, u32[]{:S(2)}, u32[]{:S(2)}) collective-permute-start(f32[4,2,16,128]{3,2,1,0:T(8,128)} %param.5), channel_id=1, source_target_pairs={{0,16},{1,17},{2,18},{3,19},{4,20},{5,21},{6,22},{7,23},{8,24},{9,... | collective-permute-start | bytes 196616 | tf_op jit(solution)/shard_map/ppermute | solution.py:32
  3.2 4.6 %collective-permute-start = (f32[8,16,128]{2,1,0:T(8,128)}, f32[8,16,128]{2,1,0:T(8,128)S(1)}, u32[]{:S(2)}, u32[]{:S(2)}) collective-permute-start(f32[8,16,128]{2,1,0:T(8,128)} %bitcast.17), channel_id=1, source_target_pairs={{0,32},{1,33},{2,34},{3,35},{4,36},{5,37},{6,38},{7,39},{8,40},{9,... | collective-permute-start | bytes 196616 | tf_op jit(solution)/shard_map/ppermute | solution.py:32
  4.4 2.2 %copy-start = (f32[1,64,4,2,16,128]{5,4,3,2,1,0:T(8,128)S(1)}, f32[1,64,4,2,16,128]{5,4,3,2,1,0:T(8,128)}, u32[]{:S(2)}) copy-start(f32[1,64,4,2,16,128]{5,4,3,2,1,0:T(8,128)} %param.7) | copy-start | bytes 12582916
  6.6 0.7 copy-start.2
  7.3 20.8 %copy-start.1 = (f32[1,64,4,2,16,128]{5,4,3,2,1,0:T(8,128)S(1)}, f32[1,64,4,2,16,128]{5,4,3,2,1,0:T(8,128)}, u32[]{:S(2)}) copy-start(f32[1,64,4,2,16,128]{5,4,3,2,1,0:T(8,128)} %param.7) | copy-start | bytes 12582916
  7.9 8.8 %collective-permute-start.2 = (f32[15,16,128]{2,1,0:T(8,128)S(1)}, f32[15,16,128]{2,1,0:T(8,128)S(1)}, u32[]{:S(2)}, u32[]{:S(2)}) collective-permute-start(f32[15,16,128]{2,1,0:T(8,128)S(1)} %get-tuple-element.52), channel_id=1, source_target_pairs={{0,1},{1,0},{2,3},{3,2},{4,5},{5,4},{6,7},{7,6},{8,9},{9,8},{10,11... | collective-permute-start | bytes 368648 | tf_op jit(solution)/shard_map/ppermute | solution.py:32
  9.4 7.3 %collective-permute-start.3 = (f32[15,16,128]{2,1,0:T(8,128)S(1)}, f32[15,16,128]{2,1,0:T(8,128)S(1)}, u32[]{:S(2)}, u32[]{:S(2)}) collective-permute-start(f32[15,16,128]{2,1,0:T(8,128)S(1)} %get-tuple-element.53), channel_id=1, source_target_pairs={{0,16},{1,2},{2,1},{3,4},{4,3},{5,6},{6,5},{7,8},{8,7},{9,10},{10,... | collective-permute-start | bytes 368648 | tf_op jit(solution)/shard_map/ppermute | solution.py:32
  9.7 6.9 %collective-permute-start.4 = (f32[8,16,128]{2,1,0:T(8,128)S(1)}, f32[8,16,128]{2,1,0:T(8,128)S(1)}, u32[]{:S(2)}, u32[]{:S(2)}) collective-permute-start(f32[8,16,128]{2,1,0:T(8,128)S(1)} %get-tuple-element.54), channel_id=1, source_target_pairs={{0,2},{1,3},{2,0},{3,1},{4,6},{5,7},{6,4},{7,5},{8,10},{9,11},{10,... | collective-permute-start | bytes 196616 | tf_op jit(solution)/shard_map/ppermute | solution.py:32
  12.0 4.6 %collective-permute-start.5 = (f32[8,16,128]{2,1,0:T(8,128)S(1)}, f32[8,16,128]{2,1,0:T(8,128)S(1)}, u32[]{:S(2)}, u32[]{:S(2)}) collective-permute-start(f32[8,16,128]{2,1,0:T(8,128)S(1)} %get-tuple-element.55), channel_id=1, source_target_pairs={{0,16},{1,17},{2,4},{3,5},{4,2},{5,3},{6,8},{7,9},{8,6},{9,7},{10,... | collective-permute-start | bytes 196616 | tf_op jit(solution)/shard_map/ppermute | solution.py:32
  17.0 17.2 %collective-permute-start.10 = (f32[8,16,128]{2,1,0:T(8,128)S(1)}, f32[8,16,128]{2,1,0:T(8,128)S(1)}, u32[]{:S(2)}, u32[]{:S(2)}) collective-permute-start(f32[8,16,128]{2,1,0:T(8,128)S(1)} %get-tuple-element.56.relaxed), channel_id=1, source_target_pairs={{0,16},{1,17},{2,18},{3,19},{4,20},{5,21},{6,22},{7,23},{8,24},{9,... | collective-permute-start | bytes 196616 | tf_op jit(solution)/shard_map/ppermute | solution.py:32
  18.4 15.8 %collective-permute-start.9 = (f32[8,16,128]{2,1,0:T(8,128)S(1)}, f32[8,16,128]{2,1,0:T(8,128)S(1)}, u32[]{:S(2)}, u32[]{:S(2)}) collective-permute-start(f32[8,16,128]{2,1,0:T(8,128)S(1)} %get-tuple-element.56.relaxed), channel_id=1, source_target_pairs={{0,16},{1,18},{2,17},{3,20},{4,19},{5,22},{6,21},{7,24},{8,23},{9,... | collective-permute-start | bytes 196616 | tf_op jit(solution)/shard_map/ppermute | solution.py:32
  18.4 15.7 %collective-permute-start.8 = (f32[8,16,128]{2,1,0:T(8,128)S(1)}, f32[8,16,128]{2,1,0:T(8,128)S(1)}, u32[]{:S(2)}, u32[]{:S(2)}) collective-permute-start(f32[8,16,128]{2,1,0:T(8,128)S(1)} %get-tuple-element.56.relaxed), channel_id=1, source_target_pairs={{0,17},{1,16},{2,19},{3,18},{4,21},{5,20},{6,23},{7,22},{8,25},{9,... | collective-permute-start | bytes 196616 | tf_op jit(solution)/shard_map/ppermute | solution.py:32
  22.4 11.7 %collective-permute-start.6 = (f32[6,16,128]{2,1,0:T(8,128)S(1)}, f32[6,16,128]{2,1,0:T(8,128)S(1)}, u32[]{:S(2)}, u32[]{:S(2)}) collective-permute-start(f32[6,16,128]{2,1,0:T(8,128)S(1)} %get-tuple-element.59), channel_id=1, source_target_pairs={{0,18},{1,19},{2,16},{3,17},{4,22},{5,23},{6,20},{7,21},{8,26},{9,... | collective-permute-start | bytes 147464 | tf_op jit(solution)/shard_map/ppermute | solution.py:32
  26.6 7.6 %collective-permute-start.7 = (f32[6,16,128]{2,1,0:T(8,128)S(1)}, f32[6,16,128]{2,1,0:T(8,128)S(1)}, u32[]{:S(2)}, u32[]{:S(2)}) collective-permute-start(f32[6,16,128]{2,1,0:T(8,128)S(1)} %get-tuple-element.60), channel_id=1, source_target_pairs={{0,16},{1,17},{2,20},{3,21},{4,18},{5,19},{6,24},{7,25},{8,22},{9,... | collective-permute-start | bytes 147464 | tf_op jit(solution)/shard_map/ppermute | solution.py:32
  53.1 7.7 %collective-permute-start.16 = (f32[16,16,128]{2,1,0:T(8,128)S(1)}, f32[16,16,128]{2,1,0:T(8,128)S(1)}, u32[]{:S(2)}, u32[]{:S(2)}) collective-permute-start(f32[16,16,128]{2,1,0:T(8,128)S(1)} %get-tuple-element.67), channel_id=1, source_target_pairs={{0,16},{1,17},{2,18},{3,19},{4,20},{5,21},{6,22},{7,23},{8,24},{9,... | collective-permute-start | bytes 393224 | tf_op jit(solution)/shard_map/ppermute | solution.py:32
  54.2 6.6 %collective-permute-start.14 = (f32[10,16,128]{2,1,0:T(8,128)S(1)}, f32[10,16,128]{2,1,0:T(8,128)S(1)}, u32[]{:S(2)}, u32[]{:S(2)}) collective-permute-start(f32[10,16,128]{2,1,0:T(8,128)S(1)} %get-tuple-element.65), channel_id=1, source_target_pairs={{0,17},{1,16},{2,19},{3,18},{4,21},{5,20},{6,23},{7,22},{8,25},{9,... | collective-permute-start | bytes 245768 | tf_op jit(solution)/shard_map/ppermute | solution.py:32
  54.3 6.4 %collective-permute-start.15 = (f32[10,16,128]{2,1,0:T(8,128)S(1)}, f32[10,16,128]{2,1,0:T(8,128)S(1)}, u32[]{:S(2)}, u32[]{:S(2)}) collective-permute-start(f32[10,16,128]{2,1,0:T(8,128)S(1)} %get-tuple-element.66), channel_id=1, source_target_pairs={{0,16},{1,18},{2,17},{3,20},{4,19},{5,22},{6,21},{7,24},{8,23},{9,... | collective-permute-start | bytes 245768 | tf_op jit(solution)/shard_map/ppermute | solution.py:32
  55.5 5.2 %collective-permute-start.12 = (f32[6,16,128]{2,1,0:T(8,128)S(1)}, f32[6,16,128]{2,1,0:T(8,128)S(1)}, u32[]{:S(2)}, u32[]{:S(2)}) collective-permute-start(f32[6,16,128]{2,1,0:T(8,128)S(1)} %get-tuple-element.63), channel_id=1, source_target_pairs={{0,18},{1,19},{2,16},{3,17},{4,22},{5,23},{6,20},{7,21},{8,26},{9,... | collective-permute-start | bytes 147464 | tf_op jit(solution)/shard_map/ppermute | solution.py:32
  58.0 2.8 %collective-permute-start.13 = (f32[6,16,128]{2,1,0:T(8,128)S(1)}, f32[6,16,128]{2,1,0:T(8,128)S(1)}, u32[]{:S(2)}, u32[]{:S(2)}) collective-permute-start(f32[6,16,128]{2,1,0:T(8,128)S(1)} %get-tuple-element.64), channel_id=1, source_target_pairs={{0,16},{1,17},{2,20},{3,21},{4,18},{5,19},{6,24},{7,25},{8,22},{9,... | collective-permute-start | bytes 147464 | tf_op jit(solution)/shard_map/ppermute | solution.py:32
  74.7 11.6 %collective-permute-start.21 = (f32[16,16,128]{2,1,0:T(8,128)S(1)}, f32[16,16,128]{2,1,0:T(8,128)S(1)}, u32[]{:S(2)}, u32[]{:S(2)}) collective-permute-start(f32[16,16,128]{2,1,0:T(8,128)S(1)} %get-tuple-element.75), channel_id=1, source_target_pairs={{0,16},{1,17},{2,18},{3,19},{4,20},{5,21},{6,22},{7,23},{8,24},{9,... | collective-permute-start | bytes 393224 | tf_op jit(solution)/shard_map/ppermute | solution.py:32
  78.7 7.6 %collective-permute-start.19 = (f32[10,16,128]{2,1,0:T(8,128)S(1)}, f32[10,16,128]{2,1,0:T(8,128)S(1)}, u32[]{:S(2)}, u32[]{:S(2)}) collective-permute-start(f32[10,16,128]{2,1,0:T(8,128)S(1)} %get-tuple-element.73), channel_id=1, source_target_pairs={{0,17},{1,16},{2,19},{3,18},{4,21},{5,20},{6,23},{7,22},{8,25},{9,... | collective-permute-start | bytes 245768 | tf_op jit(solution)/shard_map/ppermute | solution.py:32
  78.8 7.5 %collective-permute-start.20 = (f32[10,16,128]{2,1,0:T(8,128)S(1)}, f32[10,16,128]{2,1,0:T(8,128)S(1)}, u32[]{:S(2)}, u32[]{:S(2)}) collective-permute-start(f32[10,16,128]{2,1,0:T(8,128)S(1)} %get-tuple-element.74), channel_id=1, source_target_pairs={{0,16},{1,18},{2,17},{3,20},{4,19},{5,22},{6,21},{7,24},{8,23},{9,... | collective-permute-start | bytes 245768 | tf_op jit(solution)/shard_map/ppermute | solution.py:32
  80.4 5.9 %collective-permute-start.17 = (f32[6,16,128]{2,1,0:T(8,128)S(1)}, f32[6,16,128]{2,1,0:T(8,128)S(1)}, u32[]{:S(2)}, u32[]{:S(2)}) collective-permute-start(f32[6,16,128]{2,1,0:T(8,128)S(1)} %get-tuple-element.71), channel_id=1, source_target_pairs={{0,18},{1,19},{2,16},{3,17},{4,22},{5,23},{6,20},{7,21},{8,26},{9,... | collective-permute-start | bytes 147464 | tf_op jit(solution)/shard_map/ppermute | solution.py:32
  82.9 3.4 %collective-permute-start.18 = (f32[6,16,128]{2,1,0:T(8,128)S(1)}, f32[6,16,128]{2,1,0:T(8,128)S(1)}, u32[]{:S(2)}, u32[]{:S(2)}) collective-permute-start(f32[6,16,128]{2,1,0:T(8,128)S(1)} %get-tuple-element.72), channel_id=1, source_target_pairs={{0,16},{1,17},{2,20},{3,21},{4,18},{5,19},{6,24},{7,25},{8,22},{9,... | collective-permute-start | bytes 147464 | tf_op jit(solution)/shard_map/ppermute | solution.py:32
  100.0 12.1 %collective-permute-start.26 = (f32[16,16,128]{2,1,0:T(8,128)S(1)}, f32[16,16,128]{2,1,0:T(8,128)S(1)}, u32[]{:S(2)}, u32[]{:S(2)}) collective-permute-start(f32[16,16,128]{2,1,0:T(8,128)S(1)} %get-tuple-element.83), channel_id=1, source_target_pairs={{0,16},{1,17},{2,18},{3,19},{4,20},{5,21},{6,22},{7,23},{8,24},{9,... | collective-permute-start | bytes 393224 | tf_op jit(solution)/shard_map/ppermute | solution.py:32
  103.4 5.0 %collective-permute-start.22 = (f32[6,16,128]{2,1,0:T(8,128)S(1)}, f32[6,16,128]{2,1,0:T(8,128)S(1)}, u32[]{:S(2)}, u32[]{:S(2)}) collective-permute-start(f32[6,16,128]{2,1,0:T(8,128)S(1)} %get-tuple-element.79), channel_id=1, source_target_pairs={{0,18},{1,19},{2,16},{3,17},{4,22},{5,23},{6,20},{7,21},{8,26},{9,... | collective-permute-start | bytes 147464 | tf_op jit(solution)/shard_map/ppermute | solution.py:32
  104.1 8.0 %collective-permute-start.24 = (f32[10,16,128]{2,1,0:T(8,128)S(1)}, f32[10,16,128]{2,1,0:T(8,128)S(1)}, u32[]{:S(2)}, u32[]{:S(2)}) collective-permute-start(f32[10,16,128]{2,1,0:T(8,128)S(1)} %get-tuple-element.81), channel_id=1, source_target_pairs={{0,17},{1,16},{2,19},{3,18},{4,21},{5,20},{6,23},{7,22},{8,25},{9,... | collective-permute-start | bytes 245768 | tf_op jit(solution)/shard_map/ppermute | solution.py:32
  106.7 5.4 %collective-permute-start.25 = (f32[10,16,128]{2,1,0:T(8,128)S(1)}, f32[10,16,128]{2,1,0:T(8,128)S(1)}, u32[]{:S(2)}, u32[]{:S(2)}) collective-permute-start(f32[10,16,128]{2,1,0:T(8,128)S(1)} %get-tuple-element.82), channel_id=1, source_target_pairs={{0,16},{1,18},{2,17},{3,20},{4,19},{5,22},{6,21},{7,24},{8,23},{9,... | collective-permute-start | bytes 245768 | tf_op jit(solution)/shard_map/ppermute | solution.py:32
  106.8 38.7 %collective-permute-start.11 = (f32[28,16,128]{2,1,0:T(8,128)S(1)}, f32[28,16,128]{2,1,0:T(8,128)S(1)}, u32[]{:S(2)}, u32[]{:S(2)}) collective-permute-start(f32[28,16,128]{2,1,0:T(8,128)S(1)} %get-tuple-element.61), channel_id=1, source_target_pairs={{0,112},{1,113},{2,114},{3,115},{4,116},{5,117},{6,118},{7,119},{8... | collective-permute-start | bytes 688136 | tf_op jit(solution)/shard_map/ppermute | solution.py:32
  108.4 3.6 %collective-permute-start.23 = (f32[6,16,128]{2,1,0:T(8,128)S(1)}, f32[6,16,128]{2,1,0:T(8,128)S(1)}, u32[]{:S(2)}, u32[]{:S(2)}) collective-permute-start(f32[6,16,128]{2,1,0:T(8,128)S(1)} %get-tuple-element.80), channel_id=1, source_target_pairs={{0,16},{1,17},{2,20},{3,21},{4,18},{5,19},{6,24},{7,25},{8,22},{9,... | collective-permute-start | bytes 147464 | tf_op jit(solution)/shard_map/ppermute | solution.py:32
  112.4 10.5 %collective-permute-start.29 = (f32[8,16,128]{2,1,0:T(8,128)S(1)}, f32[8,16,128]{2,1,0:T(8,128)S(1)}, u32[]{:S(2)}, u32[]{:S(2)}) collective-permute-start(f32[8,16,128]{2,1,0:T(8,128)S(1)} %get-tuple-element.87), channel_id=1, source_target_pairs={{0,64},{1,65},{2,66},{3,67},{4,68},{5,69},{6,70},{7,71},{8,72},{9,... | collective-permute-start | bytes 196616 | tf_op jit(solution)/shard_map/ppermute | solution.py:32
  113.1 7.7 %collective-permute-start.27 = (f32[6,16,128]{2,1,0:T(8,128)S(1)}, f32[6,16,128]{2,1,0:T(8,128)S(1)}, u32[]{:S(2)}, u32[]{:S(2)}) collective-permute-start(f32[6,16,128]{2,1,0:T(8,128)S(1)} %get-tuple-element.85), channel_id=1, source_target_pairs={{0,64},{1,66},{2,65},{3,68},{4,67},{5,70},{6,69},{7,72},{8,71},{9,... | collective-permute-start | bytes 147464 | tf_op jit(solution)/shard_map/ppermute | solution.py:32
  115.5 7.4 %collective-permute-start.28 = (f32[6,16,128]{2,1,0:T(8,128)S(1)}, f32[6,16,128]{2,1,0:T(8,128)S(1)}, u32[]{:S(2)}, u32[]{:S(2)}) collective-permute-start(f32[6,16,128]{2,1,0:T(8,128)S(1)} %get-tuple-element.86), channel_id=1, source_target_pairs={{0,65},{1,64},{2,67},{3,66},{4,69},{5,68},{6,71},{7,70},{8,73},{9,... | collective-permute-start | bytes 147464 | tf_op jit(solution)/shard_map/ppermute | solution.py:32
  137.2 11.4 %collective-permute-start.32 = (f32[10,16,128]{2,1,0:T(8,128)S(1)}, f32[10,16,128]{2,1,0:T(8,128)S(1)}, u32[]{:S(2)}, u32[]{:S(2)}) collective-permute-start(f32[10,16,128]{2,1,0:T(8,128)S(1)} %get-tuple-element.93), channel_id=1, source_target_pairs={{0,1},{1,0},{2,3},{3,2},{4,5},{5,4},{6,7},{7,6},{8,9},{9,8},{10,11... | collective-permute-start | bytes 245768 | tf_op jit(solution)/shard_map/ppermute | solution.py:32
  137.6 11.0 %collective-permute-start.33 = (f32[10,16,128]{2,1,0:T(8,128)S(1)}, f32[10,16,128]{2,1,0:T(8,128)S(1)}, u32[]{:S(2)}, u32[]{:S(2)}) collective-permute-start(f32[10,16,128]{2,1,0:T(8,128)S(1)} %get-tuple-element.94), channel_id=1, source_target_pairs={{0,16},{1,2},{2,1},{3,4},{4,3},{5,6},{6,5},{7,8},{8,7},{9,10},{10,... | collective-permute-start | bytes 245768 | tf_op jit(solution)/shard_map/ppermute | solution.py:32
  141.9 4.4 %collective-permute-start.30 = (f32[6,16,128]{2,1,0:T(8,128)S(1)}, f32[6,16,128]{2,1,0:T(8,128)S(1)}, u32[]{:S(2)}, u32[]{:S(2)}) collective-permute-start(f32[6,16,128]{2,1,0:T(8,128)S(1)} %get-tuple-element.91), channel_id=1, source_target_pairs={{0,2},{1,3},{2,0},{3,1},{4,6},{5,7},{6,4},{7,5},{8,10},{9,11},{10,... | collective-permute-start | bytes 147464 | tf_op jit(solution)/shard_map/ppermute | solution.py:32
  141.9 6.6 %collective-permute-start.31 = (f32[6,16,128]{2,1,0:T(8,128)S(1)}, f32[6,16,128]{2,1,0:T(8,128)S(1)}, u32[]{:S(2)}, u32[]{:S(2)}) collective-permute-start(f32[6,16,128]{2,1,0:T(8,128)S(1)} %get-tuple-element.92), channel_id=1, source_target_pairs={{0,16},{1,17},{2,4},{3,5},{4,2},{5,3},{6,8},{7,9},{8,6},{9,7},{10,... | collective-permute-start | bytes 147464 | tf_op jit(solution)/shard_map/ppermute | solution.py:32
  149.3 21.0 %collective-permute-start.38 = (f32[8,16,128]{2,1,0:T(8,128)S(1)}, f32[8,16,128]{2,1,0:T(8,128)S(1)}, u32[]{:S(2)}, u32[]{:S(2)}) collective-permute-start(f32[8,16,128]{2,1,0:T(8,128)S(1)} %get-tuple-element.96.final), channel_id=1, source_target_pairs={{0,16},{1,17},{2,18},{3,19},{4,20},{5,21},{6,22},{7,23},{8,24},{9,... | collective-permute-start | bytes 196616 | tf_op jit(solution)/shard_map/ppermute | solution.py:32
  149.7 20.6 %collective-permute-start.37 = (f32[8,16,128]{2,1,0:T(8,128)S(1)}, f32[8,16,128]{2,1,0:T(8,128)S(1)}, u32[]{:S(2)}, u32[]{:S(2)}) collective-permute-start(f32[8,16,128]{2,1,0:T(8,128)S(1)} %get-tuple-element.96.final), channel_id=1, source_target_pairs={{0,16},{1,18},{2,17},{3,20},{4,19},{5,22},{6,21},{7,24},{8,23},{9,... | collective-permute-start | bytes 196616 | tf_op jit(solution)/shard_map/ppermute | solution.py:32
  150.0 20.4 %collective-permute-start.36 = (f32[8,16,128]{2,1,0:T(8,128)S(1)}, f32[8,16,128]{2,1,0:T(8,128)S(1)}, u32[]{:S(2)}, u32[]{:S(2)}) collective-permute-start(f32[8,16,128]{2,1,0:T(8,128)S(1)} %get-tuple-element.96.final), channel_id=1, source_target_pairs={{0,17},{1,16},{2,19},{3,18},{4,21},{5,20},{6,23},{7,22},{8,25},{9,... | collective-permute-start | bytes 196616 | tf_op jit(solution)/shard_map/ppermute | solution.py:32
  154.5 15.9 %collective-permute-start.34 = (f32[2,16,128]{2,1,0:T(8,128)S(1)}, f32[2,16,128]{2,1,0:T(8,128)S(1)}, u32[]{:S(2)}, u32[]{:S(2)}) collective-permute-start(f32[2,16,128]{2,1,0:T(8,128)S(1)} %get-tuple-element.97), channel_id=1, source_target_pairs={{0,18},{1,19},{2,16},{3,17},{4,22},{5,23},{6,20},{7,21},{8,26},{9,... | collective-permute-start | bytes 49160 | tf_op jit(solution)/shard_map/ppermute | solution.py:32
  158.6 11.8 %collective-permute-start.35 = (f32[2,16,128]{2,1,0:T(8,128)S(1)}, f32[2,16,128]{2,1,0:T(8,128)S(1)}, u32[]{:S(2)}, u32[]{:S(2)}) collective-permute-start(f32[2,16,128]{2,1,0:T(8,128)S(1)} %get-tuple-element.98), channel_id=1, source_target_pairs={{0,16},{1,17},{2,20},{3,21},{4,18},{5,19},{6,24},{7,25},{8,22},{9,... | collective-permute-start | bytes 49160 | tf_op jit(solution)/shard_map/ppermute | solution.py:32

commit v6 on v5

--- a/solution.py
+++ b/solution.py
@@ -228,8 +228,8 @@
         at = put(loads_out, at, load)
 
 
-def kept_loads(loads_ref, base=0):
-    starts = [base + sum(LOADS[:i]) for i in range(4)]
+def kept_loads(loads_ref):
+    starts = [sum(LOADS[:i]) for i in range(4)]
     return [loads_ref[start : start + n] for start, n in zip(starts, LOADS)]
 
 
@@ -238,7 +238,9 @@
     p, vx, vy, vz = wide(own[...], *halo_of((e1, o1), (e2, o2)), ok)
     u = advance_many(p, vx, vy, vz, med[...], DT, 4, ok[0], ok[2], kept_loads(loads_ref))[-1]
     out[...] = u - relaxed[...]
-    put(back, put(back, 0, u), loads_ref[...])
+    at = put(back, 0, u)
+    for load in kept_loads(loads_ref)[:3]:
+        at = put(back, at, load[1:-1])
 
 
 def gram_kernel(parts, basis, *refs):
@@ -434,7 +436,7 @@
     copies.append(pltpu.make_async_copy(kept_row, coords, sems.at[4]))
     copies[1].start()
     ok = flags()
-    loads = [load[1:-1] for load in kept_loads(back, 8)[:3]]
+    loads = [back[8:14], back[14:18], back[18:20]]
     b1, a1, b2, a2 = halo_of((e1, o1), (e2, o2))
     u = own[...]
     p = cat(
@@ -492,8 +494,10 @@
         o2,
     )
     near = traded((relaxed, relaxed), (e, o), relaxed, 1)
-    (gram,) = call(functools.partial(gram_kernel, (4, 8)), [(RANK, NY)], columns, gram, scratch=split, flops=50_000_000)
-    x, back = call(residue_kernel, [state, (8 + sum(LOADS), NX, NY)], relaxed, loads, med, *near)
+    (gram,) = call(
+        functools.partial(gram_kernel, (4, 8)), [(RANK, NY)], columns, gram, scratch=split, flops=50_000_000
+    )
+    x, back = call(residue_kernel, [state, (20, NX, NY)], relaxed, loads, med, *near)
     back = hop(back, -1)
     (rows,) = call(first_kernel, [(N_SP, RANK // 2 + 8, NY)], columns, x, gram, scratch=table)
     ginv, *packed = call(
@@ -512,10 +516,11 @@
         )
         packed = call(project_kernel, PROJECTED, share(rows), ginv, columns, u, scratch=table)
     gap, acc, e, o = call(gap_kernel, [state, state, *far], med, *exchanged(packed, 1), acc)
+    e = trade(e, 4, 1, True)
     o = trade(o, 4, 1, False)
-    e = trade(e, 4, 1, True)
+    gap = hop(gap, 4)
     x, rows = call(
-        chain_kernel, [state, copies], med, o, e, hop(gap, 4), acc, columns, scratch=table
+        chain_kernel, [state, copies], med, o, e, gap, acc, columns, scratch=table
     )
     packed = call(project_kernel, PROJECTED, share(rows), ginv, columns, x, scratch=table)
     final, e, o, rows = call(

time: 173 us -> 171 us (0.988)
    ppermute x39, waiting for transfers between devices: 17.2 us -> 15.5 us  [moved(): return lax.ppermute(value, ('tm', 'space'), pairs)]
  transfers between devices with their start and end apart: 39 -> 39, of which waited for: 9 -> 8; matrix products, arithmetic and copies ran while one was open for 0% -> 0% of each run, Pallas kernels for 4% -> 4%
where the time goes in v6:
time: 171 us; the launch traced here: 169 us
  starting transfers between devices  70.2 us (41%)
  blocking collectives  65.6 us (38%)
  waiting for transfers between devices  15.5 us (9%)
  Pallas kernels  14.3 us (8%)
  local copies, waits for them, and re-layouts  2.91 us (2%)
    ppermute x39, starting transfers between devices, moved(): return lax.ppermute(value, ('tm', 'space'), pairs)  70.2 us
    all_to_all x5, blocking collectives, share(): return lax.all_to_all(copies, 'space', 0, 0, tiled=True)  65.6 us
    ppermute x39, waiting for transfers between devices, moved(): return lax.ppermute(value, ('tm', 'space'), pairs)  15.5 us
    pallas_call x17, Pallas kernels, call(): pl.pallas_call(kernel, out_shape=shapes, in_specs=[VMEM] * len(args), out...  14.3 us
  transfers between devices with their start and end apart: 39, of which 8 were waited for; matrix products, arithmetic and copies ran while one was open for 0% of the time, Pallas kernels for 4%

profile of v6, /device:TPU:1, one launch (start us, length us, event | category | flops | bytes accessed | tf_op | source)
XLA Modules:
  0.0 169.5 jit_solution(1456917822389881208)
XLA Ops:
  0.6 2.6 %collective-permute-start.1 = (f32[4,2,16,128]{3,2,1,0:T(8,128)}, f32[4,2,16,128]{3,2,1,0:T(8,128)S(1)}, u32[]{:S(2)}, u32[]{:S(2)}) collective-permute-start(f32[4,2,16,128]{3,2,1,0:T(8,128)} %param.5), channel_id=1, source_target_pairs={{0,16},{1,17},{2,18},{3,19},{4,20},{5,21},{6,22},{7,23},{8,24},{9,... | collective-permute-start | bytes 196616 | tf_op jit(solution)/shard_map/ppermute | solution.py:32
  3.2 1.2 collective-permute-start
  4.4 2.2 %copy-done = f32[1,64,4,2,16,128]{5,4,3,2,1,0:T(8,128)S(1)} copy-done((f32[1,64,4,2,16,128]{5,4,3,2,1,0:T(8,128)S(1)}, f32[1,64,4,2,16,128]{5,4,3,2,1,0:T(8,128)}, u32[]{:S(2)}) %copy-start) | copy-done | bytes 4194328
  6.6 0.7 copy-done.2
  7.4 0.5 collective-permute-done.g_ref
  7.9 1.5 collective-permute-start.2
  9.4 0.3 collective-permute-start.3
  9.7 2.3 %collective-permute-start.4 = (f32[8,16,128]{2,1,0:T(8,128)S(1)}, f32[8,16,128]{2,1,0:T(8,128)S(1)}, u32[]{:S(2)}, u32[]{:S(2)}) collective-permute-start(f32[8,16,128]{2,1,0:T(8,128)S(1)} %get-tuple-element.54), channel_id=1, source_target_pairs={{0,2},{1,3},{2,0},{3,1},{4,6},{5,7},{6,4},{7,5},{8,10},{9,11},{10,... | collective-permute-start | bytes 196616 | tf_op jit(solution)/shard_map/ppermute | solution.py:32
  12.0 0.6 collective-permute-start.5
  12.6 4.0 %collective-permute-done.4.e2 = f32[8,16,128]{2,1,0:T(8,128)S(1)} collective-permute-done((f32[8,16,128]{2,1,0:T(8,128)S(1)}, f32[8,16,128]{2,1,0:T(8,128)S(1)}, u32[]{:S(2)}, u32[]{:S(2)}) %collective-permute-start.4) | collective-permute-done | bytes 65568 | tf_op jit(solution)/shard_map/ppermute | solution.py:32
  16.6 0.3 shard_map.61
  17.0 1.4 collective-permute-start.10
  18.4 4.0 %collective-permute-start.8 = (f32[8,16,128]{2,1,0:T(8,128)S(1)}, f32[8,16,128]{2,1,0:T(8,128)S(1)}, u32[]{:S(2)}, u32[]{:S(2)}) collective-permute-start(f32[8,16,128]{2,1,0:T(8,128)S(1)} %get-tuple-element.56.relaxed), channel_id=1, source_target_pairs={{0,17},{1,16},{2,19},{3,18},{4,21},{5,20},{6,23},{7,22},{8,25},{9,... | collective-permute-start | bytes 196616 | tf_op jit(solution)/shard_map/ppermute | solution.py:32
  22.4 4.2 %collective-permute-start.6 = (f32[6,16,128]{2,1,0:T(8,128)S(1)}, f32[6,16,128]{2,1,0:T(8,128)S(1)}, u32[]{:S(2)}, u32[]{:S(2)}) collective-permute-start(f32[6,16,128]{2,1,0:T(8,128)S(1)} %get-tuple-element.59), channel_id=1, source_target_pairs={{0,18},{1,19},{2,16},{3,17},{4,22},{5,23},{6,20},{7,21},{8,26},{9,... | collective-permute-start | bytes 147464 | tf_op jit(solution)/shard_map/ppermute | solution.py:32
  26.6 1.6 collective-permute-start.7
  28.1 3.0 %shard_map.63.refs_0_ = f32[64,128]{1,0:T(8,128)S(1)} custom-call(f32[8192,128]{1,0:T(8,128)S(1)} %bitcast.5), custom_call_target="tpu_custom_call" | custom-call | flops 50000000 | bytes 100000 | tf_op jit(solution)/shard_map/pallas_call | solution.py:171
  31.1 3.0 %shard_map.64.gram = f32[64,128]{1,0:T(8,128)S(1)} custom-call(f32[8192,128]{1,0:T(8,128)S(1)} %bitcast.6, f32[64,128]{1,0:T(8,128)S(1)} %shard_map.63.refs_0_), custom_call_target="tpu_custom_call" | custom-call | flops 50000000 | bytes 100000 | tf_op jit(solution)/shard_map/pallas_call | solution.py:171
  34.2 0.3 shard_map.62
  34.5 0.4 shard_map.65
  35.0 16.2 %all_to_all.25.got = f32[16,40,128]{2,1,0:T(8,128)S(1)} all-to-all(f32[16,40,128]{2,1,0:T(8,128)S(1)} %shard_map.65), channel_id=1, replica_groups=mesh['tm'=8,'space'=16] {'space'}, dimensions={0} | all-to-all | bytes 655360 | tf_op jit(solution)/shard_map/all_to_all | solution.py:49
  51.1 1.9 %shard_map.66 = (f32[64,128]{1,0:T(8,128)S(1)}, f32[16,16,128]{2,1,0:T(8,128)S(1)}, f32[10,16,128]{2,1,0:T(8,128)S(1)}, f32[10,16,128]{2,1,0:T(8,128)S(1)}, f32[...) custom-call(f32[16,40,128]{2,1,0:T(8,128)S(1)} %all_to_all.25.got, f32[8192,128]{1,0:T(8,128)S(1)} %bitcast.8, ...), custom_call_target="tpu_custom_call" | custom-call | flops 1000000 | bytes 100000 | tf_op jit(solution)/shard_map/pallas_call | solution.py:171
  53.1 1.1 collective-permute-start.16
  54.2 0.1 collective-permute-start.14
  54.3 1.2 collective-permute-start.15
  55.5 2.5 %collective-permute-start.12 = (f32[6,16,128]{2,1,0:T(8,128)S(1)}, f32[6,16,128]{2,1,0:T(8,128)S(1)}, u32[]{:S(2)}, u32[]{:S(2)}) collective-permute-start(f32[6,16,128]{2,1,0:T(8,128)S(1)} %get-tuple-element.63), channel_id=1, source_target_pairs={{0,18},{1,19},{2,16},{3,17},{4,22},{5,23},{6,20},{7,21},{8,26},{9,... | collective-permute-start | bytes 147464 | tf_op jit(solution)/shard_map/ppermute | solution.py:32
  58.0 1.4 collective-permute-start.13
  59.4 1.3 collective-permute-done.12.e2
  60.7 0.7 shard_map.67
  61.5 12.8 %all_to_all.26.got = f32[16,1,128]{2,1,0:T(1,128)S(1)} all-to-all(f32[16,1,128]{2,1,0:T(1,128)S(1)} %get-tuple-element.68), channel_id=1, replica_groups=mesh['tm'=8,'space'=16] {'space'}, dimensions={0} | all-to-all | bytes 16384 | tf_op jit(solution)/shard_map/all_to_all | solution.py:49
  74.3 0.4 shard_map.68
  74.7 4.0 %collective-permute-start.21 = (f32[16,16,128]{2,1,0:T(8,128)S(1)}, f32[16,16,128]{2,1,0:T(8,128)S(1)}, u32[]{:S(2)}, u32[]{:S(2)}) collective-permute-start(f32[16,16,128]{2,1,0:T(8,128)S(1)} %get-tuple-element.75), channel_id=1, source_target_pairs={{0,16},{1,17},{2,18},{3,19},{4,20},{5,21},{6,22},{7,23},{8,24},{9,... | collective-permute-start | bytes 393224 | tf_op jit(solution)/shard_map/ppermute | solution.py:32
  78.8 1.6 collective-permute-start.20
  80.4 2.5 %collective-permute-start.17 = (f32[6,16,128]{2,1,0:T(8,128)S(1)}, f32[6,16,128]{2,1,0:T(8,128)S(1)}, u32[]{:S(2)}, u32[]{:S(2)}) collective-permute-start(f32[6,16,128]{2,1,0:T(8,128)S(1)} %get-tuple-element.71), channel_id=1, source_target_pairs={{0,18},{1,19},{2,16},{3,17},{4,22},{5,23},{6,20},{7,21},{8,26},{9,... | collective-permute-start | bytes 147464 | tf_op jit(solution)/shard_map/ppermute | solution.py:32
  82.9 1.1 collective-permute-start.18
  84.0 2.3 %collective-permute-done.17.e2 = f32[6,16,128]{2,1,0:T(8,128)S(1)} collective-permute-done((f32[6,16,128]{2,1,0:T(8,128)S(1)}, f32[6,16,128]{2,1,0:T(8,128)S(1)}, u32[]{:S(2)}, u32[]{:S(2)}) %collective-permute-start.17) | collective-permute-done | bytes 49184 | tf_op jit(solution)/shard_map/ppermute | solution.py:32
  86.3 0.7 shard_map.69
  87.1 12.5 %all_to_all.27.got = f32[16,1,128]{2,1,0:T(1,128)S(1)} all-to-all(f32[16,1,128]{2,1,0:T(1,128)S(1)} %get-tuple-element.77), channel_id=1, replica_groups=mesh['tm'=8,'space'=16] {'space'}, dimensions={0} | all-to-all | bytes 16384 | tf_op jit(solution)/shard_map/all_to_all | solution.py:49
  99.6 0.4 shard_map.70
  100.0 3.4 %collective-permute-start.26 = (f32[16,16,128]{2,1,0:T(8,128)S(1)}, f32[16,16,128]{2,1,0:T(8,128)S(1)}, u32[]{:S(2)}, u32[]{:S(2)}) collective-permute-start(f32[16,16,128]{2,1,0:T(8,128)S(1)} %get-tuple-element.83), channel_id=1, source_target_pairs={{0,16},{1,17},{2,18},{3,19},{4,20},{5,21},{6,22},{7,23},{8,24},{9,... | collective-permute-start | bytes 393224 | tf_op jit(solution)/shard_map/ppermute | solution.py:32
  103.5 2.3 %collective-permute-start.25 = (f32[10,16,128]{2,1,0:T(8,128)S(1)}, f32[10,16,128]{2,1,0:T(8,128)S(1)}, u32[]{:S(2)}, u32[]{:S(2)}) collective-permute-start(f32[10,16,128]{2,1,0:T(8,128)S(1)} %get-tuple-element.82), channel_id=1, source_target_pairs={{0,16},{1,18},{2,17},{3,20},{4,19},{5,22},{6,21},{7,24},{8,23},{9,... | collective-permute-start | bytes 245768 | tf_op jit(solution)/shard_map/ppermute | solution.py:32
  105.8 2.5 %collective-permute-start.22 = (f32[6,16,128]{2,1,0:T(8,128)S(1)}, f32[6,16,128]{2,1,0:T(8,128)S(1)}, u32[]{:S(2)}, u32[]{:S(2)}) collective-permute-start(f32[6,16,128]{2,1,0:T(8,128)S(1)} %get-tuple-element.79), channel_id=1, source_target_pairs={{0,18},{1,19},{2,16},{3,17},{4,22},{5,23},{6,20},{7,21},{8,26},{9,... | collective-permute-start | bytes 147464 | tf_op jit(solution)/shard_map/ppermute | solution.py:32
  108.3 0.5 collective-permute-start.23
  108.7 2.8 %collective-permute-done.22.e2 = f32[6,16,128]{2,1,0:T(8,128)S(1)} collective-permute-done((f32[6,16,128]{2,1,0:T(8,128)S(1)}, f32[6,16,128]{2,1,0:T(8,128)S(1)}, u32[]{:S(2)}, u32[]{:S(2)}) %collective-permute-start.22) | collective-permute-done | bytes 49184 | tf_op jit(solution)/shard_map/ppermute | solution.py:32
  111.6 1.6 collective-permute-start.11
  113.2 0.3 shard_map.71
  113.5 0.4 collective-permute-start.29
  113.9 2.6 %collective-permute-start.27 = (f32[6,16,128]{2,1,0:T(8,128)S(1)}, f32[6,16,128]{2,1,0:T(8,128)S(1)}, u32[]{:S(2)}, u32[]{:S(2)}) collective-permute-start(f32[6,16,128]{2,1,0:T(8,128)S(1)} %get-tuple-element.85), channel_id=1, source_target_pairs={{0,64},{1,66},{2,65},{3,68},{4,67},{5,70},{6,69},{7,72},{8,71},{9,... | collective-permute-start | bytes 147464 | tf_op jit(solution)/shard_map/ppermute | solution.py:32
  116.5 3.0 %collective-permute-start.28 = (f32[6,16,128]{2,1,0:T(8,128)S(1)}, f32[6,16,128]{2,1,0:T(8,128)S(1)}, u32[]{:S(2)}, u32[]{:S(2)}) collective-permute-start(f32[6,16,128]{2,1,0:T(8,128)S(1)} %get-tuple-element.86), channel_id=1, source_target_pairs={{0,65},{1,64},{2,67},{3,66},{4,69},{5,68},{6,71},{7,70},{8,73},{9,... | collective-permute-start | bytes 147464 | tf_op jit(solution)/shard_map/ppermute | solution.py:32
  119.6 2.3 %collective-permute-done.28.e1 = f32[6,16,128]{2,1,0:T(8,128)S(1)} collective-permute-done((f32[6,16,128]{2,1,0:T(8,128)S(1)}, f32[6,16,128]{2,1,0:T(8,128)S(1)}, u32[]{:S(2)}, u32[]{:S(2)}) %collective-permute-start.28) | collective-permute-done | bytes 49184 | tf_op jit(solution)/shard_map/ppermute | solution.py:32
  121.9 0.5 shard_map.72
  122.4 13.1 %all_to_all.28.got = f32[16,1,128]{2,1,0:T(1,128)S(1)} all-to-all(f32[16,1,128]{2,1,0:T(1,128)S(1)} %get-tuple-element.89), channel_id=1, replica_groups=mesh['tm'=8,'space'=16] {'space'}, dimensions={0} | all-to-all | bytes 16384 | tf_op jit(solution)/shard_map/all_to_all | solution.py:49
  135.5 0.4 shard_map.73
  135.9 0.4 collective-permute-start.32
  136.2 4.3 %collective-permute-start.33 = (f32[10,16,128]{2,1,0:T(8,128)S(1)}, f32[10,16,128]{2,1,0:T(8,128)S(1)}, u32[]{:S(2)}, u32[]{:S(2)}) collective-permute-start(f32[10,16,128]{2,1,0:T(8,128)S(1)} %get-tuple-element.94), channel_id=1, source_target_pairs={{0,16},{1,2},{2,1},{3,4},{4,3},{5,6},{6,5},{7,8},{8,7},{9,10},{10,... | collective-permute-start | bytes 245768 | tf_op jit(solution)/shard_map/ppermute | solution.py:32
  140.5 3.5 %collective-permute-start.31 = (f32[6,16,128]{2,1,0:T(8,128)S(1)}, f32[6,16,128]{2,1,0:T(8,128)S(1)}, u32[]{:S(2)}, u32[]{:S(2)}) collective-permute-start(f32[6,16,128]{2,1,0:T(8,128)S(1)} %get-tuple-element.92), channel_id=1, source_target_pairs={{0,16},{1,17},{2,4},{3,5},{4,2},{5,3},{6,8},{7,9},{8,6},{9,7},{10,... | collective-permute-start | bytes 147464 | tf_op jit(solution)/shard_map/ppermute | solution.py:32
  144.1 1.1 collective-permute-done.30.e2
  145.2 1.0 collective-permute-done.31.o2
  146.2 0.7 shard_map.74
  146.9 1.4 collective-permute-start.38
  148.3 0.4 collective-permute-start.37
  148.7 4.3 %collective-permute-start.36 = (f32[8,16,128]{2,1,0:T(8,128)S(1)}, f32[8,16,128]{2,1,0:T(8,128)S(1)}, u32[]{:S(2)}, u32[]{:S(2)}) collective-permute-start(f32[8,16,128]{2,1,0:T(8,128)S(1)} %get-tuple-element.96.final), channel_id=1, source_target_pairs={{0,17},{1,16},{2,19},{3,18},{4,21},{5,20},{6,23},{7,22},{8,25},{9,... | collective-permute-start | bytes 196616 | tf_op jit(solution)/shard_map/ppermute | solution.py:32
  153.0 4.2 %collective-permute-start.34 = (f32[2,16,128]{2,1,0:T(8,128)S(1)}, f32[2,16,128]{2,1,0:T(8,128)S(1)}, u32[]{:S(2)}, u32[]{:S(2)}) collective-permute-start(f32[2,16,128]{2,1,0:T(8,128)S(1)} %get-tuple-element.97), channel_id=1, source_target_pairs={{0,18},{1,19},{2,16},{3,17},{4,22},{5,23},{6,20},{7,21},{8,26},{9,... | collective-permute-start | bytes 49160 | tf_op jit(solution)/shard_map/ppermute | solution.py:32
  157.3 11.1 %all_to_all.29.got = f32[16,1,128]{2,1,0:T(1,128)S(1)} all-to-all(f32[16,1,128]{2,1,0:T(1,128)S(1)} %get-tuple-element.99), channel_id=1, replica_groups=mesh['tm'=8,'space'=16] {'space'}, dimensions={0} | all-to-all | bytes 16384 | tf_op jit(solution)/shard_map/all_to_all | solution.py:49
  168.4 0.9 shard_map.75
  (42 shorter events, 0.4 us)
Async XLA Ops:
  0.6 6.7 %collective-permute-start.1 = (f32[4,2,16,128]{3,2,1,0:T(8,128)}, f32[4,2,16,128]{3,2,1,0:T(8,128)S(1)}, u32[]{:S(2)}, u32[]{:S(2)}) collective-permute-start(f32[4,2,16,128]{3,2,1,0:T(8,128)} %param.5), channel_id=1, source_target_pairs={{0,16},{1,17},{2,18},{3,19},{4,20},{5,21},{6,22},{7,23},{8,24},{9,... | collective-permute-start | bytes 196616 | tf_op jit(solution)/shard_map/ppermute | solution.py:32
  3.2 4.6 %collective-permute-start = (f32[8,16,128]{2,1,0:T(8,128)}, f32[8,16,128]{2,1,0:T(8,128)S(1)}, u32[]{:S(2)}, u32[]{:S(2)}) collective-permute-start(f32[8,16,128]{2,1,0:T(8,128)} %bitcast.17), channel_id=1, source_target_pairs={{0,32},{1,33},{2,34},{3,35},{4,36},{5,37},{6,38},{7,39},{8,40},{9,... | collective-permute-start | bytes 196616 | tf_op jit(solution)/shard_map/ppermute | solution.py:32
  4.4 2.2 %copy-start = (f32[1,64,4,2,16,128]{5,4,3,2,1,0:T(8,128)S(1)}, f32[1,64,4,2,16,128]{5,4,3,2,1,0:T(8,128)}, u32[]{:S(2)}) copy-start(f32[1,64,4,2,16,128]{5,4,3,2,1,0:T(8,128)} %param.7) | copy-start | bytes 12582916
  6.6 0.7 copy-start.2
  7.3 20.8 %copy-start.1 = (f32[1,64,4,2,16,128]{5,4,3,2,1,0:T(8,128)S(1)}, f32[1,64,4,2,16,128]{5,4,3,2,1,0:T(8,128)}, u32[]{:S(2)}) copy-start(f32[1,64,4,2,16,128]{5,4,3,2,1,0:T(8,128)} %param.7) | copy-start | bytes 12582916
  7.9 8.8 %collective-permute-start.2 = (f32[15,16,128]{2,1,0:T(8,128)S(1)}, f32[15,16,128]{2,1,0:T(8,128)S(1)}, u32[]{:S(2)}, u32[]{:S(2)}) collective-permute-start(f32[15,16,128]{2,1,0:T(8,128)S(1)} %get-tuple-element.52), channel_id=1, source_target_pairs={{0,1},{1,0},{2,3},{3,2},{4,5},{5,4},{6,7},{7,6},{8,9},{9,8},{10,11... | collective-permute-start | bytes 368648 | tf_op jit(solution)/shard_map/ppermute | solution.py:32
  9.4 7.3 %collective-permute-start.3 = (f32[15,16,128]{2,1,0:T(8,128)S(1)}, f32[15,16,128]{2,1,0:T(8,128)S(1)}, u32[]{:S(2)}, u32[]{:S(2)}) collective-permute-start(f32[15,16,128]{2,1,0:T(8,128)S(1)} %get-tuple-element.53), channel_id=1, source_target_pairs={{0,16},{1,2},{2,1},{3,4},{4,3},{5,6},{6,5},{7,8},{8,7},{9,10},{10,... | collective-permute-start | bytes 368648 | tf_op jit(solution)/shard_map/ppermute | solution.py:32
  9.7 6.9 %collective-permute-start.4 = (f32[8,16,128]{2,1,0:T(8,128)S(1)}, f32[8,16,128]{2,1,0:T(8,128)S(1)}, u32[]{:S(2)}, u32[]{:S(2)}) collective-permute-start(f32[8,16,128]{2,1,0:T(8,128)S(1)} %get-tuple-element.54), channel_id=1, source_target_pairs={{0,2},{1,3},{2,0},{3,1},{4,6},{5,7},{6,4},{7,5},{8,10},{9,11},{10,... | collective-permute-start | bytes 196616 | tf_op jit(solution)/shard_map/ppermute | solution.py:32
  12.0 4.6 %collective-permute-start.5 = (f32[8,16,128]{2,1,0:T(8,128)S(1)}, f32[8,16,128]{2,1,0:T(8,128)S(1)}, u32[]{:S(2)}, u32[]{:S(2)}) collective-permute-start(f32[8,16,128]{2,1,0:T(8,128)S(1)} %get-tuple-element.55), channel_id=1, source_target_pairs={{0,16},{1,17},{2,4},{3,5},{4,2},{5,3},{6,8},{7,9},{8,6},{9,7},{10,... | collective-permute-start | bytes 196616 | tf_op jit(solution)/shard_map/ppermute | solution.py:32
  17.0 17.2 %collective-permute-start.10 = (f32[8,16,128]{2,1,0:T(8,128)S(1)}, f32[8,16,128]{2,1,0:T(8,128)S(1)}, u32[]{:S(2)}, u32[]{:S(2)}) collective-permute-start(f32[8,16,128]{2,1,0:T(8,128)S(1)} %get-tuple-element.56.relaxed), channel_id=1, source_target_pairs={{0,16},{1,17},{2,18},{3,19},{4,20},{5,21},{6,22},{7,23},{8,24},{9,... | collective-permute-start | bytes 196616 | tf_op jit(solution)/shard_map/ppermute | solution.py:32
  18.4 15.8 %collective-permute-start.9 = (f32[8,16,128]{2,1,0:T(8,128)S(1)}, f32[8,16,128]{2,1,0:T(8,128)S(1)}, u32[]{:S(2)}, u32[]{:S(2)}) collective-permute-start(f32[8,16,128]{2,1,0:T(8,128)S(1)} %get-tuple-element.56.relaxed), channel_id=1, source_target_pairs={{0,16},{1,18},{2,17},{3,20},{4,19},{5,22},{6,21},{7,24},{8,23},{9,... | collective-permute-start | bytes 196616 | tf_op jit(solution)/shard_map/ppermute | solution.py:32
  18.4 15.7 %collective-permute-start.8 = (f32[8,16,128]{2,1,0:T(8,128)S(1)}, f32[8,16,128]{2,1,0:T(8,128)S(1)}, u32[]{:S(2)}, u32[]{:S(2)}) collective-permute-start(f32[8,16,128]{2,1,0:T(8,128)S(1)} %get-tuple-element.56.relaxed), channel_id=1, source_target_pairs={{0,17},{1,16},{2,19},{3,18},{4,21},{5,20},{6,23},{7,22},{8,25},{9,... | collective-permute-start | bytes 196616 | tf_op jit(solution)/shard_map/ppermute | solution.py:32
  22.4 11.7 %collective-permute-start.6 = (f32[6,16,128]{2,1,0:T(8,128)S(1)}, f32[6,16,128]{2,1,0:T(8,128)S(1)}, u32[]{:S(2)}, u32[]{:S(2)}) collective-permute-start(f32[6,16,128]{2,1,0:T(8,128)S(1)} %get-tuple-element.59), channel_id=1, source_target_pairs={{0,18},{1,19},{2,16},{3,17},{4,22},{5,23},{6,20},{7,21},{8,26},{9,... | collective-permute-start | bytes 147464 | tf_op jit(solution)/shard_map/ppermute | solution.py:32
  26.6 7.6 %collective-permute-start.7 = (f32[6,16,128]{2,1,0:T(8,128)S(1)}, f32[6,16,128]{2,1,0:T(8,128)S(1)}, u32[]{:S(2)}, u32[]{:S(2)}) collective-permute-start(f32[6,16,128]{2,1,0:T(8,128)S(1)} %get-tuple-element.60), channel_id=1, source_target_pairs={{0,16},{1,17},{2,20},{3,21},{4,18},{5,19},{6,24},{7,25},{8,22},{9,... | collective-permute-start | bytes 147464 | tf_op jit(solution)/shard_map/ppermute | solution.py:32
  53.1 7.7 %collective-permute-start.16 = (f32[16,16,128]{2,1,0:T(8,128)S(1)}, f32[16,16,128]{2,1,0:T(8,128)S(1)}, u32[]{:S(2)}, u32[]{:S(2)}) collective-permute-start(f32[16,16,128]{2,1,0:T(8,128)S(1)} %get-tuple-element.67), channel_id=1, source_target_pairs={{0,16},{1,17},{2,18},{3,19},{4,20},{5,21},{6,22},{7,23},{8,24},{9,... | collective-permute-start | bytes 393224 | tf_op jit(solution)/shard_map/ppermute | solution.py:32
  54.2 6.6 %collective-permute-start.14 = (f32[10,16,128]{2,1,0:T(8,128)S(1)}, f32[10,16,128]{2,1,0:T(8,128)S(1)}, u32[]{:S(2)}, u32[]{:S(2)}) collective-permute-start(f32[10,16,128]{2,1,0:T(8,128)S(1)} %get-tuple-element.65), channel_id=1, source_target_pairs={{0,17},{1,16},{2,19},{3,18},{4,21},{5,20},{6,23},{7,22},{8,25},{9,... | collective-permute-start | bytes 245768 | tf_op jit(solution)/shard_map/ppermute | solution.py:32
  54.3 6.4 %collective-permute-start.15 = (f32[10,16,128]{2,1,0:T(8,128)S(1)}, f32[10,16,128]{2,1,0:T(8,128)S(1)}, u32[]{:S(2)}, u32[]{:S(2)}) collective-permute-start(f32[10,16,128]{2,1,0:T(8,128)S(1)} %get-tuple-element.66), channel_id=1, source_target_pairs={{0,16},{1,18},{2,17},{3,20},{4,19},{5,22},{6,21},{7,24},{8,23},{9,... | collective-permute-start | bytes 245768 | tf_op jit(solution)/shard_map/ppermute | solution.py:32
  55.5 5.2 %collective-permute-start.12 = (f32[6,16,128]{2,1,0:T(8,128)S(1)}, f32[6,16,128]{2,1,0:T(8,128)S(1)}, u32[]{:S(2)}, u32[]{:S(2)}) collective-permute-start(f32[6,16,128]{2,1,0:T(8,128)S(1)} %get-tuple-element.63), channel_id=1, source_target_pairs={{0,18},{1,19},{2,16},{3,17},{4,22},{5,23},{6,20},{7,21},{8,26},{9,... | collective-permute-start | bytes 147464 | tf_op jit(solution)/shard_map/ppermute | solution.py:32
  58.0 2.8 %collective-permute-start.13 = (f32[6,16,128]{2,1,0:T(8,128)S(1)}, f32[6,16,128]{2,1,0:T(8,128)S(1)}, u32[]{:S(2)}, u32[]{:S(2)}) collective-permute-start(f32[6,16,128]{2,1,0:T(8,128)S(1)} %get-tuple-element.64), channel_id=1, source_target_pairs={{0,16},{1,17},{2,20},{3,21},{4,18},{5,19},{6,24},{7,25},{8,22},{9,... | collective-permute-start | bytes 147464 | tf_op jit(solution)/shard_map/ppermute | solution.py:32
  74.7 11.6 %collective-permute-start.21 = (f32[16,16,128]{2,1,0:T(8,128)S(1)}, f32[16,16,128]{2,1,0:T(8,128)S(1)}, u32[]{:S(2)}, u32[]{:S(2)}) collective-permute-start(f32[16,16,128]{2,1,0:T(8,128)S(1)} %get-tuple-element.75), channel_id=1, source_target_pairs={{0,16},{1,17},{2,18},{3,19},{4,20},{5,21},{6,22},{7,23},{8,24},{9,... | collective-permute-start | bytes 393224 | tf_op jit(solution)/shard_map/ppermute | solution.py:32
  78.7 7.6 %collective-permute-start.19 = (f32[10,16,128]{2,1,0:T(8,128)S(1)}, f32[10,16,128]{2,1,0:T(8,128)S(1)}, u32[]{:S(2)}, u32[]{:S(2)}) collective-permute-start(f32[10,16,128]{2,1,0:T(8,128)S(1)} %get-tuple-element.73), channel_id=1, source_target_pairs={{0,17},{1,16},{2,19},{3,18},{4,21},{5,20},{6,23},{7,22},{8,25},{9,... | collective-permute-start | bytes 245768 | tf_op jit(solution)/shard_map/ppermute | solution.py:32
  78.8 7.5 %collective-permute-start.20 = (f32[10,16,128]{2,1,0:T(8,128)S(1)}, f32[10,16,128]{2,1,0:T(8,128)S(1)}, u32[]{:S(2)}, u32[]{:S(2)}) collective-permute-start(f32[10,16,128]{2,1,0:T(8,128)S(1)} %get-tuple-element.74), channel_id=1, source_target_pairs={{0,16},{1,18},{2,17},{3,20},{4,19},{5,22},{6,21},{7,24},{8,23},{9,... | collective-permute-start | bytes 245768 | tf_op jit(solution)/shard_map/ppermute | solution.py:32
  80.4 5.9 %collective-permute-start.17 = (f32[6,16,128]{2,1,0:T(8,128)S(1)}, f32[6,16,128]{2,1,0:T(8,128)S(1)}, u32[]{:S(2)}, u32[]{:S(2)}) collective-permute-start(f32[6,16,128]{2,1,0:T(8,128)S(1)} %get-tuple-element.71), channel_id=1, source_target_pairs={{0,18},{1,19},{2,16},{3,17},{4,22},{5,23},{6,20},{7,21},{8,26},{9,... | collective-permute-start | bytes 147464 | tf_op jit(solution)/shard_map/ppermute | solution.py:32
  82.9 3.4 %collective-permute-start.18 = (f32[6,16,128]{2,1,0:T(8,128)S(1)}, f32[6,16,128]{2,1,0:T(8,128)S(1)}, u32[]{:S(2)}, u32[]{:S(2)}) collective-permute-start(f32[6,16,128]{2,1,0:T(8,128)S(1)} %get-tuple-element.72), channel_id=1, source_target_pairs={{0,16},{1,17},{2,20},{3,21},{4,18},{5,19},{6,24},{7,25},{8,22},{9,... | collective-permute-start | bytes 147464 | tf_op jit(solution)/shard_map/ppermute | solution.py:32
  100.0 13.2 %collective-permute-start.26 = (f32[16,16,128]{2,1,0:T(8,128)S(1)}, f32[16,16,128]{2,1,0:T(8,128)S(1)}, u32[]{:S(2)}, u32[]{:S(2)}) collective-permute-start(f32[16,16,128]{2,1,0:T(8,128)S(1)} %get-tuple-element.83), channel_id=1, source_target_pairs={{0,16},{1,17},{2,18},{3,19},{4,20},{5,21},{6,22},{7,23},{8,24},{9,... | collective-permute-start | bytes 393224 | tf_op jit(solution)/shard_map/ppermute | solution.py:32
  103.4 9.7 %collective-permute-start.24 = (f32[10,16,128]{2,1,0:T(8,128)S(1)}, f32[10,16,128]{2,1,0:T(8,128)S(1)}, u32[]{:S(2)}, u32[]{:S(2)}) collective-permute-start(f32[10,16,128]{2,1,0:T(8,128)S(1)} %get-tuple-element.81), channel_id=1, source_target_pairs={{0,17},{1,16},{2,19},{3,18},{4,21},{5,20},{6,23},{7,22},{8,25},{9,... | collective-permute-start | bytes 245768 | tf_op jit(solution)/shard_map/ppermute | solution.py:32
  103.5 9.6 %collective-permute-start.25 = (f32[10,16,128]{2,1,0:T(8,128)S(1)}, f32[10,16,128]{2,1,0:T(8,128)S(1)}, u32[]{:S(2)}, u32[]{:S(2)}) collective-permute-start(f32[10,16,128]{2,1,0:T(8,128)S(1)} %get-tuple-element.82), channel_id=1, source_target_pairs={{0,16},{1,18},{2,17},{3,20},{4,19},{5,22},{6,21},{7,24},{8,23},{9,... | collective-permute-start | bytes 245768 | tf_op jit(solution)/shard_map/ppermute | solution.py:32
  105.8 5.8 %collective-permute-start.22 = (f32[6,16,128]{2,1,0:T(8,128)S(1)}, f32[6,16,128]{2,1,0:T(8,128)S(1)}, u32[]{:S(2)}, u32[]{:S(2)}) collective-permute-start(f32[6,16,128]{2,1,0:T(8,128)S(1)} %get-tuple-element.79), channel_id=1, source_target_pairs={{0,18},{1,19},{2,16},{3,17},{4,22},{5,23},{6,20},{7,21},{8,26},{9,... | collective-permute-start | bytes 147464 | tf_op jit(solution)/shard_map/ppermute | solution.py:32
  108.3 4.8 %collective-permute-start.23 = (f32[6,16,128]{2,1,0:T(8,128)S(1)}, f32[6,16,128]{2,1,0:T(8,128)S(1)}, u32[]{:S(2)}, u32[]{:S(2)}) collective-permute-start(f32[6,16,128]{2,1,0:T(8,128)S(1)} %get-tuple-element.80), channel_id=1, source_target_pairs={{0,16},{1,17},{2,20},{3,21},{4,18},{5,19},{6,24},{7,25},{8,22},{9,... | collective-permute-start | bytes 147464 | tf_op jit(solution)/shard_map/ppermute | solution.py:32
  111.6 32.5 %collective-permute-start.11 = (f32[20,16,128]{2,1,0:T(8,128)S(1)}, f32[20,16,128]{2,1,0:T(8,128)S(1)}, u32[]{:S(2)}, u32[]{:S(2)}) collective-permute-start(f32[20,16,128]{2,1,0:T(8,128)S(1)} %get-tuple-element.61), channel_id=1, source_target_pairs={{0,112},{1,113},{2,114},{3,115},{4,116},{5,117},{6,118},{7,119},{8... | collective-permute-start | bytes 491528 | tf_op jit(solution)/shard_map/ppermute | solution.py:32
  113.5 8.4 %collective-permute-start.29 = (f32[8,16,128]{2,1,0:T(8,128)S(1)}, f32[8,16,128]{2,1,0:T(8,128)S(1)}, u32[]{:S(2)}, u32[]{:S(2)}) collective-permute-start(f32[8,16,128]{2,1,0:T(8,128)S(1)} %get-tuple-element.87), channel_id=1, source_target_pairs={{0,64},{1,65},{2,66},{3,67},{4,68},{5,69},{6,70},{7,71},{8,72},{9,... | collective-permute-start | bytes 196616 | tf_op jit(solution)/shard_map/ppermute | solution.py:32
  113.9 5.7 %collective-permute-start.27 = (f32[6,16,128]{2,1,0:T(8,128)S(1)}, f32[6,16,128]{2,1,0:T(8,128)S(1)}, u32[]{:S(2)}, u32[]{:S(2)}) collective-permute-start(f32[6,16,128]{2,1,0:T(8,128)S(1)} %get-tuple-element.85), channel_id=1, source_target_pairs={{0,64},{1,66},{2,65},{3,68},{4,67},{5,70},{6,69},{7,72},{8,71},{9,... | collective-permute-start | bytes 147464 | tf_op jit(solution)/shard_map/ppermute | solution.py:32
  116.5 5.3 %collective-permute-start.28 = (f32[6,16,128]{2,1,0:T(8,128)S(1)}, f32[6,16,128]{2,1,0:T(8,128)S(1)}, u32[]{:S(2)}, u32[]{:S(2)}) collective-permute-start(f32[6,16,128]{2,1,0:T(8,128)S(1)} %get-tuple-element.86), channel_id=1, source_target_pairs={{0,65},{1,64},{2,67},{3,66},{4,69},{5,68},{6,71},{7,70},{8,73},{9,... | collective-permute-start | bytes 147464 | tf_op jit(solution)/shard_map/ppermute | solution.py:32
  135.9 10.3 %collective-permute-start.32 = (f32[10,16,128]{2,1,0:T(8,128)S(1)}, f32[10,16,128]{2,1,0:T(8,128)S(1)}, u32[]{:S(2)}, u32[]{:S(2)}) collective-permute-start(f32[10,16,128]{2,1,0:T(8,128)S(1)} %get-tuple-element.93), channel_id=1, source_target_pairs={{0,1},{1,0},{2,3},{3,2},{4,5},{5,4},{6,7},{7,6},{8,9},{9,8},{10,11... | collective-permute-start | bytes 245768 | tf_op jit(solution)/shard_map/ppermute | solution.py:32
  136.2 9.9 %collective-permute-start.33 = (f32[10,16,128]{2,1,0:T(8,128)S(1)}, f32[10,16,128]{2,1,0:T(8,128)S(1)}, u32[]{:S(2)}, u32[]{:S(2)}) collective-permute-start(f32[10,16,128]{2,1,0:T(8,128)S(1)} %get-tuple-element.94), channel_id=1, source_target_pairs={{0,16},{1,2},{2,1},{3,4},{4,3},{5,6},{6,5},{7,8},{8,7},{9,10},{10,... | collective-permute-start | bytes 245768 | tf_op jit(solution)/shard_map/ppermute | solution.py:32
  140.5 4.6 %collective-permute-start.30 = (f32[6,16,128]{2,1,0:T(8,128)S(1)}, f32[6,16,128]{2,1,0:T(8,128)S(1)}, u32[]{:S(2)}, u32[]{:S(2)}) collective-permute-start(f32[6,16,128]{2,1,0:T(8,128)S(1)} %get-tuple-element.91), channel_id=1, source_target_pairs={{0,2},{1,3},{2,0},{3,1},{4,6},{5,7},{6,4},{7,5},{8,10},{9,11},{10,... | collective-permute-start | bytes 147464 | tf_op jit(solution)/shard_map/ppermute | solution.py:32
  140.5 5.6 %collective-permute-start.31 = (f32[6,16,128]{2,1,0:T(8,128)S(1)}, f32[6,16,128]{2,1,0:T(8,128)S(1)}, u32[]{:S(2)}, u32[]{:S(2)}) collective-permute-start(f32[6,16,128]{2,1,0:T(8,128)S(1)} %get-tuple-element.92), channel_id=1, source_target_pairs={{0,16},{1,17},{2,4},{3,5},{4,2},{5,3},{6,8},{7,9},{8,6},{9,7},{10,... | collective-permute-start | bytes 147464 | tf_op jit(solution)/shard_map/ppermute | solution.py:32
  146.9 21.5 %collective-permute-start.38 = (f32[8,16,128]{2,1,0:T(8,128)S(1)}, f32[8,16,128]{2,1,0:T(8,128)S(1)}, u32[]{:S(2)}, u32[]{:S(2)}) collective-permute-start(f32[8,16,128]{2,1,0:T(8,128)S(1)} %get-tuple-element.96.final), channel_id=1, source_target_pairs={{0,16},{1,17},{2,18},{3,19},{4,20},{5,21},{6,22},{7,23},{8,24},{9,... | collective-permute-start | bytes 196616 | tf_op jit(solution)/shard_map/ppermute | solution.py:32
  148.3 20.1 %collective-permute-start.37 = (f32[8,16,128]{2,1,0:T(8,128)S(1)}, f32[8,16,128]{2,1,0:T(8,128)S(1)}, u32[]{:S(2)}, u32[]{:S(2)}) collective-permute-start(f32[8,16,128]{2,1,0:T(8,128)S(1)} %get-tuple-element.96.final), channel_id=1, source_target_pairs={{0,16},{1,18},{2,17},{3,20},{4,19},{5,22},{6,21},{7,24},{8,23},{9,... | collective-permute-start | bytes 196616 | tf_op jit(solution)/shard_map/ppermute | solution.py:32
  148.7 19.7 %collective-permute-start.36 = (f32[8,16,128]{2,1,0:T(8,128)S(1)}, f32[8,16,128]{2,1,0:T(8,128)S(1)}, u32[]{:S(2)}, u32[]{:S(2)}) collective-permute-start(f32[8,16,128]{2,1,0:T(8,128)S(1)} %get-tuple-element.96.final), channel_id=1, source_target_pairs={{0,17},{1,16},{2,19},{3,18},{4,21},{5,20},{6,23},{7,22},{8,25},{9,... | collective-permute-start | bytes 196616 | tf_op jit(solution)/shard_map/ppermute | solution.py:32
  153.0 15.3 %collective-permute-start.34 = (f32[2,16,128]{2,1,0:T(8,128)S(1)}, f32[2,16,128]{2,1,0:T(8,128)S(1)}, u32[]{:S(2)}, u32[]{:S(2)}) collective-permute-start(f32[2,16,128]{2,1,0:T(8,128)S(1)} %get-tuple-element.97), channel_id=1, source_target_pairs={{0,18},{1,19},{2,16},{3,17},{4,22},{5,23},{6,20},{7,21},{8,26},{9,... | collective-permute-start | bytes 49160 | tf_op jit(solution)/shard_map/ppermute | solution.py:32
  157.3 11.1 %collective-permute-start.35 = (f32[2,16,128]{2,1,0:T(8,128)S(1)}, f32[2,16,128]{2,1,0:T(8,128)S(1)}, u32[]{:S(2)}, u32[]{:S(2)}) collective-permute-start(f32[2,16,128]{2,1,0:T(8,128)S(1)} %get-tuple-element.98), channel_id=1, source_target_pairs={{0,16},{1,17},{2,20},{3,21},{4,18},{5,19},{6,24},{7,25},{8,22},{9,... | collective-permute-start | bytes 49160 | tf_op jit(solution)/shard_map/ppermute | solution.py:32

commit v7 on v6

--- a/solution.py
+++ b/solution.py
@@ -417,12 +417,15 @@
     put_copies(row_out, inner_products(basis, x, scratch))
 
 
-def final_kernel(med, e2, o2, e1, o1, center, back, basis, out, e_out, o_out, row_out, scratch):
+def products_kernel(basis, u_ref, row_out, scratch):
+    put_copies(row_out, inner_products(basis, u_ref[...], scratch))
+
+
+def final_kernel(med, e2, o2, e1, o1, center, back, out, e_out, o_out):
     u = q_of(med, e2, o2, e1, o1, center) + back[0:8]
     out[...] = u
     up2 = ways()[1]
     put_both((e_out, o_out), up2, 0, [], [u[1:2], u[7:8]], [u[0:1], u[6:7]])
-    put_copies(row_out, inner_products(basis, u, scratch))
 
 
 def sweep_kernel(back, med, final, e2, o2, e1, o1, own, got, ginv, out, coords, kept, kept_row, sems):
@@ -523,17 +526,16 @@
         chain_kernel, [state, copies], med, o, e, gap, acc, columns, scratch=table
     )
     packed = call(project_kernel, PROJECTED, share(rows), ginv, columns, x, scratch=table)
-    final, e, o, rows = call(
+    final, e, o = call(
         final_kernel,
-        [state, (2, NX, NY), (2, NX, NY), copies],
+        [state, (2, NX, NY), (2, NX, NY)],
         med,
         *exchanged(packed, 0),
         back,
-        columns,
-        scratch=table,
-    )
+    )
+    near = traded((final, final), (e, o), final, 1)
+    (rows,) = call(products_kernel, [copies], columns, final, scratch=table)
     got = share(rows)
-    near = traded((final, final), (e, o), final, 1)
     states, coords = call(
         sweep_kernel,
         [(4, 8, NX, NY), (1, NY)],

time: 171 us -> 171 us (level)
    pallas_call x17 -> x18, Pallas kernels: 14.3 us -> 14.3 us  [call(): pl.pallas_call(kernel, out_shape=shapes, in_specs=[VMEM] * len(args), out...]
  transfers between devices with their start and end apart: 39 -> 39, of which waited for: 8 -> 8; matrix products, arithmetic and copies ran while one was open for 0% -> 0% of each run, Pallas kernels for 4% -> 5%
where the time goes in v7:
time: 171 us; the launch traced here: 170 us
  starting transfers between devices  70.3 us (41%)
  blocking collectives  65.6 us (38%)
  waiting for transfers between devices  15.5 us (9%)
  Pallas kernels  14.3 us (8%)
  local copies, waits for them, and re-layouts  2.91 us (2%)
    ppermute x39, starting transfers between devices, moved(): return lax.ppermute(value, ('tm', 'space'), pairs)  70.3 us
    all_to_all x5, blocking collectives, share(): return lax.all_to_all(copies, 'space', 0, 0, tiled=True)  65.6 us
    ppermute x39, waiting for transfers between devices, moved(): return lax.ppermute(value, ('tm', 'space'), pairs)  15.5 us
    pallas_call x18, Pallas kernels, call(): pl.pallas_call(kernel, out_shape=shapes, in_specs=[VMEM] * len(args), out...  14.3 us
  transfers between devices with their start and end apart: 39, of which 8 were waited for; matrix products, arithmetic and copies ran while one was open for 0% of the time, Pallas kernels for 5%

profile of v7, /device:TPU:1, one launch (start us, length us, event | category | flops | bytes accessed | tf_op | source)
XLA Modules:
  0.0 169.6 jit_solution(16546425930957352811)
XLA Ops:
  0.6 2.6 %collective-permute-start.1 = (f32[4,2,16,128]{3,2,1,0:T(8,128)}, f32[4,2,16,128]{3,2,1,0:T(8,128)S(1)}, u32[]{:S(2)}, u32[]{:S(2)}) collective-permute-start(f32[4,2,16,128]{3,2,1,0:T(8,128)} %param.5), channel_id=1, source_target_pairs={{0,16},{1,17},{2,18},{3,19},{4,20},{5,21},{6,22},{7,23},{8,24},{9,... | collective-permute-start | bytes 196616 | tf_op jit(solution)/shard_map/ppermute | solution.py:32
  3.2 1.2 collective-permute-start
  4.4 2.2 %copy-done = f32[1,64,4,2,16,128]{5,4,3,2,1,0:T(8,128)S(1)} copy-done((f32[1,64,4,2,16,128]{5,4,3,2,1,0:T(8,128)S(1)}, f32[1,64,4,2,16,128]{5,4,3,2,1,0:T(8,128)}, u32[]{:S(2)}) %copy-start) | copy-done | bytes 4194328
  6.6 0.7 copy-done.2
  7.4 0.5 collective-permute-done.g_ref
  7.9 1.5 collective-permute-start.2
  9.4 0.3 collective-permute-start.3
  9.7 2.3 %collective-permute-start.4 = (f32[8,16,128]{2,1,0:T(8,128)S(1)}, f32[8,16,128]{2,1,0:T(8,128)S(1)}, u32[]{:S(2)}, u32[]{:S(2)}) collective-permute-start(f32[8,16,128]{2,1,0:T(8,128)S(1)} %get-tuple-element.53), channel_id=1, source_target_pairs={{0,2},{1,3},{2,0},{3,1},{4,6},{5,7},{6,4},{7,5},{8,10},{9,11},{10,... | collective-permute-start | bytes 196616 | tf_op jit(solution)/shard_map/ppermute | solution.py:32
  12.0 0.6 collective-permute-start.5
  12.6 4.0 %collective-permute-done.4.e2 = f32[8,16,128]{2,1,0:T(8,128)S(1)} collective-permute-done((f32[8,16,128]{2,1,0:T(8,128)S(1)}, f32[8,16,128]{2,1,0:T(8,128)S(1)}, u32[]{:S(2)}, u32[]{:S(2)}) %collective-permute-start.4) | collective-permute-done | bytes 65568 | tf_op jit(solution)/shard_map/ppermute | solution.py:32
  16.6 0.3 shard_map.61
  17.0 1.4 collective-permute-start.10
  18.4 4.0 %collective-permute-start.8 = (f32[8,16,128]{2,1,0:T(8,128)S(1)}, f32[8,16,128]{2,1,0:T(8,128)S(1)}, u32[]{:S(2)}, u32[]{:S(2)}) collective-permute-start(f32[8,16,128]{2,1,0:T(8,128)S(1)} %get-tuple-element.55.relaxed), channel_id=1, source_target_pairs={{0,17},{1,16},{2,19},{3,18},{4,21},{5,20},{6,23},{7,22},{8,25},{9,... | collective-permute-start | bytes 196616 | tf_op jit(solution)/shard_map/ppermute | solution.py:32
  22.4 4.2 %collective-permute-start.6 = (f32[6,16,128]{2,1,0:T(8,128)S(1)}, f32[6,16,128]{2,1,0:T(8,128)S(1)}, u32[]{:S(2)}, u32[]{:S(2)}) collective-permute-start(f32[6,16,128]{2,1,0:T(8,128)S(1)} %get-tuple-element.58), channel_id=1, source_target_pairs={{0,18},{1,19},{2,16},{3,17},{4,22},{5,23},{6,20},{7,21},{8,26},{9,... | collective-permute-start | bytes 147464 | tf_op jit(solution)/shard_map/ppermute | solution.py:32
  26.6 1.6 collective-permute-start.7
  28.1 3.0 %shard_map.63.refs_0_ = f32[64,128]{1,0:T(8,128)S(1)} custom-call(f32[8192,128]{1,0:T(8,128)S(1)} %bitcast.5), custom_call_target="tpu_custom_call" | custom-call | flops 50000000 | bytes 100000 | tf_op jit(solution)/shard_map/pallas_call | solution.py:171
  31.1 3.0 %shard_map.64.gram = f32[64,128]{1,0:T(8,128)S(1)} custom-call(f32[8192,128]{1,0:T(8,128)S(1)} %bitcast.6, f32[64,128]{1,0:T(8,128)S(1)} %shard_map.63.refs_0_), custom_call_target="tpu_custom_call" | custom-call | flops 50000000 | bytes 100000 | tf_op jit(solution)/shard_map/pallas_call | solution.py:171
  34.2 0.3 shard_map.62
  34.5 0.4 shard_map.65
  35.0 16.2 %all_to_all.25.got = f32[16,40,128]{2,1,0:T(8,128)S(1)} all-to-all(f32[16,40,128]{2,1,0:T(8,128)S(1)} %shard_map.65), channel_id=1, replica_groups=mesh['tm'=8,'space'=16] {'space'}, dimensions={0} | all-to-all | bytes 655360 | tf_op jit(solution)/shard_map/all_to_all | solution.py:49
  51.1 1.9 %shard_map.66 = (f32[64,128]{1,0:T(8,128)S(1)}, f32[16,16,128]{2,1,0:T(8,128)S(1)}, f32[10,16,128]{2,1,0:T(8,128)S(1)}, f32[10,16,128]{2,1,0:T(8,128)S(1)}, f32[...) custom-call(f32[16,40,128]{2,1,0:T(8,128)S(1)} %all_to_all.25.got, f32[8192,128]{1,0:T(8,128)S(1)} %bitcast.8, ...), custom_call_target="tpu_custom_call" | custom-call | flops 1000000 | bytes 100000 | tf_op jit(solution)/shard_map/pallas_call | solution.py:171
  53.1 1.1 collective-permute-start.16
  54.3 1.2 collective-permute-start.15
  55.5 2.5 %collective-permute-start.12 = (f32[6,16,128]{2,1,0:T(8,128)S(1)}, f32[6,16,128]{2,1,0:T(8,128)S(1)}, u32[]{:S(2)}, u32[]{:S(2)}) collective-permute-start(f32[6,16,128]{2,1,0:T(8,128)S(1)} %get-tuple-element.62), channel_id=1, source_target_pairs={{0,18},{1,19},{2,16},{3,17},{4,22},{5,23},{6,20},{7,21},{8,26},{9,... | collective-permute-start | bytes 147464 | tf_op jit(solution)/shard_map/ppermute | solution.py:32
  58.0 1.4 collective-permute-start.13
  59.4 1.3 collective-permute-done.12.e2
  60.7 0.7 shard_map.67
  61.5 12.8 %all_to_all.26.got = f32[16,1,128]{2,1,0:T(1,128)S(1)} all-to-all(f32[16,1,128]{2,1,0:T(1,128)S(1)} %get-tuple-element.67), channel_id=1, replica_groups=mesh['tm'=8,'space'=16] {'space'}, dimensions={0} | all-to-all | bytes 16384 | tf_op jit(solution)/shard_map/all_to_all | solution.py:49
  74.3 0.4 shard_map.68
  74.7 4.0 %collective-permute-start.21 = (f32[16,16,128]{2,1,0:T(8,128)S(1)}, f32[16,16,128]{2,1,0:T(8,128)S(1)}, u32[]{:S(2)}, u32[]{:S(2)}) collective-permute-start(f32[16,16,128]{2,1,0:T(8,128)S(1)} %get-tuple-element.74), channel_id=1, source_target_pairs={{0,16},{1,17},{2,18},{3,19},{4,20},{5,21},{6,22},{7,23},{8,24},{9,... | collective-permute-start | bytes 393224 | tf_op jit(solution)/shard_map/ppermute | solution.py:32
  78.8 1.6 collective-permute-start.20
  80.4 2.5 %collective-permute-start.17 = (f32[6,16,128]{2,1,0:T(8,128)S(1)}, f32[6,16,128]{2,1,0:T(8,128)S(1)}, u32[]{:S(2)}, u32[]{:S(2)}) collective-permute-start(f32[6,16,128]{2,1,0:T(8,128)S(1)} %get-tuple-element.70), channel_id=1, source_target_pairs={{0,18},{1,19},{2,16},{3,17},{4,22},{5,23},{6,20},{7,21},{8,26},{9,... | collective-permute-start | bytes 147464 | tf_op jit(solution)/shard_map/ppermute | solution.py:32
  82.9 1.1 collective-permute-start.18
  84.0 2.3 %collective-permute-done.17.e2 = f32[6,16,128]{2,1,0:T(8,128)S(1)} collective-permute-done((f32[6,16,128]{2,1,0:T(8,128)S(1)}, f32[6,16,128]{2,1,0:T(8,128)S(1)}, u32[]{:S(2)}, u32[]{:S(2)}) %collective-permute-start.17) | collective-permute-done | bytes 49184 | tf_op jit(solution)/shard_map/ppermute | solution.py:32
  86.3 0.7 shard_map.69
  87.1 12.5 %all_to_all.27.got = f32[16,1,128]{2,1,0:T(1,128)S(1)} all-to-all(f32[16,1,128]{2,1,0:T(1,128)S(1)} %get-tuple-element.76), channel_id=1, replica_groups=mesh['tm'=8,'space'=16] {'space'}, dimensions={0} | all-to-all | bytes 16384 | tf_op jit(solution)/shard_map/all_to_all | solution.py:49
  99.6 0.4 shard_map.70
  100.0 3.4 %collective-permute-start.26 = (f32[16,16,128]{2,1,0:T(8,128)S(1)}, f32[16,16,128]{2,1,0:T(8,128)S(1)}, u32[]{:S(2)}, u32[]{:S(2)}) collective-permute-start(f32[16,16,128]{2,1,0:T(8,128)S(1)} %get-tuple-element.82), channel_id=1, source_target_pairs={{0,16},{1,17},{2,18},{3,19},{4,20},{5,21},{6,22},{7,23},{8,24},{9,... | collective-permute-start | bytes 393224 | tf_op jit(solution)/shard_map/ppermute | solution.py:32
  103.5 2.3 %collective-permute-start.25 = (f32[10,16,128]{2,1,0:T(8,128)S(1)}, f32[10,16,128]{2,1,0:T(8,128)S(1)}, u32[]{:S(2)}, u32[]{:S(2)}) collective-permute-start(f32[10,16,128]{2,1,0:T(8,128)S(1)} %get-tuple-element.81), channel_id=1, source_target_pairs={{0,16},{1,18},{2,17},{3,20},{4,19},{5,22},{6,21},{7,24},{8,23},{9,... | collective-permute-start | bytes 245768 | tf_op jit(solution)/shard_map/ppermute | solution.py:32
  105.8 2.5 %collective-permute-start.22 = (f32[6,16,128]{2,1,0:T(8,128)S(1)}, f32[6,16,128]{2,1,0:T(8,128)S(1)}, u32[]{:S(2)}, u32[]{:S(2)}) collective-permute-start(f32[6,16,128]{2,1,0:T(8,128)S(1)} %get-tuple-element.78), channel_id=1, source_target_pairs={{0,18},{1,19},{2,16},{3,17},{4,22},{5,23},{6,20},{7,21},{8,26},{9,... | collective-permute-start | bytes 147464 | tf_op jit(solution)/shard_map/ppermute | solution.py:32
  108.3 0.5 collective-permute-start.23
  108.7 2.8 %collective-permute-done.22.e2 = f32[6,16,128]{2,1,0:T(8,128)S(1)} collective-permute-done((f32[6,16,128]{2,1,0:T(8,128)S(1)}, f32[6,16,128]{2,1,0:T(8,128)S(1)}, u32[]{:S(2)}, u32[]{:S(2)}) %collective-permute-start.22) | collective-permute-done | bytes 49184 | tf_op jit(solution)/shard_map/ppermute | solution.py:32
  111.6 1.6 collective-permute-start.11
  113.2 0.3 shard_map.71
  113.5 0.4 collective-permute-start.29
  113.9 2.6 %collective-permute-start.27 = (f32[6,16,128]{2,1,0:T(8,128)S(1)}, f32[6,16,128]{2,1,0:T(8,128)S(1)}, u32[]{:S(2)}, u32[]{:S(2)}) collective-permute-start(f32[6,16,128]{2,1,0:T(8,128)S(1)} %get-tuple-element.84), channel_id=1, source_target_pairs={{0,64},{1,66},{2,65},{3,68},{4,67},{5,70},{6,69},{7,72},{8,71},{9,... | collective-permute-start | bytes 147464 | tf_op jit(solution)/shard_map/ppermute | solution.py:32
  116.5 3.0 %collective-permute-start.28 = (f32[6,16,128]{2,1,0:T(8,128)S(1)}, f32[6,16,128]{2,1,0:T(8,128)S(1)}, u32[]{:S(2)}, u32[]{:S(2)}) collective-permute-start(f32[6,16,128]{2,1,0:T(8,128)S(1)} %get-tuple-element.85), channel_id=1, source_target_pairs={{0,65},{1,64},{2,67},{3,66},{4,69},{5,68},{6,71},{7,70},{8,73},{9,... | collective-permute-start | bytes 147464 | tf_op jit(solution)/shard_map/ppermute | solution.py:32
  119.6 2.3 %collective-permute-done.28.e1 = f32[6,16,128]{2,1,0:T(8,128)S(1)} collective-permute-done((f32[6,16,128]{2,1,0:T(8,128)S(1)}, f32[6,16,128]{2,1,0:T(8,128)S(1)}, u32[]{:S(2)}, u32[]{:S(2)}) %collective-permute-start.28) | collective-permute-done | bytes 49184 | tf_op jit(solution)/shard_map/ppermute | solution.py:32
  121.9 0.5 shard_map.72
  122.4 13.1 %all_to_all.28.got = f32[16,1,128]{2,1,0:T(1,128)S(1)} all-to-all(f32[16,1,128]{2,1,0:T(1,128)S(1)} %get-tuple-element.88), channel_id=1, replica_groups=mesh['tm'=8,'space'=16] {'space'}, dimensions={0} | all-to-all | bytes 16384 | tf_op jit(solution)/shard_map/all_to_all | solution.py:49
  135.5 0.4 shard_map.73
  135.9 0.4 collective-permute-start.32
  136.2 4.3 %collective-permute-start.33 = (f32[10,16,128]{2,1,0:T(8,128)S(1)}, f32[10,16,128]{2,1,0:T(8,128)S(1)}, u32[]{:S(2)}, u32[]{:S(2)}) collective-permute-start(f32[10,16,128]{2,1,0:T(8,128)S(1)} %get-tuple-element.93), channel_id=1, source_target_pairs={{0,16},{1,2},{2,1},{3,4},{4,3},{5,6},{6,5},{7,8},{8,7},{9,10},{10,... | collective-permute-start | bytes 245768 | tf_op jit(solution)/shard_map/ppermute | solution.py:32
  140.5 3.5 %collective-permute-start.31 = (f32[6,16,128]{2,1,0:T(8,128)S(1)}, f32[6,16,128]{2,1,0:T(8,128)S(1)}, u32[]{:S(2)}, u32[]{:S(2)}) collective-permute-start(f32[6,16,128]{2,1,0:T(8,128)S(1)} %get-tuple-element.91), channel_id=1, source_target_pairs={{0,16},{1,17},{2,4},{3,5},{4,2},{5,3},{6,8},{7,9},{8,6},{9,7},{10,... | collective-permute-start | bytes 147464 | tf_op jit(solution)/shard_map/ppermute | solution.py:32
  144.1 1.1 collective-permute-done.30.e2
  145.2 1.0 collective-permute-done.31.o2
  146.2 0.3 shard_map.74
  146.5 1.4 collective-permute-start.38
  147.9 0.4 collective-permute-start.37
  148.3 4.3 %collective-permute-start.36 = (f32[8,16,128]{2,1,0:T(8,128)S(1)}, f32[8,16,128]{2,1,0:T(8,128)S(1)}, u32[]{:S(2)}, u32[]{:S(2)}) collective-permute-start(f32[8,16,128]{2,1,0:T(8,128)S(1)} %get-tuple-element.95.u_ref.final), channel_id=1, source_target_pairs={{0,17},{1,16},{2,19},{3,18},{4,21},{5,20},{6,23},{7,22},{8,25},{9,... | collective-permute-start | bytes 196616 | tf_op jit(solution)/shard_map/ppermute | solution.py:32
  152.7 4.3 %collective-permute-start.34 = (f32[2,16,128]{2,1,0:T(8,128)S(1)}, f32[2,16,128]{2,1,0:T(8,128)S(1)}, u32[]{:S(2)}, u32[]{:S(2)}) collective-permute-start(f32[2,16,128]{2,1,0:T(8,128)S(1)} %get-tuple-element.96), channel_id=1, source_target_pairs={{0,18},{1,19},{2,16},{3,17},{4,22},{5,23},{6,20},{7,21},{8,26},{9,... | collective-permute-start | bytes 49160 | tf_op jit(solution)/shard_map/ppermute | solution.py:32
  156.9 0.4 shard_map.75
  157.4 11.1 %all_to_all.29.got = f32[16,1,128]{2,1,0:T(1,128)S(1)} all-to-all(f32[16,1,128]{2,1,0:T(1,128)S(1)} %shard_map.75), channel_id=1, replica_groups=mesh['tm'=8,'space'=16] {'space'}, dimensions={0} | all-to-all | bytes 16384 | tf_op jit(solution)/shard_map/all_to_all | solution.py:49
  168.5 0.9 shard_map.76
  (43 shorter events, 0.5 us)
Async XLA Ops:
  0.6 6.7 %collective-permute-start.1 = (f32[4,2,16,128]{3,2,1,0:T(8,128)}, f32[4,2,16,128]{3,2,1,0:T(8,128)S(1)}, u32[]{:S(2)}, u32[]{:S(2)}) collective-permute-start(f32[4,2,16,128]{3,2,1,0:T(8,128)} %param.5), channel_id=1, source_target_pairs={{0,16},{1,17},{2,18},{3,19},{4,20},{5,21},{6,22},{7,23},{8,24},{9,... | collective-permute-start | bytes 196616 | tf_op jit(solution)/shard_map/ppermute | solution.py:32
  3.2 4.6 %collective-permute-start = (f32[8,16,128]{2,1,0:T(8,128)}, f32[8,16,128]{2,1,0:T(8,128)S(1)}, u32[]{:S(2)}, u32[]{:S(2)}) collective-permute-start(f32[8,16,128]{2,1,0:T(8,128)} %bitcast.17), channel_id=1, source_target_pairs={{0,32},{1,33},{2,34},{3,35},{4,36},{5,37},{6,38},{7,39},{8,40},{9,... | collective-permute-start | bytes 196616 | tf_op jit(solution)/shard_map/ppermute | solution.py:32
  4.4 2.2 %copy-start = (f32[1,64,4,2,16,128]{5,4,3,2,1,0:T(8,128)S(1)}, f32[1,64,4,2,16,128]{5,4,3,2,1,0:T(8,128)}, u32[]{:S(2)}) copy-start(f32[1,64,4,2,16,128]{5,4,3,2,1,0:T(8,128)} %param.7) | copy-start | bytes 12582916
  6.6 0.7 copy-start.2
  7.3 20.8 %copy-start.1 = (f32[1,64,4,2,16,128]{5,4,3,2,1,0:T(8,128)S(1)}, f32[1,64,4,2,16,128]{5,4,3,2,1,0:T(8,128)}, u32[]{:S(2)}) copy-start(f32[1,64,4,2,16,128]{5,4,3,2,1,0:T(8,128)} %param.7) | copy-start | bytes 12582916
  7.9 8.8 %collective-permute-start.2 = (f32[15,16,128]{2,1,0:T(8,128)S(1)}, f32[15,16,128]{2,1,0:T(8,128)S(1)}, u32[]{:S(2)}, u32[]{:S(2)}) collective-permute-start(f32[15,16,128]{2,1,0:T(8,128)S(1)} %get-tuple-element.51), channel_id=1, source_target_pairs={{0,1},{1,0},{2,3},{3,2},{4,5},{5,4},{6,7},{7,6},{8,9},{9,8},{10,11... | collective-permute-start | bytes 368648 | tf_op jit(solution)/shard_map/ppermute | solution.py:32
  9.4 7.3 %collective-permute-start.3 = (f32[15,16,128]{2,1,0:T(8,128)S(1)}, f32[15,16,128]{2,1,0:T(8,128)S(1)}, u32[]{:S(2)}, u32[]{:S(2)}) collective-permute-start(f32[15,16,128]{2,1,0:T(8,128)S(1)} %get-tuple-element.52), channel_id=1, source_target_pairs={{0,16},{1,2},{2,1},{3,4},{4,3},{5,6},{6,5},{7,8},{8,7},{9,10},{10,... | collective-permute-start | bytes 368648 | tf_op jit(solution)/shard_map/ppermute | solution.py:32
  9.7 6.9 %collective-permute-start.4 = (f32[8,16,128]{2,1,0:T(8,128)S(1)}, f32[8,16,128]{2,1,0:T(8,128)S(1)}, u32[]{:S(2)}, u32[]{:S(2)}) collective-permute-start(f32[8,16,128]{2,1,0:T(8,128)S(1)} %get-tuple-element.53), channel_id=1, source_target_pairs={{0,2},{1,3},{2,0},{3,1},{4,6},{5,7},{6,4},{7,5},{8,10},{9,11},{10,... | collective-permute-start | bytes 196616 | tf_op jit(solution)/shard_map/ppermute | solution.py:32
  12.0 4.6 %collective-permute-start.5 = (f32[8,16,128]{2,1,0:T(8,128)S(1)}, f32[8,16,128]{2,1,0:T(8,128)S(1)}, u32[]{:S(2)}, u32[]{:S(2)}) collective-permute-start(f32[8,16,128]{2,1,0:T(8,128)S(1)} %get-tuple-element.54), channel_id=1, source_target_pairs={{0,16},{1,17},{2,4},{3,5},{4,2},{5,3},{6,8},{7,9},{8,6},{9,7},{10,... | collective-permute-start | bytes 196616 | tf_op jit(solution)/shard_map/ppermute | solution.py:32
  17.0 17.2 %collective-permute-start.10 = (f32[8,16,128]{2,1,0:T(8,128)S(1)}, f32[8,16,128]{2,1,0:T(8,128)S(1)}, u32[]{:S(2)}, u32[]{:S(2)}) collective-permute-start(f32[8,16,128]{2,1,0:T(8,128)S(1)} %get-tuple-element.55.relaxed), channel_id=1, source_target_pairs={{0,16},{1,17},{2,18},{3,19},{4,20},{5,21},{6,22},{7,23},{8,24},{9,... | collective-permute-start | bytes 196616 | tf_op jit(solution)/shard_map/ppermute | solution.py:32
  18.4 15.8 %collective-permute-start.9 = (f32[8,16,128]{2,1,0:T(8,128)S(1)}, f32[8,16,128]{2,1,0:T(8,128)S(1)}, u32[]{:S(2)}, u32[]{:S(2)}) collective-permute-start(f32[8,16,128]{2,1,0:T(8,128)S(1)} %get-tuple-element.55.relaxed), channel_id=1, source_target_pairs={{0,16},{1,18},{2,17},{3,20},{4,19},{5,22},{6,21},{7,24},{8,23},{9,... | collective-permute-start | bytes 196616 | tf_op jit(solution)/shard_map/ppermute | solution.py:32
  18.4 15.7 %collective-permute-start.8 = (f32[8,16,128]{2,1,0:T(8,128)S(1)}, f32[8,16,128]{2,1,0:T(8,128)S(1)}, u32[]{:S(2)}, u32[]{:S(2)}) collective-permute-start(f32[8,16,128]{2,1,0:T(8,128)S(1)} %get-tuple-element.55.relaxed), channel_id=1, source_target_pairs={{0,17},{1,16},{2,19},{3,18},{4,21},{5,20},{6,23},{7,22},{8,25},{9,... | collective-permute-start | bytes 196616 | tf_op jit(solution)/shard_map/ppermute | solution.py:32
  22.4 11.7 %collective-permute-start.6 = (f32[6,16,128]{2,1,0:T(8,128)S(1)}, f32[6,16,128]{2,1,0:T(8,128)S(1)}, u32[]{:S(2)}, u32[]{:S(2)}) collective-permute-start(f32[6,16,128]{2,1,0:T(8,128)S(1)} %get-tuple-element.58), channel_id=1, source_target_pairs={{0,18},{1,19},{2,16},{3,17},{4,22},{5,23},{6,20},{7,21},{8,26},{9,... | collective-permute-start | bytes 147464 | tf_op jit(solution)/shard_map/ppermute | solution.py:32
  26.6 7.6 %collective-permute-start.7 = (f32[6,16,128]{2,1,0:T(8,128)S(1)}, f32[6,16,128]{2,1,0:T(8,128)S(1)}, u32[]{:S(2)}, u32[]{:S(2)}) collective-permute-start(f32[6,16,128]{2,1,0:T(8,128)S(1)} %get-tuple-element.59), channel_id=1, source_target_pairs={{0,16},{1,17},{2,20},{3,21},{4,18},{5,19},{6,24},{7,25},{8,22},{9,... | collective-permute-start | bytes 147464 | tf_op jit(solution)/shard_map/ppermute | solution.py:32
  53.1 7.7 %collective-permute-start.16 = (f32[16,16,128]{2,1,0:T(8,128)S(1)}, f32[16,16,128]{2,1,0:T(8,128)S(1)}, u32[]{:S(2)}, u32[]{:S(2)}) collective-permute-start(f32[16,16,128]{2,1,0:T(8,128)S(1)} %get-tuple-element.66), channel_id=1, source_target_pairs={{0,16},{1,17},{2,18},{3,19},{4,20},{5,21},{6,22},{7,23},{8,24},{9,... | collective-permute-start | bytes 393224 | tf_op jit(solution)/shard_map/ppermute | solution.py:32
  54.2 6.6 %collective-permute-start.14 = (f32[10,16,128]{2,1,0:T(8,128)S(1)}, f32[10,16,128]{2,1,0:T(8,128)S(1)}, u32[]{:S(2)}, u32[]{:S(2)}) collective-permute-start(f32[10,16,128]{2,1,0:T(8,128)S(1)} %get-tuple-element.64), channel_id=1, source_target_pairs={{0,17},{1,16},{2,19},{3,18},{4,21},{5,20},{6,23},{7,22},{8,25},{9,... | collective-permute-start | bytes 245768 | tf_op jit(solution)/shard_map/ppermute | solution.py:32
  54.3 6.4 %collective-permute-start.15 = (f32[10,16,128]{2,1,0:T(8,128)S(1)}, f32[10,16,128]{2,1,0:T(8,128)S(1)}, u32[]{:S(2)}, u32[]{:S(2)}) collective-permute-start(f32[10,16,128]{2,1,0:T(8,128)S(1)} %get-tuple-element.65), channel_id=1, source_target_pairs={{0,16},{1,18},{2,17},{3,20},{4,19},{5,22},{6,21},{7,24},{8,23},{9,... | collective-permute-start | bytes 245768 | tf_op jit(solution)/shard_map/ppermute | solution.py:32
  55.5 5.2 %collective-permute-start.12 = (f32[6,16,128]{2,1,0:T(8,128)S(1)}, f32[6,16,128]{2,1,0:T(8,128)S(1)}, u32[]{:S(2)}, u32[]{:S(2)}) collective-permute-start(f32[6,16,128]{2,1,0:T(8,128)S(1)} %get-tuple-element.62), channel_id=1, source_target_pairs={{0,18},{1,19},{2,16},{3,17},{4,22},{5,23},{6,20},{7,21},{8,26},{9,... | collective-permute-start | bytes 147464 | tf_op jit(solution)/shard_map/ppermute | solution.py:32
  58.0 2.8 %collective-permute-start.13 = (f32[6,16,128]{2,1,0:T(8,128)S(1)}, f32[6,16,128]{2,1,0:T(8,128)S(1)}, u32[]{:S(2)}, u32[]{:S(2)}) collective-permute-start(f32[6,16,128]{2,1,0:T(8,128)S(1)} %get-tuple-element.63), channel_id=1, source_target_pairs={{0,16},{1,17},{2,20},{3,21},{4,18},{5,19},{6,24},{7,25},{8,22},{9,... | collective-permute-start | bytes 147464 | tf_op jit(solution)/shard_map/ppermute | solution.py:32
  74.7 11.6 %collective-permute-start.21 = (f32[16,16,128]{2,1,0:T(8,128)S(1)}, f32[16,16,128]{2,1,0:T(8,128)S(1)}, u32[]{:S(2)}, u32[]{:S(2)}) collective-permute-start(f32[16,16,128]{2,1,0:T(8,128)S(1)} %get-tuple-element.74), channel_id=1, source_target_pairs={{0,16},{1,17},{2,18},{3,19},{4,20},{5,21},{6,22},{7,23},{8,24},{9,... | collective-permute-start | bytes 393224 | tf_op jit(solution)/shard_map/ppermute | solution.py:32
  78.7 7.6 %collective-permute-start.19 = (f32[10,16,128]{2,1,0:T(8,128)S(1)}, f32[10,16,128]{2,1,0:T(8,128)S(1)}, u32[]{:S(2)}, u32[]{:S(2)}) collective-permute-start(f32[10,16,128]{2,1,0:T(8,128)S(1)} %get-tuple-element.72), channel_id=1, source_target_pairs={{0,17},{1,16},{2,19},{3,18},{4,21},{5,20},{6,23},{7,22},{8,25},{9,... | collective-permute-start | bytes 245768 | tf_op jit(solution)/shard_map/ppermute | solution.py:32
  78.8 7.5 %collective-permute-start.20 = (f32[10,16,128]{2,1,0:T(8,128)S(1)}, f32[10,16,128]{2,1,0:T(8,128)S(1)}, u32[]{:S(2)}, u32[]{:S(2)}) collective-permute-start(f32[10,16,128]{2,1,0:T(8,128)S(1)} %get-tuple-element.73), channel_id=1, source_target_pairs={{0,16},{1,18},{2,17},{3,20},{4,19},{5,22},{6,21},{7,24},{8,23},{9,... | collective-permute-start | bytes 245768 | tf_op jit(solution)/shard_map/ppermute | solution.py:32
  80.4 5.9 %collective-permute-start.17 = (f32[6,16,128]{2,1,0:T(8,128)S(1)}, f32[6,16,128]{2,1,0:T(8,128)S(1)}, u32[]{:S(2)}, u32[]{:S(2)}) collective-permute-start(f32[6,16,128]{2,1,0:T(8,128)S(1)} %get-tuple-element.70), channel_id=1, source_target_pairs={{0,18},{1,19},{2,16},{3,17},{4,22},{5,23},{6,20},{7,21},{8,26},{9,... | collective-permute-start | bytes 147464 | tf_op jit(solution)/shard_map/ppermute | solution.py:32
  82.9 3.4 %collective-permute-start.18 = (f32[6,16,128]{2,1,0:T(8,128)S(1)}, f32[6,16,128]{2,1,0:T(8,128)S(1)}, u32[]{:S(2)}, u32[]{:S(2)}) collective-permute-start(f32[6,16,128]{2,1,0:T(8,128)S(1)} %get-tuple-element.71), channel_id=1, source_target_pairs={{0,16},{1,17},{2,20},{3,21},{4,18},{5,19},{6,24},{7,25},{8,22},{9,... | collective-permute-start | bytes 147464 | tf_op jit(solution)/shard_map/ppermute | solution.py:32
  100.0 13.2 %collective-permute-start.26 = (f32[16,16,128]{2,1,0:T(8,128)S(1)}, f32[16,16,128]{2,1,0:T(8,128)S(1)}, u32[]{:S(2)}, u32[]{:S(2)}) collective-permute-start(f32[16,16,128]{2,1,0:T(8,128)S(1)} %get-tuple-element.82), channel_id=1, source_target_pairs={{0,16},{1,17},{2,18},{3,19},{4,20},{5,21},{6,22},{7,23},{8,24},{9,... | collective-permute-start | bytes 393224 | tf_op jit(solution)/shard_map/ppermute | solution.py:32
  103.4 9.7 %collective-permute-start.24 = (f32[10,16,128]{2,1,0:T(8,128)S(1)}, f32[10,16,128]{2,1,0:T(8,128)S(1)}, u32[]{:S(2)}, u32[]{:S(2)}) collective-permute-start(f32[10,16,128]{2,1,0:T(8,128)S(1)} %get-tuple-element.80), channel_id=1, source_target_pairs={{0,17},{1,16},{2,19},{3,18},{4,21},{5,20},{6,23},{7,22},{8,25},{9,... | collective-permute-start | bytes 245768 | tf_op jit(solution)/shard_map/ppermute | solution.py:32
  103.5 9.6 %collective-permute-start.25 = (f32[10,16,128]{2,1,0:T(8,128)S(1)}, f32[10,16,128]{2,1,0:T(8,128)S(1)}, u32[]{:S(2)}, u32[]{:S(2)}) collective-permute-start(f32[10,16,128]{2,1,0:T(8,128)S(1)} %get-tuple-element.81), channel_id=1, source_target_pairs={{0,16},{1,18},{2,17},{3,20},{4,19},{5,22},{6,21},{7,24},{8,23},{9,... | collective-permute-start | bytes 245768 | tf_op jit(solution)/shard_map/ppermute | solution.py:32
  105.8 5.8 %collective-permute-start.22 = (f32[6,16,128]{2,1,0:T(8,128)S(1)}, f32[6,16,128]{2,1,0:T(8,128)S(1)}, u32[]{:S(2)}, u32[]{:S(2)}) collective-permute-start(f32[6,16,128]{2,1,0:T(8,128)S(1)} %get-tuple-element.78), channel_id=1, source_target_pairs={{0,18},{1,19},{2,16},{3,17},{4,22},{5,23},{6,20},{7,21},{8,26},{9,... | collective-permute-start | bytes 147464 | tf_op jit(solution)/shard_map/ppermute | solution.py:32
  108.3 4.8 %collective-permute-start.23 = (f32[6,16,128]{2,1,0:T(8,128)S(1)}, f32[6,16,128]{2,1,0:T(8,128)S(1)}, u32[]{:S(2)}, u32[]{:S(2)}) collective-permute-start(f32[6,16,128]{2,1,0:T(8,128)S(1)} %get-tuple-element.79), channel_id=1, source_target_pairs={{0,16},{1,17},{2,20},{3,21},{4,18},{5,19},{6,24},{7,25},{8,22},{9,... | collective-permute-start | bytes 147464 | tf_op jit(solution)/shard_map/ppermute | solution.py:32
  111.6 32.5 %collective-permute-start.11 = (f32[20,16,128]{2,1,0:T(8,128)S(1)}, f32[20,16,128]{2,1,0:T(8,128)S(1)}, u32[]{:S(2)}, u32[]{:S(2)}) collective-permute-start(f32[20,16,128]{2,1,0:T(8,128)S(1)} %get-tuple-element.60), channel_id=1, source_target_pairs={{0,112},{1,113},{2,114},{3,115},{4,116},{5,117},{6,118},{7,119},{8... | collective-permute-start | bytes 491528 | tf_op jit(solution)/shard_map/ppermute | solution.py:32
  113.5 8.4 %collective-permute-start.29 = (f32[8,16,128]{2,1,0:T(8,128)S(1)}, f32[8,16,128]{2,1,0:T(8,128)S(1)}, u32[]{:S(2)}, u32[]{:S(2)}) collective-permute-start(f32[8,16,128]{2,1,0:T(8,128)S(1)} %get-tuple-element.86), channel_id=1, source_target_pairs={{0,64},{1,65},{2,66},{3,67},{4,68},{5,69},{6,70},{7,71},{8,72},{9,... | collective-permute-start | bytes 196616 | tf_op jit(solution)/shard_map/ppermute | solution.py:32
  113.9 5.7 %collective-permute-start.27 = (f32[6,16,128]{2,1,0:T(8,128)S(1)}, f32[6,16,128]{2,1,0:T(8,128)S(1)}, u32[]{:S(2)}, u32[]{:S(2)}) collective-permute-start(f32[6,16,128]{2,1,0:T(8,128)S(1)} %get-tuple-element.84), channel_id=1, source_target_pairs={{0,64},{1,66},{2,65},{3,68},{4,67},{5,70},{6,69},{7,72},{8,71},{9,... | collective-permute-start | bytes 147464 | tf_op jit(solution)/shard_map/ppermute | solution.py:32
  116.5 5.3 %collective-permute-start.28 = (f32[6,16,128]{2,1,0:T(8,128)S(1)}, f32[6,16,128]{2,1,0:T(8,128)S(1)}, u32[]{:S(2)}, u32[]{:S(2)}) collective-permute-start(f32[6,16,128]{2,1,0:T(8,128)S(1)} %get-tuple-element.85), channel_id=1, source_target_pairs={{0,65},{1,64},{2,67},{3,66},{4,69},{5,68},{6,71},{7,70},{8,73},{9,... | collective-permute-start | bytes 147464 | tf_op jit(solution)/shard_map/ppermute | solution.py:32
  135.9 10.3 %collective-permute-start.32 = (f32[10,16,128]{2,1,0:T(8,128)S(1)}, f32[10,16,128]{2,1,0:T(8,128)S(1)}, u32[]{:S(2)}, u32[]{:S(2)}) collective-permute-start(f32[10,16,128]{2,1,0:T(8,128)S(1)} %get-tuple-element.92), channel_id=1, source_target_pairs={{0,1},{1,0},{2,3},{3,2},{4,5},{5,4},{6,7},{7,6},{8,9},{9,8},{10,11... | collective-permute-start | bytes 245768 | tf_op jit(solution)/shard_map/ppermute | solution.py:32
  136.2 9.9 %collective-permute-start.33 = (f32[10,16,128]{2,1,0:T(8,128)S(1)}, f32[10,16,128]{2,1,0:T(8,128)S(1)}, u32[]{:S(2)}, u32[]{:S(2)}) collective-permute-start(f32[10,16,128]{2,1,0:T(8,128)S(1)} %get-tuple-element.93), channel_id=1, source_target_pairs={{0,16},{1,2},{2,1},{3,4},{4,3},{5,6},{6,5},{7,8},{8,7},{9,10},{10,... | collective-permute-start | bytes 245768 | tf_op jit(solution)/shard_map/ppermute | solution.py:32
  140.5 4.6 %collective-permute-start.30 = (f32[6,16,128]{2,1,0:T(8,128)S(1)}, f32[6,16,128]{2,1,0:T(8,128)S(1)}, u32[]{:S(2)}, u32[]{:S(2)}) collective-permute-start(f32[6,16,128]{2,1,0:T(8,128)S(1)} %get-tuple-element.90), channel_id=1, source_target_pairs={{0,2},{1,3},{2,0},{3,1},{4,6},{5,7},{6,4},{7,5},{8,10},{9,11},{10,... | collective-permute-start | bytes 147464 | tf_op jit(solution)/shard_map/ppermute | solution.py:32
  140.5 5.6 %collective-permute-start.31 = (f32[6,16,128]{2,1,0:T(8,128)S(1)}, f32[6,16,128]{2,1,0:T(8,128)S(1)}, u32[]{:S(2)}, u32[]{:S(2)}) collective-permute-start(f32[6,16,128]{2,1,0:T(8,128)S(1)} %get-tuple-element.91), channel_id=1, source_target_pairs={{0,16},{1,17},{2,4},{3,5},{4,2},{5,3},{6,8},{7,9},{8,6},{9,7},{10,... | collective-permute-start | bytes 147464 | tf_op jit(solution)/shard_map/ppermute | solution.py:32
  146.5 21.9 %collective-permute-start.38 = (f32[8,16,128]{2,1,0:T(8,128)S(1)}, f32[8,16,128]{2,1,0:T(8,128)S(1)}, u32[]{:S(2)}, u32[]{:S(2)}) collective-permute-start(f32[8,16,128]{2,1,0:T(8,128)S(1)} %get-tuple-element.95.u_ref.final), channel_id=1, source_target_pairs={{0,16},{1,17},{2,18},{3,19},{4,20},{5,21},{6,22},{7,23},{8,24},{9,... | collective-permute-start | bytes 196616 | tf_op jit(solution)/shard_map/ppermute | solution.py:32
  147.9 20.5 %collective-permute-start.37 = (f32[8,16,128]{2,1,0:T(8,128)S(1)}, f32[8,16,128]{2,1,0:T(8,128)S(1)}, u32[]{:S(2)}, u32[]{:S(2)}) collective-permute-start(f32[8,16,128]{2,1,0:T(8,128)S(1)} %get-tuple-element.95.u_ref.final), channel_id=1, source_target_pairs={{0,16},{1,18},{2,17},{3,20},{4,19},{5,22},{6,21},{7,24},{8,23},{9,... | collective-permute-start | bytes 196616 | tf_op jit(solution)/shard_map/ppermute | solution.py:32
  148.3 20.1 %collective-permute-start.36 = (f32[8,16,128]{2,1,0:T(8,128)S(1)}, f32[8,16,128]{2,1,0:T(8,128)S(1)}, u32[]{:S(2)}, u32[]{:S(2)}) collective-permute-start(f32[8,16,128]{2,1,0:T(8,128)S(1)} %get-tuple-element.95.u_ref.final), channel_id=1, source_target_pairs={{0,17},{1,16},{2,19},{3,18},{4,21},{5,20},{6,23},{7,22},{8,25},{9,... | collective-permute-start | bytes 196616 | tf_op jit(solution)/shard_map/ppermute | solution.py:32
  152.7 15.8 %collective-permute-start.34 = (f32[2,16,128]{2,1,0:T(8,128)S(1)}, f32[2,16,128]{2,1,0:T(8,128)S(1)}, u32[]{:S(2)}, u32[]{:S(2)}) collective-permute-start(f32[2,16,128]{2,1,0:T(8,128)S(1)} %get-tuple-element.96), channel_id=1, source_target_pairs={{0,18},{1,19},{2,16},{3,17},{4,22},{5,23},{6,20},{7,21},{8,26},{9,... | collective-permute-start | bytes 49160 | tf_op jit(solution)/shard_map/ppermute | solution.py:32
  156.9 11.5 %collective-permute-start.35 = (f32[2,16,128]{2,1,0:T(8,128)S(1)}, f32[2,16,128]{2,1,0:T(8,128)S(1)}, u32[]{:S(2)}, u32[]{:S(2)}) collective-permute-start(f32[2,16,128]{2,1,0:T(8,128)S(1)} %get-tuple-element.97), channel_id=1, source_target_pairs={{0,16},{1,17},{2,20},{3,21},{4,18},{5,19},{6,24},{7,25},{8,22},{9,... | collective-permute-start | bytes 49160 | tf_op jit(solution)/shard_map/ppermute | solution.py:32
